TPU v7x, 128 devices: a whole 4x4x4 slice. The times are simulated.
128 devices in a mesh: grp: 16 (over z_hi, y, core), loc: 8 (over z_lo, x).
Axes of the slice: x: 4, y: 4, z: 4 (z_hi: 2, z_lo: 2; z = z_hi * 2 + z_lo), core: 2. Of those that a mesh axis runs over, the one named last changes fastest.
Arguments:
- tokens: bfloat16 [16384, 7168], P(('grp', 'loc')), may hold values from -6 to 6
- route: int32 [16384, 1], P(('grp', 'loc')), may hold values from 0 to 31; in each aligned block of 128 rows (0 to 127, 128 to 255, ...) at most 5 rows name the same one
- gate_prob: float32 [16384, 1], P(('grp', 'loc')), may hold values from 0.25 to 1
- w_gate: bfloat16 [128, 7168, 256], P(('grp', 'loc')), may hold values from -0.0625 to 0.0625
- w_up: bfloat16 [128, 7168, 256], P(('grp', 'loc')), may hold values from -0.0625 to 0.0625
- w_down: bfloat16 [128, 256, 7168], P(('grp', 'loc')), may hold values from -0.1875 to 0.1875
- partner: int32 [128, 2], replicated, may hold values from 0 to 127, as said below
Outputs:
- mixed: bfloat16 [16384, 7168], P(('grp', 'loc'))
Inputs may be any that keep to these rules, and one draw needn't show every extreme that they name: `route`: within the 128 rows of one device no expert is named more than 5 times, a bound that some block reaches. partner[i, h] is slot i itself, slot i - 1 or slot i + 1, cyclically over all slots.
All inputs are finite; a program needn't handle non-finite values.
Results may differ from a plain program's by a relative error of at most 0.0056.
Values may be sent and summed in bfloat16 or wider, within the bound.
No kernel may reach another device: no remote copies, remote signals or barrier semaphores. Data moves between devices by JAX's collectives and lax.ppermute only.
A program may use at most 192 MiB of HBM per device.

v0:
```python
import jax
import jax.numpy as jnp
from jax import lax
from jax.sharding import PartitionSpec as P

SPAN = 4


def shifted(block, axis, distance):
    devices = range(lax.axis_size(axis))
    route = [((i - distance) % len(devices), i) for i in devices]
    return lax.ppermute(block, axis, route)


def in_blocks(shard, dim, count):
    before, after = (shard.shape[:dim], shard.shape[dim + 1 :])
    return jnp.moveaxis(shard.reshape(*before, count, -1, *after), dim, 0)


def cut_rows(length, count):
    unit = 8 if length >= 8 * count else 1
    return [length // unit * k // count * unit for k in range(1, count)]


def joined_along(blocks, dim):
    shape = list(blocks.shape[1:])
    shape[dim] *= blocks.shape[0]
    return jnp.moveaxis(blocks, 0, dim).reshape(shape)


def several_exchanges(shard, axis, pieces, split_dim, concat_dim):
    blocks = in_blocks(shard, split_dim, lax.axis_size(axis))
    cut = max(range(1, max(2, blocks.ndim - 1)), key=lambda d: blocks.shape[d])
    done = []
    for piece in jnp.split(blocks, cut_rows(blocks.shape[cut], pieces), axis=cut):
        if piece.size:
            done.append(lax.all_to_all(piece, axis, split_axis=0, concat_axis=0, tiled=True))
    return joined_along(jnp.concatenate(done, axis=cut), concat_dim)


def expert_pass(row_block, gate_block, up_block, down_block):
    gate_part = jnp.dot(row_block, gate_block, preferred_element_type=jnp.float32)
    up_part = jnp.dot(row_block, up_block, preferred_element_type=jnp.float32)
    hidden = (jax.nn.silu(gate_part) * up_part).astype(jnp.bfloat16)
    return jnp.dot(hidden, down_block, preferred_element_type=jnp.float32).astype(jnp.bfloat16)


def migrate(w_gate, w_up, w_down, partner, own_index, slots_all):
    lower = shifted((w_gate, w_up, w_down), ("grp", "loc"), 1)
    upper = shifted((w_gate, w_up, w_down), ("grp", "loc"), -1)
    own_blocks = (w_gate, w_up, w_down)
    mine = partner[own_index]
    chosen = []
    for which in range(2):
        offset = (mine[which] - own_index) % slots_all
        chosen.append(
            tuple(
                (
                    jnp.where(
                        offset == slots_all - 1,
                        low_part,
                        jnp.where(offset == 1, up_piece, own_part),
                    )
                    for low_part, up_piece, own_part in zip(lower, upper, own_blocks)
                )
            )
        )
    half = w_gate.shape[2] // 2
    gate_block = jnp.concatenate([chosen[0][0][0][:, :half], chosen[1][0][0][:, half:]], axis=1)
    up_block = jnp.concatenate([chosen[0][1][0][:, :half], chosen[1][1][0][:, half:]], axis=1)
    down_block = jnp.concatenate([chosen[0][2][0][:half], chosen[1][2][0][half:]], axis=0)
    return (gate_block, up_block, down_block)


def make_picker(owner_expert, flat_route, slot_rank, capacity):
    matches = owner_expert[:, None] == flat_route[None, :]
    slot_match = jnp.arange(capacity, dtype=jnp.int32)[:, None] == slot_rank[None, :]
    return (matches[:, None, :] & slot_match[None, :, :]).reshape(
        owner_expert.shape[0] * capacity, -1
    )


def body(tokens, route, gate_prob, w_gate, w_up, w_down, partner):
    slots_all = lax.axis_size(("grp", "loc"))
    own_index = lax.axis_index(("grp", "loc"))
    tok_count, top_count = route.shape
    width = tokens.shape[1]
    capacity = max(2, tok_count * top_count * SPAN * 5 // (4 * slots_all))
    experts_all = slots_all // SPAN
    flat_route = route.reshape(-1)
    flat_gate = gate_prob.reshape(-1)
    onehot = (flat_route[:, None] == jnp.arange(experts_all, dtype=jnp.int32)[None, :]).astype(
        jnp.int32
    )
    slot_rank = jnp.sum(jnp.cumsum(onehot, axis=0) * onehot, axis=1) - 1
    assigned = jnp.repeat(tokens, top_count, axis=0)
    gate_block, up_block, down_block = migrate(w_gate, w_up, w_down, partner, own_index, slots_all)
    block_expert = jnp.arange(slots_all, dtype=jnp.int32) // SPAN
    picker = make_picker(block_expert, flat_route, slot_rank, capacity).astype(jnp.bfloat16)
    outgoing = jnp.dot(picker, assigned, preferred_element_type=jnp.float32).astype(jnp.bfloat16)
    outgoing = outgoing.reshape(slots_all, capacity, width)
    received = lax.all_to_all(outgoing, ("grp", "loc"), split_axis=0, concat_axis=0, tiled=True)
    result = expert_pass(received.reshape(-1, width), gate_block, up_block, down_block)
    returned = several_exchanges(result.reshape(received.shape), ("grp", "loc"), 2, 0, 0)
    returned = returned.reshape(slots_all * capacity, width)
    expert_out = lax.dot_general(
        picker, returned, (((0,), (0,)), ((), ())), preferred_element_type=jnp.float32
    )
    weighted = expert_out * flat_gate[:, None]
    return jnp.sum(weighted.reshape(tok_count, top_count, width), axis=1).astype(jnp.bfloat16)


def solution(mesh):
    return jax.shard_map(
        body,
        mesh=mesh,
        in_specs=(
            P(("grp", "loc"), None),
            P(("grp", "loc"), None),
            P(("grp", "loc"), None),
            P(("grp", "loc"), None, None),
            P(("grp", "loc"), None, None),
            P(("grp", "loc"), None, None),
            P(),
        ),
        out_specs=P(("grp", "loc"), None),
        check_vma=False,
    )
```

profile of v0, /device:TPU:7, one launch (start us, length us, event | category | flops | bytes accessed | tf_op | source)
XLA Modules:
  0.0 712.0 jit_solution(10577113730258988218)
XLA Ops:
  0.0 0.0 copy-start
  0.0 1.6 collective-permute-start
  1.6 0.7 fusion.15
  2.3 0.7 broadcast_compare_fusion
  3.0 0.2 reduce_window_sum.11
  3.2 0.8 select_reduce_fusion
  4.1 0.1 broadcast_and_fusion
  4.2 0.1 and.52
  4.3 0.0 copy-done
  4.3 6.1 convolution_convert_fusion
  10.3 14.7 %reshape.91 = bf16[128,5,7168]{2,1,0:T(8,128)(2,1)} reshape(bf16[640,7168]{1,0:T(8,128)(2,1)} %convolution_convert_fusion) | data formatting | bytes 18350080 | tf_op jit(solution)/shard_map/reshape | solution.py:101
  25.1 10.8 %all-to-all-start = ((bf16[128,5,7168]{2,1,0:T(8,128)(2,1)}), bf16[128,5,7168]{2,1,0:T(8,128)(2,1)}, u32[]{:S(2)}, u32[]{:S(2)}) async-start(bf16[128,5,7168]{2,1,0:T(8,128)(2,1)} %reshape.91), calls=%async_computation | async-start | bytes 29360128 | tf_op jit(solution)/shard_map/all_to_all | solution.py:102
  35.9 0.7 collective-permute-start.1
  36.5 3.0 collective-permute-start.2
  39.5 0.0 collective-permute-start.3
  39.5 3.6 collective-permute-start.4
  43.1 103.5 %collective-permute-done = bf16[1,7168,256]{2,1,0:T(8,128)(2,1)} collective-permute-done((bf16[1,7168,256]{2,1,0:T(8,128)(2,1)}, bf16[1,7168,256]{2,1,0:T(8,128)(2,1)}, u32[]{:S(2)}, u32[]{:S(2)}) %collective-permute-start) | collective-permute-done | bytes 3670048 | tf_op jit(solution)/shard_map/ppermute | solution.py:12
  146.6 0.0 collective-permute-start.5
  146.6 0.0 copy-done.8
  146.6 0.1 constant_dynamic-slice_fusion
  146.7 0.6 fusion.20
  148.5 153.1 %collective-permute-done.1 = bf16[1,7168,256]{2,1,0:T(8,128)(2,1)} collective-permute-done((bf16[1,7168,256]{2,1,0:T(8,128)(2,1)}, bf16[1,7168,256]{2,1,0:T(8,128)(2,1)}, u32[]{:S(2)}, u32[]{:S(2)}) %collective-permute-start.1) | collective-permute-done | bytes 3670048 | tf_op jit(solution)/shard_map/ppermute | solution.py:12
  301.6 74.1 %collective-permute-done.2 = bf16[1,7168,256]{2,1,0:T(8,128)(2,1)} collective-permute-done((bf16[1,7168,256]{2,1,0:T(8,128)(2,1)}, bf16[1,7168,256]{2,1,0:T(8,128)(2,1)}, u32[]{:S(2)}, u32[]{:S(2)}) %collective-permute-start.2) | collective-permute-done | bytes 3670048 | tf_op jit(solution)/shard_map/ppermute | solution.py:12
  375.7 4.6 collective-permute-done.3
  380.3 9.9 %select_bitcast_fusion.1 = (bf16[7168,256]{1,0:T(8,128)(2,1)}, bf16[7168,256]{1,0:T(8,128)(2,1)S(1)}, bf16[7168,256]{1,0:T(8,128)(2,1)S(1)}, bf16[7168,256]{1,0:T(8,128)(2,1)S(1)}) fusion(bf16[1,7168,256]{2,1,0:T(8,128)(2,1)} %collective-permute-done.2, bf16[1,7168,256]{2,1,0:T(8,128)(2,1)} %collective-permute-done.3, bf16[1,7168,256]{2,1,0:T(8,128)(2,1)} %param.11, ...), kind=kLoop, calls=%fused_computation.19 | loop fusion | flops 14680064 | bytes 36700164 | tf_op jit(solution)/shard_map/squeeze | solution.py:70
  390.2 1.6 slice.44
  391.8 1.4 slice.45
  393.2 1.4 slice.43
  394.6 1.4 slice.42
  396.0 58.4 %collective-permute-done.4 = bf16[1,256,7168]{2,1,0:T(8,128)(2,1)} collective-permute-done((bf16[1,256,7168]{2,1,0:T(8,128)(2,1)}, bf16[1,256,7168]{2,1,0:T(8,128)(2,1)}, u32[]{:S(2)}, u32[]{:S(2)}) %collective-permute-start.4) | collective-permute-done | bytes 3670048 | tf_op jit(solution)/shard_map/ppermute | solution.py:12
  454.3 4.6 collective-permute-done.5
  458.9 4.6 fusion.13
  463.5 0.0 all-to-all-done
  463.5 15.1 %reshape.92 = bf16[640,7168]{1,0:T(8,128)(2,1)} reshape(bf16[128,5,7168]{2,1,0:T(8,128)(2,1)} %all-to-all-done) | data formatting | bytes 18350080 | tf_op jit(solution)/shard_map/reshape | solution.py:103
  478.7 6.8 fusion.5
  485.5 0.4 copy-done.4
  485.9 0.5 copy-done.5
  486.4 2.5 fusion.1
  489.0 5.0 convolution_convert_fusion.1
  494.0 14.8 %reshape_reshape.6 = bf16[128,1,5,7168]{3,2,0,1:T(8,128)(2,1)} reshape(bf16[640,7168]{1,0:T(8,128)(2,1)} %convolution_convert_fusion.1) | data formatting | bytes 18350080 | tf_op jit(solution)/shard_map/reshape;reshape | solution.py:17
  508.7 8.3 %slice_bitcast_fusion.1 = bf16[128,1,2,7168]{3,2,1,0:T(2,128)(2,1)} fusion(bf16[128,1,5,7168]{3,2,0,1:T(8,128)(2,1)} %reshape_reshape.6), kind=kLoop, calls=%fused_computation.6 | loop fusion | bytes 7340032 | tf_op jit(solution)/shard_map/split | solution.py:35
  517.0 24.6 %all-to-all-start.1 = ((bf16[128,1,2,7168]{3,2,1,0:T(2,128)(2,1)}), bf16[128,1,2,7168]{3,2,1,0:T(2,128)(2,1)}, u32[]{:S(2)}, u32[]{:S(2)}) async-start(bf16[128,1,2,7168]{3,2,1,0:T(2,128)(2,1)} %slice_bitcast_fusion.1), calls=%async_computation.1 | async-start | bytes 7340032 | tf_op jit(solution)/shard_map/all_to_all | solution.py:37
  541.6 9.8 %slice_bitcast_fusion = bf16[128,1,3,7168]{3,2,1,0:T(4,128)(2,1)} fusion(bf16[128,1,5,7168]{3,2,0,1:T(8,128)(2,1)} %reshape_reshape.6), kind=kLoop, calls=%fused_computation.5 | loop fusion | bytes 11010048 | tf_op jit(solution)/shard_map/split | solution.py:35
  551.4 36.8 %all-to-all-done.1 = bf16[128,1,2,7168]{3,2,1,0:T(2,128)(2,1)} async-done(((bf16[128,1,2,7168]{3,2,1,0:T(2,128)(2,1)}), bf16[128,1,2,7168]{3,2,1,0:T(2,128)(2,1)}, u32[]{:S(2)}, u32[]{:S(2)}) %all-to-all-start.1) | async-done | bytes 3670048 | tf_op jit(solution)/shard_map/all_to_all | solution.py:37
  588.2 92.0 %all_to_all.15 = bf16[128,1,3,7168]{3,2,1,0:T(4,128)(2,1)S(1)} all-to-all(bf16[128,1,3,7168]{3,2,1,0:T(4,128)(2,1)} %slice_bitcast_fusion), channel_id=1, replica_groups=mesh['grp'=16,'loc'=8] {'grp','loc'}, dimensions={0} | all-to-all | bytes 11010048 | tf_op jit(solution)/shard_map/all_to_all | solution.py:37
  680.2 10.0 %pad_maximum_fusion = bf16[128,1,5,7168]{3,2,1,0:T(8,128)(2,1)} fusion(bf16[128,1,3,7168]{3,2,1,0:T(4,128)(2,1)S(1)} %all_to_all.15, bf16[128,1,2,7168]{3,2,1,0:T(2,128)(2,1)} %all-to-all-done.1), kind=kLoop, calls=%fused_computation | loop fusion | flops 18350080 | bytes 18350080 | tf_op jit(solution)/shard_map/concatenate | solution.py:38
  690.2 15.2 %reshape_reshape.7 = bf16[640,7168]{1,0:T(8,128)(2,1)} reshape(bf16[128,1,5,7168]{3,2,1,0:T(8,128)(2,1)} %pad_maximum_fusion) | data formatting | bytes 18350080 | tf_op jit(solution)/shard_map/reshape;reshape | solution.py:105
  705.3 6.6 fusion
  (18 shorter events, 0.0 us)
Async XLA Ops:
  0.0 4.3 copy-start
  0.0 146.6 %collective-permute-start = (bf16[1,7168,256]{2,1,0:T(8,128)(2,1)}, bf16[1,7168,256]{2,1,0:T(8,128)(2,1)}, u32[]{:S(2)}, u32[]{:S(2)}) collective-permute-start(bf16[1,7168,256]{2,1,0:T(8,128)(2,1)} %param.10), channel_id=1, source_target_pairs={{127,0},{0,1},{1,2},{2,3},{3,4},{4,5},{5,6},{6,7},{7,8},{8,9},{9,1... | collective-permute-start | bytes 11010056 | tf_op jit(solution)/shard_map/ppermute | solution.py:12
  25.1 121.5 %copy-start.8 = (s32[128,2]{0,1:T(2,128)S(1)}, s32[128,2]{0,1:T(2,128)}, u32[]{:S(2)}) copy-start(s32[128,2]{0,1:T(2,128)} %param.13) | copy-start | bytes 3076
  25.1 438.4 %all-to-all-start = ((bf16[128,5,7168]{2,1,0:T(8,128)(2,1)}), bf16[128,5,7168]{2,1,0:T(8,128)(2,1)}, u32[]{:S(2)}, u32[]{:S(2)}) async-start(bf16[128,5,7168]{2,1,0:T(8,128)(2,1)} %reshape.91), calls=%async_computation | async-start | bytes 29360128 | tf_op jit(solution)/shard_map/all_to_all | solution.py:102
  35.9 265.7 %collective-permute-start.1 = (bf16[1,7168,256]{2,1,0:T(8,128)(2,1)}, bf16[1,7168,256]{2,1,0:T(8,128)(2,1)}, u32[]{:S(2)}, u32[]{:S(2)}) collective-permute-start(bf16[1,7168,256]{2,1,0:T(8,128)(2,1)} %param.10), channel_id=1, source_target_pairs={{1,0},{2,1},{3,2},{4,3},{5,4},{6,5},{7,6},{8,7},{9,8},{10,9},{11,1... | collective-permute-start | bytes 11010056 | tf_op jit(solution)/shard_map/ppermute | solution.py:12
  36.5 339.2 %collective-permute-start.2 = (bf16[1,7168,256]{2,1,0:T(8,128)(2,1)}, bf16[1,7168,256]{2,1,0:T(8,128)(2,1)}, u32[]{:S(2)}, u32[]{:S(2)}) collective-permute-start(bf16[1,7168,256]{2,1,0:T(8,128)(2,1)} %param.11), channel_id=1, source_target_pairs={{127,0},{0,1},{1,2},{2,3},{3,4},{4,5},{5,6},{6,7},{7,8},{8,9},{9,1... | collective-permute-start | bytes 11010056 | tf_op jit(solution)/shard_map/ppermute | solution.py:12
  39.5 340.7 %collective-permute-start.3 = (bf16[1,7168,256]{2,1,0:T(8,128)(2,1)}, bf16[1,7168,256]{2,1,0:T(8,128)(2,1)}, u32[]{:S(2)}, u32[]{:S(2)}) collective-permute-start(bf16[1,7168,256]{2,1,0:T(8,128)(2,1)} %param.11), channel_id=1, source_target_pairs={{1,0},{2,1},{3,2},{4,3},{5,4},{6,5},{7,6},{8,7},{9,8},{10,9},{11,1... | collective-permute-start | bytes 11010056 | tf_op jit(solution)/shard_map/ppermute | solution.py:12
  39.5 414.8 %collective-permute-start.4 = (bf16[1,256,7168]{2,1,0:T(8,128)(2,1)}, bf16[1,256,7168]{2,1,0:T(8,128)(2,1)}, u32[]{:S(2)}, u32[]{:S(2)}) collective-permute-start(bf16[1,256,7168]{2,1,0:T(8,128)(2,1)} %param.12), channel_id=1, source_target_pairs={{127,0},{0,1},{1,2},{2,3},{3,4},{4,5},{5,6},{6,7},{7,8},{8,9},{9,1... | collective-permute-start | bytes 11010056 | tf_op jit(solution)/shard_map/ppermute | solution.py:12
  146.6 312.4 %collective-permute-start.5 = (bf16[1,256,7168]{2,1,0:T(8,128)(2,1)}, bf16[1,256,7168]{2,1,0:T(8,128)(2,1)}, u32[]{:S(2)}, u32[]{:S(2)}) collective-permute-start(bf16[1,256,7168]{2,1,0:T(8,128)(2,1)} %param.12), channel_id=1, source_target_pairs={{1,0},{2,1},{3,2},{4,3},{5,4},{6,5},{7,6},{8,7},{9,8},{10,9},{11,1... | collective-permute-start | bytes 11010056 | tf_op jit(solution)/shard_map/ppermute | solution.py:12
  393.2 65.7 %copy-start.3 = (bf16[1,256,7168]{2,1,0:T(8,128)(2,1)S(1)}, bf16[1,256,7168]{2,1,0:T(8,128)(2,1)}, u32[]{:S(2)}) copy-start(bf16[1,256,7168]{2,1,0:T(8,128)(2,1)} %param.12) | copy-start | bytes 11010052
  478.7 6.8 copy-start.2
  478.7 7.2 %copy-start.4 = (bf16[7168,128]{1,0:T(8,128)(2,1)S(1)}, bf16[7168,128]{1,0:T(8,128)(2,1)}, u32[]{:S(2)}) copy-start(bf16[7168,128]{1,0:T(8,128)(2,1)} %slice.43) | copy-start | bytes 5505028
  478.7 7.8 %copy-start.5 = (bf16[7168,128]{1,0:T(8,128)(2,1)S(1)}, bf16[7168,128]{1,0:T(8,128)(2,1)}, u32[]{:S(2)}) copy-start(bf16[7168,128]{1,0:T(8,128)(2,1)} %slice.42) | copy-start | bytes 5505028
  486.4 2.5 copy-start.6
  486.4 2.5 copy-start.7
  517.0 71.2 %all-to-all-start.1 = ((bf16[128,1,2,7168]{3,2,1,0:T(2,128)(2,1)}), bf16[128,1,2,7168]{3,2,1,0:T(2,128)(2,1)}, u32[]{:S(2)}, u32[]{:S(2)}) async-start(bf16[128,1,2,7168]{3,2,1,0:T(2,128)(2,1)} %slice_bitcast_fusion.1), calls=%async_computation.1 | async-start | bytes 7340032 | tf_op jit(solution)/shard_map/all_to_all | solution.py:37
  690.2 15.2 %copy-start.9 = (f32[128,1]{0,1:T(1,128)S(1)}, f32[128,1]{0,1:T(1,128)}, u32[]{:S(2)}) copy-start(f32[128,1]{0,1:T(1,128)} %param.9) | copy-start | bytes 1540
  705.3 6.6 copy-start.1
where the time goes:
time: 714 us; the launch traced here: 712 us
  waiting for transfers between devices  435 us (61%)
  blocking collectives  92 us (13%)
  local copies, waits for them, and re-layouts  85.4 us (12%)
  starting transfers between devices  44.2 us (6%)
  other arithmetic  27 us (4%)
  matrix products  27 us (4%)
    ppermute x6, waiting for transfers between devices, shifted(): return lax.ppermute(block, axis, route)  398 us
    all_to_all x1, blocking collectives, several_exchanges(): lax.all_to_all(piece, axis, split_axis=0, concat_axis=0, tiled=True)  92 us
    all_to_all x1, waiting for transfers between devices, several_exchanges(): lax.all_to_all(piece, axis, split_axis=0, concat_axis=0, tiled=True)  36.8 us
    all_to_all x1, starting transfers between devices, several_exchanges(): lax.all_to_all(piece, axis, split_axis=0, concat_axis=0, tiled=True)  24.6 us
    split x2, local copies, waits for them, and re-layouts, several_exchanges(): jnp.split(blocks, cut_rows(blocks.shape[cut], pieces), axis=cut)  18 us
    another operation x1, local copies, waits for them, and re-layouts, body(): returned = returned.reshape(slots_all * capacity, width)  15.2 us
    reshape x1, local copies, waits for them, and re-layouts, body(): received.reshape(-1, width)  15.1 us
    another operation x1, local copies, waits for them, and re-layouts, in_blocks(): return jnp.moveaxis(shard.reshape(*before, count, -1, *after), dim, 0)  14.8 us
  transfers between devices with their start and end apart: 8, of which 7 were waited for; matrix products, arithmetic and copies ran while one was open for 8% of the time, Pallas kernels for 0%

commit v1 on v0

v1 whole, which is shorter than its diff:
```python
import jax
import jax.numpy as jnp
from jax import lax
from jax.sharding import Mesh, PartitionSpec as P

SPAN = 4
CAPACITY = 5
PLANE = ("zh", "y", "c", "zl")
EVERY = PLANE + ("x",)
LANES = 128


def neighbours(step):
    return [(i, (i + step) % SPAN) for i in range(SPAN)]


def shift(block, step):
    return lax.ppermute(block, "x", neighbours(step))


def edge_pairs(which, experts):
    pairs = []
    for e in range(experts):
        pairs.append((SPAN * e + SPAN - 1, SPAN * ((e + 1) % experts) + which))
        pairs.append((SPAN * e, SPAN * ((e - 1) % experts) + SPAN - 1 - which))
    return pairs


def edge_blocks(w_gate, w_up, w_down, experts):
    quarter = w_gate.shape[1] // SPAN
    into, out = [], []
    for which in range(SPAN):
        cut = slice(which * quarter, (which + 1) * quarter)
        pairs = edge_pairs(which, experts)
        into.append(lax.ppermute(jnp.concatenate([w_gate[:, cut], w_up[:, cut]], axis=1), EVERY, pairs))
        out.append(lax.ppermute(w_down[cut], EVERY, pairs))
    return into, out


def multiplicities(partner, own, slots):
    expert, place = own // SPAN, own % SPAN
    first = expert * SPAN
    mine = lax.dynamic_slice_in_dim(partner, first, SPAN, 0)
    kept = jnp.sum((mine == own).astype(jnp.float32), axis=0)
    low = (mine[0] == (first - 1) % slots).astype(jnp.float32)
    high = (mine[SPAN - 1] == (first + SPAN) % slots).astype(jnp.float32)
    early = jnp.where(place < 2, low[0], high[0])
    late = jnp.where(place < 2, high[1], low[1])
    return kept, early, late


def dot(a, b):
    return jnp.dot(a, b, preferred_element_type=jnp.float32)


def body(tokens, route, gate_prob, w_gate, w_up, w_down, partner):
    slots = lax.axis_size(EVERY)
    own = lax.axis_index(EVERY)
    experts = slots // SPAN
    place = own % SPAN
    width = tokens.shape[1]
    w_gate, w_up, w_down = w_gate[0], w_up[0], w_down[0]
    quarter = w_gate.shape[1] // SPAN
    into, out = edge_blocks(w_gate, w_up, w_down, experts)

    flat_route = route.reshape(-1)
    onehot = (flat_route[:, None] == jnp.arange(experts, dtype=jnp.int32)[None, :]).astype(jnp.int32)
    rank = jnp.sum(jnp.cumsum(onehot, axis=0) * onehot, axis=1) - 1
    row = flat_route * CAPACITY + rank
    rows = experts * CAPACITY
    picker = (jnp.arange(rows, dtype=jnp.int32)[:, None] == row[None, :]).astype(jnp.bfloat16)
    outgoing = dot(picker, tokens).astype(jnp.bfloat16)
    tiled = (experts, CAPACITY, width // LANES, LANES)
    arrived = lax.all_to_all(outgoing.reshape(tiled), PLANE, 0, 0, tiled=True)
    mid = arrived.reshape(rows, width)
    half = rows // 2

    a, b = mid[:half], mid[half:]
    from_left_a = shift(a, 1)
    from_right_b = shift(b, -1)
    from_left_b = shift(b, 1)
    from_right_a = shift(a, -1)
    far_a = shift(from_left_a, 1)
    far_b = shift(from_right_b, -1)

    kept, early, late = multiplicities(partner, own, slots)
    scale = jnp.repeat(kept, 2 * quarter)[None, :]
    outer = (place == 0) | (place == SPAN - 1)
    piece_into = jnp.concatenate(
        [jnp.where(outer, into[0], into[1]), jnp.where(outer, into[3], into[2])], axis=1
    )
    piece_out = jnp.concatenate(
        [jnp.where(outer, out[0], out[1]), jnp.where(outer, out[3], out[2])], axis=0
    )
    down = jnp.concatenate([w_down, piece_out], axis=0)

    def partial(block):
        kept_hidden = jax.nn.silu(dot(block, w_gate)) * dot(block, w_up) * scale
        both = dot(block, piece_into)
        q = quarter
        hidden_early = jax.nn.silu(both[:, :q]) * both[:, q : 2 * q] * early
        hidden_late = jax.nn.silu(both[:, 2 * q : 3 * q]) * both[:, 3 * q :] * late
        hidden = jnp.concatenate([kept_hidden, hidden_early, hidden_late], axis=1).astype(jnp.bfloat16)
        return dot(hidden, down).astype(jnp.bfloat16)

    far = partial(jnp.concatenate([far_a, far_b], axis=0))
    right = partial(jnp.concatenate([from_right_a, from_right_b], axis=0))
    left = partial(jnp.concatenate([from_left_a, from_left_b], axis=0))
    home = partial(mid)

    def added(u, v):
        return (u.astype(jnp.float32) + v.astype(jnp.float32)).astype(jnp.bfloat16)

    to_right_a = shift(added(right[:half], shift(far[:half], 1)), 1)
    to_right_b = shift(right[half:], 1)
    to_left_b = shift(added(left[half:], shift(far[half:], -1)), -1)
    to_left_a = shift(left[:half], -1)
    f32 = jnp.float32
    total_a = home[:half].astype(f32) + to_right_a.astype(f32) + to_left_a.astype(f32)
    total_b = home[half:].astype(f32) + to_right_b.astype(f32) + to_left_b.astype(f32)
    total = jnp.concatenate([total_a, total_b], axis=0).astype(jnp.bfloat16)
    returned = lax.all_to_all(total.reshape(tiled), PLANE, 0, 0, tiled=True).reshape(rows, width)
    expert_out = lax.dot_general(picker, returned, (((0,), (0,)), ((), ())), preferred_element_type=f32)
    return (expert_out * gate_prob.reshape(-1)[:, None]).astype(jnp.bfloat16)


def solution(mesh):
    grid = Mesh(mesh.devices.reshape(2, 4, 2, 2, 4), EVERY)
    spec2, spec3 = P(EVERY, None), P(EVERY, None, None)
    return jax.shard_map(
        body,
        mesh=grid,
        in_specs=(spec2, spec2, spec2, spec3, spec3, spec3, P()),
        out_specs=spec2,
        check_vma=False,
    )
```

time: 714 us -> 422 us (0.59)
  waiting for transfers between devices: 435 us -> 263 us
  local copies, waits for them, and re-layouts: 85.4 us -> 18.2 us
  blocking collectives: 92 us -> 48.3 us
  matrix products: 27 us -> 18.6 us
    ppermute x6 -> x20, waiting for transfers between devices: 398 us -> 263 us  [the longest x12 122 us: shift(): return lax.ppermute(block, 'x', neighbours(step))]
    all_to_all x1, blocking collectives: 92 us -> 48.3 us  [body(): lax.all_to_all(total.reshape(tiled), PLANE, 0, 0, tiled=True)]
    all_to_all x2 -> x1, waiting for transfers between devices: 36.8 us -> 0.01 us  [body(): arrived = lax.all_to_all(outgoing.reshape(tiled), PLANE, 0, 0, tiled=True)]
    another operation x2 -> x0, local copies, waits for them, and re-layouts: 29.9 us -> none  [the longest x1 15.2 us: body(): returned = returned.reshape(slots_all * capacity, width)]
    reshape x2 -> x0, local copies, waits for them, and re-layouts: 29.9 us -> none  [the longest x1 15.1 us: body(): received.reshape(-1, width)]
    ppermute x6 -> x20, starting transfers between devices: 8.78 us -> 37 us  [the longest x12 14.9 us: shift(): return lax.ppermute(block, 'x', neighbours(step))]
    all_to_all x2 -> x1, starting transfers between devices: 35.4 us -> 8.2 us  [body(): arrived = lax.all_to_all(outgoing.reshape(tiled), PLANE, 0, 0, tiled=True)]
    split x2 -> x0, local copies, waits for them, and re-layouts: 18 us -> none  [several_exchanges(): jnp.split(blocks, cut_rows(blocks.shape[cut], pieces), axis=cut)]
  transfers between devices with their start and end apart: 8 -> 21, of which waited for: 7 -> 9; matrix products, arithmetic and copies ran while one was open for 8% -> 9% of each run, Pallas kernels for 0% -> 0%
where the time goes in v1:
time: 422 us; the launch traced here: 417 us
  waiting for transfers between devices  263 us (62%)
  blocking collectives  48.3 us (11%)
  starting transfers between devices  45.2 us (11%)
  other arithmetic  21.3 us (5%)
  matrix products  18.6 us (4%)
  local copies, waits for them, and re-layouts  18.2 us (4%)
    ppermute x12, waiting for transfers between devices, shift(): return lax.ppermute(block, 'x', neighbours(step))  122 us
    ppermute x4, waiting for transfers between devices, edge_blocks(): out.append(lax.ppermute(w_down[cut], EVERY, pairs))  106 us
    all_to_all x1, blocking collectives, body(): lax.all_to_all(total.reshape(tiled), PLANE, 0, 0, tiled=True)  48.3 us
    ppermute x4, waiting for transfers between devices, edge_blocks(): lax.ppermute(jnp.concatenate([w_gate[:, cut], w_up[:, cut]], axis=1), EVE...  34.2 us
    dot_general x17, matrix products, dot(): return jnp.dot(a, b, preferred_element_type=jnp.float32)  16.7 us
    ppermute x12, starting transfers between devices, shift(): return lax.ppermute(block, 'x', neighbours(step))  14.9 us
    ppermute x4, starting transfers between devices, edge_blocks(): lax.ppermute(jnp.concatenate([w_gate[:, cut], w_up[:, cut]], axis=1), EVE...  13.3 us
    concatenate x4, other arithmetic, edge_blocks(): jnp.concatenate([w_gate[:, cut], w_up[:, cut]], axis=1)  11.3 us
  transfers between devices with their start and end apart: 21, of which 9 were waited for; matrix products, arithmetic and copies ran while one was open for 9% of the time, Pallas kernels for 0%

profile of v1, /device:TPU:7, one launch (start us, length us, event | category | flops | bytes accessed | tf_op | source)
XLA Modules:
  0.0 417.2 jit_solution(15611313636561327940)
XLA Ops:
  0.0 7.8 %fusion.89 = (bf16[7168,64]{1,0:T(8,128)(2,1)S(1)}, bf16[7168,64]{1,0:T(8,128)(2,1)S(1)}, bf16[7168,64]{1,0:T(8,128)(2,1)S(1)}, bf16[7168,64]{1,0:T(8,128)(2,1)}...) fusion(bf16[7168,256]{1,0:T(8,128)(2,1)} %bitcast.90, ...), kind=kLoop, calls=%fused_computation.130 | loop fusion | bytes 14680064 | tf_op jit(solution)/shard_map/slice | solution.py:35
  7.8 2.3 pad_maximum_fusion.2
  10.1 3.4 collective-permute-start
  13.6 2.3 pad_maximum_fusion.3
  15.9 4.1 collective-permute-start.1
  20.0 2.3 pad_maximum_fusion.4
  22.3 3.3 collective-permute-start.2
  26.8 1.9 copy.8
  28.7 8.2 %all-to-all-start = ((bf16[32,5,56,128]{3,2,1,0:T(8,128)(2,1)}), bf16[32,5,56,128]{3,2,1,0:T(8,128)(2,1)S(1)}, u32[]{:S(2)}, u32[]{:S(2)}) async-start(bf16[32,5,56,128]{3,2,1,0:T(8,128)(2,1)} %bitcast.95), calls=%async_computation | async-start | bytes 4587520 | tf_op jit(solution)/shard_map/all_to_all | solution.py:74
  36.9 3.6 slice_bitcast_fusion.2
  40.5 3.2 collective-permute-start.6
  43.7 2.2 collective-permute-start.7
  49.4 4.4 %pad_maximum_fusion.5 = bf16[7168,128]{1,0:T(8,128)(2,1)} fusion(bf16[7168,64]{1,0:T(8,128)(2,1)} %get-tuple-element.41, bf16[7168,64]{1,0:T(8,128)(2,1)} %get-tuple-element.14), kind=kLoop, calls=%fused_computation.25 | loop fusion | flops 3670016 | bytes 3670016 | tf_op jit(solution)/shard_map/concatenate | solution.py:35
  53.8 86.3 %collective-permute-done.6 = bf16[64,7168]{1,0:T(8,128)(2,1)} collective-permute-done((bf16[64,7168]{1,0:T(8,128)(2,1)}, bf16[64,7168]{1,0:T(8,128)(2,1)}, u32[]{:S(2)}, u32[]{:S(2)}) %collective-permute-start.6) | collective-permute-done | bytes 917536 | tf_op jit(solution)/shard_map/ppermute | solution.py:36
  140.1 1.9 collective-permute-start.4
  142.0 1.3 collective-permute-start.5
  143.3 2.2 broadcast_select_fusion.2
  145.6 20.0 %collective-permute-done.4 = bf16[64,7168]{1,0:T(8,128)(2,1)S(1)} collective-permute-done((bf16[64,7168]{1,0:T(8,128)(2,1)S(1)}, bf16[64,7168]{1,0:T(8,128)(2,1)S(1)}, u32[]{:S(2)}, u32[]{:S(2)}) %collective-permute-start.4) | collective-permute-done | bytes 917536 | tf_op jit(solution)/shard_map/ppermute | solution.py:36
  165.6 2.5 collective-permute-start.3
  168.2 2.9 broadcast_select_fusion.1
  171.9 34.2 %collective-permute-done.3 = bf16[7168,128]{1,0:T(8,128)(2,1)} collective-permute-done((bf16[7168,128]{1,0:T(8,128)(2,1)}, bf16[7168,128]{1,0:T(8,128)(2,1)}, u32[]{:S(2)}, u32[]{:S(2)}) %collective-permute-start.3) | collective-permute-done | bytes 1835040 | tf_op jit(solution)/shard_map/ppermute | solution.py:35
  206.0 1.8 broadcast_select_fusion
  208.2 1.5 collective-permute-start.9
  209.7 1.2 collective-permute-start.15
  211.7 18.8 %collective-permute-done.8 = bf16[80,7168]{1,0:T(8,128)(2,1)S(1)} collective-permute-done((bf16[80,7168]{1,0:T(8,128)(2,1)S(1)}, bf16[80,7168]{1,0:T(8,128)(2,1)S(1)}, u32[]{:S(2)}, u32[]{:S(2)}) %collective-permute-start.8) | collective-permute-done | bytes 1146912 | tf_op jit(solution)/shard_map/ppermute | solution.py:18
  230.6 24.5 %collective-permute-done.9 = bf16[80,7168]{1,0:T(8,128)(2,1)S(1)} collective-permute-done((bf16[80,7168]{1,0:T(8,128)(2,1)S(1)}, bf16[80,7168]{1,0:T(8,128)(2,1)S(1)}, u32[]{:S(2)}, u32[]{:S(2)}) %collective-permute-start.9) | collective-permute-done | bytes 1146912 | tf_op jit(solution)/shard_map/ppermute | solution.py:18
  255.2 0.8 fusion.88
  256.0 2.3 collective-permute-start.12
  258.4 0.8 fusion.83
  259.2 1.2 copy-done.3
  260.4 0.8 multiply_convert_fusion.2
  262.7 1.6 convolution_convert_fusion.2
  265.3 20.9 %collective-permute-done.11 = bf16[80,7168]{1,0:T(8,128)(2,1)S(1)} collective-permute-done((bf16[80,7168]{1,0:T(8,128)(2,1)S(1)}, bf16[80,7168]{1,0:T(8,128)(2,1)S(1)}, u32[]{:S(2)}, u32[]{:S(2)}) %collective-permute-start.11) | collective-permute-done | bytes 1146912 | tf_op jit(solution)/shard_map/ppermute | solution.py:18
  286.4 0.8 fusion.87
  287.2 0.8 fusion.81
  288.1 0.8 multiply_convert_fusion.1
  289.0 1.6 convolution_convert_fusion.1
  292.0 2.4 collective-permute-start.17
  295.3 1.6 convolution_convert_fusion
  297.1 2.7 collective-permute-start.13
  299.8 16.3 %collective-permute-done.18 = bf16[80,7168]{1,0:T(8,128)(2,1)S(1)} collective-permute-done((bf16[80,7168]{1,0:T(8,128)(2,1)S(1)}, bf16[80,7168]{1,0:T(8,128)(2,1)S(1)}, u32[]{:S(2)}, u32[]{:S(2)}) %collective-permute-start.18) | collective-permute-done | bytes 1146912 | tf_op jit(solution)/shard_map/ppermute | solution.py:18
  316.6 24.0 %collective-permute-done.13 = bf16[80,7168]{1,0:T(8,128)(2,1)S(1)} collective-permute-done((bf16[80,7168]{1,0:T(8,128)(2,1)S(1)}, bf16[80,7168]{1,0:T(8,128)(2,1)S(1)}, u32[]{:S(2)}, u32[]{:S(2)}) %collective-permute-start.13) | collective-permute-done | bytes 1146912 | tf_op jit(solution)/shard_map/ppermute | solution.py:18
  340.9 3.4 collective-permute-start.14
  345.9 1.6 convolution_convert_fusion.3
  347.6 17.6 %collective-permute-done.19 = bf16[80,7168]{1,0:T(8,128)(2,1)S(1)} collective-permute-done((bf16[80,7168]{1,0:T(8,128)(2,1)S(1)}, bf16[80,7168]{1,0:T(8,128)(2,1)S(1)}, u32[]{:S(2)}, u32[]{:S(2)}) %collective-permute-start.19) | collective-permute-done | bytes 1146912 | tf_op jit(solution)/shard_map/ppermute | solution.py:18
  365.2 1.1 add_convert_fusion.2
  367.0 48.3 %all_to_all.10 = bf16[32,5,56,128]{3,2,1,0:T(8,128)(2,1)S(1)} all-to-all(bf16[32,5,56,128]{3,2,1,0:T(8,128)(2,1)S(1)} %bitcast.96), channel_id=1, replica_groups=mesh['zh'=2,'y'=4,'c'=2,'zl'=2,'x'=4] {'zh','y','c','zl'}, dimensions={0} | all-to-all | bytes 4587520 | tf_op jit(solution)/shard_map/all_to_all | solution.py:122
  415.2 1.9 fusion
  (75 shorter events, 12.4 us)
Async XLA Ops:
  0.0 26.1 %copy-start = (bf16[128,7168]{1,0:T(8,128)(2,1)S(1)}, bf16[128,7168]{1,0:T(8,128)(2,1)}, u32[]{:S(2)}) copy-start(bf16[128,7168]{1,0:T(8,128)(2,1)} %param.7) | copy-start | bytes 5505028
  10.1 158.1 %collective-permute-start = (bf16[7168,128]{1,0:T(8,128)(2,1)}, bf16[7168,128]{1,0:T(8,128)(2,1)}, u32[]{:S(2)}, u32[]{:S(2)}) collective-permute-start(bf16[7168,128]{1,0:T(8,128)(2,1)} %pad_maximum_fusion.2), channel_id=1, source_target_pairs={{3,4},{0,127},{7,8},{4,3},{11,12},{8,7},{15,16},{12,11},{19,20},{1... | collective-permute-start | bytes 5505032 | tf_op jit(solution)/shard_map/ppermute | solution.py:35
  15.9 152.3 %collective-permute-start.1 = (bf16[7168,128]{1,0:T(8,128)(2,1)}, bf16[7168,128]{1,0:T(8,128)(2,1)}, u32[]{:S(2)}, u32[]{:S(2)}) collective-permute-start(bf16[7168,128]{1,0:T(8,128)(2,1)} %pad_maximum_fusion.3), channel_id=1, source_target_pairs={{3,5},{0,126},{7,9},{4,2},{11,13},{8,6},{15,17},{12,10},{19,21},{1... | collective-permute-start | bytes 5505032 | tf_op jit(solution)/shard_map/ppermute | solution.py:35
  20.0 5.6 %copy-start.8 = (s32[128,1]{0,1:T(1,128)S(1)}, s32[128,1]{0,1:T(1,128)}, u32[]{:S(2)}) copy-start(s32[128,1]{0,1:T(1,128)} %param.8) | copy-start | bytes 1540
  22.3 149.6 %collective-permute-start.2 = (bf16[7168,128]{1,0:T(8,128)(2,1)}, bf16[7168,128]{1,0:T(8,128)(2,1)}, u32[]{:S(2)}, u32[]{:S(2)}) collective-permute-start(bf16[7168,128]{1,0:T(8,128)(2,1)} %pad_maximum_fusion.4), channel_id=1, source_target_pairs={{3,7},{0,124},{7,11},{4,0},{11,15},{8,4},{15,19},{12,8},{19,23},{1... | collective-permute-start | bytes 5505032 | tf_op jit(solution)/shard_map/ppermute | solution.py:35
  28.7 142.5 %all-to-all-start = ((bf16[32,5,56,128]{3,2,1,0:T(8,128)(2,1)}), bf16[32,5,56,128]{3,2,1,0:T(8,128)(2,1)S(1)}, u32[]{:S(2)}, u32[]{:S(2)}) async-start(bf16[32,5,56,128]{3,2,1,0:T(8,128)(2,1)} %bitcast.95), calls=%async_computation | async-start | bytes 4587520 | tf_op jit(solution)/shard_map/all_to_all | solution.py:74
  36.9 9.1 %copy-start.9 = (s32[128,2]{0,1:T(2,128)S(1)}, s32[128,2]{0,1:T(2,128)}, u32[]{:S(2)}) copy-start(s32[128,2]{0,1:T(2,128)} %param.13) | copy-start | bytes 3076
  40.5 99.6 %collective-permute-start.6 = (bf16[64,7168]{1,0:T(8,128)(2,1)}, bf16[64,7168]{1,0:T(8,128)(2,1)}, u32[]{:S(2)}, u32[]{:S(2)}) collective-permute-start(bf16[64,7168]{1,0:T(8,128)(2,1)} %get-tuple-element.10), channel_id=1, source_target_pairs={{3,7},{0,124},{7,11},{4,0},{11,15},{8,4},{15,19},{12,8},{19,23},{1... | collective-permute-start | bytes 2752520 | tf_op jit(solution)/shard_map/ppermute | solution.py:36
  43.7 98.2 %collective-permute-start.7 = (bf16[64,7168]{1,0:T(8,128)(2,1)}, bf16[64,7168]{1,0:T(8,128)(2,1)}, u32[]{:S(2)}, u32[]{:S(2)}) collective-permute-start(bf16[64,7168]{1,0:T(8,128)(2,1)} %get-tuple-element.9), channel_id=1, source_target_pairs={{3,6},{0,125},{7,10},{4,1},{11,14},{8,5},{15,18},{12,9},{19,22},{1... | collective-permute-start | bytes 2752520 | tf_op jit(solution)/shard_map/ppermute | solution.py:36
  49.4 90.6 %copy-start.6 = (bf16[64,7168]{1,0:T(8,128)(2,1)S(1)}, bf16[64,7168]{1,0:T(8,128)(2,1)}, u32[]{:S(2)}) copy-start(bf16[64,7168]{1,0:T(8,128)(2,1)} %get-tuple-element.8) | copy-start | bytes 2752516
  140.1 25.5 %collective-permute-start.4 = (bf16[64,7168]{1,0:T(8,128)(2,1)S(1)}, bf16[64,7168]{1,0:T(8,128)(2,1)S(1)}, u32[]{:S(2)}, u32[]{:S(2)}) collective-permute-start(bf16[64,7168]{1,0:T(8,128)(2,1)S(1)} %copy-done.6), channel_id=1, source_target_pairs={{3,4},{0,127},{7,8},{4,3},{11,12},{8,7},{15,16},{12,11},{19,20},{1... | collective-permute-start | bytes 2752520 | tf_op jit(solution)/shard_map/ppermute | solution.py:36
  142.0 26.1 %collective-permute-start.5 = (bf16[64,7168]{1,0:T(8,128)(2,1)S(1)}, bf16[64,7168]{1,0:T(8,128)(2,1)S(1)}, u32[]{:S(2)}, u32[]{:S(2)}) collective-permute-start(bf16[64,7168]{1,0:T(8,128)(2,1)S(1)} %get-tuple-element.7), channel_id=1, source_target_pairs={{3,5},{0,126},{7,9},{4,2},{11,13},{8,6},{15,17},{12,10},{19,21},{1... | collective-permute-start | bytes 2752520 | tf_op jit(solution)/shard_map/ppermute | solution.py:36
  165.6 40.4 %collective-permute-start.3 = (bf16[7168,128]{1,0:T(8,128)(2,1)}, bf16[7168,128]{1,0:T(8,128)(2,1)}, u32[]{:S(2)}, u32[]{:S(2)}) collective-permute-start(bf16[7168,128]{1,0:T(8,128)(2,1)} %pad_maximum_fusion.5), channel_id=1, source_target_pairs={{3,6},{0,125},{7,10},{4,1},{11,14},{8,5},{15,18},{12,9},{19,22},{1... | collective-permute-start | bytes 5505032 | tf_op jit(solution)/shard_map/ppermute | solution.py:35
  171.8 58.7 %collective-permute-start.8 = (bf16[80,7168]{1,0:T(8,128)(2,1)S(1)}, bf16[80,7168]{1,0:T(8,128)(2,1)S(1)}, u32[]{:S(2)}, u32[]{:S(2)}) collective-permute-start(bf16[80,7168]{1,0:T(8,128)(2,1)S(1)} %bitcast.104), channel_id=1, source_target_pairs={{0,3},{1,0},{2,1},{3,2},{4,7},{5,4},{6,5},{7,6},{8,11},{9,8},{10,9... | collective-permute-start | bytes 3440648 | tf_op jit(solution)/shard_map/ppermute | solution.py:18
  206.0 4.9 %copy-start.2 = (bf16[1,7168,256]{2,1,0:T(8,128)(2,1)S(1)}, bf16[1,7168,256]{2,1,0:T(8,128)(2,1)}, u32[]{:S(2)}) copy-start(bf16[1,7168,256]{2,1,0:T(8,128)(2,1)} %param.10) | copy-start | bytes 11010052
  207.9 53.4 %collective-permute-start.10 = (bf16[80,7168]{1,0:T(8,128)(2,1)S(1)}, bf16[80,7168]{1,0:T(8,128)(2,1)S(1)}, u32[]{:S(2)}, u32[]{:S(2)}) collective-permute-start(bf16[80,7168]{1,0:T(8,128)(2,1)S(1)} %bitcast.105), channel_id=1, source_target_pairs={{0,1},{1,2},{2,3},{3,0},{4,5},{5,6},{6,7},{7,4},{8,9},{9,10},{10,1... | collective-permute-start | bytes 3440648 | tf_op jit(solution)/shard_map/ppermute | solution.py:18
  208.2 46.9 %collective-permute-start.9 = (bf16[80,7168]{1,0:T(8,128)(2,1)S(1)}, bf16[80,7168]{1,0:T(8,128)(2,1)S(1)}, u32[]{:S(2)}, u32[]{:S(2)}) collective-permute-start(bf16[80,7168]{1,0:T(8,128)(2,1)S(1)} %bitcast.106), channel_id=1, source_target_pairs={{0,3},{1,0},{2,1},{3,2},{4,7},{5,4},{6,5},{7,6},{8,11},{9,8},{10,9... | collective-permute-start | bytes 3440648 | tf_op jit(solution)/shard_map/ppermute | solution.py:18
  209.7 54.8 %collective-permute-start.15 = (bf16[80,7168]{1,0:T(8,128)(2,1)S(1)}, bf16[80,7168]{1,0:T(8,128)(2,1)S(1)}, u32[]{:S(2)}, u32[]{:S(2)}) collective-permute-start(bf16[80,7168]{1,0:T(8,128)(2,1)S(1)} %bitcast.107), channel_id=1, source_target_pairs={{0,1},{1,2},{2,3},{3,0},{4,5},{5,6},{6,7},{7,4},{8,9},{9,10},{10,1... | collective-permute-start | bytes 3440648 | tf_op jit(solution)/shard_map/ppermute | solution.py:18
  211.7 43.5 %copy-start.5 = (bf16[7168,128]{1,0:T(8,128)(2,1)S(1)}, bf16[7168,128]{1,0:T(8,128)(2,1)}, u32[]{:S(2)}) copy-start(bf16[7168,128]{1,0:T(8,128)(2,1)} %broadcast_select_fusion.1) | copy-start | bytes 5505028
  256.0 30.3 %collective-permute-start.12 = (bf16[80,7168]{1,0:T(8,128)(2,1)S(1)}, bf16[80,7168]{1,0:T(8,128)(2,1)S(1)}, u32[]{:S(2)}, u32[]{:S(2)}) collective-permute-start(bf16[80,7168]{1,0:T(8,128)(2,1)S(1)} %collective-permute-done.9), channel_id=1, source_target_pairs={{0,3},{1,0},{2,1},{3,2},{4,7},{5,4},{6,5},{7,6},{8,11},{9,8},{10,9... | collective-permute-start | bytes 3440648 | tf_op jit(solution)/shard_map/ppermute | solution.py:18
  258.4 2.0 copy-start.3
  260.4 2.0 copy-start.4
  260.4 2.3 copy-start.7
  261.3 24.9 %collective-permute-start.11 = (bf16[80,7168]{1,0:T(8,128)(2,1)S(1)}, bf16[80,7168]{1,0:T(8,128)(2,1)S(1)}, u32[]{:S(2)}, u32[]{:S(2)}) collective-permute-start(bf16[80,7168]{1,0:T(8,128)(2,1)S(1)} %collective-permute-done.10), channel_id=1, source_target_pairs={{0,1},{1,2},{2,3},{3,0},{4,5},{5,6},{6,7},{7,4},{8,9},{9,10},{10,1... | collective-permute-start | bytes 3440648 | tf_op jit(solution)/shard_map/ppermute | solution.py:18
  290.8 25.3 %collective-permute-start.18 = (bf16[80,7168]{1,0:T(8,128)(2,1)S(1)}, bf16[80,7168]{1,0:T(8,128)(2,1)S(1)}, u32[]{:S(2)}, u32[]{:S(2)}) collective-permute-start(bf16[80,7168]{1,0:T(8,128)(2,1)S(1)} %get-tuple-element.22), channel_id=1, source_target_pairs={{0,3},{1,0},{2,1},{3,2},{4,7},{5,4},{6,5},{7,6},{8,11},{9,8},{10,9... | collective-permute-start | bytes 3440648 | tf_op jit(solution)/shard_map/ppermute | solution.py:18
  292.0 55.6 %collective-permute-start.17 = (bf16[80,7168]{1,0:T(8,128)(2,1)S(1)}, bf16[80,7168]{1,0:T(8,128)(2,1)S(1)}, u32[]{:S(2)}, u32[]{:S(2)}) collective-permute-start(bf16[80,7168]{1,0:T(8,128)(2,1)S(1)} %slice.235), channel_id=1, source_target_pairs={{0,1},{1,2},{2,3},{3,0},{4,5},{5,6},{6,7},{7,4},{8,9},{9,10},{10,1... | collective-permute-start | bytes 3440648 | tf_op jit(solution)/shard_map/ppermute | solution.py:18
  297.0 50.5 %collective-permute-start.16 = (bf16[80,7168]{1,0:T(8,128)(2,1)S(1)}, bf16[80,7168]{1,0:T(8,128)(2,1)S(1)}, u32[]{:S(2)}, u32[]{:S(2)}) collective-permute-start(bf16[80,7168]{1,0:T(8,128)(2,1)S(1)} %slice.233), channel_id=1, source_target_pairs={{0,3},{1,0},{2,1},{3,2},{4,7},{5,4},{6,5},{7,6},{8,11},{9,8},{10,9... | collective-permute-start | bytes 3440648 | tf_op jit(solution)/shard_map/ppermute | solution.py:18
  297.1 43.5 %collective-permute-start.13 = (bf16[80,7168]{1,0:T(8,128)(2,1)S(1)}, bf16[80,7168]{1,0:T(8,128)(2,1)S(1)}, u32[]{:S(2)}, u32[]{:S(2)}) collective-permute-start(bf16[80,7168]{1,0:T(8,128)(2,1)S(1)} %get-tuple-element.21), channel_id=1, source_target_pairs={{0,1},{1,2},{2,3},{3,0},{4,5},{5,6},{6,7},{7,4},{8,9},{9,10},{10,1... | collective-permute-start | bytes 3440648 | tf_op jit(solution)/shard_map/ppermute | solution.py:18
  316.3 48.9 %collective-permute-start.19 = (bf16[80,7168]{1,0:T(8,128)(2,1)S(1)}, bf16[80,7168]{1,0:T(8,128)(2,1)S(1)}, u32[]{:S(2)}, u32[]{:S(2)}) collective-permute-start(bf16[80,7168]{1,0:T(8,128)(2,1)S(1)} %add_convert_fusion.1), channel_id=1, source_target_pairs={{0,3},{1,0},{2,1},{3,2},{4,7},{5,4},{6,5},{7,6},{8,11},{9,8},{10,9... | collective-permute-start | bytes 3440648 | tf_op jit(solution)/shard_map/ppermute | solution.py:18
  340.9 24.3 %collective-permute-start.14 = (bf16[80,7168]{1,0:T(8,128)(2,1)S(1)}, bf16[80,7168]{1,0:T(8,128)(2,1)S(1)}, u32[]{:S(2)}, u32[]{:S(2)}) collective-permute-start(bf16[80,7168]{1,0:T(8,128)(2,1)S(1)} %add_convert_fusion.3), channel_id=1, source_target_pairs={{0,1},{1,2},{2,3},{3,0},{4,5},{5,6},{6,7},{7,4},{8,9},{9,10},{10,1... | collective-permute-start | bytes 3440648 | tf_op jit(solution)/shard_map/ppermute | solution.py:18
  366.9 48.3 %copy-start.10 = (f32[128,1]{0,1:T(1,128)S(1)}, f32[128,1]{0,1:T(1,128)}, u32[]{:S(2)}) copy-start(f32[128,1]{0,1:T(1,128)} %param.9) | copy-start | bytes 1540
  367.0 50.2 %copy-start.1 = (bf16[128,7168]{1,0:T(8,128)(2,1)S(1)}, bf16[128,7168]{1,0:T(8,128)(2,1)}, u32[]{:S(2)}) copy-start(bf16[128,7168]{1,0:T(8,128)(2,1)} %param.7) | copy-start | bytes 5505028

commit v2 on v1

--- a/solution.py
+++ b/solution.py
@@ -1,13 +1,17 @@
 import jax
 import jax.numpy as jnp
 from jax import lax
+from jax.experimental import pallas as pl
+from jax.experimental.pallas import tpu as pltpu
 from jax.sharding import Mesh, PartitionSpec as P
+
 
 SPAN = 4
 CAPACITY = 5
 PLANE = ("zh", "y", "c", "zl")
 EVERY = PLANE + ("x",)
 LANES = 128
+CHUNK = 1024
 
 
 def neighbours(step):
@@ -26,15 +30,76 @@
     return pairs
 
 
-def edge_blocks(w_gate, w_up, w_down, experts):
-    quarter = w_gate.shape[1] // SPAN
-    into, out = [], []
-    for which in range(SPAN):
-        cut = slice(which * quarter, (which + 1) * quarter)
-        pairs = edge_pairs(which, experts)
-        into.append(lax.ppermute(jnp.concatenate([w_gate[:, cut], w_up[:, cut]], axis=1), EVERY, pairs))
-        out.append(lax.ppermute(w_down[cut], EVERY, pairs))
-    return into, out
+def split_kernel(gate, up, down, *pieces):
+    quarter = gate.shape[1] // SPAN
+    for q, piece in enumerate(pieces):
+        cut = slice(q * quarter, (q + 1) * quarter)
+        piece[:CHUNK, :] = jnp.concatenate([gate[:, cut], up[:, cut]], axis=1)
+        for t in range(CHUNK // LANES):
+            piece[pl.ds(CHUNK + t * quarter, quarter), :] = down[cut, t * LANES : (t + 1) * LANES]
+
+
+def split_pieces(w_gate, w_up, w_down):
+    width, hidden = w_gate.shape
+    chunks = width // CHUNK
+    rows = CHUNK + CHUNK // LANES * (hidden // SPAN)
+    return pl.pallas_call(
+        split_kernel,
+        grid=(chunks,),
+        in_specs=[
+            pl.BlockSpec((CHUNK, hidden), lambda i: (i, 0)),
+            pl.BlockSpec((CHUNK, hidden), lambda i: (i, 0)),
+            pl.BlockSpec((hidden, CHUNK), lambda i: (0, i)),
+        ],
+        out_specs=[pl.BlockSpec((rows, LANES), lambda i: (i, 0))] * SPAN,
+        out_shape=[jax.ShapeDtypeStruct((chunks * rows, LANES), jnp.bfloat16)] * SPAN,
+        name="split_pieces",
+    )(w_gate, w_up, w_down)
+
+
+def join_kernel(outer, p0, p1, p2, p3, into, down):
+    quarter = LANES // 2
+
+    def fill(first, second):
+        gate = [first[:CHUNK, :quarter], second[:CHUNK, :quarter]]
+        up = [first[:CHUNK, quarter:], second[:CHUNK, quarter:]]
+        into[...] = jnp.concatenate(gate + up, axis=1)
+        for t in range(CHUNK // LANES):
+            lanes = slice(t * LANES, (t + 1) * LANES)
+            down[:quarter, lanes] = first[pl.ds(CHUNK + t * quarter, quarter), :]
+            down[quarter:, lanes] = second[pl.ds(CHUNK + t * quarter, quarter), :]
+
+    @pl.when(outer[0] == 1)
+    def _():
+        fill(p0, p3)
+
+    @pl.when(outer[0] == 0)
+    def _():
+        fill(p1, p2)
+
+
+def join_pieces(outer, pieces, width):
+    chunks = width // CHUNK
+    rows = pieces[0].shape[0] // chunks
+    on = pl.BlockSpec((rows, LANES), lambda i, s: (i * s[0], 0))
+    off = pl.BlockSpec((rows, LANES), lambda i, s: (i * (1 - s[0]), 0))
+    return pl.pallas_call(
+        join_kernel,
+        grid_spec=pltpu.PrefetchScalarGridSpec(
+            num_scalar_prefetch=1,
+            grid=(chunks,),
+            in_specs=[on, off, off, on],
+            out_specs=[
+                pl.BlockSpec((CHUNK, 2 * LANES), lambda i, s: (i, 0)),
+                pl.BlockSpec((LANES, CHUNK), lambda i, s: (0, i)),
+            ],
+        ),
+        out_shape=[
+            jax.ShapeDtypeStruct((width, 2 * LANES), jnp.bfloat16),
+            jax.ShapeDtypeStruct((LANES, width), jnp.bfloat16),
+        ],
+        name="join_pieces",
+    )(outer, *pieces)
 
 
 def multiplicities(partner, own, slots):
@@ -46,7 +111,7 @@
     high = (mine[SPAN - 1] == (first + SPAN) % slots).astype(jnp.float32)
     early = jnp.where(place < 2, low[0], high[0])
     late = jnp.where(place < 2, high[1], low[1])
-    return kept, early, late
+    return kept, jnp.stack([early, late])
 
 
 def dot(a, b):
@@ -57,11 +122,10 @@
     slots = lax.axis_size(EVERY)
     own = lax.axis_index(EVERY)
     experts = slots // SPAN
-    place = own % SPAN
+    place = lax.axis_index("x")
     width = tokens.shape[1]
     w_gate, w_up, w_down = w_gate[0], w_up[0], w_down[0]
-    quarter = w_gate.shape[1] // SPAN
-    into, out = edge_blocks(w_gate, w_up, w_down, experts)
+    hidden = w_gate.shape[1]
 
     flat_route = route.reshape(-1)
     onehot = (flat_route[:, None] == jnp.arange(experts, dtype=jnp.int32)[None, :]).astype(jnp.int32)
@@ -71,7 +135,9 @@
     picker = (jnp.arange(rows, dtype=jnp.int32)[:, None] == row[None, :]).astype(jnp.bfloat16)
     outgoing = dot(picker, tokens).astype(jnp.bfloat16)
     tiled = (experts, CAPACITY, width // LANES, LANES)
-    arrived = lax.all_to_all(outgoing.reshape(tiled), PLANE, 0, 0, tiled=True)
+    outgoing, *held = lax.optimization_barrier((outgoing.reshape(tiled), w_gate, w_up, w_down))
+    arrived = lax.all_to_all(outgoing, PLANE, 0, 0, tiled=True)
+    pieces = [lax.ppermute(p, EVERY, edge_pairs(q, experts)) for q, p in enumerate(split_pieces(*held))]
     mid = arrived.reshape(rows, width)
     half = rows // 2
 
@@ -83,25 +149,21 @@
     far_a = shift(from_left_a, 1)
     far_b = shift(from_right_b, -1)
 
-    kept, early, late = multiplicities(partner, own, slots)
-    scale = jnp.repeat(kept, 2 * quarter)[None, :]
-    outer = (place == 0) | (place == SPAN - 1)
-    piece_into = jnp.concatenate(
-        [jnp.where(outer, into[0], into[1]), jnp.where(outer, into[3], into[2])], axis=1
-    )
-    piece_out = jnp.concatenate(
-        [jnp.where(outer, out[0], out[1]), jnp.where(outer, out[3], out[2])], axis=0
-    )
-    down = jnp.concatenate([w_down, piece_out], axis=0)
+    kept, edge = multiplicities(partner, own, slots)
+    scale = jnp.repeat(kept, hidden // 2)[None, :]
+    edge_scale = jnp.repeat(edge, LANES // 2)[None, :]
+    outer = ((place == 0) | (place == SPAN - 1)).astype(jnp.int32).reshape(1)
+    *pieces, far_a, far_b = lax.optimization_barrier((*pieces, far_a, far_b))
+    edge_into, edge_down = join_pieces(outer, pieces, width)
+    down = jnp.concatenate([w_down, edge_down], axis=0)
 
     def partial(block):
         kept_hidden = jax.nn.silu(dot(block, w_gate)) * dot(block, w_up) * scale
-        both = dot(block, piece_into)
-        q = quarter
-        hidden_early = jax.nn.silu(both[:, :q]) * both[:, q : 2 * q] * early
-        hidden_late = jax.nn.silu(both[:, 2 * q : 3 * q]) * both[:, 3 * q :] * late
-        hidden = jnp.concatenate([kept_hidden, hidden_early, hidden_late], axis=1).astype(jnp.bfloat16)
-        return dot(hidden, down).astype(jnp.bfloat16)
+        both = dot(block, edge_into)
+        edge_hidden = jax.nn.silu(both[:, :LANES]) * both[:, LANES:] * edge_scale
+        return dot(
+            jnp.concatenate([kept_hidden, edge_hidden], axis=1).astype(jnp.bfloat16), down
+        ).astype(jnp.bfloat16)
 
     far = partial(jnp.concatenate([far_a, far_b], axis=0))
     right = partial(jnp.concatenate([from_right_a, from_right_b], axis=0))

time: 422 us -> 439 us (1.040)
  blocking collectives: 48.3 us -> 81.9 us
  waiting for transfers between devices: 263 us -> 236 us
  Pallas kernels: 0 us -> 19.7 us
  other arithmetic: 21.3 us -> 4.78 us
  matrix products: 18.6 us -> 26.1 us
  starting transfers between devices: 45.2 us -> 52 us
    ppermute x8 -> x4, waiting for transfers between devices: 140 us -> 0.01 us  [body(): lax.ppermute(p, EVERY, edge_pairs(q, experts))]
    ppermute x12, waiting for transfers between devices: 122 us -> 235 us  [shift(): return lax.ppermute(block, 'x', neighbours(step))]
    all_to_all x0 -> x1, blocking collectives: none -> 39.2 us  [body(): arrived = lax.all_to_all(outgoing, PLANE, 0, 0, tiled=True)]
    ppermute x12, starting transfers between devices: 14.9 us -> 39.2 us  [shift(): return lax.ppermute(block, 'x', neighbours(step))]
    pallas_call x0 -> x2, Pallas kernels: none -> 19.7 us  [the longest x1 11.2 us: split_pieces(): pl.pallas_call(split_kernel, grid=(chunks,), in_specs=[pl.BlockSpec((CHUN...]
    slice x2 -> x0, local copies, waits for them, and re-layouts: 11.4 us -> none  [the longest x1 7.82 us: edge_blocks(): w_gate[:, cut]]
    concatenate x4 -> x0, other arithmetic: 11.3 us -> none  [edge_blocks(): jnp.concatenate([w_gate[:, cut], w_up[:, cut]], axis=1)]
    ppermute x8 -> x4, starting transfers between devices: 22.1 us -> 12.8 us  [body(): lax.ppermute(p, EVERY, edge_pairs(q, experts))]
  transfers between devices with their start and end apart: 21 -> 16, of which waited for: 9 -> 9; matrix products, arithmetic and copies ran while one was open for 9% -> 4% of each run, Pallas kernels for 0% -> 3%
where the time goes in v2:
time: 439 us; the launch traced here: 438 us
  waiting for transfers between devices  236 us (54%)
  blocking collectives  81.9 us (19%)
  starting transfers between devices  52 us (12%)
  matrix products  26.1 us (6%)
  Pallas kernels  19.7 us (4%)
  local copies, waits for them, and re-layouts  15.3 us (3%)
  other arithmetic  4.78 us (1%)
    ppermute x12, waiting for transfers between devices, shift(): return lax.ppermute(block, 'x', neighbours(step))  235 us
    all_to_all x1, blocking collectives, body(): lax.all_to_all(total.reshape(tiled), PLANE, 0, 0, tiled=True)  42.8 us
    ppermute x12, starting transfers between devices, shift(): return lax.ppermute(block, 'x', neighbours(step))  39.2 us
    all_to_all x1, blocking collectives, body(): arrived = lax.all_to_all(outgoing, PLANE, 0, 0, tiled=True)  39.2 us
    dot_general x17, matrix products, dot(): return jnp.dot(a, b, preferred_element_type=jnp.float32)  24.2 us
    ppermute x4, starting transfers between devices, body(): lax.ppermute(p, EVERY, edge_pairs(q, experts))  12.8 us
    unnamed x41, local copies, waits for them, and re-layouts  12.5 us
    pallas_call x1, Pallas kernels, split_pieces(): pl.pallas_call(split_kernel, grid=(chunks,), in_specs=[pl.BlockSpec((CHUN...  11.2 us
  transfers between devices with their start and end apart: 16, of which 9 were waited for; matrix products, arithmetic and copies ran while one was open for 4% of the time, Pallas kernels for 3%

profile of v2, /device:TPU:7, one launch (start us, length us, event | category | flops | bytes accessed | tf_op | source)
XLA Modules:
  0.0 438.2 jit_solution(3511811760470345027)
XLA Ops:
  0.0 0.9 fusion.44
  1.1 0.8 select_reduce_fusion
  3.8 39.2 %all_to_all.10 = bf16[32,5,56,128]{3,2,1,0:T(8,128)(2,1)S(1)} all-to-all(bf16[32,5,56,128]{3,2,1,0:T(8,128)(2,1)S(1)} %bitcast.91), channel_id=1, replica_groups=mesh['zh'=2,'y'=4,'c'=2,'zl'=2,'x'=4] {'zh','y','c','zl'}, dimensions={0} | all-to-all | bytes 4587520 | tf_op jit(solution)/shard_map/all_to_all | solution.py:139
  43.4 1.0 copy-done.7
  44.4 1.2 copy.39
  45.8 11.2 %split_pieces.1 = (bf16[10752,128]{1,0:T(8,128)(2,1)}, bf16[10752,128]{1,0:T(8,128)(2,1)}, bf16[10752,128]{1,0:T(8,128)(2,1)}, bf16[10752,128]{1,0:T(8,128)(2,1)}) custom-call(bf16[7168,256]{1,0:T(8,128)(2,1)} %bitcast.87, bf16[7168,256]{1,0:T(8,128)(2,1)} %bitcast.95, bf16[256,7168]{1,0:T(8,128)(2,1)} %bitcast.96), custom_call_target="tpu_custom_call" | custom-call | tf_op jit(solution)/shard_map/split_pieces/pallas_call | solution.py:46
  57.0 3.0 collective-permute-start
  60.1 4.7 %collective-permute-start.1 = (bf16[10752,128]{1,0:T(8,128)(2,1)}, bf16[10752,128]{1,0:T(8,128)(2,1)}, u32[]{:S(2)}, u32[]{:S(2)}) collective-permute-start(bf16[10752,128]{1,0:T(8,128)(2,1)} %get-tuple-element.26), channel_id=1, source_target_pairs={{3,5},{0,126},{7,9},{4,2},{11,13},{8,6},{15,17},{12,10},{19,21},{1... | collective-permute-start | bytes 8257544 | tf_op jit(solution)/shard_map/ppermute | solution.py:140
  64.7 2.9 collective-permute-start.2
  71.0 1.3 copy.38
  72.3 2.6 collective-permute-start.11
  75.3 78.0 %collective-permute-done.11 = bf16[80,7168]{1,0:T(8,128)(2,1)S(1)} collective-permute-done((bf16[80,7168]{1,0:T(8,128)(2,1)}, bf16[80,7168]{1,0:T(8,128)(2,1)S(1)}, u32[]{:S(2)}, u32[]{:S(2)}) %collective-permute-start.11) | collective-permute-done | bytes 1146912 | tf_op jit(solution)/shard_map/ppermute | solution.py:22
  153.3 2.1 collective-permute-start.3
  155.5 56.9 %collective-permute-done.8 = bf16[80,7168]{1,0:T(8,128)(2,1)S(1)} collective-permute-done((bf16[80,7168]{1,0:T(8,128)(2,1)}, bf16[80,7168]{1,0:T(8,128)(2,1)S(1)}, u32[]{:S(2)}, u32[]{:S(2)}) %collective-permute-start.8) | collective-permute-done | bytes 1146912 | tf_op jit(solution)/shard_map/ppermute | solution.py:22
  212.4 2.1 collective-permute-start.6
  215.3 1.1 constant_dynamic-update-slice_fusion.1
  216.4 5.1 %collective-permute-start.5 = (bf16[80,7168]{1,0:T(8,128)(2,1)S(1)}, bf16[80,7168]{1,0:T(8,128)(2,1)S(1)}, u32[]{:S(2)}, u32[]{:S(2)}) collective-permute-start(bf16[80,7168]{1,0:T(8,128)(2,1)S(1)} %collective-permute-done.4), channel_id=1, source_target_pairs={{0,1},{1,2},{2,3},{3,0},{4,5},{5,6},{6,7},{7,4},{8,9},{9,10},{10,1... | collective-permute-start | bytes 3440648 | tf_op jit(solution)/shard_map/ppermute | solution.py:22
  221.5 15.9 %collective-permute-done.6 = bf16[80,7168]{1,0:T(8,128)(2,1)S(1)} collective-permute-done((bf16[80,7168]{1,0:T(8,128)(2,1)}, bf16[80,7168]{1,0:T(8,128)(2,1)S(1)}, u32[]{:S(2)}, u32[]{:S(2)}) %collective-permute-start.6) | collective-permute-done | bytes 1146912 | tf_op jit(solution)/shard_map/ppermute | solution.py:22
  237.4 4.5 %collective-permute-start.7 = (bf16[80,7168]{1,0:T(8,128)(2,1)S(1)}, bf16[80,7168]{1,0:T(8,128)(2,1)S(1)}, u32[]{:S(2)}, u32[]{:S(2)}) collective-permute-start(bf16[80,7168]{1,0:T(8,128)(2,1)S(1)} %collective-permute-done.6), channel_id=1, source_target_pairs={{0,3},{1,0},{2,1},{3,2},{4,7},{5,4},{6,5},{7,6},{8,11},{9,8},{10,9... | collective-permute-start | bytes 3440648 | tf_op jit(solution)/shard_map/ppermute | solution.py:22
  241.9 0.8 multiply_convert_fusion
  242.7 1.1 constant_dynamic-update-slice_fusion
  244.2 16.9 %collective-permute-done.7 = bf16[80,7168]{1,0:T(8,128)(2,1)S(1)} collective-permute-done((bf16[80,7168]{1,0:T(8,128)(2,1)S(1)}, bf16[80,7168]{1,0:T(8,128)(2,1)S(1)}, u32[]{:S(2)}, u32[]{:S(2)}) %collective-permute-start.7) | collective-permute-done | bytes 1146912 | tf_op jit(solution)/shard_map/ppermute | solution.py:22
  261.1 1.0 copy-done.12
  262.1 1.1 constant_dynamic-update-slice_fusion.3
  263.2 8.4 %join_pieces.1 = (bf16[7168,256]{1,0:T(8,128)(2,1)}, bf16[128,7168]{1,0:T(8,128)(2,1)}) custom-call(s32[1]{0:T(128)} %bitcast.5.outer, bf16[10752,128]{1,0:T(8,128)(2,1)} %collective-permute-done.p0, bf16[10752,128]{1,0:T(8,128)(2,1)} %collective-permute-done.1.p1, bf16[10752,128]{1,0:T(8,128)(2,1)} %collective-permute-done.2.p2, ...), custom_call_target="tpu_custom_call" | custom-call | tf_op jit(solution)/shard_map/join_pieces/pallas_call | solution.py:86
  271.7 3.6 fusion.75
  276.9 1.3 copy-done.3
  279.0 0.9 copy-done.8
  280.6 2.6 fusion.73
  283.4 0.8 fusion.20
  284.3 1.1 copy-done.11
  286.0 1.6 convolution_convert_fusion.1
  287.7 18.0 %collective-permute-start.9 = (bf16[80,7168]{1,0:T(8,128)(2,1)S(1)}, bf16[80,7168]{1,0:T(8,128)(2,1)S(1)}, u32[]{:S(2)}, u32[]{:S(2)}) collective-permute-start(bf16[80,7168]{1,0:T(8,128)(2,1)S(1)} %get-tuple-element.41), channel_id=1, source_target_pairs={{0,1},{1,2},{2,3},{3,0},{4,5},{5,6},{6,7},{7,4},{8,9},{9,10},{10,1... | collective-permute-start | bytes 3440648 | tf_op jit(solution)/shard_map/ppermute | solution.py:22
  305.7 2.4 fusion.66
  308.1 2.4 multiply_convert_fusion.1
  310.5 1.6 convolution_convert_fusion
  312.3 1.6 convolution_convert_fusion.2
  314.0 2.7 collective-permute-start.13
  316.7 13.4 %collective-permute-done.9 = bf16[80,7168]{1,0:T(8,128)(2,1)S(1)} collective-permute-done((bf16[80,7168]{1,0:T(8,128)(2,1)S(1)}, bf16[80,7168]{1,0:T(8,128)(2,1)S(1)}, u32[]{:S(2)}, u32[]{:S(2)}) %collective-permute-start.9) | collective-permute-done | bytes 1146912 | tf_op jit(solution)/shard_map/ppermute | solution.py:22
  330.4 3.5 collective-permute-start.10
  333.9 30.5 %collective-permute-done.14 = bf16[80,7168]{1,0:T(8,128)(2,1)S(1)} collective-permute-done((bf16[80,7168]{1,0:T(8,128)(2,1)S(1)}, bf16[80,7168]{1,0:T(8,128)(2,1)S(1)}, u32[]{:S(2)}, u32[]{:S(2)}) %collective-permute-start.14) | collective-permute-done | bytes 1146912 | tf_op jit(solution)/shard_map/ppermute | solution.py:22
  365.7 0.8 fusion.21
  366.5 1.6 convolution_convert_fusion.3
  368.1 11.1 %collective-permute-done.10 = bf16[80,7168]{1,0:T(8,128)(2,1)S(1)} collective-permute-done((bf16[80,7168]{1,0:T(8,128)(2,1)S(1)}, bf16[80,7168]{1,0:T(8,128)(2,1)S(1)}, u32[]{:S(2)}, u32[]{:S(2)}) %collective-permute-start.10) | collective-permute-done | bytes 1146912 | tf_op jit(solution)/shard_map/ppermute | solution.py:22
  379.3 12.4 %collective-permute-done.15 = bf16[80,7168]{1,0:T(8,128)(2,1)S(1)} collective-permute-done((bf16[80,7168]{1,0:T(8,128)(2,1)S(1)}, bf16[80,7168]{1,0:T(8,128)(2,1)S(1)}, u32[]{:S(2)}, u32[]{:S(2)}) %collective-permute-start.15) | collective-permute-done | bytes 1146912 | tf_op jit(solution)/shard_map/ppermute | solution.py:22
  391.7 1.1 add_convert_fusion.2
  393.5 42.8 %all_to_all.11 = bf16[32,5,56,128]{3,2,1,0:T(8,128)(2,1)S(1)} all-to-all(bf16[32,5,56,128]{3,2,1,0:T(8,128)(2,1)S(1)} %bitcast.92), channel_id=1, replica_groups=mesh['zh'=2,'y'=4,'c'=2,'zl'=2,'x'=4] {'zh','y','c','zl'}, dimensions={0} | all-to-all | bytes 4587520 | tf_op jit(solution)/shard_map/all_to_all | solution.py:184
  436.2 1.9 fusion
  (70 shorter events, 11.8 us)
Async XLA Ops:
  0.0 2.6 copy-start
  43.0 1.4 copy-start.7
  45.6 22.1 %copy-start.14 = (s32[128,2]{0,1:T(2,128)S(1)}, s32[128,2]{0,1:T(2,128)}, u32[]{:S(2)}) copy-start(s32[128,2]{0,1:T(2,128)} %param.13) | copy-start | bytes 3076
  45.6 29.7 %collective-permute-start.4 = (bf16[80,7168]{1,0:T(8,128)(2,1)}, bf16[80,7168]{1,0:T(8,128)(2,1)S(1)}, u32[]{:S(2)}, u32[]{:S(2)}) collective-permute-start(bf16[80,7168]{1,0:T(8,128)(2,1)} %bitcast.86), channel_id=1, source_target_pairs={{0,1},{1,2},{2,3},{3,0},{4,5},{5,6},{6,7},{7,4},{8,9},{9,10},{10,1... | collective-permute-start | bytes 3440648 | tf_op jit(solution)/shard_map/ppermute | solution.py:22
  57.0 159.4 %collective-permute-start = (bf16[10752,128]{1,0:T(8,128)(2,1)}, bf16[10752,128]{1,0:T(8,128)(2,1)}, u32[]{:S(2)}, u32[]{:S(2)}) collective-permute-start(bf16[10752,128]{1,0:T(8,128)(2,1)} %get-tuple-element.25), channel_id=1, source_target_pairs={{3,4},{0,127},{7,8},{4,3},{11,12},{8,7},{15,16},{12,11},{19,20},{1... | collective-permute-start | bytes 8257544 | tf_op jit(solution)/shard_map/ppermute | solution.py:140
  60.1 183.8 %collective-permute-start.1 = (bf16[10752,128]{1,0:T(8,128)(2,1)}, bf16[10752,128]{1,0:T(8,128)(2,1)}, u32[]{:S(2)}, u32[]{:S(2)}) collective-permute-start(bf16[10752,128]{1,0:T(8,128)(2,1)} %get-tuple-element.26), channel_id=1, source_target_pairs={{3,5},{0,126},{7,9},{4,2},{11,13},{8,6},{15,17},{12,10},{19,21},{1... | collective-permute-start | bytes 8257544 | tf_op jit(solution)/shard_map/ppermute | solution.py:140
  64.7 179.1 %collective-permute-start.2 = (bf16[10752,128]{1,0:T(8,128)(2,1)}, bf16[10752,128]{1,0:T(8,128)(2,1)}, u32[]{:S(2)}, u32[]{:S(2)}) collective-permute-start(bf16[10752,128]{1,0:T(8,128)(2,1)} %get-tuple-element.27), channel_id=1, source_target_pairs={{3,6},{0,125},{7,10},{4,1},{11,14},{8,5},{15,18},{12,9},{19,22},{1... | collective-permute-start | bytes 8257544 | tf_op jit(solution)/shard_map/ppermute | solution.py:140
  72.3 81.0 %collective-permute-start.11 = (bf16[80,7168]{1,0:T(8,128)(2,1)}, bf16[80,7168]{1,0:T(8,128)(2,1)S(1)}, u32[]{:S(2)}, u32[]{:S(2)}) collective-permute-start(bf16[80,7168]{1,0:T(8,128)(2,1)} %bitcast.85), channel_id=1, source_target_pairs={{0,1},{1,2},{2,3},{3,0},{4,5},{5,6},{6,7},{7,4},{8,9},{9,10},{10,1... | collective-permute-start | bytes 3440648 | tf_op jit(solution)/shard_map/ppermute | solution.py:22
  75.2 139.3 %copy-start.2 = (bf16[1,7168,256]{2,1,0:T(8,128)(2,1)S(1)}, bf16[1,7168,256]{2,1,0:T(8,128)(2,1)}, u32[]{:S(2)}) copy-start(bf16[1,7168,256]{2,1,0:T(8,128)(2,1)} %param.10) | copy-start | bytes 11010052
  75.2 137.2 %collective-permute-start.8 = (bf16[80,7168]{1,0:T(8,128)(2,1)}, bf16[80,7168]{1,0:T(8,128)(2,1)S(1)}, u32[]{:S(2)}, u32[]{:S(2)}) collective-permute-start(bf16[80,7168]{1,0:T(8,128)(2,1)} %bitcast.86), channel_id=1, source_target_pairs={{0,3},{1,0},{2,1},{3,2},{4,7},{5,4},{6,5},{7,6},{8,11},{9,8},{10,9... | collective-permute-start | bytes 3440648 | tf_op jit(solution)/shard_map/ppermute | solution.py:22
  153.3 90.5 %collective-permute-start.3 = (bf16[10752,128]{1,0:T(8,128)(2,1)}, bf16[10752,128]{1,0:T(8,128)(2,1)}, u32[]{:S(2)}, u32[]{:S(2)}) collective-permute-start(bf16[10752,128]{1,0:T(8,128)(2,1)} %get-tuple-element.28), channel_id=1, source_target_pairs={{3,7},{0,124},{7,11},{4,0},{11,15},{8,4},{15,19},{12,8},{19,23},{1... | collective-permute-start | bytes 8257544 | tf_op jit(solution)/shard_map/ppermute | solution.py:140
  155.5 86.4 %copy-start.6 = (bf16[160,7168]{1,0:T(8,128)(2,1)}, bf16[160,7168]{1,0:T(8,128)(2,1)S(1)}, u32[]{:S(2)}) copy-start(bf16[160,7168]{1,0:T(8,128)(2,1)S(1)} %constant_dynamic-update-slice_fusion.4) | copy-start | bytes 6881284
  212.4 24.9 %collective-permute-start.6 = (bf16[80,7168]{1,0:T(8,128)(2,1)}, bf16[80,7168]{1,0:T(8,128)(2,1)S(1)}, u32[]{:S(2)}, u32[]{:S(2)}) collective-permute-start(bf16[80,7168]{1,0:T(8,128)(2,1)} %bitcast.85), channel_id=1, source_target_pairs={{0,3},{1,0},{2,1},{3,2},{4,7},{5,4},{6,5},{7,6},{8,11},{9,8},{10,9... | collective-permute-start | bytes 3440648 | tf_op jit(solution)/shard_map/ppermute | solution.py:22
  214.5 27.4 %copy-start.9 = (bf16[1,7168,256]{2,1,0:T(8,128)(2,1)S(1)}, bf16[1,7168,256]{2,1,0:T(8,128)(2,1)}, u32[]{:S(2)}) copy-start(bf16[1,7168,256]{2,1,0:T(8,128)(2,1)} %param.11) | copy-start | bytes 11010052
  216.4 27.8 %collective-permute-start.5 = (bf16[80,7168]{1,0:T(8,128)(2,1)S(1)}, bf16[80,7168]{1,0:T(8,128)(2,1)S(1)}, u32[]{:S(2)}, u32[]{:S(2)}) collective-permute-start(bf16[80,7168]{1,0:T(8,128)(2,1)S(1)} %collective-permute-done.4), channel_id=1, source_target_pairs={{0,1},{1,2},{2,3},{3,0},{4,5},{5,6},{6,7},{7,4},{8,9},{9,10},{10,1... | collective-permute-start | bytes 3440648 | tf_op jit(solution)/shard_map/ppermute | solution.py:22
  237.4 23.7 %collective-permute-start.7 = (bf16[80,7168]{1,0:T(8,128)(2,1)S(1)}, bf16[80,7168]{1,0:T(8,128)(2,1)S(1)}, u32[]{:S(2)}, u32[]{:S(2)}) collective-permute-start(bf16[80,7168]{1,0:T(8,128)(2,1)S(1)} %collective-permute-done.6), channel_id=1, source_target_pairs={{0,3},{1,0},{2,1},{3,2},{4,7},{5,4},{6,5},{7,6},{8,11},{9,8},{10,9... | collective-permute-start | bytes 3440648 | tf_op jit(solution)/shard_map/ppermute | solution.py:22
  261.1 1.0 copy-start.12
  263.2 12.1 %copy-start.13 = (bf16[80,7168]{1,0:T(8,128)(2,1)S(1)}, bf16[80,7168]{1,0:T(8,128)(2,1)}, u32[]{:S(2)}) copy-start(bf16[80,7168]{1,0:T(8,128)(2,1)} %copy-done.12) | copy-start | bytes 3440644
  271.7 3.7 copy-start.5
  271.7 4.5 %copy-start.4 = (bf16[7168,256]{1,0:T(8,128)(2,1)S(1)}, bf16[7168,256]{1,0:T(8,128)(2,1)}, u32[]{:S(2)}) copy-start(bf16[7168,256]{1,0:T(8,128)(2,1)} %get-tuple-element.33) | copy-start | bytes 11010052
  276.2 2.0 copy-start.3
  278.2 1.6 copy-start.8
  280.6 2.7 copy-start.10
  283.4 2.0 copy-start.11
  283.4 2.6 copy-start.15
  287.7 42.4 %collective-permute-start.9 = (bf16[80,7168]{1,0:T(8,128)(2,1)S(1)}, bf16[80,7168]{1,0:T(8,128)(2,1)S(1)}, u32[]{:S(2)}, u32[]{:S(2)}) collective-permute-start(bf16[80,7168]{1,0:T(8,128)(2,1)S(1)} %get-tuple-element.41), channel_id=1, source_target_pairs={{0,1},{1,2},{2,3},{3,0},{4,5},{5,6},{6,7},{7,4},{8,9},{9,10},{10,1... | collective-permute-start | bytes 3440648 | tf_op jit(solution)/shard_map/ppermute | solution.py:22
  312.2 55.9 %collective-permute-start.12 = (bf16[80,7168]{1,0:T(8,128)(2,1)S(1)}, bf16[80,7168]{1,0:T(8,128)(2,1)S(1)}, u32[]{:S(2)}, u32[]{:S(2)}) collective-permute-start(bf16[80,7168]{1,0:T(8,128)(2,1)S(1)} %slice.121), channel_id=1, source_target_pairs={{0,3},{1,0},{2,1},{3,2},{4,7},{5,4},{6,5},{7,6},{8,11},{9,8},{10,9... | collective-permute-start | bytes 3440648 | tf_op jit(solution)/shard_map/ppermute | solution.py:22
  312.3 52.1 %collective-permute-start.14 = (bf16[80,7168]{1,0:T(8,128)(2,1)S(1)}, bf16[80,7168]{1,0:T(8,128)(2,1)S(1)}, u32[]{:S(2)}, u32[]{:S(2)}) collective-permute-start(bf16[80,7168]{1,0:T(8,128)(2,1)S(1)} %get-tuple-element.42), channel_id=1, source_target_pairs={{0,3},{1,0},{2,1},{3,2},{4,7},{5,4},{6,5},{7,6},{8,11},{9,8},{10,9... | collective-permute-start | bytes 3440648 | tf_op jit(solution)/shard_map/ppermute | solution.py:22
  314.0 54.1 %collective-permute-start.13 = (bf16[80,7168]{1,0:T(8,128)(2,1)S(1)}, bf16[80,7168]{1,0:T(8,128)(2,1)S(1)}, u32[]{:S(2)}, u32[]{:S(2)}) collective-permute-start(bf16[80,7168]{1,0:T(8,128)(2,1)S(1)} %slice.123), channel_id=1, source_target_pairs={{0,1},{1,2},{2,3},{3,0},{4,5},{5,6},{6,7},{7,4},{8,9},{9,10},{10,1... | collective-permute-start | bytes 3440648 | tf_op jit(solution)/shard_map/ppermute | solution.py:22
  330.4 48.9 %collective-permute-start.10 = (bf16[80,7168]{1,0:T(8,128)(2,1)S(1)}, bf16[80,7168]{1,0:T(8,128)(2,1)S(1)}, u32[]{:S(2)}, u32[]{:S(2)}) collective-permute-start(bf16[80,7168]{1,0:T(8,128)(2,1)S(1)} %add_convert_fusion.3), channel_id=1, source_target_pairs={{0,1},{1,2},{2,3},{3,0},{4,5},{5,6},{6,7},{7,4},{8,9},{9,10},{10,1... | collective-permute-start | bytes 3440648 | tf_op jit(solution)/shard_map/ppermute | solution.py:22
  364.7 27.0 %collective-permute-start.15 = (bf16[80,7168]{1,0:T(8,128)(2,1)S(1)}, bf16[80,7168]{1,0:T(8,128)(2,1)S(1)}, u32[]{:S(2)}, u32[]{:S(2)}) collective-permute-start(bf16[80,7168]{1,0:T(8,128)(2,1)S(1)} %add_convert_fusion.1), channel_id=1, source_target_pairs={{0,3},{1,0},{2,1},{3,2},{4,7},{5,4},{6,5},{7,6},{8,11},{9,8},{10,9... | collective-permute-start | bytes 3440648 | tf_op jit(solution)/shard_map/ppermute | solution.py:22
  393.4 42.8 %copy-start.16 = (f32[128,1]{0,1:T(1,128)S(1)}, f32[128,1]{0,1:T(1,128)}, u32[]{:S(2)}) copy-start(f32[128,1]{0,1:T(1,128)} %param.9) | copy-start | bytes 1540
  393.5 44.7 %copy-start.1 = (bf16[128,7168]{1,0:T(8,128)(2,1)S(1)}, bf16[128,7168]{1,0:T(8,128)(2,1)}, u32[]{:S(2)}) copy-start(bf16[128,7168]{1,0:T(8,128)(2,1)} %param.7) | copy-start | bytes 5505028

commit v3 on v2

--- a/solution.py
+++ b/solution.py
@@ -22,11 +22,15 @@
     return lax.ppermute(block, "x", neighbours(step))
 
 
-def edge_pairs(which, experts):
+def cross_pairs(which):
+    return [(SPAN - 1, which), (0, SPAN - 1 - which)]
+
+
+def pass_pairs(which, experts):
     pairs = []
     for e in range(experts):
-        pairs.append((SPAN * e + SPAN - 1, SPAN * ((e + 1) % experts) + which))
-        pairs.append((SPAN * e, SPAN * ((e - 1) % experts) + SPAN - 1 - which))
+        pairs.append((SPAN * e + which, SPAN * ((e + 1) % experts) + which))
+        pairs.append((SPAN * e + SPAN - 1 - which, SPAN * ((e - 1) % experts) + SPAN - 1 - which))
     return pairs
 
 
@@ -61,9 +65,8 @@
     quarter = LANES // 2
 
     def fill(first, second):
-        gate = [first[:CHUNK, :quarter], second[:CHUNK, :quarter]]
-        up = [first[:CHUNK, quarter:], second[:CHUNK, quarter:]]
-        into[...] = jnp.concatenate(gate + up, axis=1)
+        into[:, :LANES] = first[:CHUNK, :]
+        into[:, LANES:] = second[:CHUNK, :]
         for t in range(CHUNK // LANES):
             lanes = slice(t * LANES, (t + 1) * LANES)
             down[:quarter, lanes] = first[pl.ds(CHUNK + t * quarter, quarter), :]
@@ -137,7 +140,11 @@
     tiled = (experts, CAPACITY, width // LANES, LANES)
     outgoing, *held = lax.optimization_barrier((outgoing.reshape(tiled), w_gate, w_up, w_down))
     arrived = lax.all_to_all(outgoing, PLANE, 0, 0, tiled=True)
-    pieces = [lax.ppermute(p, EVERY, edge_pairs(q, experts)) for q, p in enumerate(split_pieces(*held))]
+    pieces = list(split_pieces(*held))
+    for q in (2, 0, 1):
+        pieces[q] = lax.ppermute(pieces[q], "x", cross_pairs(q))
+    for q in (3, 2, 0, 1):
+        pieces[q] = lax.ppermute(pieces[q], EVERY, pass_pairs(q, experts))
     mid = arrived.reshape(rows, width)
     half = rows // 2
 
@@ -153,22 +160,29 @@
     scale = jnp.repeat(kept, hidden // 2)[None, :]
     edge_scale = jnp.repeat(edge, LANES // 2)[None, :]
     outer = ((place == 0) | (place == SPAN - 1)).astype(jnp.int32).reshape(1)
-    *pieces, far_a, far_b = lax.optimization_barrier((*pieces, far_a, far_b))
+    blocks = [
+        jnp.concatenate([far_a, far_b], axis=0),
+        jnp.concatenate([from_right_a, from_right_b], axis=0),
+        jnp.concatenate([from_left_a, from_left_b], axis=0),
+        mid,
+    ]
+    kept_hidden = [
+        (jax.nn.silu(dot(block, w_gate)) * dot(block, w_up) * scale).astype(jnp.bfloat16) for block in blocks
+    ]
+    tied = lax.optimization_barrier((*pieces, *kept_hidden))
+    pieces, kept_hidden = tied[:SPAN], tied[SPAN:]
     edge_into, edge_down = join_pieces(outer, pieces, width)
     down = jnp.concatenate([w_down, edge_down], axis=0)
-
-    def partial(block):
-        kept_hidden = jax.nn.silu(dot(block, w_gate)) * dot(block, w_up) * scale
+    quarter = LANES // 2
+
+    def partial(block, own_hidden):
         both = dot(block, edge_into)
-        edge_hidden = jax.nn.silu(both[:, :LANES]) * both[:, LANES:] * edge_scale
-        return dot(
-            jnp.concatenate([kept_hidden, edge_hidden], axis=1).astype(jnp.bfloat16), down
-        ).astype(jnp.bfloat16)
-
-    far = partial(jnp.concatenate([far_a, far_b], axis=0))
-    right = partial(jnp.concatenate([from_right_a, from_right_b], axis=0))
-    left = partial(jnp.concatenate([from_left_a, from_left_b], axis=0))
-    home = partial(mid)
+        gate = jnp.concatenate([both[:, :quarter], both[:, LANES : LANES + quarter]], axis=1)
+        up = jnp.concatenate([both[:, quarter:LANES], both[:, LANES + quarter :]], axis=1)
+        edge_hidden = (jax.nn.silu(gate) * up * edge_scale).astype(jnp.bfloat16)
+        return dot(jnp.concatenate([own_hidden, edge_hidden], axis=1), down).astype(jnp.bfloat16)
+
+    far, right, left, home = [partial(block, h) for block, h in zip(blocks, kept_hidden)]
 
     def added(u, v):
         return (u.astype(jnp.float32) + v.astype(jnp.float32)).astype(jnp.bfloat16)

time: 439 us -> 455 us (1.036)
  waiting for transfers between devices: 236 us -> 276 us
  blocking collectives: 81.9 us -> 62 us
    ppermute x4 -> x7, waiting for transfers between devices: 0.01 us -> 44 us  [the longest x4 44 us: body(): pieces[q] = lax.ppermute(pieces[q], EVERY, pass_pairs(q, experts))]
    all_to_all x1 -> x0, blocking collectives: 39.2 us -> none  [body(): arrived = lax.all_to_all(outgoing, PLANE, 0, 0, tiled=True)]
    ppermute x12, starting transfers between devices: 39.2 us -> 19.3 us  [shift(): return lax.ppermute(block, 'x', neighbours(step))]
    all_to_all x1, blocking collectives: 42.8 us -> 62 us  [body(): lax.all_to_all(total.reshape(tiled), PLANE, 0, 0, tiled=True)]
    ppermute x12, waiting for transfers between devices: 235 us -> 225 us  [shift(): return lax.ppermute(block, 'x', neighbours(step))]
    all_to_all x0 -> x1, starting transfers between devices: none -> 8.82 us  [body(): arrived = lax.all_to_all(outgoing, PLANE, 0, 0, tiled=True)]
    ppermute x4 -> x7, starting transfers between devices: 12.8 us -> 21.1 us  [the longest x4 11.5 us: body(): pieces[q] = lax.ppermute(pieces[q], EVERY, pass_pairs(q, experts))]
    all_to_all x0 -> x1, waiting for transfers between devices: none -> 6.08 us  [body(): arrived = lax.all_to_all(outgoing, PLANE, 0, 0, tiled=True)]
  transfers between devices with their start and end apart: 16 -> 20, of which waited for: 9 -> 11; matrix products, arithmetic and copies ran while one was open for 4% -> 5% of each run, Pallas kernels for 3% -> 2%
where the time goes in v3:
time: 455 us; the launch traced here: 453 us
  waiting for transfers between devices  276 us (61%)
  blocking collectives  62 us (14%)
  starting transfers between devices  49.3 us (11%)
  matrix products  27.3 us (6%)
  Pallas kernels  19.3 us (4%)
  local copies, waits for them, and re-layouts  12 us (3%)
  other arithmetic  4.88 us (1%)
    ppermute x12, waiting for transfers between devices, shift(): return lax.ppermute(block, 'x', neighbours(step))  225 us
    all_to_all x1, blocking collectives, body(): lax.all_to_all(total.reshape(tiled), PLANE, 0, 0, tiled=True)  62 us
    ppermute x4, waiting for transfers between devices, body(): pieces[q] = lax.ppermute(pieces[q], EVERY, pass_pairs(q, experts))  44 us
    dot_general x17, matrix products, dot(): return jnp.dot(a, b, preferred_element_type=jnp.float32)  25.4 us
    ppermute x12, starting transfers between devices, shift(): return lax.ppermute(block, 'x', neighbours(step))  19.3 us
    ppermute x4, starting transfers between devices, body(): pieces[q] = lax.ppermute(pieces[q], EVERY, pass_pairs(q, experts))  11.5 us
    pallas_call x1, Pallas kernels, split_pieces(): pl.pallas_call(split_kernel, grid=(chunks,), in_specs=[pl.BlockSpec((CHUN...  11.3 us
    ppermute x3, starting transfers between devices, body(): pieces[q] = lax.ppermute(pieces[q], 'x', cross_pairs(q))  9.63 us
  transfers between devices with their start and end apart: 20, of which 11 were waited for; matrix products, arithmetic and copies ran while one was open for 5% of the time, Pallas kernels for 2%

profile of v3, /device:TPU:7, one launch (start us, length us, event | category | flops | bytes accessed | tf_op | source)
XLA Modules:
  0.0 453.4 jit_solution(4953556588030461361)
XLA Ops:
  0.0 0.9 fusion.42
  1.1 0.8 select_reduce_fusion
  3.3 1.9 copy.8
  5.2 8.8 %all-to-all-start = ((bf16[32,5,56,128]{3,2,1,0:T(8,128)(2,1)}), bf16[32,5,56,128]{3,2,1,0:T(8,128)(2,1)}, u32[]{:S(2)}, u32[]{:S(2)}) async-start(bf16[32,5,56,128]{3,2,1,0:T(8,128)(2,1)} %bitcast.90), calls=%async_computation | async-start | bytes 4587520 | tf_op jit(solution)/shard_map/all_to_all | solution.py:142
  14.0 11.3 %split_pieces.1 = (bf16[10752,128]{1,0:T(8,128)(2,1)}, bf16[10752,128]{1,0:T(8,128)(2,1)}, bf16[10752,128]{1,0:T(8,128)(2,1)}, bf16[10752,128]{1,0:T(8,128)(2,1)}) custom-call(bf16[7168,256]{1,0:T(8,128)(2,1)} %bitcast.89, bf16[7168,256]{1,0:T(8,128)(2,1)} %bitcast.94, bf16[256,7168]{1,0:T(8,128)(2,1)} %bitcast.95), custom_call_target="tpu_custom_call" | custom-call | tf_op jit(solution)/shard_map/split_pieces/pallas_call | solution.py:50
  25.3 2.1 collective-permute-start
  27.4 4.7 %collective-permute-start.2 = (bf16[10752,128]{1,0:T(8,128)(2,1)}, bf16[10752,128]{1,0:T(8,128)(2,1)}, u32[]{:S(2)}, u32[]{:S(2)}) collective-permute-start(bf16[10752,128]{1,0:T(8,128)(2,1)} %get-tuple-element.27), channel_id=1, source_target_pairs={{3,1},{0,2},{7,5},{4,6},{11,9},{8,10},{15,13},{12,14},{19,17},{16,... | collective-permute-start | bytes 8257544 | tf_op jit(solution)/shard_map/ppermute | solution.py:145
  32.1 2.9 collective-permute-start.4
  38.4 6.1 %all-to-all-done = bf16[32,5,56,128]{3,2,1,0:T(8,128)(2,1)} async-done(((bf16[32,5,56,128]{3,2,1,0:T(8,128)(2,1)}), bf16[32,5,56,128]{3,2,1,0:T(8,128)(2,1)}, u32[]{:S(2)}, u32[]{:S(2)}) %all-to-all-start) | async-done | bytes 2293792 | tf_op jit(solution)/shard_map/all_to_all | solution.py:142
  44.5 2.0 fusion.71
  47.6 2.1 collective-permute-start.7
  49.9 3.6 fusion.7
  53.7 2.4 fusion.19
  56.2 116.9 %collective-permute-done.11 = bf16[80,7168]{1,0:T(8,128)(2,1)} collective-permute-done((bf16[80,7168]{1,0:T(8,128)(2,1)S(1)}, bf16[80,7168]{1,0:T(8,128)(2,1)}, u32[]{:S(2)}, u32[]{:S(2)}) %collective-permute-start.11) | collective-permute-done | bytes 1146912 | tf_op jit(solution)/shard_map/ppermute | solution.py:22
  173.0 2.3 collective-permute-start.9
  175.3 1.3 constant_dynamic-update-slice_fusion.3
  177.2 3.4 collective-permute-start.6
  180.7 3.6 collective-permute-start.1
  184.3 2.3 collective-permute-start.3
  186.6 13.4 %collective-permute-done.9 = bf16[80,7168]{1,0:T(8,128)(2,1)S(1)} collective-permute-done((bf16[80,7168]{1,0:T(8,128)(2,1)S(1)}, bf16[80,7168]{1,0:T(8,128)(2,1)S(1)}, u32[]{:S(2)}, u32[]{:S(2)}) %collective-permute-start.9) | collective-permute-done | bytes 1146912 | tf_op jit(solution)/shard_map/ppermute | solution.py:22
  200.0 2.2 collective-permute-start.5
  202.3 1.5 collective-permute-start.8
  205.5 0.8 multiply_convert_fusion.1
  206.3 21.5 %collective-permute-done.8 = bf16[80,7168]{1,0:T(8,128)(2,1)S(1)} collective-permute-done((bf16[80,7168]{1,0:T(8,128)(2,1)S(1)}, bf16[80,7168]{1,0:T(8,128)(2,1)S(1)}, u32[]{:S(2)}, u32[]{:S(2)}) %collective-permute-start.8) | collective-permute-done | bytes 1146912 | tf_op jit(solution)/shard_map/ppermute | solution.py:22
  227.7 2.1 collective-permute-start.10
  230.6 22.3 %collective-permute-done.10 = bf16[80,7168]{1,0:T(8,128)(2,1)S(1)} collective-permute-done((bf16[80,7168]{1,0:T(8,128)(2,1)S(1)}, bf16[80,7168]{1,0:T(8,128)(2,1)S(1)}, u32[]{:S(2)}, u32[]{:S(2)}) %collective-permute-start.10) | collective-permute-done | bytes 1146912 | tf_op jit(solution)/shard_map/ppermute | solution.py:22
  255.2 12.1 %collective-permute-done.6.p3 = bf16[10752,128]{1,0:T(8,128)(2,1)} collective-permute-done((bf16[10752,128]{1,0:T(8,128)(2,1)S(1)}, bf16[10752,128]{1,0:T(8,128)(2,1)}, u32[]{:S(2)}, u32[]{:S(2)}) %collective-permute-start.6) | collective-permute-done | bytes 2752544 | tf_op jit(solution)/shard_map/ppermute | solution.py:147
  267.4 31.9 %collective-permute-done.1.p0 = bf16[10752,128]{1,0:T(8,128)(2,1)} collective-permute-done((bf16[10752,128]{1,0:T(8,128)(2,1)}, bf16[10752,128]{1,0:T(8,128)(2,1)}, u32[]{:S(2)}, u32[]{:S(2)}) %collective-permute-start.1) | collective-permute-done | bytes 2752544 | tf_op jit(solution)/shard_map/ppermute | solution.py:147
  299.2 8.1 %join_pieces.1 = (bf16[7168,256]{1,0:T(8,128)(2,1)}, bf16[128,7168]{1,0:T(8,128)(2,1)}) custom-call(s32[1]{0:T(128)} %bitcast.5.outer, bf16[10752,128]{1,0:T(8,128)(2,1)} %collective-permute-done.1.p0, bf16[10752,128]{1,0:T(8,128)(2,1)} %collective-permute-done.3.p1, bf16[10752,128]{1,0:T(8,128)(2,1)} %collective-permute-done.5.p2, ...), custom_call_target="tpu_custom_call" | custom-call | tf_op jit(solution)/shard_map/join_pieces/pallas_call | solution.py:89
  307.3 3.6 fusion.80
  312.6 0.9 copy-done.6
  314.2 2.5 fusion.3
  317.4 1.4 copy-done.10
  318.8 1.6 convolution_convert_fusion.1
  320.6 1.5 collective-permute-start.13
  322.1 1.6 convolution_convert_fusion.2
  323.7 5.0 %collective-permute-start.16 = (bf16[80,7168]{1,0:T(8,128)(2,1)S(1)}, bf16[80,7168]{1,0:T(8,128)(2,1)S(1)}, u32[]{:S(2)}, u32[]{:S(2)}) collective-permute-start(bf16[80,7168]{1,0:T(8,128)(2,1)S(1)} %slice.163), channel_id=1, source_target_pairs={{0,1},{1,2},{2,3},{3,0},{4,5},{5,6},{6,7},{7,4},{8,9},{9,10},{10,1... | collective-permute-start | bytes 3440648 | tf_op jit(solution)/shard_map/ppermute | solution.py:22
  328.7 1.6 convolution_convert_fusion
  330.4 1.1 collective-permute-start.15
  331.4 1.4 collective-permute-start.17
  332.9 16.6 %collective-permute-done.13 = bf16[80,7168]{1,0:T(8,128)(2,1)S(1)} collective-permute-done((bf16[80,7168]{1,0:T(8,128)(2,1)S(1)}, bf16[80,7168]{1,0:T(8,128)(2,1)S(1)}, u32[]{:S(2)}, u32[]{:S(2)}) %collective-permute-start.13) | collective-permute-done | bytes 1146912 | tf_op jit(solution)/shard_map/ppermute | solution.py:22
  349.8 1.0 collective-permute-start.14
  350.8 20.5 %collective-permute-done.17 = bf16[80,7168]{1,0:T(8,128)(2,1)S(1)} collective-permute-done((bf16[80,7168]{1,0:T(8,128)(2,1)S(1)}, bf16[80,7168]{1,0:T(8,128)(2,1)S(1)}, u32[]{:S(2)}, u32[]{:S(2)}) %collective-permute-start.17) | collective-permute-done | bytes 1146912 | tf_op jit(solution)/shard_map/ppermute | solution.py:22
  371.8 1.6 convolution_convert_fusion.3
  373.8 13.9 %collective-permute-done.18 = bf16[80,7168]{1,0:T(8,128)(2,1)S(1)} collective-permute-done((bf16[80,7168]{1,0:T(8,128)(2,1)S(1)}, bf16[80,7168]{1,0:T(8,128)(2,1)S(1)}, u32[]{:S(2)}, u32[]{:S(2)}) %collective-permute-start.18) | collective-permute-done | bytes 1146912 | tf_op jit(solution)/shard_map/ppermute | solution.py:22
  387.7 1.1 add_convert_fusion.2
  389.5 62.0 %all_to_all.10 = bf16[32,5,56,128]{3,2,1,0:T(8,128)(2,1)S(1)} all-to-all(bf16[32,5,56,128]{3,2,1,0:T(8,128)(2,1)S(1)} %bitcast.91), channel_id=1, replica_groups=mesh['zh'=2,'y'=4,'c'=2,'zl'=2,'x'=4] {'zh','y','c','zl'}, dimensions={0} | all-to-all | bytes 4587520 | tf_op jit(solution)/shard_map/all_to_all | solution.py:198
  451.5 1.9 fusion
  (75 shorter events, 14.4 us)
Async XLA Ops:
  0.0 2.6 copy-start
  5.2 39.3 %all-to-all-start = ((bf16[32,5,56,128]{3,2,1,0:T(8,128)(2,1)}), bf16[32,5,56,128]{3,2,1,0:T(8,128)(2,1)}, u32[]{:S(2)}, u32[]{:S(2)}) async-start(bf16[32,5,56,128]{3,2,1,0:T(8,128)(2,1)} %bitcast.90), calls=%async_computation | async-start | bytes 4587520 | tf_op jit(solution)/shard_map/all_to_all | solution.py:142
  14.0 20.9 %copy-start.11 = (s32[128,2]{0,1:T(2,128)S(1)}, s32[128,2]{0,1:T(2,128)}, u32[]{:S(2)}) copy-start(s32[128,2]{0,1:T(2,128)} %param.13) | copy-start | bytes 3076
  25.3 151.9 %collective-permute-start = (bf16[10752,128]{1,0:T(8,128)(2,1)}, bf16[10752,128]{1,0:T(8,128)(2,1)}, u32[]{:S(2)}, u32[]{:S(2)}) collective-permute-start(bf16[10752,128]{1,0:T(8,128)(2,1)} %get-tuple-element.26), channel_id=1, source_target_pairs={{3,0},{0,3},{7,4},{4,7},{11,8},{8,11},{15,12},{12,15},{19,16},{16,... | collective-permute-start | bytes 8257544 | tf_op jit(solution)/shard_map/ppermute | solution.py:145
  27.4 153.3 %collective-permute-start.2 = (bf16[10752,128]{1,0:T(8,128)(2,1)}, bf16[10752,128]{1,0:T(8,128)(2,1)}, u32[]{:S(2)}, u32[]{:S(2)}) collective-permute-start(bf16[10752,128]{1,0:T(8,128)(2,1)} %get-tuple-element.27), channel_id=1, source_target_pairs={{3,1},{0,2},{7,5},{4,6},{11,9},{8,10},{15,13},{12,14},{19,17},{16,... | collective-permute-start | bytes 8257544 | tf_op jit(solution)/shard_map/ppermute | solution.py:145
  32.1 152.3 %collective-permute-start.4 = (bf16[10752,128]{1,0:T(8,128)(2,1)}, bf16[10752,128]{1,0:T(8,128)(2,1)}, u32[]{:S(2)}, u32[]{:S(2)}) collective-permute-start(bf16[10752,128]{1,0:T(8,128)(2,1)} %get-tuple-element.28), channel_id=1, source_target_pairs={{3,2},{0,1},{7,6},{4,5},{11,10},{8,9},{15,14},{12,13},{19,18},{16,... | collective-permute-start | bytes 8257544 | tf_op jit(solution)/shard_map/ppermute | solution.py:145
  46.7 126.3 %collective-permute-start.11 = (bf16[80,7168]{1,0:T(8,128)(2,1)S(1)}, bf16[80,7168]{1,0:T(8,128)(2,1)}, u32[]{:S(2)}, u32[]{:S(2)}) collective-permute-start(bf16[80,7168]{1,0:T(8,128)(2,1)S(1)} %bitcast.103), channel_id=1, source_target_pairs={{0,3},{1,0},{2,1},{3,2},{4,7},{5,4},{6,5},{7,6},{8,11},{9,8},{10,9... | collective-permute-start | bytes 3440648 | tf_op jit(solution)/shard_map/ppermute | solution.py:22
  47.6 129.1 %collective-permute-start.7 = (bf16[80,7168]{1,0:T(8,128)(2,1)S(1)}, bf16[80,7168]{1,0:T(8,128)(2,1)S(1)}, u32[]{:S(2)}, u32[]{:S(2)}) collective-permute-start(bf16[80,7168]{1,0:T(8,128)(2,1)S(1)} %bitcast.104), channel_id=1, source_target_pairs={{0,1},{1,2},{2,3},{3,0},{4,5},{5,6},{6,7},{7,4},{8,9},{9,10},{10,1... | collective-permute-start | bytes 3440648 | tf_op jit(solution)/shard_map/ppermute | solution.py:22
  49.9 3.8 copy-start.9
  173.0 4.2 copy-start.12
  173.0 27.0 %collective-permute-start.9 = (bf16[80,7168]{1,0:T(8,128)(2,1)S(1)}, bf16[80,7168]{1,0:T(8,128)(2,1)S(1)}, u32[]{:S(2)}, u32[]{:S(2)}) collective-permute-start(bf16[80,7168]{1,0:T(8,128)(2,1)S(1)} %bitcast.101), channel_id=1, source_target_pairs={{0,3},{1,0},{2,1},{3,2},{4,7},{5,4},{6,5},{7,6},{8,11},{9,8},{10,9... | collective-permute-start | bytes 3440648 | tf_op jit(solution)/shard_map/ppermute | solution.py:22
  176.7 25.6 %collective-permute-start.12 = (bf16[80,7168]{1,0:T(8,128)(2,1)S(1)}, bf16[80,7168]{1,0:T(8,128)(2,1)S(1)}, u32[]{:S(2)}, u32[]{:S(2)}) collective-permute-start(bf16[80,7168]{1,0:T(8,128)(2,1)S(1)} %bitcast.102), channel_id=1, source_target_pairs={{0,1},{1,2},{2,3},{3,0},{4,5},{5,6},{6,7},{7,4},{8,9},{9,10},{10,1... | collective-permute-start | bytes 3440648 | tf_op jit(solution)/shard_map/ppermute | solution.py:22
  177.2 26.7 %copy-start.2 = (bf16[1,7168,256]{2,1,0:T(8,128)(2,1)S(1)}, bf16[1,7168,256]{2,1,0:T(8,128)(2,1)}, u32[]{:S(2)}) copy-start(bf16[1,7168,256]{2,1,0:T(8,128)(2,1)} %param.10) | copy-start | bytes 11010052
  177.2 90.1 %collective-permute-start.6 = (bf16[10752,128]{1,0:T(8,128)(2,1)S(1)}, bf16[10752,128]{1,0:T(8,128)(2,1)}, u32[]{:S(2)}, u32[]{:S(2)}) collective-permute-start(bf16[10752,128]{1,0:T(8,128)(2,1)S(1)} %copy-done.12), channel_id=1, source_target_pairs={{3,7},{0,124},{7,11},{4,0},{11,15},{8,4},{15,19},{12,8},{19,23},{1... | collective-permute-start | bytes 8257544 | tf_op jit(solution)/shard_map/ppermute | solution.py:147
  180.7 118.6 %collective-permute-start.1 = (bf16[10752,128]{1,0:T(8,128)(2,1)}, bf16[10752,128]{1,0:T(8,128)(2,1)}, u32[]{:S(2)}, u32[]{:S(2)}) collective-permute-start(bf16[10752,128]{1,0:T(8,128)(2,1)} %collective-permute-done), channel_id=1, source_target_pairs={{0,4},{3,127},{4,8},{7,3},{8,12},{11,7},{12,16},{15,11},{16,20},{1... | collective-permute-start | bytes 8257544 | tf_op jit(solution)/shard_map/ppermute | solution.py:147
  184.3 114.9 %collective-permute-start.3 = (bf16[10752,128]{1,0:T(8,128)(2,1)}, bf16[10752,128]{1,0:T(8,128)(2,1)}, u32[]{:S(2)}, u32[]{:S(2)}) collective-permute-start(bf16[10752,128]{1,0:T(8,128)(2,1)} %collective-permute-done.2), channel_id=1, source_target_pairs={{1,5},{2,126},{5,9},{6,2},{9,13},{10,6},{13,17},{14,10},{17,21},{1... | collective-permute-start | bytes 8257544 | tf_op jit(solution)/shard_map/ppermute | solution.py:147
  200.0 99.2 %collective-permute-start.5 = (bf16[10752,128]{1,0:T(8,128)(2,1)}, bf16[10752,128]{1,0:T(8,128)(2,1)}, u32[]{:S(2)}, u32[]{:S(2)}) collective-permute-start(bf16[10752,128]{1,0:T(8,128)(2,1)} %collective-permute-done.4), channel_id=1, source_target_pairs={{2,6},{1,125},{6,10},{5,1},{10,14},{9,5},{14,18},{13,9},{18,22},{1... | collective-permute-start | bytes 8257544 | tf_op jit(solution)/shard_map/ppermute | solution.py:147
  202.3 3.2 copy-start.5
  202.3 25.4 %collective-permute-start.8 = (bf16[80,7168]{1,0:T(8,128)(2,1)S(1)}, bf16[80,7168]{1,0:T(8,128)(2,1)S(1)}, u32[]{:S(2)}, u32[]{:S(2)}) collective-permute-start(bf16[80,7168]{1,0:T(8,128)(2,1)S(1)} %collective-permute-done.7), channel_id=1, source_target_pairs={{0,1},{1,2},{2,3},{3,0},{4,5},{5,6},{6,7},{7,4},{8,9},{9,10},{10,1... | collective-permute-start | bytes 3440648 | tf_op jit(solution)/shard_map/ppermute | solution.py:22
  203.9 25.9 %copy-start.4 = (bf16[160,7168]{1,0:T(8,128)(2,1)}, bf16[160,7168]{1,0:T(8,128)(2,1)S(1)}, u32[]{:S(2)}) copy-start(bf16[160,7168]{1,0:T(8,128)(2,1)S(1)} %constant_dynamic-update-slice_fusion.4) | copy-start | bytes 6881284
  227.7 25.2 %collective-permute-start.10 = (bf16[80,7168]{1,0:T(8,128)(2,1)S(1)}, bf16[80,7168]{1,0:T(8,128)(2,1)S(1)}, u32[]{:S(2)}, u32[]{:S(2)}) collective-permute-start(bf16[80,7168]{1,0:T(8,128)(2,1)S(1)} %collective-permute-done.9), channel_id=1, source_target_pairs={{0,3},{1,0},{2,1},{3,2},{4,7},{5,4},{6,5},{7,6},{8,11},{9,8},{10,9... | collective-permute-start | bytes 3440648 | tf_op jit(solution)/shard_map/ppermute | solution.py:22
  253.0 1.5 copy-start.7
  307.3 3.8 copy-start.3
  307.3 4.5 copy-start.8
  311.8 1.6 copy-start.6
  314.2 3.2 copy-start.13
  316.8 2.0 copy-start.10
  320.6 29.0 %collective-permute-start.13 = (bf16[80,7168]{1,0:T(8,128)(2,1)S(1)}, bf16[80,7168]{1,0:T(8,128)(2,1)S(1)}, u32[]{:S(2)}, u32[]{:S(2)}) collective-permute-start(bf16[80,7168]{1,0:T(8,128)(2,1)S(1)} %get-tuple-element.45), channel_id=1, source_target_pairs={{0,1},{1,2},{2,3},{3,0},{4,5},{5,6},{6,7},{7,4},{8,9},{9,10},{10,1... | collective-permute-start | bytes 3440648 | tf_op jit(solution)/shard_map/ppermute | solution.py:22
  323.7 49.7 %collective-permute-start.16 = (bf16[80,7168]{1,0:T(8,128)(2,1)S(1)}, bf16[80,7168]{1,0:T(8,128)(2,1)S(1)}, u32[]{:S(2)}, u32[]{:S(2)}) collective-permute-start(bf16[80,7168]{1,0:T(8,128)(2,1)S(1)} %slice.163), channel_id=1, source_target_pairs={{0,1},{1,2},{2,3},{3,0},{4,5},{5,6},{6,7},{7,4},{8,9},{9,10},{10,1... | collective-permute-start | bytes 3440648 | tf_op jit(solution)/shard_map/ppermute | solution.py:22
  330.4 43.1 %collective-permute-start.15 = (bf16[80,7168]{1,0:T(8,128)(2,1)S(1)}, bf16[80,7168]{1,0:T(8,128)(2,1)S(1)}, u32[]{:S(2)}, u32[]{:S(2)}) collective-permute-start(bf16[80,7168]{1,0:T(8,128)(2,1)S(1)} %slice.161), channel_id=1, source_target_pairs={{0,3},{1,0},{2,1},{3,2},{4,7},{5,4},{6,5},{7,6},{8,11},{9,8},{10,9... | collective-permute-start | bytes 3440648 | tf_op jit(solution)/shard_map/ppermute | solution.py:22
  331.4 39.8 %collective-permute-start.17 = (bf16[80,7168]{1,0:T(8,128)(2,1)S(1)}, bf16[80,7168]{1,0:T(8,128)(2,1)S(1)}, u32[]{:S(2)}, u32[]{:S(2)}) collective-permute-start(bf16[80,7168]{1,0:T(8,128)(2,1)S(1)} %get-tuple-element.46), channel_id=1, source_target_pairs={{0,3},{1,0},{2,1},{3,2},{4,7},{5,4},{6,5},{7,6},{8,11},{9,8},{10,9... | collective-permute-start | bytes 3440648 | tf_op jit(solution)/shard_map/ppermute | solution.py:22
  349.8 24.0 %collective-permute-start.14 = (bf16[80,7168]{1,0:T(8,128)(2,1)S(1)}, bf16[80,7168]{1,0:T(8,128)(2,1)S(1)}, u32[]{:S(2)}, u32[]{:S(2)}) collective-permute-start(bf16[80,7168]{1,0:T(8,128)(2,1)S(1)} %add_convert_fusion.3), channel_id=1, source_target_pairs={{0,1},{1,2},{2,3},{3,0},{4,5},{5,6},{6,7},{7,4},{8,9},{9,10},{10,1... | collective-permute-start | bytes 3440648 | tf_op jit(solution)/shard_map/ppermute | solution.py:22
  371.5 16.2 %collective-permute-start.18 = (bf16[80,7168]{1,0:T(8,128)(2,1)S(1)}, bf16[80,7168]{1,0:T(8,128)(2,1)S(1)}, u32[]{:S(2)}, u32[]{:S(2)}) collective-permute-start(bf16[80,7168]{1,0:T(8,128)(2,1)S(1)} %add_convert_fusion.1), channel_id=1, source_target_pairs={{0,3},{1,0},{2,1},{3,2},{4,7},{5,4},{6,5},{7,6},{8,11},{9,8},{10,9... | collective-permute-start | bytes 3440648 | tf_op jit(solution)/shard_map/ppermute | solution.py:22
  389.5 62.0 %copy-start.14 = (f32[128,1]{0,1:T(1,128)S(1)}, f32[128,1]{0,1:T(1,128)}, u32[]{:S(2)}) copy-start(f32[128,1]{0,1:T(1,128)} %param.9) | copy-start | bytes 1540
  389.5 64.0 %copy-start.1 = (bf16[128,7168]{1,0:T(8,128)(2,1)S(1)}, bf16[128,7168]{1,0:T(8,128)(2,1)}, u32[]{:S(2)}) copy-start(bf16[128,7168]{1,0:T(8,128)(2,1)} %param.7) | copy-start | bytes 5505028

commit v4 on v1

v4 whole, which is shorter than its diff:
```python
import jax
import jax.numpy as jnp
from jax import lax
from jax.sharding import Mesh, PartitionSpec as P


SPAN = 4
CAPACITY = 5
PLANE = ("zh", "y", "c", "zl")
EVERY = PLANE + ("x",)
LANES = 128
MIRROR = [(0, 3), (3, 0), (1, 2), (2, 1)]
SIDE = [(0, 1), (1, 0), (2, 3), (3, 2)]
INWARD = [(0, 1), (3, 2)]


def passing(last, first, experts):
    pairs = []
    for e in range(experts):
        pairs.append((SPAN * e + last, SPAN * ((e + 1) % experts) + last))
        pairs.append((SPAN * e + first, SPAN * ((e - 1) % experts) + first))
    return pairs


def multiplicities(partner, own, slots):
    expert, place = own // SPAN, own % SPAN
    start = expert * SPAN
    mine = lax.dynamic_slice_in_dim(partner, start, SPAN, 0)
    kept = jnp.sum((mine == own).astype(jnp.float32), axis=0)
    below = (mine[0] == (start - 1) % slots).astype(jnp.float32)
    above = (mine[SPAN - 1] == (start + SPAN) % slots).astype(jnp.float32)
    sent = jnp.stack([above[0], above[1], below[1], below[0]])
    return kept, sent[place]


def dot(a, b):
    return jnp.dot(a, b, preferred_element_type=jnp.float32)


def body(tokens, route, gate_prob, w_gate, w_up, w_down, partner):
    slots = lax.axis_size(EVERY)
    own = lax.axis_index(EVERY)
    experts = slots // SPAN
    place = lax.axis_index("x")
    width = tokens.shape[1]
    w_gate, w_up, w_down = w_gate[0], w_up[0], w_down[0]
    hidden = w_gate.shape[1]

    flat_route = route.reshape(-1)
    onehot = (flat_route[:, None] == jnp.arange(experts, dtype=jnp.int32)[None, :]).astype(jnp.int32)
    rank = jnp.sum(jnp.cumsum(onehot, axis=0) * onehot, axis=1) - 1
    row = flat_route * CAPACITY + rank
    rows = experts * CAPACITY
    picker = (jnp.arange(rows, dtype=jnp.int32)[:, None] == row[None, :]).astype(jnp.bfloat16)
    outgoing = dot(picker, tokens).astype(jnp.bfloat16)
    tiled = (experts, CAPACITY, width // LANES, LANES)
    outgoing = outgoing.reshape(tiled)
    inner = hidden // 2
    inward_gate = lax.ppermute(w_gate[:, inner:], "x", INWARD)
    inward_up = lax.ppermute(w_up[:, inner:], "x", INWARD)
    arrived = lax.all_to_all(outgoing, PLANE, 0, 0, tiled=True)
    straight, turned = passing(3, 0, experts), passing(2, 1, experts)
    outer_gate = lax.ppermute(w_gate[:, :inner], EVERY, straight)
    outer_up = lax.ppermute(w_up[:, :inner], EVERY, straight)
    outer_down = lax.ppermute(w_down[:inner], EVERY, straight)
    inner_gate = lax.ppermute(inward_gate, EVERY, turned)
    mid = arrived.reshape(rows, width)
    half = rows // 2

    mirror = lax.ppermute(mid, "x", MIRROR)
    side_a = lax.ppermute(mid[:half], "x", SIDE)
    side_b = lax.ppermute(mid[half:], "x", SIDE)
    cut = inner + inner // 2
    inward_down = [lax.ppermute(w, "x", INWARD) for w in (w_down[inner:cut], w_down[cut:])]
    inner_up = lax.ppermute(inward_up, EVERY, turned)
    far_a = lax.ppermute(side_a, "x", MIRROR)
    far_b = lax.ppermute(side_b, "x", MIRROR)
    inner_down = [lax.ppermute(w, EVERY, turned) for w in inward_down]

    kept, edge = multiplicities(partner, own, slots)
    scale = jnp.repeat(kept, inner)[None, :]
    outer = (place == 0) | (place == SPAN - 1)
    edge_into = jnp.concatenate(
        [jnp.where(outer, outer_gate, inner_gate), jnp.where(outer, outer_up, inner_up)], axis=1
    )
    blocks = [
        jnp.concatenate([far_a, far_b], axis=0),
        mirror,
        jnp.concatenate([side_a, side_b], axis=0),
        mid,
    ]

    def hidden_of(block):
        own_hidden = jax.nn.silu(dot(block, w_gate)) * dot(block, w_up) * scale
        both = dot(block, edge_into)
        edge_hidden = jax.nn.silu(both[:, :inner]) * both[:, inner:] * edge
        return jnp.concatenate([own_hidden, edge_hidden], axis=1).astype(jnp.bfloat16)

    tied = lax.optimization_barrier((*inner_down, outer_down, *[hidden_of(block) for block in blocks]))
    inner_down = jnp.concatenate(tied[:2], axis=0)
    down = jnp.concatenate([w_down, jnp.where(outer, tied[2], inner_down)], axis=0)
    far, mirror, side, home = [dot(h, down).astype(jnp.bfloat16) for h in tied[3:]]

    def added(u, v):
        return (u.astype(jnp.float32) + v.astype(jnp.float32)).astype(jnp.bfloat16)

    far_a = lax.ppermute(far[:half], "x", MIRROR)
    far_b = lax.ppermute(far[half:], "x", SIDE)
    mirror_a = lax.ppermute(mirror[:half], "x", MIRROR)
    side_b = lax.ppermute(side[half:], "x", SIDE)
    side_a = lax.ppermute(added(side[:half], far_a), "x", SIDE)
    mirror_b = lax.ppermute(added(mirror[half:], far_b), "x", MIRROR)
    f32 = jnp.float32
    total_a = home[:half].astype(f32) + mirror_a.astype(f32) + side_a.astype(f32)
    total_b = home[half:].astype(f32) + mirror_b.astype(f32) + side_b.astype(f32)
    total = jnp.concatenate([total_a, total_b], axis=0).astype(jnp.bfloat16)
    returned = lax.all_to_all(total.reshape(tiled), PLANE, 0, 0, tiled=True).reshape(rows, width)
    expert_out = lax.dot_general(picker, returned, (((0,), (0,)), ((), ())), preferred_element_type=f32)
    return (expert_out * gate_prob.reshape(-1)[:, None]).astype(jnp.bfloat16)


def solution(mesh):
    grid = Mesh(mesh.devices.reshape(2, 4, 2, 2, 4), EVERY)
    spec2, spec3 = P(EVERY, None), P(EVERY, None, None)
    return jax.shard_map(
        body,
        mesh=grid,
        in_specs=(spec2, spec2, spec2, spec3, spec3, spec3, P()),
        out_specs=spec2,
        check_vma=False,
    )
```

time: 422 us -> 425 us (level)
  starting transfers between devices: 45.2 us -> 70.8 us
  other arithmetic: 21.3 us -> 9.2 us
  blocking collectives: 48.3 us -> 38.3 us
    ppermute x20 -> x22, waiting for transfers between devices: 263 us -> 219 us  [the longest x1 47.2 us: body(): mirror = lax.ppermute(mid, 'x', MIRROR)]
    all_to_all x1, waiting for transfers between devices: 0.01 us -> 43.5 us  [body(): arrived = lax.all_to_all(outgoing, PLANE, 0, 0, tiled=True)]
    ppermute x20 -> x22, starting transfers between devices: 37 us -> 61.9 us  [the longest x1 25.9 us: body(): mirror = lax.ppermute(mid, 'x', MIRROR)]
    concatenate x4 -> x3, other arithmetic: 11.3 us -> 0.06 us  [hidden_of(): jnp.concatenate([own_hidden, edge_hidden], axis=1).astype(jnp.bfloat16)]
    all_to_all x1, blocking collectives: 48.3 us -> 38.3 us  [body(): lax.all_to_all(total.reshape(tiled), PLANE, 0, 0, tiled=True)]
    select_n x4 -> x3, other arithmetic: 7.12 us -> 2.39 us  [the longest x1 1.75 us: body(): jnp.where(outer, outer_up, inner_up)]
    slice x7 -> x9, local copies, waits for them, and re-layouts: 12.7 us -> 13.4 us  [the longest x1 4.26 us: body(): inward_up = lax.ppermute(w_up[:, inner:], 'x', INWARD)]
  transfers between devices with their start and end apart: 21 -> 23, of which waited for: 9 -> 13; matrix products, arithmetic and copies ran while one was open for 9% -> 9% of each run, Pallas kernels for 0% -> 0%
where the time goes in v4:
time: 425 us; the launch traced here: 422 us
  waiting for transfers between devices  262 us (62%)
  starting transfers between devices  70.8 us (17%)
  blocking collectives  38.3 us (9%)
  local copies, waits for them, and re-layouts  22.2 us (5%)
  matrix products  18.3 us (4%)
  other arithmetic  9.2 us (2%)
    ppermute x1, waiting for transfers between devices, body(): mirror = lax.ppermute(mid, 'x', MIRROR)  47.2 us
    all_to_all x1, waiting for transfers between devices, body(): arrived = lax.all_to_all(outgoing, PLANE, 0, 0, tiled=True)  43.5 us
    all_to_all x1, blocking collectives, body(): lax.all_to_all(total.reshape(tiled), PLANE, 0, 0, tiled=True)  38.3 us
    ppermute x2, waiting for transfers between devices, body(): lax.ppermute(w, 'x', INWARD)  29 us
    ppermute x1, waiting for transfers between devices, body(): far_a = lax.ppermute(far[:half], 'x', MIRROR)  28.3 us
    ppermute x1, starting transfers between devices, body(): mirror = lax.ppermute(mid, 'x', MIRROR)  25.9 us
    ppermute x1, waiting for transfers between devices, body(): side_b = lax.ppermute(mid[half:], 'x', SIDE)  22.4 us
    ppermute x1, waiting for transfers between devices, body(): side_a = lax.ppermute(mid[:half], 'x', SIDE)  19.7 us
  transfers between devices with their start and end apart: 23, of which 13 were waited for; matrix products, arithmetic and copies ran while one was open for 9% of the time, Pallas kernels for 0%

profile of v4, /device:TPU:7, one launch (start us, length us, event | category | flops | bytes accessed | tf_op | source)
XLA Modules:
  0.0 421.7 jit_solution(10340116590155400597)
XLA Ops:
  0.0 4.3 %fusion.45 = (bf16[7168,128]{1,0:T(8,128)(2,1)}, bf16[7168,128]{1,0:T(8,128)(2,1)}) fusion(bf16[7168,256]{1,0:T(8,128)(2,1)} %bitcast.93), kind=kLoop, calls=%fused_computation.87 | loop fusion | bytes 7340032 | tf_op jit(solution)/shard_map/slice | solution.py:60
  4.3 3.7 collective-permute-start.13
  8.0 3.5 collective-permute-start.12
  11.5 2.2 fusion.44
  13.7 2.6 collective-permute-start.10
  17.5 1.9 copy.8
  19.4 8.9 %all-to-all-start = ((bf16[32,5,56,128]{3,2,1,0:T(8,128)(2,1)}), bf16[32,5,56,128]{3,2,1,0:T(8,128)(2,1)S(1)}, u32[]{:S(2)}, u32[]{:S(2)}) async-start(bf16[32,5,56,128]{3,2,1,0:T(8,128)(2,1)} %bitcast.89), calls=%async_computation | async-start | bytes 4587520 | tf_op jit(solution)/shard_map/all_to_all | solution.py:61
  28.4 2.8 slice_bitcast_fusion.1
  31.5 2.8 slice_bitcast_fusion
  34.9 43.5 %all-to-all-done = bf16[32,5,56,128]{3,2,1,0:T(8,128)(2,1)S(1)} async-done(((bf16[32,5,56,128]{3,2,1,0:T(8,128)(2,1)}), bf16[32,5,56,128]{3,2,1,0:T(8,128)(2,1)S(1)}, u32[]{:S(2)}, u32[]{:S(2)}) %all-to-all-start) | async-done | bytes 2293792 | tf_op jit(solution)/shard_map/all_to_all | solution.py:61
  78.8 1.2 copy.26
  80.0 1.3 pad_maximum_fusion.6
  82.7 1.5 collective-permute-start.7
  86.5 3.4 collective-permute-start
  89.9 19.7 %collective-permute-done.5 = bf16[80,7168]{1,0:T(8,128)(2,1)} collective-permute-done((bf16[80,7168]{1,0:T(8,128)(2,1)}, bf16[80,7168]{1,0:T(8,128)(2,1)}, u32[]{:S(2)}, u32[]{:S(2)}) %collective-permute-start.5) | collective-permute-done | bytes 1146912 | tf_op jit(solution)/shard_map/ppermute | solution.py:71
  109.6 0.8 collective-permute-start.14
  110.4 1.3 constant_dynamic-update-slice_fusion.3
  111.7 22.4 %collective-permute-done.7 = bf16[80,7168]{1,0:T(8,128)(2,1)S(1)} collective-permute-done((bf16[80,7168]{1,0:T(8,128)(2,1)S(1)}, bf16[80,7168]{1,0:T(8,128)(2,1)S(1)}, u32[]{:S(2)}, u32[]{:S(2)}) %collective-permute-start.7) | collective-permute-done | bytes 1146912 | tf_op jit(solution)/shard_map/ppermute | solution.py:72
  134.1 4.2 collective-permute-start.2
  139.1 14.6 %collective-permute-done = bf16[64,7168]{1,0:T(8,128)(2,1)S(1)} collective-permute-done((bf16[64,7168]{1,0:T(8,128)(2,1)S(1)}, bf16[64,7168]{1,0:T(8,128)(2,1)S(1)}, u32[]{:S(2)}, u32[]{:S(2)}) %collective-permute-start) | collective-permute-done | bytes 917536 | tf_op jit(solution)/shard_map/ppermute | solution.py:74
  153.8 3.7 collective-permute-start.9
  157.4 0.8 collective-permute-start.11
  159.0 14.4 %collective-permute-done.2 = bf16[64,7168]{1,0:T(8,128)(2,1)S(1)} collective-permute-done((bf16[64,7168]{1,0:T(8,128)(2,1)S(1)}, bf16[64,7168]{1,0:T(8,128)(2,1)S(1)}, u32[]{:S(2)}, u32[]{:S(2)}) %collective-permute-start.2) | collective-permute-done | bytes 917536 | tf_op jit(solution)/shard_map/ppermute | solution.py:74
  173.4 3.5 collective-permute-start.4
  178.4 1.8 broadcast_select_fusion
  180.2 13.9 %collective-permute-done.9 = bf16[7168,128]{1,0:T(8,128)(2,1)S(1)} collective-permute-done((bf16[7168,128]{1,0:T(8,128)(2,1)S(1)}, bf16[7168,128]{1,0:T(8,128)(2,1)S(1)}, u32[]{:S(2)}, u32[]{:S(2)}) %collective-permute-start.9) | collective-permute-done | bytes 1835040 | tf_op jit(solution)/shard_map/ppermute | solution.py:63
  194.1 25.9 %collective-permute-start.15 = (bf16[160,7168]{1,0:T(8,128)(2,1)S(1)}, bf16[160,7168]{1,0:T(8,128)(2,1)S(1)}, u32[]{:S(2)}, u32[]{:S(2)}) collective-permute-start(bf16[160,7168]{1,0:T(8,128)(2,1)S(1)} %bitcast.98), channel_id=1, source_target_pairs={{0,3},{3,0},{1,2},{2,1},{4,7},{7,4},{5,6},{6,5},{8,11},{11,8},{9,1... | collective-permute-start | bytes 6881288 | tf_op jit(solution)/shard_map/ppermute | solution.py:70
  223.2 47.2 %collective-permute-done.15 = bf16[160,7168]{1,0:T(8,128)(2,1)S(1)} collective-permute-done((bf16[160,7168]{1,0:T(8,128)(2,1)S(1)}, bf16[160,7168]{1,0:T(8,128)(2,1)S(1)}, u32[]{:S(2)}, u32[]{:S(2)}) %collective-permute-start.15) | collective-permute-done | bytes 2293792 | tf_op jit(solution)/shard_map/ppermute | solution.py:70
  270.4 2.7 collective-permute-start.8
  275.4 15.5 %collective-permute-done.6 = bf16[80,7168]{1,0:T(8,128)(2,1)S(1)} collective-permute-done((bf16[80,7168]{1,0:T(8,128)(2,1)}, bf16[80,7168]{1,0:T(8,128)(2,1)S(1)}, u32[]{:S(2)}, u32[]{:S(2)}) %collective-permute-start.6) | collective-permute-done | bytes 1146912 | tf_op jit(solution)/shard_map/ppermute | solution.py:76
  290.9 14.1 %collective-permute-done.8 = bf16[80,7168]{1,0:T(8,128)(2,1)S(1)} collective-permute-done((bf16[80,7168]{1,0:T(8,128)(2,1)S(1)}, bf16[80,7168]{1,0:T(8,128)(2,1)S(1)}, u32[]{:S(2)}, u32[]{:S(2)}) %collective-permute-start.8) | collective-permute-done | bytes 1146912 | tf_op jit(solution)/shard_map/ppermute | solution.py:77
  305.9 0.8 fusion.43
  307.4 0.8 fusion.38
  308.3 0.8 multiply_convert_fusion.2
  309.6 1.6 copy-done.5
  311.2 1.6 convolution_convert_fusion
  313.0 1.6 convolution_convert_fusion.2
  314.7 2.8 collective-permute-start.16
  317.5 1.6 convolution_convert_fusion.1
  319.2 0.9 collective-permute-start.21
  320.1 15.6 %collective-permute-done.19 = bf16[80,7168]{1,0:T(8,128)(2,1)S(1)} collective-permute-done((bf16[80,7168]{1,0:T(8,128)(2,1)S(1)}, bf16[80,7168]{1,0:T(8,128)(2,1)S(1)}, u32[]{:S(2)}, u32[]{:S(2)}) %collective-permute-start.19) | collective-permute-done | bytes 1146912 | tf_op jit(solution)/shard_map/ppermute | solution.py:108
  336.2 28.3 %collective-permute-done.17 = bf16[80,7168]{1,0:T(8,128)(2,1)S(1)} collective-permute-done((bf16[80,7168]{1,0:T(8,128)(2,1)S(1)}, bf16[80,7168]{1,0:T(8,128)(2,1)S(1)}, u32[]{:S(2)}, u32[]{:S(2)}) %collective-permute-start.17) | collective-permute-done | bytes 1146912 | tf_op jit(solution)/shard_map/ppermute | solution.py:107
  364.9 1.6 convolution_convert_fusion.3
  366.6 10.3 %collective-permute-done.20 = bf16[80,7168]{1,0:T(8,128)(2,1)S(1)} collective-permute-done((bf16[80,7168]{1,0:T(8,128)(2,1)S(1)}, bf16[80,7168]{1,0:T(8,128)(2,1)S(1)}, u32[]{:S(2)}, u32[]{:S(2)}) %collective-permute-start.20) | collective-permute-done | bytes 1146912 | tf_op jit(solution)/shard_map/ppermute | solution.py:112
  376.9 2.8 collective-permute-done.18
  379.6 1.1 add_convert_fusion.2
  381.5 38.3 %all_to_all.10 = bf16[32,5,56,128]{3,2,1,0:T(8,128)(2,1)S(1)} all-to-all(bf16[32,5,56,128]{3,2,1,0:T(8,128)(2,1)S(1)} %bitcast.90), channel_id=1, replica_groups=mesh['zh'=2,'y'=4,'c'=2,'zl'=2,'x'=4] {'zh','y','c','zl'}, dimensions={0} | all-to-all | bytes 4587520 | tf_op jit(solution)/shard_map/all_to_all | solution.py:117
  419.8 1.9 fusion
  (85 shorter events, 18.8 us)
Async XLA Ops:
  0.0 16.8 %copy-start = (bf16[128,7168]{1,0:T(8,128)(2,1)S(1)}, bf16[128,7168]{1,0:T(8,128)(2,1)}, u32[]{:S(2)}) copy-start(bf16[128,7168]{1,0:T(8,128)(2,1)} %param.7) | copy-start | bytes 5505028
  0.0 11.5 %copy-start.2 = (bf16[1,7168,256]{2,1,0:T(8,128)(2,1)S(1)}, bf16[1,7168,256]{2,1,0:T(8,128)(2,1)}, u32[]{:S(2)}) copy-start(bf16[1,7168,256]{2,1,0:T(8,128)(2,1)} %param.10) | copy-start | bytes 11010052
  4.3 81.9 %collective-permute-start.13 = (bf16[7168,128]{1,0:T(8,128)(2,1)}, bf16[7168,128]{1,0:T(8,128)(2,1)}, u32[]{:S(2)}, u32[]{:S(2)}) collective-permute-start(bf16[7168,128]{1,0:T(8,128)(2,1)} %get-tuple-element.23), channel_id=1, source_target_pairs={{0,1},{3,2},{4,5},{7,6},{8,9},{11,10},{12,13},{15,14},{16,17},{19,... | collective-permute-start | bytes 5505032 | tf_op jit(solution)/shard_map/ppermute | solution.py:60
  8.0 169.0 %collective-permute-start.12 = (bf16[7168,128]{1,0:T(8,128)(2,1)}, bf16[7168,128]{1,0:T(8,128)(2,1)}, u32[]{:S(2)}, u32[]{:S(2)}) collective-permute-start(bf16[7168,128]{1,0:T(8,128)(2,1)} %get-tuple-element.24), channel_id=1, source_target_pairs={{3,7},{0,124},{7,11},{4,0},{11,15},{8,4},{15,19},{12,8},{19,23},{1... | collective-permute-start | bytes 5505032 | tf_op jit(solution)/shard_map/ppermute | solution.py:64
  11.5 4.8 %copy-start.10 = (s32[128,1]{0,1:T(1,128)S(1)}, s32[128,1]{0,1:T(1,128)}, u32[]{:S(2)}) copy-start(s32[128,1]{0,1:T(1,128)} %param.8) | copy-start | bytes 1540
  13.7 143.7 %collective-permute-start.10 = (bf16[7168,128]{1,0:T(8,128)(2,1)}, bf16[7168,128]{1,0:T(8,128)(2,1)}, u32[]{:S(2)}, u32[]{:S(2)}) collective-permute-start(bf16[7168,128]{1,0:T(8,128)(2,1)} %get-tuple-element.21), channel_id=1, source_target_pairs={{0,1},{3,2},{4,5},{7,6},{8,9},{11,10},{12,13},{15,14},{16,17},{19,... | collective-permute-start | bytes 5505032 | tf_op jit(solution)/shard_map/ppermute | solution.py:59
  19.4 59.0 %all-to-all-start = ((bf16[32,5,56,128]{3,2,1,0:T(8,128)(2,1)}), bf16[32,5,56,128]{3,2,1,0:T(8,128)(2,1)S(1)}, u32[]{:S(2)}, u32[]{:S(2)}) async-start(bf16[32,5,56,128]{3,2,1,0:T(8,128)(2,1)} %bitcast.89), calls=%async_computation | async-start | bytes 4587520 | tf_op jit(solution)/shard_map/all_to_all | solution.py:61
  28.3 2.9 copy-start.11
  80.0 29.6 %collective-permute-start.5 = (bf16[80,7168]{1,0:T(8,128)(2,1)}, bf16[80,7168]{1,0:T(8,128)(2,1)}, u32[]{:S(2)}, u32[]{:S(2)}) collective-permute-start(bf16[80,7168]{1,0:T(8,128)(2,1)} %bitcast.83), channel_id=1, source_target_pairs={{0,1},{1,0},{2,3},{3,2},{4,5},{5,4},{6,7},{7,6},{8,9},{9,8},{10,11... | collective-permute-start | bytes 3440648 | tf_op jit(solution)/shard_map/ppermute | solution.py:71
  82.0 2.2 copy-start.3
  82.7 2.7 copy-start.4
  82.7 51.4 %collective-permute-start.7 = (bf16[80,7168]{1,0:T(8,128)(2,1)S(1)}, bf16[80,7168]{1,0:T(8,128)(2,1)S(1)}, u32[]{:S(2)}, u32[]{:S(2)}) collective-permute-start(bf16[80,7168]{1,0:T(8,128)(2,1)S(1)} %bitcast.100), channel_id=1, source_target_pairs={{0,1},{1,0},{2,3},{3,2},{4,5},{5,4},{6,7},{7,6},{8,9},{9,8},{10,11... | collective-permute-start | bytes 3440648 | tf_op jit(solution)/shard_map/ppermute | solution.py:72
  85.3 1.2 copy-start.9
  86.1 48.0 %copy-start.8 = (bf16[64,7168]{1,0:T(8,128)(2,1)S(1)}, bf16[64,7168]{1,0:T(8,128)(2,1)}, u32[]{:S(2)}) copy-start(bf16[64,7168]{1,0:T(8,128)(2,1)} %get-tuple-element.25) | copy-start | bytes 2752516
  86.5 67.2 %collective-permute-start = (bf16[64,7168]{1,0:T(8,128)(2,1)S(1)}, bf16[64,7168]{1,0:T(8,128)(2,1)S(1)}, u32[]{:S(2)}, u32[]{:S(2)}) collective-permute-start(bf16[64,7168]{1,0:T(8,128)(2,1)S(1)} %copy-done.9), channel_id=1, source_target_pairs={{0,1},{3,2},{4,5},{7,6},{8,9},{11,10},{12,13},{15,14},{16,17},{19,... | collective-permute-start | bytes 2752520 | tf_op jit(solution)/shard_map/ppermute | solution.py:74
  109.6 68.1 %collective-permute-start.14 = (bf16[7168,128]{1,0:T(8,128)(2,1)}, bf16[7168,128]{1,0:T(8,128)(2,1)S(1)}, u32[]{:S(2)}, u32[]{:S(2)}) collective-permute-start(bf16[7168,128]{1,0:T(8,128)(2,1)} %collective-permute-done.13), channel_id=1, source_target_pairs={{2,6},{1,125},{6,10},{5,1},{10,14},{9,5},{14,18},{13,9},{18,22},{1... | collective-permute-start | bytes 5505032 | tf_op jit(solution)/shard_map/ppermute | solution.py:75
  134.1 39.3 %collective-permute-start.2 = (bf16[64,7168]{1,0:T(8,128)(2,1)S(1)}, bf16[64,7168]{1,0:T(8,128)(2,1)S(1)}, u32[]{:S(2)}, u32[]{:S(2)}) collective-permute-start(bf16[64,7168]{1,0:T(8,128)(2,1)S(1)} %copy-done.8), channel_id=1, source_target_pairs={{0,1},{3,2},{4,5},{7,6},{8,9},{11,10},{12,13},{15,14},{16,17},{19,... | collective-permute-start | bytes 2752520 | tf_op jit(solution)/shard_map/ppermute | solution.py:74
  138.3 15.4 %copy-start.6 = (bf16[7168,128]{1,0:T(8,128)(2,1)S(1)}, bf16[7168,128]{1,0:T(8,128)(2,1)}, u32[]{:S(2)}) copy-start(bf16[7168,128]{1,0:T(8,128)(2,1)} %get-tuple-element.22) | copy-start | bytes 5505028
  153.7 19.7 %copy-start.7 = (bf16[128,7168]{1,0:T(8,128)(2,1)S(1)}, bf16[128,7168]{1,0:T(8,128)(2,1)}, u32[]{:S(2)}) copy-start(bf16[128,7168]{1,0:T(8,128)(2,1)} %slice_bitcast_fusion) | copy-start | bytes 5505028
  153.8 40.4 %collective-permute-start.9 = (bf16[7168,128]{1,0:T(8,128)(2,1)S(1)}, bf16[7168,128]{1,0:T(8,128)(2,1)S(1)}, u32[]{:S(2)}, u32[]{:S(2)}) collective-permute-start(bf16[7168,128]{1,0:T(8,128)(2,1)S(1)} %copy-done.6), channel_id=1, source_target_pairs={{3,7},{0,124},{7,11},{4,0},{11,15},{8,4},{15,19},{12,8},{19,23},{1... | collective-permute-start | bytes 5505032 | tf_op jit(solution)/shard_map/ppermute | solution.py:63
  157.4 62.6 %collective-permute-start.11 = (bf16[7168,128]{1,0:T(8,128)(2,1)}, bf16[7168,128]{1,0:T(8,128)(2,1)S(1)}, u32[]{:S(2)}, u32[]{:S(2)}) collective-permute-start(bf16[7168,128]{1,0:T(8,128)(2,1)} %collective-permute-done.10), channel_id=1, source_target_pairs={{2,6},{1,125},{6,10},{5,1},{10,14},{9,5},{14,18},{13,9},{18,22},{1... | collective-permute-start | bytes 5505032 | tf_op jit(solution)/shard_map/ppermute | solution.py:66
  173.4 135.7 %collective-permute-start.4 = (bf16[128,7168]{1,0:T(8,128)(2,1)S(1)}, bf16[128,7168]{1,0:T(8,128)(2,1)S(1)}, u32[]{:S(2)}, u32[]{:S(2)}) collective-permute-start(bf16[128,7168]{1,0:T(8,128)(2,1)S(1)} %copy-done.7), channel_id=1, source_target_pairs={{3,7},{0,124},{7,11},{4,0},{11,15},{8,4},{15,19},{12,8},{19,23},{1... | collective-permute-start | bytes 5505032 | tf_op jit(solution)/shard_map/ppermute | solution.py:65
  177.0 132.1 %collective-permute-start.1 = (bf16[64,7168]{1,0:T(8,128)(2,1)S(1)}, bf16[64,7168]{1,0:T(8,128)(2,1)S(1)}, u32[]{:S(2)}, u32[]{:S(2)}) collective-permute-start(bf16[64,7168]{1,0:T(8,128)(2,1)S(1)} %collective-permute-done), channel_id=1, source_target_pairs={{2,6},{1,125},{6,10},{5,1},{10,14},{9,5},{14,18},{13,9},{18,22},{1... | collective-permute-start | bytes 2752520 | tf_op jit(solution)/shard_map/ppermute | solution.py:78
  177.7 131.4 %collective-permute-start.3 = (bf16[64,7168]{1,0:T(8,128)(2,1)S(1)}, bf16[64,7168]{1,0:T(8,128)(2,1)S(1)}, u32[]{:S(2)}, u32[]{:S(2)}) collective-permute-start(bf16[64,7168]{1,0:T(8,128)(2,1)S(1)} %collective-permute-done.2), channel_id=1, source_target_pairs={{2,6},{1,125},{6,10},{5,1},{10,14},{9,5},{14,18},{13,9},{18,22},{1... | collective-permute-start | bytes 2752520 | tf_op jit(solution)/shard_map/ppermute | solution.py:78
  194.1 76.3 %collective-permute-start.15 = (bf16[160,7168]{1,0:T(8,128)(2,1)S(1)}, bf16[160,7168]{1,0:T(8,128)(2,1)S(1)}, u32[]{:S(2)}, u32[]{:S(2)}) collective-permute-start(bf16[160,7168]{1,0:T(8,128)(2,1)S(1)} %bitcast.98), channel_id=1, source_target_pairs={{0,3},{3,0},{1,2},{2,1},{4,7},{7,4},{5,6},{6,5},{8,11},{11,8},{9,1... | collective-permute-start | bytes 6881288 | tf_op jit(solution)/shard_map/ppermute | solution.py:70
  220.0 70.9 %collective-permute-start.6 = (bf16[80,7168]{1,0:T(8,128)(2,1)}, bf16[80,7168]{1,0:T(8,128)(2,1)S(1)}, u32[]{:S(2)}, u32[]{:S(2)}) collective-permute-start(bf16[80,7168]{1,0:T(8,128)(2,1)} %collective-permute-done.5), channel_id=1, source_target_pairs={{0,3},{3,0},{1,2},{2,1},{4,7},{7,4},{5,6},{6,5},{8,11},{11,8},{9,1... | collective-permute-start | bytes 3440648 | tf_op jit(solution)/shard_map/ppermute | solution.py:76
  270.4 34.7 %collective-permute-start.8 = (bf16[80,7168]{1,0:T(8,128)(2,1)S(1)}, bf16[80,7168]{1,0:T(8,128)(2,1)S(1)}, u32[]{:S(2)}, u32[]{:S(2)}) collective-permute-start(bf16[80,7168]{1,0:T(8,128)(2,1)S(1)} %collective-permute-done.7), channel_id=1, source_target_pairs={{0,3},{3,0},{1,2},{2,1},{4,7},{7,4},{5,6},{6,5},{8,11},{11,8},{9,1... | collective-permute-start | bytes 3440648 | tf_op jit(solution)/shard_map/ppermute | solution.py:77
  309.1 2.0 copy-start.5
  312.9 22.8 %collective-permute-start.19 = (bf16[80,7168]{1,0:T(8,128)(2,1)S(1)}, bf16[80,7168]{1,0:T(8,128)(2,1)S(1)}, u32[]{:S(2)}, u32[]{:S(2)}) collective-permute-start(bf16[80,7168]{1,0:T(8,128)(2,1)S(1)} %get-tuple-element.30), channel_id=1, source_target_pairs={{0,1},{1,0},{2,3},{3,2},{4,5},{5,4},{6,7},{7,6},{8,9},{9,8},{10,11... | collective-permute-start | bytes 3440648 | tf_op jit(solution)/shard_map/ppermute | solution.py:108
  314.7 51.9 %collective-permute-start.16 = (bf16[80,7168]{1,0:T(8,128)(2,1)S(1)}, bf16[80,7168]{1,0:T(8,128)(2,1)S(1)}, u32[]{:S(2)}, u32[]{:S(2)}) collective-permute-start(bf16[80,7168]{1,0:T(8,128)(2,1)S(1)} %slice.162), channel_id=1, source_target_pairs={{0,3},{3,0},{1,2},{2,1},{4,7},{7,4},{5,6},{6,5},{8,11},{11,8},{9,1... | collective-permute-start | bytes 3440648 | tf_op jit(solution)/shard_map/ppermute | solution.py:109
  317.4 47.1 %collective-permute-start.17 = (bf16[80,7168]{1,0:T(8,128)(2,1)S(1)}, bf16[80,7168]{1,0:T(8,128)(2,1)S(1)}, u32[]{:S(2)}, u32[]{:S(2)}) collective-permute-start(bf16[80,7168]{1,0:T(8,128)(2,1)S(1)} %get-tuple-element.29), channel_id=1, source_target_pairs={{0,3},{3,0},{1,2},{2,1},{4,7},{7,4},{5,6},{6,5},{8,11},{11,8},{9,1... | collective-permute-start | bytes 3440648 | tf_op jit(solution)/shard_map/ppermute | solution.py:107
  319.2 47.4 %collective-permute-start.21 = (bf16[80,7168]{1,0:T(8,128)(2,1)S(1)}, bf16[80,7168]{1,0:T(8,128)(2,1)S(1)}, u32[]{:S(2)}, u32[]{:S(2)}) collective-permute-start(bf16[80,7168]{1,0:T(8,128)(2,1)S(1)} %slice.168), channel_id=1, source_target_pairs={{0,1},{1,0},{2,3},{3,2},{4,5},{5,4},{6,7},{7,6},{8,9},{9,8},{10,11... | collective-permute-start | bytes 3440648 | tf_op jit(solution)/shard_map/ppermute | solution.py:110
  336.0 40.9 %collective-permute-start.20 = (bf16[80,7168]{1,0:T(8,128)(2,1)S(1)}, bf16[80,7168]{1,0:T(8,128)(2,1)S(1)}, u32[]{:S(2)}, u32[]{:S(2)}) collective-permute-start(bf16[80,7168]{1,0:T(8,128)(2,1)S(1)} %add_convert_fusion.1), channel_id=1, source_target_pairs={{0,3},{3,0},{1,2},{2,1},{4,7},{7,4},{5,6},{6,5},{8,11},{11,8},{9,1... | collective-permute-start | bytes 3440648 | tf_op jit(solution)/shard_map/ppermute | solution.py:112
  364.9 14.8 %collective-permute-start.18 = (bf16[80,7168]{1,0:T(8,128)(2,1)S(1)}, bf16[80,7168]{1,0:T(8,128)(2,1)S(1)}, u32[]{:S(2)}, u32[]{:S(2)}) collective-permute-start(bf16[80,7168]{1,0:T(8,128)(2,1)S(1)} %add_convert_fusion.3), channel_id=1, source_target_pairs={{0,1},{1,0},{2,3},{3,2},{4,5},{5,4},{6,7},{7,6},{8,9},{9,8},{10,11... | collective-permute-start | bytes 3440648 | tf_op jit(solution)/shard_map/ppermute | solution.py:111
  381.4 38.3 %copy-start.12 = (f32[128,1]{0,1:T(1,128)S(1)}, f32[128,1]{0,1:T(1,128)}, u32[]{:S(2)}) copy-start(f32[128,1]{0,1:T(1,128)} %param.9) | copy-start | bytes 1540
  381.4 40.2 %copy-start.1 = (bf16[128,7168]{1,0:T(8,128)(2,1)S(1)}, bf16[128,7168]{1,0:T(8,128)(2,1)}, u32[]{:S(2)}) copy-start(bf16[128,7168]{1,0:T(8,128)(2,1)} %param.7) | copy-start | bytes 5505028

commit v5 on v4

v5 whole, which is shorter than its diff:
```python
import jax
import jax.numpy as jnp
from jax import lax
from jax.sharding import Mesh, PartitionSpec as P


SPAN = 4
CAPACITY = 5
PLANE = ("zh", "y", "c", "zl")
EVERY = PLANE + ("x",)
LANES = 128
MIRROR = [(0, 3), (3, 0), (1, 2), (2, 1)]
SIDE = [(0, 1), (1, 0), (2, 3), (3, 2)]
INWARD = [(0, 1), (3, 2)]


def passing(last, first, experts):
    pairs = []
    for e in range(experts):
        pairs.append((SPAN * e + last, SPAN * ((e + 1) % experts) + last))
        pairs.append((SPAN * e + first, SPAN * ((e - 1) % experts) + first))
    return pairs


def multiplicities(partner, own, slots):
    expert, place = own // SPAN, own % SPAN
    start = expert * SPAN
    mine = lax.dynamic_slice_in_dim(partner, start, SPAN, 0)
    kept = jnp.sum((mine == own).astype(jnp.float32), axis=0)
    below = (mine[0] == (start - 1) % slots).astype(jnp.float32)
    above = (mine[SPAN - 1] == (start + SPAN) % slots).astype(jnp.float32)
    sent = jnp.stack([above[0], above[1], below[1], below[0]])
    return kept, sent[place]


def dot(a, b):
    return jnp.dot(a, b, preferred_element_type=jnp.float32)


def body(tokens, route, gate_prob, w_gate, w_up, w_down, partner):
    slots = lax.axis_size(EVERY)
    own = lax.axis_index(EVERY)
    experts = slots // SPAN
    place = lax.axis_index("x")
    width = tokens.shape[1]
    w_gate, w_up, w_down = w_gate[0], w_up[0], w_down[0]
    hidden = w_gate.shape[1]

    flat_route = route.reshape(-1)
    onehot = (flat_route[:, None] == jnp.arange(experts, dtype=jnp.int32)[None, :]).astype(jnp.int32)
    rank = jnp.sum(jnp.cumsum(onehot, axis=0) * onehot, axis=1) - 1
    row = flat_route * CAPACITY + rank
    rows = experts * CAPACITY
    picker = (jnp.arange(rows, dtype=jnp.int32)[:, None] == row[None, :]).astype(jnp.bfloat16)
    outgoing = dot(picker, tokens).astype(jnp.bfloat16)
    tiled = (experts, CAPACITY, width // LANES, LANES)
    outgoing = outgoing.reshape(tiled)
    inner = hidden // 2
    first_down = inner + inner * 3 // 4
    straight, turned = passing(3, 0, experts), passing(2, 1, experts)

    def cross(block):
        return lax.ppermute(block, "x", INWARD)

    def over(block, pairs):
        return lax.ppermute(block, "x", pairs)

    inward_down = cross(w_down[inner:first_down])
    inward_gate = cross(w_gate[:, inner:])
    arrived = lax.all_to_all(outgoing, PLANE, 0, 0, tiled=True)
    mid = arrived.reshape(rows, width)

    kept, edge = multiplicities(partner, own, slots)
    scale = jnp.repeat(kept, inner)[None, :]

    def own_hidden(block):
        return (jax.nn.silu(dot(block, w_gate)) * dot(block, w_up) * scale).astype(jnp.bfloat16)

    mirror = over(mid, MIRROR)
    outer_gate = lax.ppermute(w_gate[:, :inner], EVERY, straight)
    outer_up = lax.ppermute(w_up[:, :inner], EVERY, straight)
    outer_down = lax.ppermute(w_down[:inner], EVERY, straight)
    side_a = over(mid[:64], SIDE)
    inward_up = cross(w_up[:, inner:])
    side_b = over(mid[64:128], SIDE)
    side_c = over(mid[128:], SIDE)
    inward_last = cross(w_down[first_down:])
    inner_down = lax.ppermute(inward_down, EVERY, turned)
    inner_gate = lax.ppermute(inward_gate, EVERY, turned)
    far_a = over(side_a, MIRROR)
    inner_up = lax.ppermute(inward_up, EVERY, turned)
    home_own, mirror_own = own_hidden(mid), own_hidden(mirror)
    side_b, home_own, mirror_own = lax.optimization_barrier((side_b, home_own, mirror_own))
    far_b = over(side_b, MIRROR)
    far_c = over(side_c, MIRROR)
    inner_last = lax.ppermute(inward_last, EVERY, turned)

    outer = (place == 0) | (place == SPAN - 1)
    edge_into = jnp.concatenate(
        [jnp.where(outer, outer_gate, inner_gate), jnp.where(outer, outer_up, inner_up)], axis=1
    )
    side = jnp.concatenate([side_a, side_b, side_c], axis=0)
    far = jnp.concatenate([far_a, far_b, far_c], axis=0)

    def full_hidden(block, mine):
        both = dot(block, edge_into)
        edge_hidden = jax.nn.silu(both[:, :inner]) * both[:, inner:] * edge
        return jnp.concatenate([mine, edge_hidden.astype(jnp.bfloat16)], axis=1)

    pairs = ((far, own_hidden(far)), (mirror, mirror_own), (side, own_hidden(side)), (mid, home_own))
    tied = lax.optimization_barrier((inner_down, inner_last, outer_down, *[full_hidden(*p) for p in pairs]))
    edge_down = jnp.where(outer, tied[2], jnp.concatenate(tied[:2], axis=0))
    down = jnp.concatenate([w_down, edge_down], axis=0)
    far, mirror, side, home = [dot(h, down).astype(jnp.bfloat16) for h in tied[3:]]

    def added(u, v):
        return (u.astype(jnp.float32) + v.astype(jnp.float32)).astype(jnp.bfloat16)

    f32 = jnp.float32
    half = rows // 2
    upper, lower = slice(None, half), slice(half, None)
    outs = []
    for lo, hi in ((0, 4096), (4096, width)):
        cols = slice(lo, hi)
        far_a = over(far[upper, cols], MIRROR)
        far_b = over(far[lower, cols], SIDE)
        mirror_a = over(mirror[upper, cols], MIRROR)
        side_b = over(side[lower, cols], SIDE)
        side_a = over(added(side[upper, cols], far_a), SIDE)
        mirror_b = over(added(mirror[lower, cols], far_b), MIRROR)
        total_a = home[upper, cols].astype(f32) + mirror_a.astype(f32) + side_a.astype(f32)
        total_b = home[lower, cols].astype(f32) + mirror_b.astype(f32) + side_b.astype(f32)
        total = jnp.concatenate([total_a, total_b], axis=0).astype(jnp.bfloat16)
        total = total.reshape(experts, CAPACITY, (hi - lo) // LANES, LANES)
        returned = lax.all_to_all(total, PLANE, 0, 0, tiled=True).reshape(rows, hi - lo)
        expert_out = lax.dot_general(picker, returned, (((0,), (0,)), ((), ())), preferred_element_type=f32)
        outs.append((expert_out * gate_prob.reshape(-1)[:, None]).astype(jnp.bfloat16))
    return jnp.concatenate(outs, axis=1)


def solution(mesh):
    grid = Mesh(mesh.devices.reshape(2, 4, 2, 2, 4), EVERY)
    spec2, spec3 = P(EVERY, None), P(EVERY, None, None)
    return jax.shard_map(
        body,
        mesh=grid,
        in_specs=(spec2, spec2, spec2, spec3, spec3, spec3, P()),
        out_specs=spec2,
        check_vma=False,
    )
```

time: 425 us -> 436 us (1.026)
  blocking collectives: 38.3 us -> 0 us
  starting transfers between devices: 70.8 us -> 104 us
  matrix products: 18.3 us -> 25.9 us
  local copies, waits for them, and re-layouts: 22.2 us -> 28.9 us
  other arithmetic: 9.2 us -> 14.1 us
    all_to_all x1 -> x0, blocking collectives: 38.3 us -> none  [body(): lax.all_to_all(total.reshape(tiled), PLANE, 0, 0, tiled=True)]
    all_to_all x0 -> x2, starting transfers between devices: none -> 25.1 us  [body(): lax.all_to_all(total, PLANE, 0, 0, tiled=True).reshape(rows, hi - lo)]
    all_to_all x0 -> x2, waiting for transfers between devices: none -> 18 us  [body(): lax.all_to_all(total, PLANE, 0, 0, tiled=True).reshape(rows, hi - lo)]
    ppermute x1, waiting for transfers between devices: 13.9 us -> 0.01 us  [body(): outer_gate = lax.ppermute(w_gate[:, :inner], EVERY, straight)]
    all_to_all x1, waiting for transfers between devices: 43.5 us -> 31 us  [body(): arrived = lax.all_to_all(outgoing, PLANE, 0, 0, tiled=True)]
    ppermute x17 -> x25, starting transfers between devices: 49.6 us -> 56.7 us  [the longest x19 43.4 us: over(): return lax.ppermute(block, 'x', pairs)]
    dot_general x17, matrix products: 16.4 us -> 22.8 us  [dot(): return jnp.dot(a, b, preferred_element_type=jnp.float32)]
    ppermute x17 -> x25, waiting for transfers between devices: 205 us -> 210 us  [the longest x19 163 us: over(): return lax.ppermute(block, 'x', pairs)]
  transfers between devices with their start and end apart: 23 -> 33, of which waited for: 13 -> 15; matrix products, arithmetic and copies ran while one was open for 9% -> 13% of each run, Pallas kernels for 0% -> 0%
where the time goes in v5:
time: 436 us; the launch traced here: 432 us
  waiting for transfers between devices  259 us (59%)
  starting transfers between devices  104 us (24%)
  local copies, waits for them, and re-layouts  28.9 us (7%)
  matrix products  25.9 us (6%)
  other arithmetic  14.1 us (3%)
    ppermute x19, waiting for transfers between devices, over(): return lax.ppermute(block, 'x', pairs)  163 us
    ppermute x4, waiting for transfers between devices, cross(): return lax.ppermute(block, 'x', INWARD)  46.4 us
    ppermute x19, starting transfers between devices, over(): return lax.ppermute(block, 'x', pairs)  43.4 us
    all_to_all x1, waiting for transfers between devices, body(): arrived = lax.all_to_all(outgoing, PLANE, 0, 0, tiled=True)  31 us
    all_to_all x2, starting transfers between devices, body(): lax.all_to_all(total, PLANE, 0, 0, tiled=True).reshape(rows, hi - lo)  25.1 us
    dot_general x17, matrix products, dot(): return jnp.dot(a, b, preferred_element_type=jnp.float32)  22.8 us
    all_to_all x2, waiting for transfers between devices, body(): lax.all_to_all(total, PLANE, 0, 0, tiled=True).reshape(rows, hi - lo)  18 us
    unnamed x46, local copies, waits for them, and re-layouts  12.4 us
  transfers between devices with their start and end apart: 33, of which 15 were waited for; matrix products, arithmetic and copies ran while one was open for 13% of the time, Pallas kernels for 0%

profile of v5, /device:TPU:7, one launch (start us, length us, event | category | flops | bytes accessed | tf_op | source)
XLA Modules:
  0.0 432.3 jit_solution(7383559093710999491)
XLA Ops:
  0.0 4.3 fusion.49
  4.3 3.8 collective-permute-start.16
  8.1 3.5 collective-permute-start.15
  11.6 2.0 fusion.48
  13.7 2.5 collective-permute-start.13
  17.4 1.9 copy.8
  19.3 8.9 %all-to-all-start = ((bf16[32,5,56,128]{3,2,1,0:T(8,128)(2,1)}), bf16[32,5,56,128]{3,2,1,0:T(8,128)(2,1)}, u32[]{:S(2)}, u32[]{:S(2)}) async-start(bf16[32,5,56,128]{3,2,1,0:T(8,128)(2,1)} %bitcast.87), calls=%async_computation | async-start | bytes 4587520 | tf_op jit(solution)/shard_map/all_to_all | solution.py:70
  33.2 2.8 slice_bitcast_fusion
  36.0 9.7 %collective-permute-done.16 = bf16[7168,128]{1,0:T(8,128)(2,1)} collective-permute-done((bf16[7168,128]{1,0:T(8,128)(2,1)}, bf16[7168,128]{1,0:T(8,128)(2,1)}, u32[]{:S(2)}, u32[]{:S(2)}) %collective-permute-start.16) | collective-permute-done | bytes 1835040 | tf_op jit(solution)/shard_map/ppermute | solution.py:63
  45.7 1.9 collective-permute-start.17
  47.7 31.0 %all-to-all-done = bf16[32,5,56,128]{3,2,1,0:T(8,128)(2,1)} async-done(((bf16[32,5,56,128]{3,2,1,0:T(8,128)(2,1)}), bf16[32,5,56,128]{3,2,1,0:T(8,128)(2,1)}, u32[]{:S(2)}, u32[]{:S(2)}) %all-to-all-start) | async-done | bytes 2293792 | tf_op jit(solution)/shard_map/all_to_all | solution.py:70
  78.6 2.1 copy.26
  85.5 9.3 %collective-permute-done.2 = bf16[32,7168]{1,0:T(8,128)(2,1)S(1)} collective-permute-done((bf16[32,7168]{1,0:T(8,128)(2,1)S(1)}, bf16[32,7168]{1,0:T(8,128)(2,1)S(1)}, u32[]{:S(2)}, u32[]{:S(2)}) %collective-permute-start.2) | collective-permute-done | bytes 458784 | tf_op jit(solution)/shard_map/ppermute | solution.py:63
  94.8 4.2 collective-permute-start
  99.0 3.5 fusion.42
  102.6 2.6 fusion.6
  105.2 3.5 collective-permute-start.12
  108.7 5.8 %collective-permute-done.5 = bf16[64,7168]{1,0:T(8,128)(2,1)} collective-permute-done((bf16[64,7168]{1,0:T(8,128)(2,1)}, bf16[64,7168]{1,0:T(8,128)(2,1)}, u32[]{:S(2)}, u32[]{:S(2)}) %collective-permute-start.5) | collective-permute-done | bytes 917536 | tf_op jit(solution)/shard_map/ppermute | solution.py:66
  116.6 27.4 %collective-permute-done = bf16[96,7168]{1,0:T(8,128)(2,1)S(1)} collective-permute-done((bf16[96,7168]{1,0:T(8,128)(2,1)S(1)}, bf16[96,7168]{1,0:T(8,128)(2,1)S(1)}, u32[]{:S(2)}, u32[]{:S(2)}) %collective-permute-start) | collective-permute-done | bytes 1376288 | tf_op jit(solution)/shard_map/ppermute | solution.py:63
  143.9 3.5 collective-permute-start.4
  149.0 1.7 broadcast_select_fusion
  150.7 20.9 %collective-permute-start.8 = (bf16[160,7168]{1,0:T(8,128)(2,1)S(1)}, bf16[160,7168]{1,0:T(8,128)(2,1)S(1)}, u32[]{:S(2)}, u32[]{:S(2)}) collective-permute-start(bf16[160,7168]{1,0:T(8,128)(2,1)S(1)} %bitcast.86), channel_id=1, source_target_pairs={{0,3},{3,0},{1,2},{2,1},{4,7},{7,4},{5,6},{6,5},{8,11},{11,8},{9,1... | collective-permute-start | bytes 6881288 | tf_op jit(solution)/shard_map/ppermute | solution.py:66
  171.8 2.5 fusion.44
  175.1 51.5 %collective-permute-done.6 = bf16[64,7168]{1,0:T(8,128)(2,1)S(1)} collective-permute-done((bf16[64,7168]{1,0:T(8,128)(2,1)}, bf16[64,7168]{1,0:T(8,128)(2,1)S(1)}, u32[]{:S(2)}, u32[]{:S(2)}) %collective-permute-start.6) | collective-permute-done | bytes 917536 | tf_op jit(solution)/shard_map/ppermute | solution.py:66
  226.6 11.9 %collective-permute-done.10 = bf16[32,7168]{1,0:T(8,128)(2,1)S(1)} collective-permute-done((bf16[32,7168]{1,0:T(8,128)(2,1)S(1)}, bf16[32,7168]{1,0:T(8,128)(2,1)S(1)}, u32[]{:S(2)}, u32[]{:S(2)}) %collective-permute-start.10) | collective-permute-done | bytes 458784 | tf_op jit(solution)/shard_map/ppermute | solution.py:66
  238.5 3.5 collective-permute-start.11
  245.1 14.4 %collective-permute-done.7 = bf16[64,7168]{1,0:T(8,128)(2,1)S(1)} collective-permute-done((bf16[64,7168]{1,0:T(8,128)(2,1)S(1)}, bf16[64,7168]{1,0:T(8,128)(2,1)S(1)}, u32[]{:S(2)}, u32[]{:S(2)}) %collective-permute-start.7) | collective-permute-done | bytes 917536 | tf_op jit(solution)/shard_map/ppermute | solution.py:66
  259.5 2.9 collective-permute-start.9
  265.6 15.5 %collective-permute-done.9 = bf16[64,7168]{1,0:T(8,128)(2,1)S(1)} collective-permute-done((bf16[64,7168]{1,0:T(8,128)(2,1)S(1)}, bf16[64,7168]{1,0:T(8,128)(2,1)S(1)}, u32[]{:S(2)}, u32[]{:S(2)}) %collective-permute-start.9) | collective-permute-done | bytes 917536 | tf_op jit(solution)/shard_map/ppermute | solution.py:66
  285.0 1.6 copy-done.7
  286.6 1.6 convolution_convert_fusion
  288.3 1.6 convolution_convert_fusion.2
  291.2 1.6 convolution_convert_fusion.1
  295.0 3.3 collective-permute-start.19
  298.4 2.7 collective-permute-start.24
  301.0 1.6 convolution_convert_fusion.3
  302.6 1.7 collective-permute-start.25
  304.4 41.5 %collective-permute-done.25 = bf16[80,3072]{1,0:T(8,128)(2,1)S(1)} collective-permute-done((bf16[80,3072]{1,0:T(8,128)(2,1)S(1)}, bf16[80,3072]{1,0:T(8,128)(2,1)S(1)}, u32[]{:S(2)}, u32[]{:S(2)}) %collective-permute-start.25) | collective-permute-done | bytes 491552 | tf_op jit(solution)/shard_map/ppermute | solution.py:66
  346.0 2.8 collective-permute-start.28
  352.3 3.2 collective-permute-done.29
  355.4 2.7 collective-permute-start.22
  358.1 7.8 %collective-permute-done.26 = bf16[80,3072]{1,0:T(8,128)(2,1)S(1)} collective-permute-done((bf16[80,3072]{1,0:T(8,128)(2,1)S(1)}, bf16[80,3072]{1,0:T(8,128)(2,1)S(1)}, u32[]{:S(2)}, u32[]{:S(2)}) %collective-permute-start.26) | collective-permute-done | bytes 491552 | tf_op jit(solution)/shard_map/ppermute | solution.py:66
  367.6 14.9 %all-to-all-start.2 = ((bf16[32,5,24,128]{3,2,1,0:T(8,128)(2,1)}), bf16[32,5,24,128]{3,2,1,0:T(8,128)(2,1)S(1)}, u32[]{:S(2)}, u32[]{:S(2)}) async-start(bf16[32,5,24,128]{3,2,1,0:T(8,128)(2,1)} %bitcast.26), calls=%async_computation.2 | async-start | bytes 1966080 | tf_op jit(solution)/shard_map/all_to_all | solution.py:135
  382.6 11.6 %collective-permute-done.20 = bf16[80,4096]{1,0:T(8,128)(2,1)} collective-permute-done((bf16[80,4096]{1,0:T(8,128)(2,1)}, bf16[80,4096]{1,0:T(8,128)(2,1)}, u32[]{:S(2)}, u32[]{:S(2)}) %collective-permute-start.20) | collective-permute-done | bytes 655392 | tf_op jit(solution)/shard_map/ppermute | solution.py:66
  394.2 2.5 add_convert_fusion.2
  399.8 10.2 %all-to-all-start.1 = ((bf16[32,5,32,128]{3,2,1,0:T(8,128)(2,1)}), bf16[32,5,32,128]{3,2,1,0:T(8,128)(2,1)S(1)}, u32[]{:S(2)}, u32[]{:S(2)}) async-start(bf16[32,5,32,128]{3,2,1,0:T(8,128)(2,1)} %bitcast.20), calls=%async_computation.1 | async-start | bytes 2621440 | tf_op jit(solution)/shard_map/all_to_all | solution.py:135
  410.0 2.5 fusion.1
  412.5 17.3 %all-to-all-done.1 = bf16[32,5,32,128]{3,2,1,0:T(8,128)(2,1)S(1)} async-done(((bf16[32,5,32,128]{3,2,1,0:T(8,128)(2,1)}), bf16[32,5,32,128]{3,2,1,0:T(8,128)(2,1)S(1)}, u32[]{:S(2)}, u32[]{:S(2)}) %all-to-all-start.1) | async-done | bytes 1310752 | tf_op jit(solution)/shard_map/all_to_all | solution.py:135
  (127 shorter events, 40.1 us)
Async XLA Ops:
  0.0 16.6 %copy-start = (bf16[128,7168]{1,0:T(8,128)(2,1)S(1)}, bf16[128,7168]{1,0:T(8,128)(2,1)}, u32[]{:S(2)}) copy-start(bf16[128,7168]{1,0:T(8,128)(2,1)} %param.7) | copy-start | bytes 5505028
  0.0 11.6 %copy-start.2 = (bf16[1,7168,256]{2,1,0:T(8,128)(2,1)S(1)}, bf16[1,7168,256]{2,1,0:T(8,128)(2,1)}, u32[]{:S(2)}) copy-start(bf16[1,7168,256]{2,1,0:T(8,128)(2,1)} %param.10) | copy-start | bytes 11010052
  4.3 41.4 %collective-permute-start.16 = (bf16[7168,128]{1,0:T(8,128)(2,1)}, bf16[7168,128]{1,0:T(8,128)(2,1)}, u32[]{:S(2)}, u32[]{:S(2)}) collective-permute-start(bf16[7168,128]{1,0:T(8,128)(2,1)} %get-tuple-element.29), channel_id=1, source_target_pairs={{0,1},{3,2},{4,5},{7,6},{8,9},{11,10},{12,13},{15,14},{16,17},{19,... | collective-permute-start | bytes 5505032 | tf_op jit(solution)/shard_map/ppermute | solution.py:63
  8.1 139.4 %collective-permute-start.15 = (bf16[7168,128]{1,0:T(8,128)(2,1)}, bf16[7168,128]{1,0:T(8,128)(2,1)}, u32[]{:S(2)}, u32[]{:S(2)}) collective-permute-start(bf16[7168,128]{1,0:T(8,128)(2,1)} %get-tuple-element.30), channel_id=1, source_target_pairs={{3,7},{0,124},{7,11},{4,0},{11,15},{8,4},{15,19},{12,8},{19,23},{1... | collective-permute-start | bytes 5505032 | tf_op jit(solution)/shard_map/ppermute | solution.py:81
  11.6 4.6 %copy-start.14 = (s32[128,1]{0,1:T(1,128)S(1)}, s32[128,1]{0,1:T(1,128)}, u32[]{:S(2)}) copy-start(s32[128,1]{0,1:T(1,128)} %param.8) | copy-start | bytes 1540
  13.7 91.5 %collective-permute-start.13 = (bf16[7168,128]{1,0:T(8,128)(2,1)}, bf16[7168,128]{1,0:T(8,128)(2,1)}, u32[]{:S(2)}, u32[]{:S(2)}) collective-permute-start(bf16[7168,128]{1,0:T(8,128)(2,1)} %get-tuple-element.27), channel_id=1, source_target_pairs={{0,1},{3,2},{4,5},{7,6},{8,9},{11,10},{12,13},{15,14},{16,17},{19,... | collective-permute-start | bytes 5505032 | tf_op jit(solution)/shard_map/ppermute | solution.py:63
  19.3 59.3 %all-to-all-start = ((bf16[32,5,56,128]{3,2,1,0:T(8,128)(2,1)}), bf16[32,5,56,128]{3,2,1,0:T(8,128)(2,1)}, u32[]{:S(2)}, u32[]{:S(2)}) async-start(bf16[32,5,56,128]{3,2,1,0:T(8,128)(2,1)} %bitcast.87), calls=%async_computation | async-start | bytes 4587520 | tf_op jit(solution)/shard_map/all_to_all | solution.py:70
  28.2 3.9 copy-start.15
  29.3 65.5 %collective-permute-start.2 = (bf16[32,7168]{1,0:T(8,128)(2,1)S(1)}, bf16[32,7168]{1,0:T(8,128)(2,1)S(1)}, u32[]{:S(2)}, u32[]{:S(2)}) collective-permute-start(bf16[32,7168]{1,0:T(8,128)(2,1)S(1)} %slice_bitcast_fusion.2), channel_id=1, source_target_pairs={{0,1},{3,2},{4,5},{7,6},{8,9},{11,10},{12,13},{15,14},{16,17},{19,... | collective-permute-start | bytes 1376264 | tf_op jit(solution)/shard_map/ppermute | solution.py:63
  45.7 102.5 %collective-permute-start.17 = (bf16[7168,128]{1,0:T(8,128)(2,1)}, bf16[7168,128]{1,0:T(8,128)(2,1)}, u32[]{:S(2)}, u32[]{:S(2)}) collective-permute-start(bf16[7168,128]{1,0:T(8,128)(2,1)} %collective-permute-done.16), channel_id=1, source_target_pairs={{2,6},{1,125},{6,10},{5,1},{10,14},{9,5},{14,18},{13,9},{18,22},{1... | collective-permute-start | bytes 5505032 | tf_op jit(solution)/shard_map/ppermute | solution.py:91
  83.5 31.0 %collective-permute-start.5 = (bf16[64,7168]{1,0:T(8,128)(2,1)}, bf16[64,7168]{1,0:T(8,128)(2,1)}, u32[]{:S(2)}, u32[]{:S(2)}) collective-permute-start(bf16[64,7168]{1,0:T(8,128)(2,1)} %get-tuple-element.40), channel_id=1, source_target_pairs={{0,1},{1,0},{2,3},{3,2},{4,5},{5,4},{6,7},{7,6},{8,9},{9,8},{10,11... | collective-permute-start | bytes 2752520 | tf_op jit(solution)/shard_map/ppermute | solution.py:66
  85.5 17.0 %copy-start.5 = (bf16[20,8,56,128]{3,1,2,0:T(8,128)(2,1)S(1)}, bf16[20,8,56,128]{3,1,2,0:T(8,128)(2,1)}, u32[]{:S(2)}) copy-start(bf16[20,8,56,128]{3,1,2,0:T(8,128)(2,1)} %copy-done.4) | copy-start | bytes 6881284
  85.5 17.0 %copy-start.6 = (bf16[1,7168,256]{2,1,0:T(8,128)(2,1)S(1)}, bf16[1,7168,256]{2,1,0:T(8,128)(2,1)}, u32[]{:S(2)}) copy-start(bf16[1,7168,256]{2,1,0:T(8,128)(2,1)} %param.11) | copy-start | bytes 11010052
  94.8 7.7 %copy-start.16 = (bf16[32,7168]{1,0:T(8,128)(2,1)}, bf16[32,7168]{1,0:T(8,128)(2,1)S(1)}, u32[]{:S(2)}) copy-start(bf16[32,7168]{1,0:T(8,128)(2,1)S(1)} %collective-permute-done.2) | copy-start | bytes 1376260
  94.8 49.2 %collective-permute-start = (bf16[96,7168]{1,0:T(8,128)(2,1)S(1)}, bf16[96,7168]{1,0:T(8,128)(2,1)S(1)}, u32[]{:S(2)}, u32[]{:S(2)}) collective-permute-start(bf16[96,7168]{1,0:T(8,128)(2,1)S(1)} %slice_bitcast_fusion.1), channel_id=1, source_target_pairs={{0,1},{3,2},{4,5},{7,6},{8,9},{11,10},{12,13},{15,14},{16,17},{19,... | collective-permute-start | bytes 4128776 | tf_op jit(solution)/shard_map/ppermute | solution.py:63
  102.6 2.6 copy-start.9
  102.6 41.4 %copy-start.10 = (bf16[128,7168]{1,0:T(8,128)(2,1)S(1)}, bf16[128,7168]{1,0:T(8,128)(2,1)}, u32[]{:S(2)}) copy-start(bf16[128,7168]{1,0:T(8,128)(2,1)} %slice_bitcast_fusion) | copy-start | bytes 5505028
  102.6 44.9 %copy-start.17 = (bf16[32,7168]{1,0:T(8,128)(2,1)S(1)}, bf16[32,7168]{1,0:T(8,128)(2,1)}, u32[]{:S(2)}) copy-start(bf16[32,7168]{1,0:T(8,128)(2,1)} %copy-done.16) | copy-start | bytes 1376260
  105.2 45.5 %collective-permute-start.12 = (bf16[7168,128]{1,0:T(8,128)(2,1)S(1)}, bf16[7168,128]{1,0:T(8,128)(2,1)S(1)}, u32[]{:S(2)}, u32[]{:S(2)}) collective-permute-start(bf16[7168,128]{1,0:T(8,128)(2,1)S(1)} %copy-done.9), channel_id=1, source_target_pairs={{3,7},{0,124},{7,11},{4,0},{11,15},{8,4},{15,19},{12,8},{19,23},{1... | collective-permute-start | bytes 5505032 | tf_op jit(solution)/shard_map/ppermute | solution.py:80
  114.6 57.0 %collective-permute-start.14 = (bf16[7168,128]{1,0:T(8,128)(2,1)}, bf16[7168,128]{1,0:T(8,128)(2,1)S(1)}, u32[]{:S(2)}, u32[]{:S(2)}) collective-permute-start(bf16[7168,128]{1,0:T(8,128)(2,1)} %collective-permute-done.13), channel_id=1, source_target_pairs={{2,6},{1,125},{6,10},{5,1},{10,14},{9,5},{14,18},{13,9},{18,22},{1... | collective-permute-start | bytes 5505032 | tf_op jit(solution)/shard_map/ppermute | solution.py:89
  143.9 140.6 %collective-permute-start.4 = (bf16[128,7168]{1,0:T(8,128)(2,1)S(1)}, bf16[128,7168]{1,0:T(8,128)(2,1)S(1)}, u32[]{:S(2)}, u32[]{:S(2)}) collective-permute-start(bf16[128,7168]{1,0:T(8,128)(2,1)S(1)} %copy-done.10), channel_id=1, source_target_pairs={{3,7},{0,124},{7,11},{4,0},{11,15},{8,4},{15,19},{12,8},{19,23},{1... | collective-permute-start | bytes 5505032 | tf_op jit(solution)/shard_map/ppermute | solution.py:82
  147.5 137.0 %collective-permute-start.3 = (bf16[32,7168]{1,0:T(8,128)(2,1)S(1)}, bf16[32,7168]{1,0:T(8,128)(2,1)S(1)}, u32[]{:S(2)}, u32[]{:S(2)}) collective-permute-start(bf16[32,7168]{1,0:T(8,128)(2,1)S(1)} %copy-done.17), channel_id=1, source_target_pairs={{2,6},{1,125},{6,10},{5,1},{10,14},{9,5},{14,18},{13,9},{18,22},{1... | collective-permute-start | bytes 1376264 | tf_op jit(solution)/shard_map/ppermute | solution.py:96
  148.2 136.3 %collective-permute-start.1 = (bf16[96,7168]{1,0:T(8,128)(2,1)S(1)}, bf16[96,7168]{1,0:T(8,128)(2,1)S(1)}, u32[]{:S(2)}, u32[]{:S(2)}) collective-permute-start(bf16[96,7168]{1,0:T(8,128)(2,1)S(1)} %collective-permute-done), channel_id=1, source_target_pairs={{2,6},{1,125},{6,10},{5,1},{10,14},{9,5},{14,18},{13,9},{18,22},{1... | collective-permute-start | bytes 4128776 | tf_op jit(solution)/shard_map/ppermute | solution.py:88
  150.7 87.8 %collective-permute-start.8 = (bf16[160,7168]{1,0:T(8,128)(2,1)S(1)}, bf16[160,7168]{1,0:T(8,128)(2,1)S(1)}, u32[]{:S(2)}, u32[]{:S(2)}) collective-permute-start(bf16[160,7168]{1,0:T(8,128)(2,1)S(1)} %bitcast.86), channel_id=1, source_target_pairs={{0,3},{3,0},{1,2},{2,1},{4,7},{7,4},{5,6},{6,5},{8,11},{11,8},{9,1... | collective-permute-start | bytes 6881288 | tf_op jit(solution)/shard_map/ppermute | solution.py:66
  171.6 55.0 %collective-permute-start.6 = (bf16[64,7168]{1,0:T(8,128)(2,1)}, bf16[64,7168]{1,0:T(8,128)(2,1)S(1)}, u32[]{:S(2)}, u32[]{:S(2)}) collective-permute-start(bf16[64,7168]{1,0:T(8,128)(2,1)} %collective-permute-done.5), channel_id=1, source_target_pairs={{0,3},{3,0},{1,2},{2,1},{4,7},{7,4},{5,6},{6,5},{8,11},{11,8},{9,1... | collective-permute-start | bytes 2752520 | tf_op jit(solution)/shard_map/ppermute | solution.py:66
  171.8 66.7 %copy-start.12 = (bf16[64,7168]{1,0:T(8,128)(2,1)S(1)}, bf16[64,7168]{1,0:T(8,128)(2,1)}, u32[]{:S(2)}) copy-start(bf16[64,7168]{1,0:T(8,128)(2,1)} %get-tuple-element.39) | copy-start | bytes 2752516
  226.5 12.0 %collective-permute-start.10 = (bf16[32,7168]{1,0:T(8,128)(2,1)S(1)}, bf16[32,7168]{1,0:T(8,128)(2,1)S(1)}, u32[]{:S(2)}, u32[]{:S(2)}) collective-permute-start(bf16[32,7168]{1,0:T(8,128)(2,1)S(1)} %slice.177), channel_id=1, source_target_pairs={{0,1},{1,0},{2,3},{3,2},{4,5},{5,4},{6,7},{7,6},{8,9},{9,8},{10,11... | collective-permute-start | bytes 1376264 | tf_op jit(solution)/shard_map/ppermute | solution.py:66
  238.5 5.0 %copy-start.3 = (bf16[1,7168,256]{2,1,0:T(8,128)(2,1)S(1)}, bf16[1,7168,256]{2,1,0:T(8,128)(2,1)}, u32[]{:S(2)}) copy-start(bf16[1,7168,256]{2,1,0:T(8,128)(2,1)} %param.10) | copy-start | bytes 11010052
  238.5 20.9 %collective-permute-start.7 = (bf16[64,7168]{1,0:T(8,128)(2,1)S(1)}, bf16[64,7168]{1,0:T(8,128)(2,1)S(1)}, u32[]{:S(2)}, u32[]{:S(2)}) collective-permute-start(bf16[64,7168]{1,0:T(8,128)(2,1)S(1)} %copy-done.12), channel_id=1, source_target_pairs={{0,1},{1,0},{2,3},{3,2},{4,5},{5,4},{6,7},{7,6},{8,9},{9,8},{10,11... | collective-permute-start | bytes 2752520 | tf_op jit(solution)/shard_map/ppermute | solution.py:66
  238.5 42.6 %collective-permute-start.11 = (bf16[32,7168]{1,0:T(8,128)(2,1)S(1)}, bf16[32,7168]{1,0:T(8,128)(2,1)S(1)}, u32[]{:S(2)}, u32[]{:S(2)}) collective-permute-start(bf16[32,7168]{1,0:T(8,128)(2,1)S(1)} %collective-permute-done.10), channel_id=1, source_target_pairs={{0,3},{3,0},{1,2},{2,1},{4,7},{7,4},{5,6},{6,5},{8,11},{11,8},{9,1... | collective-permute-start | bytes 1376264 | tf_op jit(solution)/shard_map/ppermute | solution.py:66
  259.5 21.7 %collective-permute-start.9 = (bf16[64,7168]{1,0:T(8,128)(2,1)S(1)}, bf16[64,7168]{1,0:T(8,128)(2,1)S(1)}, u32[]{:S(2)}, u32[]{:S(2)}) collective-permute-start(bf16[64,7168]{1,0:T(8,128)(2,1)S(1)} %collective-permute-done.7), channel_id=1, source_target_pairs={{0,3},{3,0},{1,2},{2,1},{4,7},{7,4},{5,6},{6,5},{8,11},{11,8},{9,1... | collective-permute-start | bytes 2752520 | tf_op jit(solution)/shard_map/ppermute | solution.py:66
  289.9 12.7 %collective-permute-start.27 = (bf16[80,3072]{1,0:T(8,128)(2,1)S(1)}, bf16[80,3072]{1,0:T(8,128)(2,1)S(1)}, u32[]{:S(2)}, u32[]{:S(2)}) collective-permute-start(bf16[80,3072]{1,0:T(8,128)(2,1)S(1)} %get-tuple-element.38), channel_id=1, source_target_pairs={{0,1},{1,0},{2,3},{3,2},{4,5},{5,4},{6,7},{7,6},{8,9},{9,8},{10,11... | collective-permute-start | bytes 1474568 | tf_op jit(solution)/shard_map/ppermute | solution.py:66
  294.7 51.3 %collective-permute-start.21 = (bf16[80,4096]{1,0:T(8,128)(2,1)S(1)}, bf16[80,4096]{1,0:T(8,128)(2,1)S(1)}, u32[]{:S(2)}, u32[]{:S(2)}) collective-permute-start(bf16[80,4096]{1,0:T(8,128)(2,1)S(1)} %get-tuple-element.34), channel_id=1, source_target_pairs={{0,1},{1,0},{2,3},{3,2},{4,5},{5,4},{6,7},{7,6},{8,9},{9,8},{10,11... | collective-permute-start | bytes 1966088 | tf_op jit(solution)/shard_map/ppermute | solution.py:66
  295.0 54.8 %collective-permute-start.19 = (bf16[80,4096]{1,0:T(8,128)(2,1)S(1)}, bf16[80,4096]{1,0:T(8,128)(2,1)S(1)}, u32[]{:S(2)}, u32[]{:S(2)}) collective-permute-start(bf16[80,4096]{1,0:T(8,128)(2,1)S(1)} %get-tuple-element.33), channel_id=1, source_target_pairs={{0,3},{3,0},{1,2},{2,1},{4,7},{7,4},{5,6},{6,5},{8,11},{11,8},{9,1... | collective-permute-start | bytes 1966088 | tf_op jit(solution)/shard_map/ppermute | solution.py:66
  298.4 84.2 %collective-permute-start.18 = (bf16[80,4096]{1,0:T(8,128)(2,1)}, bf16[80,4096]{1,0:T(8,128)(2,1)S(1)}, u32[]{:S(2)}, u32[]{:S(2)}) collective-permute-start(bf16[80,4096]{1,0:T(8,128)(2,1)} %slice.191), channel_id=1, source_target_pairs={{0,3},{3,0},{1,2},{2,1},{4,7},{7,4},{5,6},{6,5},{8,11},{11,8},{9,1... | collective-permute-start | bytes 1966088 | tf_op jit(solution)/shard_map/ppermute | solution.py:66
  298.4 53.3 %collective-permute-start.24 = (bf16[80,3072]{1,0:T(8,128)(2,1)S(1)}, bf16[80,3072]{1,0:T(8,128)(2,1)S(1)}, u32[]{:S(2)}, u32[]{:S(2)}) collective-permute-start(bf16[80,3072]{1,0:T(8,128)(2,1)S(1)} %slice.199), channel_id=1, source_target_pairs={{0,3},{3,0},{1,2},{2,1},{4,7},{7,4},{5,6},{6,5},{8,11},{11,8},{9,1... | collective-permute-start | bytes 1474568 | tf_op jit(solution)/shard_map/ppermute | solution.py:66
  302.6 63.4 %copy-start.8 = (bf16[160,7168]{1,0:T(8,128)(2,1)}, bf16[160,7168]{1,0:T(8,128)(2,1)S(1)}, u32[]{:S(2)}) copy-start(bf16[160,7168]{1,0:T(8,128)(2,1)S(1)} %convolution_convert_fusion.3) | copy-start | bytes 6881284
  302.6 43.3 %collective-permute-start.25 = (bf16[80,3072]{1,0:T(8,128)(2,1)S(1)}, bf16[80,3072]{1,0:T(8,128)(2,1)S(1)}, u32[]{:S(2)}, u32[]{:S(2)}) collective-permute-start(bf16[80,3072]{1,0:T(8,128)(2,1)S(1)} %get-tuple-element.37), channel_id=1, source_target_pairs={{0,3},{3,0},{1,2},{2,1},{4,7},{7,4},{5,6},{6,5},{8,11},{11,8},{9,1... | collective-permute-start | bytes 1474568 | tf_op jit(solution)/shard_map/ppermute | solution.py:66
  345.9 9.5 %collective-permute-start.29 = (bf16[80,3072]{1,0:T(8,128)(2,1)S(1)}, bf16[80,3072]{1,0:T(8,128)(2,1)S(1)}, u32[]{:S(2)}, u32[]{:S(2)}) collective-permute-start(bf16[80,3072]{1,0:T(8,128)(2,1)S(1)} %slice.205), channel_id=1, source_target_pairs={{0,1},{1,0},{2,3},{3,2},{4,5},{5,4},{6,7},{7,6},{8,9},{9,8},{10,11... | collective-permute-start | bytes 1474568 | tf_op jit(solution)/shard_map/ppermute | solution.py:66
  346.0 12.1 %collective-permute-start.28 = (bf16[80,3072]{1,0:T(8,128)(2,1)S(1)}, bf16[80,3072]{1,0:T(8,128)(2,1)S(1)}, u32[]{:S(2)}, u32[]{:S(2)}) collective-permute-start(bf16[80,3072]{1,0:T(8,128)(2,1)S(1)} %add_convert_fusion.5), channel_id=1, source_target_pairs={{0,3},{3,0},{1,2},{2,1},{4,7},{7,4},{5,6},{6,5},{8,11},{11,8},{9,1... | collective-permute-start | bytes 1474568 | tf_op jit(solution)/shard_map/ppermute | solution.py:66
  349.8 16.2 %collective-permute-start.26 = (bf16[80,3072]{1,0:T(8,128)(2,1)S(1)}, bf16[80,3072]{1,0:T(8,128)(2,1)S(1)}, u32[]{:S(2)}, u32[]{:S(2)}) collective-permute-start(bf16[80,3072]{1,0:T(8,128)(2,1)S(1)} %add_convert_fusion.7), channel_id=1, source_target_pairs={{0,1},{1,0},{2,3},{3,2},{4,5},{5,4},{6,7},{7,6},{8,9},{9,8},{10,11... | collective-permute-start | bytes 1474568 | tf_op jit(solution)/shard_map/ppermute | solution.py:66
  351.6 30.9 %collective-permute-start.23 = (bf16[80,4096]{1,0:T(8,128)(2,1)}, bf16[80,4096]{1,0:T(8,128)(2,1)}, u32[]{:S(2)}, u32[]{:S(2)}) collective-permute-start(bf16[80,4096]{1,0:T(8,128)(2,1)} %slice.197), channel_id=1, source_target_pairs={{0,1},{1,0},{2,3},{3,2},{4,5},{5,4},{6,7},{7,6},{8,9},{9,8},{10,11... | collective-permute-start | bytes 1966088 | tf_op jit(solution)/shard_map/ppermute | solution.py:66
  355.4 27.1 %collective-permute-start.22 = (bf16[80,4096]{1,0:T(8,128)(2,1)}, bf16[80,4096]{1,0:T(8,128)(2,1)}, u32[]{:S(2)}, u32[]{:S(2)}) collective-permute-start(bf16[80,4096]{1,0:T(8,128)(2,1)} %add_convert_fusion.1), channel_id=1, source_target_pairs={{0,3},{3,0},{1,2},{2,1},{4,7},{7,4},{5,6},{6,5},{8,11},{11,8},{9,1... | collective-permute-start | bytes 1966088 | tf_op jit(solution)/shard_map/ppermute | solution.py:66
  358.1 36.0 %collective-permute-start.20 = (bf16[80,4096]{1,0:T(8,128)(2,1)}, bf16[80,4096]{1,0:T(8,128)(2,1)}, u32[]{:S(2)}, u32[]{:S(2)}) collective-permute-start(bf16[80,4096]{1,0:T(8,128)(2,1)} %add_convert_fusion.3), channel_id=1, source_target_pairs={{0,1},{1,0},{2,3},{3,2},{4,5},{5,4},{6,7},{7,6},{8,9},{9,8},{10,11... | collective-permute-start | bytes 1966088 | tf_op jit(solution)/shard_map/ppermute | solution.py:66
  367.6 31.2 %all-to-all-start.2 = ((bf16[32,5,24,128]{3,2,1,0:T(8,128)(2,1)}), bf16[32,5,24,128]{3,2,1,0:T(8,128)(2,1)S(1)}, u32[]{:S(2)}, u32[]{:S(2)}) async-start(bf16[32,5,24,128]{3,2,1,0:T(8,128)(2,1)} %bitcast.26), calls=%async_computation.2 | async-start | bytes 1966080 | tf_op jit(solution)/shard_map/all_to_all | solution.py:135
  396.8 13.2 %copy-start.18 = (f32[128,1]{0,1:T(1,128)S(1)}, f32[128,1]{0,1:T(1,128)}, u32[]{:S(2)}) copy-start(f32[128,1]{0,1:T(1,128)} %param.9) | copy-start | bytes 1540
  399.8 30.0 %all-to-all-start.1 = ((bf16[32,5,32,128]{3,2,1,0:T(8,128)(2,1)}), bf16[32,5,32,128]{3,2,1,0:T(8,128)(2,1)S(1)}, u32[]{:S(2)}, u32[]{:S(2)}) async-start(bf16[32,5,32,128]{3,2,1,0:T(8,128)(2,1)} %bitcast.20), calls=%async_computation.1 | async-start | bytes 2621440 | tf_op jit(solution)/shard_map/all_to_all | solution.py:135
  429.8 2.5 copy-start.1
  (4 other events, 5.6 us)

commit v6 on v5

--- a/solution.py
+++ b/solution.py
@@ -67,6 +67,7 @@
 
     inward_down = cross(w_down[inner:first_down])
     inward_gate = cross(w_gate[:, inner:])
+    inward_up = cross(w_up[:, inner:])
     arrived = lax.all_to_all(outgoing, PLANE, 0, 0, tiled=True)
     mid = arrived.reshape(rows, width)
 
@@ -81,7 +82,6 @@
     outer_up = lax.ppermute(w_up[:, :inner], EVERY, straight)
     outer_down = lax.ppermute(w_down[:inner], EVERY, straight)
     side_a = over(mid[:64], SIDE)
-    inward_up = cross(w_up[:, inner:])
     side_b = over(mid[64:128], SIDE)
     side_c = over(mid[128:], SIDE)
     inward_last = cross(w_down[first_down:])
@@ -96,9 +96,9 @@
     inner_last = lax.ppermute(inward_last, EVERY, turned)
 
     outer = (place == 0) | (place == SPAN - 1)
-    edge_into = jnp.concatenate(
-        [jnp.where(outer, outer_gate, inner_gate), jnp.where(outer, outer_up, inner_up)], axis=1
-    )
+    edge_gate = jnp.where(outer, outer_gate, inner_gate)
+    edge_up = jnp.where(outer, outer_up, inner_up)
+    edge_into = jnp.concatenate([edge_gate, edge_up], axis=1)
     side = jnp.concatenate([side_a, side_b, side_c], axis=0)
     far = jnp.concatenate([far_a, far_b, far_c], axis=0)
 
@@ -111,7 +111,9 @@
     tied = lax.optimization_barrier((inner_down, inner_last, outer_down, *[full_hidden(*p) for p in pairs]))
     edge_down = jnp.where(outer, tied[2], jnp.concatenate(tied[:2], axis=0))
     down = jnp.concatenate([w_down, edge_down], axis=0)
-    far, mirror, side, home = [dot(h, down).astype(jnp.bfloat16) for h in tied[3:]]
+    far = dot(tied[3], down).astype(jnp.bfloat16)
+    far, *rest = lax.optimization_barrier((far, *tied[4:]))
+    mirror, side, home = [dot(h, down).astype(jnp.bfloat16) for h in rest]
 
     def added(u, v):
         return (u.astype(jnp.float32) + v.astype(jnp.float32)).astype(jnp.bfloat16)
@@ -126,8 +128,10 @@
         far_b = over(far[lower, cols], SIDE)
         mirror_a = over(mirror[upper, cols], MIRROR)
         side_b = over(side[lower, cols], SIDE)
-        side_a = over(added(side[upper, cols], far_a), SIDE)
-        mirror_b = over(added(mirror[lower, cols], far_b), MIRROR)
+        side_a = added(side[upper, cols], far_a)
+        mirror_b = added(mirror[lower, cols], far_b)
+        side_a = over(side_a, SIDE)
+        mirror_b = over(mirror_b, MIRROR)
         total_a = home[upper, cols].astype(f32) + mirror_a.astype(f32) + side_a.astype(f32)
         total_b = home[lower, cols].astype(f32) + mirror_b.astype(f32) + side_b.astype(f32)
         total = jnp.concatenate([total_a, total_b], axis=0).astype(jnp.bfloat16)

time: 436 us -> 436 us (level)
  no operation moved by 1% of the time
where the time goes in v6:
time: 436 us; the launch traced here: 432 us
  waiting for transfers between devices  259 us (59%)
  starting transfers between devices  104 us (24%)
  local copies, waits for them, and re-layouts  28.9 us (7%)
  matrix products  25.9 us (6%)
  other arithmetic  14.1 us (3%)
    ppermute x19, waiting for transfers between devices, over(): return lax.ppermute(block, 'x', pairs)  163 us
    ppermute x4, waiting for transfers between devices, cross(): return lax.ppermute(block, 'x', INWARD)  46.4 us
    ppermute x19, starting transfers between devices, over(): return lax.ppermute(block, 'x', pairs)  43.4 us
    all_to_all x1, waiting for transfers between devices, body(): arrived = lax.all_to_all(outgoing, PLANE, 0, 0, tiled=True)  31 us
    all_to_all x2, starting transfers between devices, body(): lax.all_to_all(total, PLANE, 0, 0, tiled=True).reshape(rows, hi - lo)  25.1 us
    dot_general x17, matrix products, dot(): return jnp.dot(a, b, preferred_element_type=jnp.float32)  22.8 us
    all_to_all x2, waiting for transfers between devices, body(): lax.all_to_all(total, PLANE, 0, 0, tiled=True).reshape(rows, hi - lo)  18 us
    unnamed x46, local copies, waits for them, and re-layouts  12.4 us
  transfers between devices with their start and end apart: 33, of which 15 were waited for; matrix products, arithmetic and copies ran while one was open for 13% of the time, Pallas kernels for 0%

profile of v6, /device:TPU:7, one launch (start us, length us, event | category | flops | bytes accessed | tf_op | source)
XLA Modules:
  0.0 432.3 jit_solution(7383559093710999491)
XLA Ops:
  0.0 4.3 fusion.49
  4.3 3.8 collective-permute-start.16
  8.1 3.5 collective-permute-start.15
  11.6 2.0 fusion.48
  13.7 2.5 collective-permute-start.13
  17.4 1.9 copy.8
  19.3 8.9 %all-to-all-start = ((bf16[32,5,56,128]{3,2,1,0:T(8,128)(2,1)}), bf16[32,5,56,128]{3,2,1,0:T(8,128)(2,1)}, u32[]{:S(2)}, u32[]{:S(2)}) async-start(bf16[32,5,56,128]{3,2,1,0:T(8,128)(2,1)} %bitcast.87), calls=%async_computation | async-start | bytes 4587520 | tf_op jit(solution)/shard_map/all_to_all | solution.py:71
  33.2 2.8 slice_bitcast_fusion
  36.0 9.7 %collective-permute-done.16 = bf16[7168,128]{1,0:T(8,128)(2,1)} collective-permute-done((bf16[7168,128]{1,0:T(8,128)(2,1)}, bf16[7168,128]{1,0:T(8,128)(2,1)}, u32[]{:S(2)}, u32[]{:S(2)}) %collective-permute-start.16) | collective-permute-done | bytes 1835040 | tf_op jit(solution)/shard_map/ppermute | solution.py:63
  45.7 1.9 collective-permute-start.17
  47.7 31.0 %all-to-all-done = bf16[32,5,56,128]{3,2,1,0:T(8,128)(2,1)} async-done(((bf16[32,5,56,128]{3,2,1,0:T(8,128)(2,1)}), bf16[32,5,56,128]{3,2,1,0:T(8,128)(2,1)}, u32[]{:S(2)}, u32[]{:S(2)}) %all-to-all-start) | async-done | bytes 2293792 | tf_op jit(solution)/shard_map/all_to_all | solution.py:71
  78.6 2.1 copy.26
  85.5 9.3 %collective-permute-done.2 = bf16[32,7168]{1,0:T(8,128)(2,1)S(1)} collective-permute-done((bf16[32,7168]{1,0:T(8,128)(2,1)S(1)}, bf16[32,7168]{1,0:T(8,128)(2,1)S(1)}, u32[]{:S(2)}, u32[]{:S(2)}) %collective-permute-start.2) | collective-permute-done | bytes 458784 | tf_op jit(solution)/shard_map/ppermute | solution.py:63
  94.8 4.2 collective-permute-start
  99.0 3.5 fusion.42
  102.6 2.6 fusion.6
  105.2 3.5 collective-permute-start.12
  108.7 5.8 %collective-permute-done.5 = bf16[64,7168]{1,0:T(8,128)(2,1)} collective-permute-done((bf16[64,7168]{1,0:T(8,128)(2,1)}, bf16[64,7168]{1,0:T(8,128)(2,1)}, u32[]{:S(2)}, u32[]{:S(2)}) %collective-permute-start.5) | collective-permute-done | bytes 917536 | tf_op jit(solution)/shard_map/ppermute | solution.py:66
  116.6 27.4 %collective-permute-done = bf16[96,7168]{1,0:T(8,128)(2,1)S(1)} collective-permute-done((bf16[96,7168]{1,0:T(8,128)(2,1)S(1)}, bf16[96,7168]{1,0:T(8,128)(2,1)S(1)}, u32[]{:S(2)}, u32[]{:S(2)}) %collective-permute-start) | collective-permute-done | bytes 1376288 | tf_op jit(solution)/shard_map/ppermute | solution.py:63
  143.9 3.5 collective-permute-start.4
  149.0 1.7 broadcast_select_fusion
  150.7 20.9 %collective-permute-start.8 = (bf16[160,7168]{1,0:T(8,128)(2,1)S(1)}, bf16[160,7168]{1,0:T(8,128)(2,1)S(1)}, u32[]{:S(2)}, u32[]{:S(2)}) collective-permute-start(bf16[160,7168]{1,0:T(8,128)(2,1)S(1)} %bitcast.86), channel_id=1, source_target_pairs={{0,3},{3,0},{1,2},{2,1},{4,7},{7,4},{5,6},{6,5},{8,11},{11,8},{9,1... | collective-permute-start | bytes 6881288 | tf_op jit(solution)/shard_map/ppermute | solution.py:66
  171.8 2.5 fusion.44
  175.1 51.5 %collective-permute-done.6 = bf16[64,7168]{1,0:T(8,128)(2,1)S(1)} collective-permute-done((bf16[64,7168]{1,0:T(8,128)(2,1)}, bf16[64,7168]{1,0:T(8,128)(2,1)S(1)}, u32[]{:S(2)}, u32[]{:S(2)}) %collective-permute-start.6) | collective-permute-done | bytes 917536 | tf_op jit(solution)/shard_map/ppermute | solution.py:66
  226.6 11.9 %collective-permute-done.10 = bf16[32,7168]{1,0:T(8,128)(2,1)S(1)} collective-permute-done((bf16[32,7168]{1,0:T(8,128)(2,1)S(1)}, bf16[32,7168]{1,0:T(8,128)(2,1)S(1)}, u32[]{:S(2)}, u32[]{:S(2)}) %collective-permute-start.10) | collective-permute-done | bytes 458784 | tf_op jit(solution)/shard_map/ppermute | solution.py:66
  238.5 3.5 collective-permute-start.11
  245.1 14.4 %collective-permute-done.7 = bf16[64,7168]{1,0:T(8,128)(2,1)S(1)} collective-permute-done((bf16[64,7168]{1,0:T(8,128)(2,1)S(1)}, bf16[64,7168]{1,0:T(8,128)(2,1)S(1)}, u32[]{:S(2)}, u32[]{:S(2)}) %collective-permute-start.7) | collective-permute-done | bytes 917536 | tf_op jit(solution)/shard_map/ppermute | solution.py:66
  259.5 2.9 collective-permute-start.9
  265.6 15.5 %collective-permute-done.9 = bf16[64,7168]{1,0:T(8,128)(2,1)S(1)} collective-permute-done((bf16[64,7168]{1,0:T(8,128)(2,1)S(1)}, bf16[64,7168]{1,0:T(8,128)(2,1)S(1)}, u32[]{:S(2)}, u32[]{:S(2)}) %collective-permute-start.9) | collective-permute-done | bytes 917536 | tf_op jit(solution)/shard_map/ppermute | solution.py:66
  285.0 1.6 copy-done.7
  286.6 1.6 convolution_convert_fusion.3
  288.3 1.6 convolution_convert_fusion.1
  291.2 1.6 convolution_convert_fusion
  295.0 3.3 collective-permute-start.19
  298.4 2.7 collective-permute-start.24
  301.0 1.6 convolution_convert_fusion.2
  302.6 1.7 collective-permute-start.25
  304.4 41.5 %collective-permute-done.25 = bf16[80,3072]{1,0:T(8,128)(2,1)S(1)} collective-permute-done((bf16[80,3072]{1,0:T(8,128)(2,1)S(1)}, bf16[80,3072]{1,0:T(8,128)(2,1)S(1)}, u32[]{:S(2)}, u32[]{:S(2)}) %collective-permute-start.25) | collective-permute-done | bytes 491552 | tf_op jit(solution)/shard_map/ppermute | solution.py:66
  346.0 2.8 collective-permute-start.28
  352.3 3.2 collective-permute-done.29
  355.4 2.7 collective-permute-start.22
  358.1 7.8 %collective-permute-done.26 = bf16[80,3072]{1,0:T(8,128)(2,1)S(1)} collective-permute-done((bf16[80,3072]{1,0:T(8,128)(2,1)S(1)}, bf16[80,3072]{1,0:T(8,128)(2,1)S(1)}, u32[]{:S(2)}, u32[]{:S(2)}) %collective-permute-start.26) | collective-permute-done | bytes 491552 | tf_op jit(solution)/shard_map/ppermute | solution.py:66
  367.6 14.9 %all-to-all-start.2 = ((bf16[32,5,24,128]{3,2,1,0:T(8,128)(2,1)}), bf16[32,5,24,128]{3,2,1,0:T(8,128)(2,1)S(1)}, u32[]{:S(2)}, u32[]{:S(2)}) async-start(bf16[32,5,24,128]{3,2,1,0:T(8,128)(2,1)} %bitcast.26), calls=%async_computation.2 | async-start | bytes 1966080 | tf_op jit(solution)/shard_map/all_to_all | solution.py:139
  382.6 11.6 %collective-permute-done.20 = bf16[80,4096]{1,0:T(8,128)(2,1)} collective-permute-done((bf16[80,4096]{1,0:T(8,128)(2,1)}, bf16[80,4096]{1,0:T(8,128)(2,1)}, u32[]{:S(2)}, u32[]{:S(2)}) %collective-permute-start.20) | collective-permute-done | bytes 655392 | tf_op jit(solution)/shard_map/ppermute | solution.py:66
  394.2 2.5 add_convert_fusion.2
  399.8 10.2 %all-to-all-start.1 = ((bf16[32,5,32,128]{3,2,1,0:T(8,128)(2,1)}), bf16[32,5,32,128]{3,2,1,0:T(8,128)(2,1)S(1)}, u32[]{:S(2)}, u32[]{:S(2)}) async-start(bf16[32,5,32,128]{3,2,1,0:T(8,128)(2,1)} %bitcast.20), calls=%async_computation.1 | async-start | bytes 2621440 | tf_op jit(solution)/shard_map/all_to_all | solution.py:139
  410.0 2.5 fusion.1
  412.5 17.3 %all-to-all-done.1 = bf16[32,5,32,128]{3,2,1,0:T(8,128)(2,1)S(1)} async-done(((bf16[32,5,32,128]{3,2,1,0:T(8,128)(2,1)}), bf16[32,5,32,128]{3,2,1,0:T(8,128)(2,1)S(1)}, u32[]{:S(2)}, u32[]{:S(2)}) %all-to-all-start.1) | async-done | bytes 1310752 | tf_op jit(solution)/shard_map/all_to_all | solution.py:139
  (127 shorter events, 40.1 us)
Async XLA Ops:
  0.0 16.6 %copy-start = (bf16[128,7168]{1,0:T(8,128)(2,1)S(1)}, bf16[128,7168]{1,0:T(8,128)(2,1)}, u32[]{:S(2)}) copy-start(bf16[128,7168]{1,0:T(8,128)(2,1)} %param.7) | copy-start | bytes 5505028
  0.0 11.6 %copy-start.2 = (bf16[1,7168,256]{2,1,0:T(8,128)(2,1)S(1)}, bf16[1,7168,256]{2,1,0:T(8,128)(2,1)}, u32[]{:S(2)}) copy-start(bf16[1,7168,256]{2,1,0:T(8,128)(2,1)} %param.10) | copy-start | bytes 11010052
  4.3 41.4 %collective-permute-start.16 = (bf16[7168,128]{1,0:T(8,128)(2,1)}, bf16[7168,128]{1,0:T(8,128)(2,1)}, u32[]{:S(2)}, u32[]{:S(2)}) collective-permute-start(bf16[7168,128]{1,0:T(8,128)(2,1)} %get-tuple-element.37), channel_id=1, source_target_pairs={{0,1},{3,2},{4,5},{7,6},{8,9},{11,10},{12,13},{15,14},{16,17},{19,... | collective-permute-start | bytes 5505032 | tf_op jit(solution)/shard_map/ppermute | solution.py:63
  8.1 139.4 %collective-permute-start.15 = (bf16[7168,128]{1,0:T(8,128)(2,1)}, bf16[7168,128]{1,0:T(8,128)(2,1)}, u32[]{:S(2)}, u32[]{:S(2)}) collective-permute-start(bf16[7168,128]{1,0:T(8,128)(2,1)} %get-tuple-element.38), channel_id=1, source_target_pairs={{3,7},{0,124},{7,11},{4,0},{11,15},{8,4},{15,19},{12,8},{19,23},{1... | collective-permute-start | bytes 5505032 | tf_op jit(solution)/shard_map/ppermute | solution.py:82
  11.6 4.6 %copy-start.14 = (s32[128,1]{0,1:T(1,128)S(1)}, s32[128,1]{0,1:T(1,128)}, u32[]{:S(2)}) copy-start(s32[128,1]{0,1:T(1,128)} %param.8) | copy-start | bytes 1540
  13.7 91.5 %collective-permute-start.13 = (bf16[7168,128]{1,0:T(8,128)(2,1)}, bf16[7168,128]{1,0:T(8,128)(2,1)}, u32[]{:S(2)}, u32[]{:S(2)}) collective-permute-start(bf16[7168,128]{1,0:T(8,128)(2,1)} %get-tuple-element.35), channel_id=1, source_target_pairs={{0,1},{3,2},{4,5},{7,6},{8,9},{11,10},{12,13},{15,14},{16,17},{19,... | collective-permute-start | bytes 5505032 | tf_op jit(solution)/shard_map/ppermute | solution.py:63
  19.3 59.3 %all-to-all-start = ((bf16[32,5,56,128]{3,2,1,0:T(8,128)(2,1)}), bf16[32,5,56,128]{3,2,1,0:T(8,128)(2,1)}, u32[]{:S(2)}, u32[]{:S(2)}) async-start(bf16[32,5,56,128]{3,2,1,0:T(8,128)(2,1)} %bitcast.87), calls=%async_computation | async-start | bytes 4587520 | tf_op jit(solution)/shard_map/all_to_all | solution.py:71
  28.2 3.9 copy-start.15
  29.3 65.5 %collective-permute-start.2 = (bf16[32,7168]{1,0:T(8,128)(2,1)S(1)}, bf16[32,7168]{1,0:T(8,128)(2,1)S(1)}, u32[]{:S(2)}, u32[]{:S(2)}) collective-permute-start(bf16[32,7168]{1,0:T(8,128)(2,1)S(1)} %slice_bitcast_fusion.2), channel_id=1, source_target_pairs={{0,1},{3,2},{4,5},{7,6},{8,9},{11,10},{12,13},{15,14},{16,17},{19,... | collective-permute-start | bytes 1376264 | tf_op jit(solution)/shard_map/ppermute | solution.py:63
  45.7 102.5 %collective-permute-start.17 = (bf16[7168,128]{1,0:T(8,128)(2,1)}, bf16[7168,128]{1,0:T(8,128)(2,1)}, u32[]{:S(2)}, u32[]{:S(2)}) collective-permute-start(bf16[7168,128]{1,0:T(8,128)(2,1)} %collective-permute-done.16), channel_id=1, source_target_pairs={{2,6},{1,125},{6,10},{5,1},{10,14},{9,5},{14,18},{13,9},{18,22},{1... | collective-permute-start | bytes 5505032 | tf_op jit(solution)/shard_map/ppermute | solution.py:91
  83.5 31.0 %collective-permute-start.5 = (bf16[64,7168]{1,0:T(8,128)(2,1)}, bf16[64,7168]{1,0:T(8,128)(2,1)}, u32[]{:S(2)}, u32[]{:S(2)}) collective-permute-start(bf16[64,7168]{1,0:T(8,128)(2,1)} %get-tuple-element.48), channel_id=1, source_target_pairs={{0,1},{1,0},{2,3},{3,2},{4,5},{5,4},{6,7},{7,6},{8,9},{9,8},{10,11... | collective-permute-start | bytes 2752520 | tf_op jit(solution)/shard_map/ppermute | solution.py:66
  85.5 17.0 %copy-start.5 = (bf16[20,8,56,128]{3,1,2,0:T(8,128)(2,1)S(1)}, bf16[20,8,56,128]{3,1,2,0:T(8,128)(2,1)}, u32[]{:S(2)}) copy-start(bf16[20,8,56,128]{3,1,2,0:T(8,128)(2,1)} %copy-done.4) | copy-start | bytes 6881284
  85.5 17.0 %copy-start.6 = (bf16[1,7168,256]{2,1,0:T(8,128)(2,1)S(1)}, bf16[1,7168,256]{2,1,0:T(8,128)(2,1)}, u32[]{:S(2)}) copy-start(bf16[1,7168,256]{2,1,0:T(8,128)(2,1)} %param.11) | copy-start | bytes 11010052
  94.8 7.7 %copy-start.16 = (bf16[32,7168]{1,0:T(8,128)(2,1)}, bf16[32,7168]{1,0:T(8,128)(2,1)S(1)}, u32[]{:S(2)}) copy-start(bf16[32,7168]{1,0:T(8,128)(2,1)S(1)} %collective-permute-done.2) | copy-start | bytes 1376260
  94.8 49.2 %collective-permute-start = (bf16[96,7168]{1,0:T(8,128)(2,1)S(1)}, bf16[96,7168]{1,0:T(8,128)(2,1)S(1)}, u32[]{:S(2)}, u32[]{:S(2)}) collective-permute-start(bf16[96,7168]{1,0:T(8,128)(2,1)S(1)} %slice_bitcast_fusion.1), channel_id=1, source_target_pairs={{0,1},{3,2},{4,5},{7,6},{8,9},{11,10},{12,13},{15,14},{16,17},{19,... | collective-permute-start | bytes 4128776 | tf_op jit(solution)/shard_map/ppermute | solution.py:63
  102.6 2.6 copy-start.9
  102.6 41.4 %copy-start.10 = (bf16[128,7168]{1,0:T(8,128)(2,1)S(1)}, bf16[128,7168]{1,0:T(8,128)(2,1)}, u32[]{:S(2)}) copy-start(bf16[128,7168]{1,0:T(8,128)(2,1)} %slice_bitcast_fusion) | copy-start | bytes 5505028
  102.6 44.9 %copy-start.17 = (bf16[32,7168]{1,0:T(8,128)(2,1)S(1)}, bf16[32,7168]{1,0:T(8,128)(2,1)}, u32[]{:S(2)}) copy-start(bf16[32,7168]{1,0:T(8,128)(2,1)} %copy-done.16) | copy-start | bytes 1376260
  105.2 45.5 %collective-permute-start.12 = (bf16[7168,128]{1,0:T(8,128)(2,1)S(1)}, bf16[7168,128]{1,0:T(8,128)(2,1)S(1)}, u32[]{:S(2)}, u32[]{:S(2)}) collective-permute-start(bf16[7168,128]{1,0:T(8,128)(2,1)S(1)} %copy-done.9), channel_id=1, source_target_pairs={{3,7},{0,124},{7,11},{4,0},{11,15},{8,4},{15,19},{12,8},{19,23},{1... | collective-permute-start | bytes 5505032 | tf_op jit(solution)/shard_map/ppermute | solution.py:81
  114.6 57.0 %collective-permute-start.14 = (bf16[7168,128]{1,0:T(8,128)(2,1)}, bf16[7168,128]{1,0:T(8,128)(2,1)S(1)}, u32[]{:S(2)}, u32[]{:S(2)}) collective-permute-start(bf16[7168,128]{1,0:T(8,128)(2,1)} %collective-permute-done.13), channel_id=1, source_target_pairs={{2,6},{1,125},{6,10},{5,1},{10,14},{9,5},{14,18},{13,9},{18,22},{1... | collective-permute-start | bytes 5505032 | tf_op jit(solution)/shard_map/ppermute | solution.py:89
  143.9 140.6 %collective-permute-start.4 = (bf16[128,7168]{1,0:T(8,128)(2,1)S(1)}, bf16[128,7168]{1,0:T(8,128)(2,1)S(1)}, u32[]{:S(2)}, u32[]{:S(2)}) collective-permute-start(bf16[128,7168]{1,0:T(8,128)(2,1)S(1)} %copy-done.10), channel_id=1, source_target_pairs={{3,7},{0,124},{7,11},{4,0},{11,15},{8,4},{15,19},{12,8},{19,23},{1... | collective-permute-start | bytes 5505032 | tf_op jit(solution)/shard_map/ppermute | solution.py:83
  147.5 137.0 %collective-permute-start.3 = (bf16[32,7168]{1,0:T(8,128)(2,1)S(1)}, bf16[32,7168]{1,0:T(8,128)(2,1)S(1)}, u32[]{:S(2)}, u32[]{:S(2)}) collective-permute-start(bf16[32,7168]{1,0:T(8,128)(2,1)S(1)} %copy-done.17), channel_id=1, source_target_pairs={{2,6},{1,125},{6,10},{5,1},{10,14},{9,5},{14,18},{13,9},{18,22},{1... | collective-permute-start | bytes 1376264 | tf_op jit(solution)/shard_map/ppermute | solution.py:96
  148.2 136.3 %collective-permute-start.1 = (bf16[96,7168]{1,0:T(8,128)(2,1)S(1)}, bf16[96,7168]{1,0:T(8,128)(2,1)S(1)}, u32[]{:S(2)}, u32[]{:S(2)}) collective-permute-start(bf16[96,7168]{1,0:T(8,128)(2,1)S(1)} %collective-permute-done), channel_id=1, source_target_pairs={{2,6},{1,125},{6,10},{5,1},{10,14},{9,5},{14,18},{13,9},{18,22},{1... | collective-permute-start | bytes 4128776 | tf_op jit(solution)/shard_map/ppermute | solution.py:88
  150.7 87.8 %collective-permute-start.8 = (bf16[160,7168]{1,0:T(8,128)(2,1)S(1)}, bf16[160,7168]{1,0:T(8,128)(2,1)S(1)}, u32[]{:S(2)}, u32[]{:S(2)}) collective-permute-start(bf16[160,7168]{1,0:T(8,128)(2,1)S(1)} %bitcast.86), channel_id=1, source_target_pairs={{0,3},{3,0},{1,2},{2,1},{4,7},{7,4},{5,6},{6,5},{8,11},{11,8},{9,1... | collective-permute-start | bytes 6881288 | tf_op jit(solution)/shard_map/ppermute | solution.py:66
  171.6 55.0 %collective-permute-start.6 = (bf16[64,7168]{1,0:T(8,128)(2,1)}, bf16[64,7168]{1,0:T(8,128)(2,1)S(1)}, u32[]{:S(2)}, u32[]{:S(2)}) collective-permute-start(bf16[64,7168]{1,0:T(8,128)(2,1)} %collective-permute-done.5), channel_id=1, source_target_pairs={{0,3},{3,0},{1,2},{2,1},{4,7},{7,4},{5,6},{6,5},{8,11},{11,8},{9,1... | collective-permute-start | bytes 2752520 | tf_op jit(solution)/shard_map/ppermute | solution.py:66
  171.8 66.7 %copy-start.12 = (bf16[64,7168]{1,0:T(8,128)(2,1)S(1)}, bf16[64,7168]{1,0:T(8,128)(2,1)}, u32[]{:S(2)}) copy-start(bf16[64,7168]{1,0:T(8,128)(2,1)} %get-tuple-element.47) | copy-start | bytes 2752516
  226.5 12.0 %collective-permute-start.10 = (bf16[32,7168]{1,0:T(8,128)(2,1)S(1)}, bf16[32,7168]{1,0:T(8,128)(2,1)S(1)}, u32[]{:S(2)}, u32[]{:S(2)}) collective-permute-start(bf16[32,7168]{1,0:T(8,128)(2,1)S(1)} %slice.177), channel_id=1, source_target_pairs={{0,1},{1,0},{2,3},{3,2},{4,5},{5,4},{6,7},{7,6},{8,9},{9,8},{10,11... | collective-permute-start | bytes 1376264 | tf_op jit(solution)/shard_map/ppermute | solution.py:66
  238.5 5.0 %copy-start.3 = (bf16[1,7168,256]{2,1,0:T(8,128)(2,1)S(1)}, bf16[1,7168,256]{2,1,0:T(8,128)(2,1)}, u32[]{:S(2)}) copy-start(bf16[1,7168,256]{2,1,0:T(8,128)(2,1)} %param.10) | copy-start | bytes 11010052
  238.5 20.9 %collective-permute-start.7 = (bf16[64,7168]{1,0:T(8,128)(2,1)S(1)}, bf16[64,7168]{1,0:T(8,128)(2,1)S(1)}, u32[]{:S(2)}, u32[]{:S(2)}) collective-permute-start(bf16[64,7168]{1,0:T(8,128)(2,1)S(1)} %copy-done.12), channel_id=1, source_target_pairs={{0,1},{1,0},{2,3},{3,2},{4,5},{5,4},{6,7},{7,6},{8,9},{9,8},{10,11... | collective-permute-start | bytes 2752520 | tf_op jit(solution)/shard_map/ppermute | solution.py:66
  238.5 42.6 %collective-permute-start.11 = (bf16[32,7168]{1,0:T(8,128)(2,1)S(1)}, bf16[32,7168]{1,0:T(8,128)(2,1)S(1)}, u32[]{:S(2)}, u32[]{:S(2)}) collective-permute-start(bf16[32,7168]{1,0:T(8,128)(2,1)S(1)} %collective-permute-done.10), channel_id=1, source_target_pairs={{0,3},{3,0},{1,2},{2,1},{4,7},{7,4},{5,6},{6,5},{8,11},{11,8},{9,1... | collective-permute-start | bytes 1376264 | tf_op jit(solution)/shard_map/ppermute | solution.py:66
  259.5 21.7 %collective-permute-start.9 = (bf16[64,7168]{1,0:T(8,128)(2,1)S(1)}, bf16[64,7168]{1,0:T(8,128)(2,1)S(1)}, u32[]{:S(2)}, u32[]{:S(2)}) collective-permute-start(bf16[64,7168]{1,0:T(8,128)(2,1)S(1)} %collective-permute-done.7), channel_id=1, source_target_pairs={{0,3},{3,0},{1,2},{2,1},{4,7},{7,4},{5,6},{6,5},{8,11},{11,8},{9,1... | collective-permute-start | bytes 2752520 | tf_op jit(solution)/shard_map/ppermute | solution.py:66
  289.9 12.7 %collective-permute-start.27 = (bf16[80,3072]{1,0:T(8,128)(2,1)S(1)}, bf16[80,3072]{1,0:T(8,128)(2,1)S(1)}, u32[]{:S(2)}, u32[]{:S(2)}) collective-permute-start(bf16[80,3072]{1,0:T(8,128)(2,1)S(1)} %get-tuple-element.46), channel_id=1, source_target_pairs={{0,1},{1,0},{2,3},{3,2},{4,5},{5,4},{6,7},{7,6},{8,9},{9,8},{10,11... | collective-permute-start | bytes 1474568 | tf_op jit(solution)/shard_map/ppermute | solution.py:66
  294.7 51.3 %collective-permute-start.21 = (bf16[80,4096]{1,0:T(8,128)(2,1)S(1)}, bf16[80,4096]{1,0:T(8,128)(2,1)S(1)}, u32[]{:S(2)}, u32[]{:S(2)}) collective-permute-start(bf16[80,4096]{1,0:T(8,128)(2,1)S(1)} %get-tuple-element.42), channel_id=1, source_target_pairs={{0,1},{1,0},{2,3},{3,2},{4,5},{5,4},{6,7},{7,6},{8,9},{9,8},{10,11... | collective-permute-start | bytes 1966088 | tf_op jit(solution)/shard_map/ppermute | solution.py:66
  295.0 54.8 %collective-permute-start.19 = (bf16[80,4096]{1,0:T(8,128)(2,1)S(1)}, bf16[80,4096]{1,0:T(8,128)(2,1)S(1)}, u32[]{:S(2)}, u32[]{:S(2)}) collective-permute-start(bf16[80,4096]{1,0:T(8,128)(2,1)S(1)} %get-tuple-element.41), channel_id=1, source_target_pairs={{0,3},{3,0},{1,2},{2,1},{4,7},{7,4},{5,6},{6,5},{8,11},{11,8},{9,1... | collective-permute-start | bytes 1966088 | tf_op jit(solution)/shard_map/ppermute | solution.py:66
  298.4 84.2 %collective-permute-start.18 = (bf16[80,4096]{1,0:T(8,128)(2,1)}, bf16[80,4096]{1,0:T(8,128)(2,1)S(1)}, u32[]{:S(2)}, u32[]{:S(2)}) collective-permute-start(bf16[80,4096]{1,0:T(8,128)(2,1)} %slice.191), channel_id=1, source_target_pairs={{0,3},{3,0},{1,2},{2,1},{4,7},{7,4},{5,6},{6,5},{8,11},{11,8},{9,1... | collective-permute-start | bytes 1966088 | tf_op jit(solution)/shard_map/ppermute | solution.py:66
  298.4 53.3 %collective-permute-start.24 = (bf16[80,3072]{1,0:T(8,128)(2,1)S(1)}, bf16[80,3072]{1,0:T(8,128)(2,1)S(1)}, u32[]{:S(2)}, u32[]{:S(2)}) collective-permute-start(bf16[80,3072]{1,0:T(8,128)(2,1)S(1)} %slice.197), channel_id=1, source_target_pairs={{0,3},{3,0},{1,2},{2,1},{4,7},{7,4},{5,6},{6,5},{8,11},{11,8},{9,1... | collective-permute-start | bytes 1474568 | tf_op jit(solution)/shard_map/ppermute | solution.py:66
  302.6 63.4 %copy-start.8 = (bf16[160,7168]{1,0:T(8,128)(2,1)}, bf16[160,7168]{1,0:T(8,128)(2,1)S(1)}, u32[]{:S(2)}) copy-start(bf16[160,7168]{1,0:T(8,128)(2,1)S(1)} %convolution_convert_fusion.2) | copy-start | bytes 6881284
  302.6 43.3 %collective-permute-start.25 = (bf16[80,3072]{1,0:T(8,128)(2,1)S(1)}, bf16[80,3072]{1,0:T(8,128)(2,1)S(1)}, u32[]{:S(2)}, u32[]{:S(2)}) collective-permute-start(bf16[80,3072]{1,0:T(8,128)(2,1)S(1)} %get-tuple-element.45), channel_id=1, source_target_pairs={{0,3},{3,0},{1,2},{2,1},{4,7},{7,4},{5,6},{6,5},{8,11},{11,8},{9,1... | collective-permute-start | bytes 1474568 | tf_op jit(solution)/shard_map/ppermute | solution.py:66
  345.9 9.5 %collective-permute-start.29 = (bf16[80,3072]{1,0:T(8,128)(2,1)S(1)}, bf16[80,3072]{1,0:T(8,128)(2,1)S(1)}, u32[]{:S(2)}, u32[]{:S(2)}) collective-permute-start(bf16[80,3072]{1,0:T(8,128)(2,1)S(1)} %slice.201), channel_id=1, source_target_pairs={{0,1},{1,0},{2,3},{3,2},{4,5},{5,4},{6,7},{7,6},{8,9},{9,8},{10,11... | collective-permute-start | bytes 1474568 | tf_op jit(solution)/shard_map/ppermute | solution.py:66
  346.0 12.1 %collective-permute-start.28 = (bf16[80,3072]{1,0:T(8,128)(2,1)S(1)}, bf16[80,3072]{1,0:T(8,128)(2,1)S(1)}, u32[]{:S(2)}, u32[]{:S(2)}) collective-permute-start(bf16[80,3072]{1,0:T(8,128)(2,1)S(1)} %add_convert_fusion.5), channel_id=1, source_target_pairs={{0,3},{3,0},{1,2},{2,1},{4,7},{7,4},{5,6},{6,5},{8,11},{11,8},{9,1... | collective-permute-start | bytes 1474568 | tf_op jit(solution)/shard_map/ppermute | solution.py:66
  349.8 16.2 %collective-permute-start.26 = (bf16[80,3072]{1,0:T(8,128)(2,1)S(1)}, bf16[80,3072]{1,0:T(8,128)(2,1)S(1)}, u32[]{:S(2)}, u32[]{:S(2)}) collective-permute-start(bf16[80,3072]{1,0:T(8,128)(2,1)S(1)} %add_convert_fusion.7), channel_id=1, source_target_pairs={{0,1},{1,0},{2,3},{3,2},{4,5},{5,4},{6,7},{7,6},{8,9},{9,8},{10,11... | collective-permute-start | bytes 1474568 | tf_op jit(solution)/shard_map/ppermute | solution.py:66
  351.6 30.9 %collective-permute-start.23 = (bf16[80,4096]{1,0:T(8,128)(2,1)}, bf16[80,4096]{1,0:T(8,128)(2,1)}, u32[]{:S(2)}, u32[]{:S(2)}) collective-permute-start(bf16[80,4096]{1,0:T(8,128)(2,1)} %slice.195), channel_id=1, source_target_pairs={{0,1},{1,0},{2,3},{3,2},{4,5},{5,4},{6,7},{7,6},{8,9},{9,8},{10,11... | collective-permute-start | bytes 1966088 | tf_op jit(solution)/shard_map/ppermute | solution.py:66
  355.4 27.1 %collective-permute-start.22 = (bf16[80,4096]{1,0:T(8,128)(2,1)}, bf16[80,4096]{1,0:T(8,128)(2,1)}, u32[]{:S(2)}, u32[]{:S(2)}) collective-permute-start(bf16[80,4096]{1,0:T(8,128)(2,1)} %add_convert_fusion.1), channel_id=1, source_target_pairs={{0,3},{3,0},{1,2},{2,1},{4,7},{7,4},{5,6},{6,5},{8,11},{11,8},{9,1... | collective-permute-start | bytes 1966088 | tf_op jit(solution)/shard_map/ppermute | solution.py:66
  358.1 36.0 %collective-permute-start.20 = (bf16[80,4096]{1,0:T(8,128)(2,1)}, bf16[80,4096]{1,0:T(8,128)(2,1)}, u32[]{:S(2)}, u32[]{:S(2)}) collective-permute-start(bf16[80,4096]{1,0:T(8,128)(2,1)} %add_convert_fusion.3), channel_id=1, source_target_pairs={{0,1},{1,0},{2,3},{3,2},{4,5},{5,4},{6,7},{7,6},{8,9},{9,8},{10,11... | collective-permute-start | bytes 1966088 | tf_op jit(solution)/shard_map/ppermute | solution.py:66
  367.6 31.2 %all-to-all-start.2 = ((bf16[32,5,24,128]{3,2,1,0:T(8,128)(2,1)}), bf16[32,5,24,128]{3,2,1,0:T(8,128)(2,1)S(1)}, u32[]{:S(2)}, u32[]{:S(2)}) async-start(bf16[32,5,24,128]{3,2,1,0:T(8,128)(2,1)} %bitcast.26), calls=%async_computation.2 | async-start | bytes 1966080 | tf_op jit(solution)/shard_map/all_to_all | solution.py:139
  396.8 13.2 %copy-start.18 = (f32[128,1]{0,1:T(1,128)S(1)}, f32[128,1]{0,1:T(1,128)}, u32[]{:S(2)}) copy-start(f32[128,1]{0,1:T(1,128)} %param.9) | copy-start | bytes 1540
  399.8 30.0 %all-to-all-start.1 = ((bf16[32,5,32,128]{3,2,1,0:T(8,128)(2,1)}), bf16[32,5,32,128]{3,2,1,0:T(8,128)(2,1)S(1)}, u32[]{:S(2)}, u32[]{:S(2)}) async-start(bf16[32,5,32,128]{3,2,1,0:T(8,128)(2,1)} %bitcast.20), calls=%async_computation.1 | async-start | bytes 2621440 | tf_op jit(solution)/shard_map/all_to_all | solution.py:139
  429.8 2.5 copy-start.1
  (4 other events, 5.6 us)

commit v7 on v6

--- a/solution.py
+++ b/solution.py
@@ -100,20 +100,20 @@
     edge_up = jnp.where(outer, outer_up, inner_up)
     edge_into = jnp.concatenate([edge_gate, edge_up], axis=1)
     side = jnp.concatenate([side_a, side_b, side_c], axis=0)
-    far = jnp.concatenate([far_a, far_b, far_c], axis=0)
+    far = jnp.concatenate(lax.optimization_barrier((far_a, far_b, far_c)), axis=0)
 
     def full_hidden(block, mine):
         both = dot(block, edge_into)
         edge_hidden = jax.nn.silu(both[:, :inner]) * both[:, inner:] * edge
         return jnp.concatenate([mine, edge_hidden.astype(jnp.bfloat16)], axis=1)
 
-    pairs = ((far, own_hidden(far)), (mirror, mirror_own), (side, own_hidden(side)), (mid, home_own))
+    pairs = ((far, own_hidden(far)), (mirror, mirror_own), (side, own_hidden(side)))
     tied = lax.optimization_barrier((inner_down, inner_last, outer_down, *[full_hidden(*p) for p in pairs]))
     edge_down = jnp.where(outer, tied[2], jnp.concatenate(tied[:2], axis=0))
     down = jnp.concatenate([w_down, edge_down], axis=0)
     far = dot(tied[3], down).astype(jnp.bfloat16)
-    far, *rest = lax.optimization_barrier((far, *tied[4:]))
-    mirror, side, home = [dot(h, down).astype(jnp.bfloat16) for h in rest]
+    far, mirror, side, mid, home_own = lax.optimization_barrier((far, *tied[4:], mid, home_own))
+    mirror, side, home = [dot(h, down).astype(jnp.bfloat16) for h in (mirror, side, full_hidden(mid, home_own))]
 
     def added(u, v):
         return (u.astype(jnp.float32) + v.astype(jnp.float32)).astype(jnp.bfloat16)
@@ -121,7 +121,7 @@
     f32 = jnp.float32
     half = rows // 2
     upper, lower = slice(None, half), slice(half, None)
-    outs = []
+    result = jnp.zeros(tokens.shape, jnp.bfloat16)
     for lo, hi in ((0, 4096), (4096, width)):
         cols = slice(lo, hi)
         far_a = over(far[upper, cols], MIRROR)
@@ -138,8 +138,9 @@
         total = total.reshape(experts, CAPACITY, (hi - lo) // LANES, LANES)
         returned = lax.all_to_all(total, PLANE, 0, 0, tiled=True).reshape(rows, hi - lo)
         expert_out = lax.dot_general(picker, returned, (((0,), (0,)), ((), ())), preferred_element_type=f32)
-        outs.append((expert_out * gate_prob.reshape(-1)[:, None]).astype(jnp.bfloat16))
-    return jnp.concatenate(outs, axis=1)
+        mixed = (expert_out * gate_prob.reshape(-1)[:, None]).astype(jnp.bfloat16)
+        result = lax.dynamic_update_slice(result, mixed, (0, lo))
+    return result
 
 
 def solution(mesh):

time: 436 us -> 389 us (0.89)
  waiting for transfers between devices: 259 us -> 220 us
  starting transfers between devices: 104 us -> 94.8 us
    all_to_all x1, waiting for transfers between devices: 31 us -> 0.01 us  [body(): arrived = lax.all_to_all(outgoing, PLANE, 0, 0, tiled=True)]
    ppermute x1, waiting for transfers between devices: 0.01 us -> 9.91 us  [body(): outer_down = lax.ppermute(w_down[:inner], EVERY, straight)]
    ppermute x19, waiting for transfers between devices: 163 us -> 154 us  [over(): return lax.ppermute(block, 'x', pairs)]
    ppermute x4, waiting for transfers between devices: 46.4 us -> 39.6 us  [cross(): return lax.ppermute(block, 'x', INWARD)]
    all_to_all x2, starting transfers between devices: 25.1 us -> 19 us  [body(): lax.all_to_all(total, PLANE, 0, 0, tiled=True).reshape(rows, hi - lo)]
    unnamed x46 -> x40, local copies, waits for them, and re-layouts: 12.4 us -> 11.7 us
  transfers between devices with their start and end apart: 33 -> 33, of which waited for: 15 -> 16; matrix products, arithmetic and copies ran while one was open for 13% -> 14% of each run, Pallas kernels for 0% -> 0%
where the time goes in v7:
time: 389 us; the launch traced here: 386 us
  waiting for transfers between devices  220 us (57%)
  starting transfers between devices  94.8 us (24%)
  local copies, waits for them, and re-layouts  29.3 us (8%)
  matrix products  24.5 us (6%)
  other arithmetic  16.8 us (4%)
    ppermute x19, waiting for transfers between devices, over(): return lax.ppermute(block, 'x', pairs)  154 us
    ppermute x19, starting transfers between devices, over(): return lax.ppermute(block, 'x', pairs)  40.2 us
    ppermute x4, waiting for transfers between devices, cross(): return lax.ppermute(block, 'x', INWARD)  39.6 us
    dot_general x17, matrix products, dot(): return jnp.dot(a, b, preferred_element_type=jnp.float32)  21.3 us
    all_to_all x2, starting transfers between devices, body(): lax.all_to_all(total, PLANE, 0, 0, tiled=True).reshape(rows, hi - lo)  19 us
    all_to_all x2, waiting for transfers between devices, body(): lax.all_to_all(total, PLANE, 0, 0, tiled=True).reshape(rows, hi - lo)  17.3 us
    ppermute x4, starting transfers between devices, cross(): return lax.ppermute(block, 'x', INWARD)  12.6 us
    unnamed x40, local copies, waits for them, and re-layouts  11.7 us
  transfers between devices with their start and end apart: 33, of which 16 were waited for; matrix products, arithmetic and copies ran while one was open for 14% of the time, Pallas kernels for 0%

profile of v7, /device:TPU:7, one launch (start us, length us, event | category | flops | bytes accessed | tf_op | source)
XLA Modules:
  0.0 386.5 jit_solution(4121319189547692714)
XLA Ops:
  3.3 1.9 copy.8
  5.2 8.8 %all-to-all-start = ((bf16[32,5,56,128]{3,2,1,0:T(8,128)(2,1)}), bf16[32,5,56,128]{3,2,1,0:T(8,128)(2,1)}, u32[]{:S(2)}, u32[]{:S(2)}) async-start(bf16[32,5,56,128]{3,2,1,0:T(8,128)(2,1)} %bitcast.85), calls=%async_computation | async-start | bytes 4587520 | tf_op jit(solution)/shard_map/all_to_all | solution.py:71
  14.0 4.3 %fusion.52 = (bf16[7168,128]{1,0:T(8,128)(2,1)}, bf16[7168,128]{1,0:T(8,128)(2,1)}) fusion(bf16[7168,256]{1,0:T(8,128)(2,1)} %bitcast.86), kind=kLoop, calls=%fused_computation.102 | loop fusion | bytes 7340032 | tf_op jit(solution)/shard_map/slice | solution.py:70
  18.3 3.7 collective-permute-start.16
  22.0 3.2 collective-permute-start.15
  26.8 2.8 collective-permute-start.13
  29.5 3.6 collective-permute-start.12
  34.7 1.8 slice_bitcast_fusion.2
  37.5 2.9 slice_bitcast_fusion
  40.4 19.8 %collective-permute-done.16 = bf16[7168,128]{1,0:T(8,128)(2,1)} collective-permute-done((bf16[7168,128]{1,0:T(8,128)(2,1)}, bf16[7168,128]{1,0:T(8,128)(2,1)}, u32[]{:S(2)}, u32[]{:S(2)}) %collective-permute-start.16) | collective-permute-done | bytes 1835040 | tf_op jit(solution)/shard_map/ppermute | solution.py:63
  60.1 1.9 collective-permute-start.17
  62.0 2.1 copy.25
  66.9 3.5 collective-permute-start.5
  73.3 3.6 fusion.45
  77.1 2.6 fusion.7
  79.7 19.8 %collective-permute-done.13 = bf16[7168,128]{1,0:T(8,128)(2,1)} collective-permute-done((bf16[7168,128]{1,0:T(8,128)(2,1)}, bf16[7168,128]{1,0:T(8,128)(2,1)}, u32[]{:S(2)}, u32[]{:S(2)}) %collective-permute-start.13) | collective-permute-done | bytes 1835040 | tf_op jit(solution)/shard_map/ppermute | solution.py:63
  99.5 4.2 %collective-permute-start = (bf16[96,7168]{1,0:T(8,128)(2,1)S(1)}, bf16[96,7168]{1,0:T(8,128)(2,1)S(1)}, u32[]{:S(2)}, u32[]{:S(2)}) collective-permute-start(bf16[96,7168]{1,0:T(8,128)(2,1)S(1)} %slice_bitcast_fusion.1), channel_id=1, source_target_pairs={{0,1},{3,2},{4,5},{7,6},{8,9},{11,10},{12,13},{15,14},{16,17},{19,... | collective-permute-start | bytes 4128776 | tf_op jit(solution)/shard_map/ppermute | solution.py:63
  103.7 15.5 %collective-permute-done.5 = bf16[64,7168]{1,0:T(8,128)(2,1)} collective-permute-done((bf16[64,7168]{1,0:T(8,128)(2,1)}, bf16[64,7168]{1,0:T(8,128)(2,1)}, u32[]{:S(2)}, u32[]{:S(2)}) %collective-permute-start.5) | collective-permute-done | bytes 917536 | tf_op jit(solution)/shard_map/ppermute | solution.py:66
  122.1 6.0 %collective-permute-start.10 = (bf16[32,7168]{1,0:T(8,128)(2,1)S(1)}, bf16[32,7168]{1,0:T(8,128)(2,1)S(1)}, u32[]{:S(2)}, u32[]{:S(2)}) collective-permute-start(bf16[32,7168]{1,0:T(8,128)(2,1)S(1)} %slice.177), channel_id=1, source_target_pairs={{0,1},{1,0},{2,3},{3,2},{4,5},{5,4},{6,7},{7,6},{8,9},{9,8},{10,11... | collective-permute-start | bytes 1376264 | tf_op jit(solution)/shard_map/ppermute | solution.py:66
  128.1 1.7 broadcast_select_fusion
  129.8 1.9 collective-permute-start.2
  131.8 26.6 %collective-permute-done.10 = bf16[32,7168]{1,0:T(8,128)(2,1)S(1)} collective-permute-done((bf16[32,7168]{1,0:T(8,128)(2,1)S(1)}, bf16[32,7168]{1,0:T(8,128)(2,1)S(1)}, u32[]{:S(2)}, u32[]{:S(2)}) %collective-permute-start.10) | collective-permute-done | bytes 458784 | tf_op jit(solution)/shard_map/ppermute | solution.py:66
  158.4 2.2 collective-permute-start.7
  161.4 1.7 broadcast_select_fusion.1
  163.1 8.8 %collective-permute-done.8 = bf16[160,7168]{1,0:T(8,128)(2,1)S(1)} collective-permute-done((bf16[160,7168]{1,0:T(8,128)(2,1)S(1)}, bf16[160,7168]{1,0:T(8,128)(2,1)S(1)}, u32[]{:S(2)}, u32[]{:S(2)}) %collective-permute-start.8) | collective-permute-done | bytes 2293792 | tf_op jit(solution)/shard_map/ppermute | solution.py:66
  174.5 13.4 %collective-permute-done.7 = bf16[64,7168]{1,0:T(8,128)(2,1)S(1)} collective-permute-done((bf16[64,7168]{1,0:T(8,128)(2,1)S(1)}, bf16[64,7168]{1,0:T(8,128)(2,1)S(1)}, u32[]{:S(2)}, u32[]{:S(2)}) %collective-permute-start.7) | collective-permute-done | bytes 917536 | tf_op jit(solution)/shard_map/ppermute | solution.py:66
  193.5 3.2 collective-permute-start.4
  198.1 3.3 collective-permute-done.6
  201.5 19.7 %collective-permute-done.9 = bf16[64,7168]{1,0:T(8,128)(2,1)S(1)} collective-permute-done((bf16[64,7168]{1,0:T(8,128)(2,1)S(1)}, bf16[64,7168]{1,0:T(8,128)(2,1)S(1)}, u32[]{:S(2)}, u32[]{:S(2)}) %collective-permute-start.9) | collective-permute-done | bytes 917536 | tf_op jit(solution)/shard_map/ppermute | solution.py:66
  224.6 9.9 %collective-permute-done.4 = bf16[128,7168]{1,0:T(8,128)(2,1)S(1)} collective-permute-done((bf16[128,7168]{1,0:T(8,128)(2,1)S(1)}, bf16[128,7168]{1,0:T(8,128)(2,1)S(1)}, u32[]{:S(2)}, u32[]{:S(2)}) %collective-permute-start.4) | collective-permute-done | bytes 1835040 | tf_op jit(solution)/shard_map/ppermute | solution.py:83
  236.7 1.6 convolution_convert_fusion.1
  241.7 2.5 collective-permute-start.21
  244.2 5.2 %collective-permute-start.19 = (bf16[80,4096]{1,0:T(8,128)(2,1)S(1)}, bf16[80,4096]{1,0:T(8,128)(2,1)S(1)}, u32[]{:S(2)}, u32[]{:S(2)}) collective-permute-start(bf16[80,4096]{1,0:T(8,128)(2,1)S(1)} %get-tuple-element.47), channel_id=1, source_target_pairs={{0,3},{3,0},{1,2},{2,1},{4,7},{7,4},{5,6},{6,5},{8,11},{11,8},{9,1... | collective-permute-start | bytes 1966088 | tf_op jit(solution)/shard_map/ppermute | solution.py:66
  250.4 2.6 collective-permute-start.24
  255.3 12.2 %collective-permute-done.27 = bf16[80,3072]{1,0:T(8,128)(2,1)S(1)} collective-permute-done((bf16[80,3072]{1,0:T(8,128)(2,1)S(1)}, bf16[80,3072]{1,0:T(8,128)(2,1)S(1)}, u32[]{:S(2)}, u32[]{:S(2)}) %collective-permute-start.27) | collective-permute-done | bytes 491552 | tf_op jit(solution)/shard_map/ppermute | solution.py:66
  267.5 7.7 %collective-permute-start.25 = (bf16[80,3072]{1,0:T(8,128)(2,1)S(1)}, bf16[80,3072]{1,0:T(8,128)(2,1)S(1)}, u32[]{:S(2)}, u32[]{:S(2)}) collective-permute-start(bf16[80,3072]{1,0:T(8,128)(2,1)S(1)} %get-tuple-element.51), channel_id=1, source_target_pairs={{0,3},{3,0},{1,2},{2,1},{4,7},{7,4},{5,6},{6,5},{8,11},{11,8},{9,1... | collective-permute-start | bytes 1474568 | tf_op jit(solution)/shard_map/ppermute | solution.py:66
  275.3 24.0 %collective-permute-done.25 = bf16[80,3072]{1,0:T(8,128)(2,1)S(1)} collective-permute-done((bf16[80,3072]{1,0:T(8,128)(2,1)S(1)}, bf16[80,3072]{1,0:T(8,128)(2,1)S(1)}, u32[]{:S(2)}, u32[]{:S(2)}) %collective-permute-start.25) | collective-permute-done | bytes 491552 | tf_op jit(solution)/shard_map/ppermute | solution.py:66
  299.4 2.9 collective-permute-start.28
  305.8 5.3 %collective-permute-done.29 = bf16[80,3072]{1,0:T(8,128)(2,1)S(1)} collective-permute-done((bf16[80,3072]{1,0:T(8,128)(2,1)S(1)}, bf16[80,3072]{1,0:T(8,128)(2,1)S(1)}, u32[]{:S(2)}, u32[]{:S(2)}) %collective-permute-start.29) | collective-permute-done | bytes 491552 | tf_op jit(solution)/shard_map/ppermute | solution.py:66
  311.1 2.5 collective-permute-start.22
  313.6 8.1 %collective-permute-done.26 = bf16[80,3072]{1,0:T(8,128)(2,1)S(1)} collective-permute-done((bf16[80,3072]{1,0:T(8,128)(2,1)S(1)}, bf16[80,3072]{1,0:T(8,128)(2,1)S(1)}, u32[]{:S(2)}, u32[]{:S(2)}) %collective-permute-start.26) | collective-permute-done | bytes 491552 | tf_op jit(solution)/shard_map/ppermute | solution.py:66
  323.4 9.6 %all-to-all-start.2 = ((bf16[32,5,24,128]{3,2,1,0:T(8,128)(2,1)}), bf16[32,5,24,128]{3,2,1,0:T(8,128)(2,1)S(1)}, u32[]{:S(2)}, u32[]{:S(2)}) async-start(bf16[32,5,24,128]{3,2,1,0:T(8,128)(2,1)} %bitcast.26), calls=%async_computation.2 | async-start | bytes 1966080 | tf_op jit(solution)/shard_map/all_to_all | solution.py:139
  333.0 2.7 collective-permute-done.23
  335.8 14.0 %collective-permute-done.20 = bf16[80,4096]{1,0:T(8,128)(2,1)} collective-permute-done((bf16[80,4096]{1,0:T(8,128)(2,1)}, bf16[80,4096]{1,0:T(8,128)(2,1)}, u32[]{:S(2)}, u32[]{:S(2)}) %collective-permute-start.20) | collective-permute-done | bytes 655392 | tf_op jit(solution)/shard_map/ppermute | solution.py:66
  349.8 2.5 add_convert_fusion.2
  354.8 9.4 %all-to-all-start.1 = ((bf16[32,5,32,128]{3,2,1,0:T(8,128)(2,1)}), bf16[32,5,32,128]{3,2,1,0:T(8,128)(2,1)S(1)}, u32[]{:S(2)}, u32[]{:S(2)}) async-start(bf16[32,5,32,128]{3,2,1,0:T(8,128)(2,1)} %bitcast.20), calls=%async_computation.1 | async-start | bytes 2621440 | tf_op jit(solution)/shard_map/all_to_all | solution.py:139
  364.2 2.5 fusion.1
  366.7 17.3 %all-to-all-done.1 = bf16[32,5,32,128]{3,2,1,0:T(8,128)(2,1)S(1)} async-done(((bf16[32,5,32,128]{3,2,1,0:T(8,128)(2,1)}), bf16[32,5,32,128]{3,2,1,0:T(8,128)(2,1)S(1)}, u32[]{:S(2)}, u32[]{:S(2)}) %all-to-all-start.1) | async-done | bytes 1310752 | tf_op jit(solution)/shard_map/all_to_all | solution.py:139
  (121 shorter events, 48.8 us)
Async XLA Ops:
  0.0 2.6 copy-start
  5.2 56.9 %all-to-all-start = ((bf16[32,5,56,128]{3,2,1,0:T(8,128)(2,1)}), bf16[32,5,56,128]{3,2,1,0:T(8,128)(2,1)}, u32[]{:S(2)}, u32[]{:S(2)}) async-start(bf16[32,5,56,128]{3,2,1,0:T(8,128)(2,1)} %bitcast.85), calls=%async_computation | async-start | bytes 4587520 | tf_op jit(solution)/shard_map/all_to_all | solution.py:71
  14.0 11.3 %copy-start.2 = (bf16[1,7168,256]{2,1,0:T(8,128)(2,1)S(1)}, bf16[1,7168,256]{2,1,0:T(8,128)(2,1)}, u32[]{:S(2)}) copy-start(bf16[1,7168,256]{2,1,0:T(8,128)(2,1)} %param.10) | copy-start | bytes 11010052
  18.3 41.8 %collective-permute-start.16 = (bf16[7168,128]{1,0:T(8,128)(2,1)}, bf16[7168,128]{1,0:T(8,128)(2,1)}, u32[]{:S(2)}, u32[]{:S(2)}) collective-permute-start(bf16[7168,128]{1,0:T(8,128)(2,1)} %get-tuple-element.43), channel_id=1, source_target_pairs={{0,1},{3,2},{4,5},{7,6},{8,9},{11,10},{12,13},{15,14},{16,17},{19,... | collective-permute-start | bytes 5505032 | tf_op jit(solution)/shard_map/ppermute | solution.py:63
  22.0 99.1 %collective-permute-start.15 = (bf16[7168,128]{1,0:T(8,128)(2,1)}, bf16[7168,128]{1,0:T(8,128)(2,1)}, u32[]{:S(2)}, u32[]{:S(2)}) collective-permute-start(bf16[7168,128]{1,0:T(8,128)(2,1)} %get-tuple-element.44), channel_id=1, source_target_pairs={{3,7},{0,124},{7,11},{4,0},{11,15},{8,4},{15,19},{12,8},{19,23},{1... | collective-permute-start | bytes 5505032 | tf_op jit(solution)/shard_map/ppermute | solution.py:82
  26.8 9.7 %copy-start.14 = (s32[128,2]{0,1:T(2,128)S(1)}, s32[128,2]{0,1:T(2,128)}, u32[]{:S(2)}) copy-start(s32[128,2]{0,1:T(2,128)} %param.13) | copy-start | bytes 3076
  26.8 72.7 %collective-permute-start.13 = (bf16[7168,128]{1,0:T(8,128)(2,1)}, bf16[7168,128]{1,0:T(8,128)(2,1)}, u32[]{:S(2)}, u32[]{:S(2)}) collective-permute-start(bf16[7168,128]{1,0:T(8,128)(2,1)} %get-tuple-element.41), channel_id=1, source_target_pairs={{0,1},{3,2},{4,5},{7,6},{8,9},{11,10},{12,13},{15,14},{16,17},{19,... | collective-permute-start | bytes 5505032 | tf_op jit(solution)/shard_map/ppermute | solution.py:63
  29.5 100.3 %collective-permute-start.12 = (bf16[7168,128]{1,0:T(8,128)(2,1)S(1)}, bf16[7168,128]{1,0:T(8,128)(2,1)}, u32[]{:S(2)}, u32[]{:S(2)}) collective-permute-start(bf16[7168,128]{1,0:T(8,128)(2,1)S(1)} %get-tuple-element.42), channel_id=1, source_target_pairs={{3,7},{0,124},{7,11},{4,0},{11,15},{8,4},{15,19},{12,8},{19,23},{1... | collective-permute-start | bytes 5505032 | tf_op jit(solution)/shard_map/ppermute | solution.py:81
  60.1 62.0 %collective-permute-start.17 = (bf16[7168,128]{1,0:T(8,128)(2,1)}, bf16[7168,128]{1,0:T(8,128)(2,1)}, u32[]{:S(2)}, u32[]{:S(2)}) collective-permute-start(bf16[7168,128]{1,0:T(8,128)(2,1)} %collective-permute-done.16), channel_id=1, source_target_pairs={{2,6},{1,125},{6,10},{5,1},{10,14},{9,5},{14,18},{13,9},{18,22},{1... | collective-permute-start | bytes 5505032 | tf_op jit(solution)/shard_map/ppermute | solution.py:91
  64.1 1.4 copy-start.4
  66.9 52.2 %collective-permute-start.5 = (bf16[64,7168]{1,0:T(8,128)(2,1)}, bf16[64,7168]{1,0:T(8,128)(2,1)}, u32[]{:S(2)}, u32[]{:S(2)}) collective-permute-start(bf16[64,7168]{1,0:T(8,128)(2,1)} %get-tuple-element.54), channel_id=1, source_target_pairs={{0,1},{1,0},{2,3},{3,2},{4,5},{5,4},{6,7},{7,6},{8,9},{9,8},{10,11... | collective-permute-start | bytes 2752520 | tf_op jit(solution)/shard_map/ppermute | solution.py:66
  73.3 3.8 copy-start.6
  77.1 44.1 %copy-start.5 = (bf16[20,8,56,128]{3,1,2,0:T(8,128)(2,1)S(1)}, bf16[20,8,56,128]{3,1,2,0:T(8,128)(2,1)}, u32[]{:S(2)}) copy-start(bf16[20,8,56,128]{3,1,2,0:T(8,128)(2,1)} %copy-done.4) | copy-start | bytes 6881284
  99.5 97.2 %collective-permute-start = (bf16[96,7168]{1,0:T(8,128)(2,1)S(1)}, bf16[96,7168]{1,0:T(8,128)(2,1)S(1)}, u32[]{:S(2)}, u32[]{:S(2)}) collective-permute-start(bf16[96,7168]{1,0:T(8,128)(2,1)S(1)} %slice_bitcast_fusion.1), channel_id=1, source_target_pairs={{0,1},{3,2},{4,5},{7,6},{8,9},{11,10},{12,13},{15,14},{16,17},{19,... | collective-permute-start | bytes 4128776 | tf_op jit(solution)/shard_map/ppermute | solution.py:63
  119.1 41.4 %collective-permute-start.14 = (bf16[7168,128]{1,0:T(8,128)(2,1)}, bf16[7168,128]{1,0:T(8,128)(2,1)S(1)}, u32[]{:S(2)}, u32[]{:S(2)}) collective-permute-start(bf16[7168,128]{1,0:T(8,128)(2,1)} %collective-permute-done.13), channel_id=1, source_target_pairs={{2,6},{1,125},{6,10},{5,1},{10,14},{9,5},{14,18},{13,9},{18,22},{1... | collective-permute-start | bytes 5505032 | tf_op jit(solution)/shard_map/ppermute | solution.py:89
  121.1 8.7 %copy-start.13 = (bf16[32,7168]{1,0:T(8,128)(2,1)S(1)}, bf16[32,7168]{1,0:T(8,128)(2,1)}, u32[]{:S(2)}) copy-start(bf16[32,7168]{1,0:T(8,128)(2,1)} %slice_bitcast_fusion.2) | copy-start | bytes 1376260
  121.2 37.2 %copy-start.11 = (bf16[64,7168]{1,0:T(8,128)(2,1)S(1)}, bf16[64,7168]{1,0:T(8,128)(2,1)}, u32[]{:S(2)}) copy-start(bf16[64,7168]{1,0:T(8,128)(2,1)} %get-tuple-element.53) | copy-start | bytes 2752516
  121.2 50.8 %collective-permute-start.8 = (bf16[160,7168]{1,0:T(8,128)(2,1)S(1)}, bf16[160,7168]{1,0:T(8,128)(2,1)S(1)}, u32[]{:S(2)}, u32[]{:S(2)}) collective-permute-start(bf16[160,7168]{1,0:T(8,128)(2,1)S(1)} %bitcast.83), channel_id=1, source_target_pairs={{0,3},{3,0},{1,2},{2,1},{4,7},{7,4},{5,6},{6,5},{8,11},{11,8},{9,1... | collective-permute-start | bytes 6881288 | tf_op jit(solution)/shard_map/ppermute | solution.py:66
  122.1 36.2 %collective-permute-start.10 = (bf16[32,7168]{1,0:T(8,128)(2,1)S(1)}, bf16[32,7168]{1,0:T(8,128)(2,1)S(1)}, u32[]{:S(2)}, u32[]{:S(2)}) collective-permute-start(bf16[32,7168]{1,0:T(8,128)(2,1)S(1)} %slice.177), channel_id=1, source_target_pairs={{0,1},{1,0},{2,3},{3,2},{4,5},{5,4},{6,7},{7,6},{8,9},{9,8},{10,11... | collective-permute-start | bytes 1376264 | tf_op jit(solution)/shard_map/ppermute | solution.py:66
  129.8 63.0 %collective-permute-start.2 = (bf16[32,7168]{1,0:T(8,128)(2,1)S(1)}, bf16[32,7168]{1,0:T(8,128)(2,1)S(1)}, u32[]{:S(2)}, u32[]{:S(2)}) collective-permute-start(bf16[32,7168]{1,0:T(8,128)(2,1)S(1)} %copy-done.13), channel_id=1, source_target_pairs={{0,1},{3,2},{4,5},{7,6},{8,9},{11,10},{12,13},{15,14},{16,17},{19,... | collective-permute-start | bytes 1376264 | tf_op jit(solution)/shard_map/ppermute | solution.py:63
  158.4 14.5 %copy-start.3 = (bf16[1,7168,256]{2,1,0:T(8,128)(2,1)S(1)}, bf16[1,7168,256]{2,1,0:T(8,128)(2,1)}, u32[]{:S(2)}) copy-start(bf16[1,7168,256]{2,1,0:T(8,128)(2,1)} %param.10) | copy-start | bytes 11010052
  158.4 29.5 %collective-permute-start.7 = (bf16[64,7168]{1,0:T(8,128)(2,1)S(1)}, bf16[64,7168]{1,0:T(8,128)(2,1)S(1)}, u32[]{:S(2)}, u32[]{:S(2)}) collective-permute-start(bf16[64,7168]{1,0:T(8,128)(2,1)S(1)} %copy-done.11), channel_id=1, source_target_pairs={{0,1},{1,0},{2,3},{3,2},{4,5},{5,4},{6,7},{7,6},{8,9},{9,8},{10,11... | collective-permute-start | bytes 2752520 | tf_op jit(solution)/shard_map/ppermute | solution.py:66
  160.6 36.8 %collective-permute-start.11 = (bf16[32,7168]{1,0:T(8,128)(2,1)S(1)}, bf16[32,7168]{1,0:T(8,128)(2,1)S(1)}, u32[]{:S(2)}, u32[]{:S(2)}) collective-permute-start(bf16[32,7168]{1,0:T(8,128)(2,1)S(1)} %collective-permute-done.10), channel_id=1, source_target_pairs={{0,3},{3,0},{1,2},{2,1},{4,7},{7,4},{5,6},{6,5},{8,11},{11,8},{9,1... | collective-permute-start | bytes 1376264 | tf_op jit(solution)/shard_map/ppermute | solution.py:66
  172.0 29.5 %collective-permute-start.6 = (bf16[64,7168]{1,0:T(8,128)(2,1)}, bf16[64,7168]{1,0:T(8,128)(2,1)S(1)}, u32[]{:S(2)}, u32[]{:S(2)}) collective-permute-start(bf16[64,7168]{1,0:T(8,128)(2,1)} %collective-permute-done.5), channel_id=1, source_target_pairs={{0,3},{3,0},{1,2},{2,1},{4,7},{7,4},{5,6},{6,5},{8,11},{11,8},{9,1... | collective-permute-start | bytes 2752520 | tf_op jit(solution)/shard_map/ppermute | solution.py:66
  187.8 33.3 %collective-permute-start.9 = (bf16[64,7168]{1,0:T(8,128)(2,1)S(1)}, bf16[64,7168]{1,0:T(8,128)(2,1)S(1)}, u32[]{:S(2)}, u32[]{:S(2)}) collective-permute-start(bf16[64,7168]{1,0:T(8,128)(2,1)S(1)} %collective-permute-done.7), channel_id=1, source_target_pairs={{0,3},{3,0},{1,2},{2,1},{4,7},{7,4},{5,6},{6,5},{8,11},{11,8},{9,1... | collective-permute-start | bytes 2752520 | tf_op jit(solution)/shard_map/ppermute | solution.py:66
  192.0 1.5 copy-start.9
  193.5 41.0 %collective-permute-start.4 = (bf16[128,7168]{1,0:T(8,128)(2,1)S(1)}, bf16[128,7168]{1,0:T(8,128)(2,1)S(1)}, u32[]{:S(2)}, u32[]{:S(2)}) collective-permute-start(bf16[128,7168]{1,0:T(8,128)(2,1)S(1)} %copy-done.9), channel_id=1, source_target_pairs={{3,7},{0,124},{7,11},{4,0},{11,15},{8,4},{15,19},{12,8},{19,23},{1... | collective-permute-start | bytes 5505032 | tf_op jit(solution)/shard_map/ppermute | solution.py:83
  196.7 27.9 %collective-permute-start.3 = (bf16[32,7168]{1,0:T(8,128)(2,1)S(1)}, bf16[32,7168]{1,0:T(8,128)(2,1)S(1)}, u32[]{:S(2)}, u32[]{:S(2)}) collective-permute-start(bf16[32,7168]{1,0:T(8,128)(2,1)S(1)} %collective-permute-done.2), channel_id=1, source_target_pairs={{2,6},{1,125},{6,10},{5,1},{10,14},{9,5},{14,18},{13,9},{18,22},{1... | collective-permute-start | bytes 1376264 | tf_op jit(solution)/shard_map/ppermute | solution.py:96
  197.4 37.1 %collective-permute-start.1 = (bf16[96,7168]{1,0:T(8,128)(2,1)S(1)}, bf16[96,7168]{1,0:T(8,128)(2,1)S(1)}, u32[]{:S(2)}, u32[]{:S(2)}) collective-permute-start(bf16[96,7168]{1,0:T(8,128)(2,1)S(1)} %collective-permute-done), channel_id=1, source_target_pairs={{2,6},{1,125},{6,10},{5,1},{10,14},{9,5},{14,18},{13,9},{18,22},{1... | collective-permute-start | bytes 4128776 | tf_op jit(solution)/shard_map/ppermute | solution.py:88
  224.5 10.4 %copy-start.7 = (bf16[1,256,7168]{2,1,0:T(8,128)(2,1)S(1)}, bf16[1,256,7168]{2,1,0:T(8,128)(2,1)}, u32[]{:S(2)}) copy-start(bf16[1,256,7168]{2,1,0:T(8,128)(2,1)} %param.12) | copy-start | bytes 11010052
  241.7 57.7 %collective-permute-start.21 = (bf16[80,4096]{1,0:T(8,128)(2,1)S(1)}, bf16[80,4096]{1,0:T(8,128)(2,1)S(1)}, u32[]{:S(2)}, u32[]{:S(2)}) collective-permute-start(bf16[80,4096]{1,0:T(8,128)(2,1)S(1)} %get-tuple-element.48), channel_id=1, source_target_pairs={{0,1},{1,0},{2,3},{3,2},{4,5},{5,4},{6,7},{7,6},{8,9},{9,8},{10,11... | collective-permute-start | bytes 1966088 | tf_op jit(solution)/shard_map/ppermute | solution.py:66
  244.2 59.1 %collective-permute-start.19 = (bf16[80,4096]{1,0:T(8,128)(2,1)S(1)}, bf16[80,4096]{1,0:T(8,128)(2,1)S(1)}, u32[]{:S(2)}, u32[]{:S(2)}) collective-permute-start(bf16[80,4096]{1,0:T(8,128)(2,1)S(1)} %get-tuple-element.47), channel_id=1, source_target_pairs={{0,3},{3,0},{1,2},{2,1},{4,7},{7,4},{5,6},{6,5},{8,11},{11,8},{9,1... | collective-permute-start | bytes 1966088 | tf_op jit(solution)/shard_map/ppermute | solution.py:66
  250.2 82.8 %collective-permute-start.18 = (bf16[80,4096]{1,0:T(8,128)(2,1)}, bf16[80,4096]{1,0:T(8,128)(2,1)S(1)}, u32[]{:S(2)}, u32[]{:S(2)}) collective-permute-start(bf16[80,4096]{1,0:T(8,128)(2,1)} %slice.191), channel_id=1, source_target_pairs={{0,3},{3,0},{1,2},{2,1},{4,7},{7,4},{5,6},{6,5},{8,11},{11,8},{9,1... | collective-permute-start | bytes 1966088 | tf_op jit(solution)/shard_map/ppermute | solution.py:66
  250.3 17.2 %collective-permute-start.27 = (bf16[80,3072]{1,0:T(8,128)(2,1)S(1)}, bf16[80,3072]{1,0:T(8,128)(2,1)S(1)}, u32[]{:S(2)}, u32[]{:S(2)}) collective-permute-start(bf16[80,3072]{1,0:T(8,128)(2,1)S(1)} %get-tuple-element.52), channel_id=1, source_target_pairs={{0,1},{1,0},{2,3},{3,2},{4,5},{5,4},{6,7},{7,6},{8,9},{9,8},{10,11... | collective-permute-start | bytes 1474568 | tf_op jit(solution)/shard_map/ppermute | solution.py:66
  250.4 54.8 %collective-permute-start.24 = (bf16[80,3072]{1,0:T(8,128)(2,1)S(1)}, bf16[80,3072]{1,0:T(8,128)(2,1)S(1)}, u32[]{:S(2)}, u32[]{:S(2)}) collective-permute-start(bf16[80,3072]{1,0:T(8,128)(2,1)S(1)} %slice.197), channel_id=1, source_target_pairs={{0,3},{3,0},{1,2},{2,1},{4,7},{7,4},{5,6},{6,5},{8,11},{11,8},{9,1... | collective-permute-start | bytes 1474568 | tf_op jit(solution)/shard_map/ppermute | solution.py:66
  255.2 66.5 %copy-start.8 = (bf16[160,7168]{1,0:T(8,128)(2,1)}, bf16[160,7168]{1,0:T(8,128)(2,1)S(1)}, u32[]{:S(2)}) copy-start(bf16[160,7168]{1,0:T(8,128)(2,1)S(1)} %convolution_convert_fusion.2) | copy-start | bytes 6881284
  267.5 31.8 %collective-permute-start.25 = (bf16[80,3072]{1,0:T(8,128)(2,1)S(1)}, bf16[80,3072]{1,0:T(8,128)(2,1)S(1)}, u32[]{:S(2)}, u32[]{:S(2)}) collective-permute-start(bf16[80,3072]{1,0:T(8,128)(2,1)S(1)} %get-tuple-element.51), channel_id=1, source_target_pairs={{0,3},{3,0},{1,2},{2,1},{4,7},{7,4},{5,6},{6,5},{8,11},{11,8},{9,1... | collective-permute-start | bytes 1474568 | tf_op jit(solution)/shard_map/ppermute | solution.py:66
  299.3 11.8 %collective-permute-start.29 = (bf16[80,3072]{1,0:T(8,128)(2,1)S(1)}, bf16[80,3072]{1,0:T(8,128)(2,1)S(1)}, u32[]{:S(2)}, u32[]{:S(2)}) collective-permute-start(bf16[80,3072]{1,0:T(8,128)(2,1)S(1)} %slice.201), channel_id=1, source_target_pairs={{0,1},{1,0},{2,3},{3,2},{4,5},{5,4},{6,7},{7,6},{8,9},{9,8},{10,11... | collective-permute-start | bytes 1474568 | tf_op jit(solution)/shard_map/ppermute | solution.py:66
  299.4 14.2 %collective-permute-start.28 = (bf16[80,3072]{1,0:T(8,128)(2,1)S(1)}, bf16[80,3072]{1,0:T(8,128)(2,1)S(1)}, u32[]{:S(2)}, u32[]{:S(2)}) collective-permute-start(bf16[80,3072]{1,0:T(8,128)(2,1)S(1)} %add_convert_fusion.5), channel_id=1, source_target_pairs={{0,3},{3,0},{1,2},{2,1},{4,7},{7,4},{5,6},{6,5},{8,11},{11,8},{9,1... | collective-permute-start | bytes 1474568 | tf_op jit(solution)/shard_map/ppermute | solution.py:66
  303.3 18.4 %collective-permute-start.26 = (bf16[80,3072]{1,0:T(8,128)(2,1)S(1)}, bf16[80,3072]{1,0:T(8,128)(2,1)S(1)}, u32[]{:S(2)}, u32[]{:S(2)}) collective-permute-start(bf16[80,3072]{1,0:T(8,128)(2,1)S(1)} %add_convert_fusion.7), channel_id=1, source_target_pairs={{0,1},{1,0},{2,3},{3,2},{4,5},{5,4},{6,7},{7,6},{8,9},{9,8},{10,11... | collective-permute-start | bytes 1474568 | tf_op jit(solution)/shard_map/ppermute | solution.py:66
  305.2 30.6 %collective-permute-start.23 = (bf16[80,4096]{1,0:T(8,128)(2,1)}, bf16[80,4096]{1,0:T(8,128)(2,1)}, u32[]{:S(2)}, u32[]{:S(2)}) collective-permute-start(bf16[80,4096]{1,0:T(8,128)(2,1)} %slice.195), channel_id=1, source_target_pairs={{0,1},{1,0},{2,3},{3,2},{4,5},{5,4},{6,7},{7,6},{8,9},{9,8},{10,11... | collective-permute-start | bytes 1966088 | tf_op jit(solution)/shard_map/ppermute | solution.py:66
  311.1 24.7 %collective-permute-start.22 = (bf16[80,4096]{1,0:T(8,128)(2,1)}, bf16[80,4096]{1,0:T(8,128)(2,1)}, u32[]{:S(2)}, u32[]{:S(2)}) collective-permute-start(bf16[80,4096]{1,0:T(8,128)(2,1)} %add_convert_fusion.1), channel_id=1, source_target_pairs={{0,3},{3,0},{1,2},{2,1},{4,7},{7,4},{5,6},{6,5},{8,11},{11,8},{9,1... | collective-permute-start | bytes 1966088 | tf_op jit(solution)/shard_map/ppermute | solution.py:66
  313.6 36.2 %collective-permute-start.20 = (bf16[80,4096]{1,0:T(8,128)(2,1)}, bf16[80,4096]{1,0:T(8,128)(2,1)}, u32[]{:S(2)}, u32[]{:S(2)}) collective-permute-start(bf16[80,4096]{1,0:T(8,128)(2,1)} %add_convert_fusion.3), channel_id=1, source_target_pairs={{0,1},{1,0},{2,3},{3,2},{4,5},{5,4},{6,7},{7,6},{8,9},{9,8},{10,11... | collective-permute-start | bytes 1966088 | tf_op jit(solution)/shard_map/ppermute | solution.py:66
  323.4 30.4 %all-to-all-start.2 = ((bf16[32,5,24,128]{3,2,1,0:T(8,128)(2,1)}), bf16[32,5,24,128]{3,2,1,0:T(8,128)(2,1)S(1)}, u32[]{:S(2)}, u32[]{:S(2)}) async-start(bf16[32,5,24,128]{3,2,1,0:T(8,128)(2,1)} %bitcast.26), calls=%async_computation.2 | async-start | bytes 1966080 | tf_op jit(solution)/shard_map/all_to_all | solution.py:139
  352.4 11.8 %copy-start.15 = (f32[128,1]{0,1:T(1,128)S(1)}, f32[128,1]{0,1:T(1,128)}, u32[]{:S(2)}) copy-start(f32[128,1]{0,1:T(1,128)} %param.9) | copy-start | bytes 1540
  354.8 29.2 %all-to-all-start.1 = ((bf16[32,5,32,128]{3,2,1,0:T(8,128)(2,1)}), bf16[32,5,32,128]{3,2,1,0:T(8,128)(2,1)S(1)}, u32[]{:S(2)}, u32[]{:S(2)}) async-start(bf16[32,5,32,128]{3,2,1,0:T(8,128)(2,1)} %bitcast.20), calls=%async_computation.1 | async-start | bytes 2621440 | tf_op jit(solution)/shard_map/all_to_all | solution.py:139
  384.0 1.1 copy-start.12
  384.0 2.5 copy-start.1
  (1 other events, 1.0 us)

commit v8 on v7

--- a/solution.py
+++ b/solution.py
@@ -69,6 +69,7 @@
     inward_gate = cross(w_gate[:, inner:])
     inward_up = cross(w_up[:, inner:])
     arrived = lax.all_to_all(outgoing, PLANE, 0, 0, tiled=True)
+    outer_early = lax.ppermute(w_down[: inner // 2], EVERY, straight)
     mid = arrived.reshape(rows, width)
 
     kept, edge = multiplicities(partner, own, slots)
@@ -80,7 +81,7 @@
     mirror = over(mid, MIRROR)
     outer_gate = lax.ppermute(w_gate[:, :inner], EVERY, straight)
     outer_up = lax.ppermute(w_up[:, :inner], EVERY, straight)
-    outer_down = lax.ppermute(w_down[:inner], EVERY, straight)
+    outer_late = lax.ppermute(w_down[inner // 2 : inner], EVERY, straight)
     side_a = over(mid[:64], SIDE)
     side_b = over(mid[64:128], SIDE)
     side_c = over(mid[128:], SIDE)
@@ -108,12 +109,14 @@
         return jnp.concatenate([mine, edge_hidden.astype(jnp.bfloat16)], axis=1)
 
     pairs = ((far, own_hidden(far)), (mirror, mirror_own), (side, own_hidden(side)))
-    tied = lax.optimization_barrier((inner_down, inner_last, outer_down, *[full_hidden(*p) for p in pairs]))
-    edge_down = jnp.where(outer, tied[2], jnp.concatenate(tied[:2], axis=0))
-    down = jnp.concatenate([w_down, edge_down], axis=0)
-    far = dot(tied[3], down).astype(jnp.bfloat16)
-    far, mirror, side, mid, home_own = lax.optimization_barrier((far, *tied[4:], mid, home_own))
-    mirror, side, home = [dot(h, down).astype(jnp.bfloat16) for h in (mirror, side, full_hidden(mid, home_own))]
+    downs = (outer_early, outer_late, inner_down, inner_last)
+    tied = lax.optimization_barrier((*downs, *[full_hidden(*p) for p in pairs]))
+    outer_down, inner_down = jnp.concatenate(tied[:2], axis=0), jnp.concatenate(tied[2:4], axis=0)
+    down = jnp.concatenate([w_down, jnp.where(outer, outer_down, inner_down)], axis=0)
+    far = dot(tied[4], down).astype(jnp.bfloat16)
+    far, mirror, side, mid, home_own = lax.optimization_barrier((far, *tied[5:], mid, home_own))
+    mirror, side = [dot(h, down).astype(jnp.bfloat16) for h in (mirror, side)]
+    home = dot(full_hidden(mid, home_own), down).astype(jnp.bfloat16)
 
     def added(u, v):
         return (u.astype(jnp.float32) + v.astype(jnp.float32)).astype(jnp.bfloat16)

time: 389 us -> 391 us (level)
  waiting for transfers between devices: 220 us -> 224 us
    ppermute x19, starting transfers between devices: 40.2 us -> 30.6 us  [over(): return lax.ppermute(block, 'x', pairs)]
    ppermute x1 -> x2, starting transfers between devices: 3.15 us -> 7.66 us  [the longest x1 4.51 us: body(): outer_late = lax.ppermute(w_down[inner // 2:inner], EVERY, straight)]
    unnamed x40 -> x42, local copies, waits for them, and re-layouts: 11.7 us -> 11.3 us
    ppermute x1 -> x2, waiting for transfers between devices: 9.91 us -> 9.66 us  [the longest x1 9.66 us: body(): outer_late = lax.ppermute(w_down[inner // 2:inner], EVERY, straight)]
  transfers between devices with their start and end apart: 33 -> 34, of which waited for: 16 -> 15; matrix products, arithmetic and copies ran while one was open for 14% -> 13% of each run, Pallas kernels for 0% -> 0%
where the time goes in v8:
time: 391 us; the launch traced here: 388 us
  waiting for transfers between devices  224 us (57%)
  starting transfers between devices  93.2 us (24%)
  local copies, waits for them, and re-layouts  28.9 us (7%)
  matrix products  24.6 us (6%)
  other arithmetic  16.7 us (4%)
    ppermute x19, waiting for transfers between devices, over(): return lax.ppermute(block, 'x', pairs)  158 us
    ppermute x4, waiting for transfers between devices, cross(): return lax.ppermute(block, 'x', INWARD)  39.7 us
    ppermute x19, starting transfers between devices, over(): return lax.ppermute(block, 'x', pairs)  30.6 us
    all_to_all x2, starting transfers between devices, body(): lax.all_to_all(total, PLANE, 0, 0, tiled=True).reshape(rows, hi - lo)  22.7 us
    dot_general x17, matrix products, dot(): return jnp.dot(a, b, preferred_element_type=jnp.float32)  21.5 us
    all_to_all x2, waiting for transfers between devices, body(): lax.all_to_all(total, PLANE, 0, 0, tiled=True).reshape(rows, hi - lo)  17.3 us
    ppermute x4, starting transfers between devices, cross(): return lax.ppermute(block, 'x', INWARD)  12.4 us
    unnamed x42, local copies, waits for them, and re-layouts  11.3 us
  transfers between devices with their start and end apart: 34, of which 15 were waited for; matrix products, arithmetic and copies ran while one was open for 13% of the time, Pallas kernels for 0%

profile of v8, /device:TPU:7, one launch (start us, length us, event | category | flops | bytes accessed | tf_op | source)
XLA Modules:
  0.0 388.3 jit_solution(3589460073183192375)
XLA Ops:
  3.3 1.9 copy.8
  5.2 8.8 %all-to-all-start = ((bf16[32,5,56,128]{3,2,1,0:T(8,128)(2,1)}), bf16[32,5,56,128]{3,2,1,0:T(8,128)(2,1)}, u32[]{:S(2)}, u32[]{:S(2)}) async-start(bf16[32,5,56,128]{3,2,1,0:T(8,128)(2,1)} %bitcast.87), calls=%async_computation | async-start | bytes 4587520 | tf_op jit(solution)/shard_map/all_to_all | solution.py:71
  14.0 4.3 %fusion.52 = (bf16[7168,128]{1,0:T(8,128)(2,1)}, bf16[7168,128]{1,0:T(8,128)(2,1)}) fusion(bf16[7168,256]{1,0:T(8,128)(2,1)} %bitcast.88), kind=kLoop, calls=%fused_computation.103 | loop fusion | bytes 7340032 | tf_op jit(solution)/shard_map/slice | solution.py:70
  18.3 3.7 collective-permute-start.17
  22.0 3.2 collective-permute-start.16
  25.3 1.5 fusion.51
  26.8 2.6 collective-permute-start.14
  29.4 3.6 collective-permute-start.13
  33.1 2.8 slice_bitcast_fusion.1
  35.9 1.8 slice_bitcast_fusion.3
  38.8 1.4 slice_bitcast_fusion
  40.2 19.9 %collective-permute-done.17 = bf16[7168,128]{1,0:T(8,128)(2,1)} collective-permute-done((bf16[7168,128]{1,0:T(8,128)(2,1)}, bf16[7168,128]{1,0:T(8,128)(2,1)}, u32[]{:S(2)}, u32[]{:S(2)}) %collective-permute-start.17) | collective-permute-done | bytes 1835040 | tf_op jit(solution)/shard_map/ppermute | solution.py:63
  60.1 1.9 collective-permute-start.18
  62.0 2.1 copy.25
  66.9 3.5 collective-permute-start.6
  73.4 3.6 fusion.45
  77.2 2.6 fusion.7
  79.7 19.7 %collective-permute-done.14 = bf16[7168,128]{1,0:T(8,128)(2,1)} collective-permute-done((bf16[7168,128]{1,0:T(8,128)(2,1)}, bf16[7168,128]{1,0:T(8,128)(2,1)}, u32[]{:S(2)}, u32[]{:S(2)}) %collective-permute-start.14) | collective-permute-done | bytes 1835040 | tf_op jit(solution)/shard_map/ppermute | solution.py:63
  99.5 4.2 %collective-permute-start.2 = (bf16[96,7168]{1,0:T(8,128)(2,1)S(1)}, bf16[96,7168]{1,0:T(8,128)(2,1)S(1)}, u32[]{:S(2)}, u32[]{:S(2)}) collective-permute-start(bf16[96,7168]{1,0:T(8,128)(2,1)S(1)} %slice_bitcast_fusion), channel_id=1, source_target_pairs={{0,1},{3,2},{4,5},{7,6},{8,9},{11,10},{12,13},{15,14},{16,17},{19,... | collective-permute-start | bytes 4128776 | tf_op jit(solution)/shard_map/ppermute | solution.py:63
  103.7 15.5 %collective-permute-done.6 = bf16[64,7168]{1,0:T(8,128)(2,1)} collective-permute-done((bf16[64,7168]{1,0:T(8,128)(2,1)}, bf16[64,7168]{1,0:T(8,128)(2,1)}, u32[]{:S(2)}, u32[]{:S(2)}) %collective-permute-start.6) | collective-permute-done | bytes 917536 | tf_op jit(solution)/shard_map/ppermute | solution.py:66
  122.1 6.0 %collective-permute-start.11 = (bf16[32,7168]{1,0:T(8,128)(2,1)S(1)}, bf16[32,7168]{1,0:T(8,128)(2,1)S(1)}, u32[]{:S(2)}, u32[]{:S(2)}) collective-permute-start(bf16[32,7168]{1,0:T(8,128)(2,1)S(1)} %slice.185), channel_id=1, source_target_pairs={{0,1},{1,0},{2,3},{3,2},{4,5},{5,4},{6,7},{7,6},{8,9},{9,8},{10,11... | collective-permute-start | bytes 1376264 | tf_op jit(solution)/shard_map/ppermute | solution.py:66
  128.1 1.7 broadcast_select_fusion
  129.8 1.9 collective-permute-start.4
  131.8 26.6 %collective-permute-done.11 = bf16[32,7168]{1,0:T(8,128)(2,1)S(1)} collective-permute-done((bf16[32,7168]{1,0:T(8,128)(2,1)S(1)}, bf16[32,7168]{1,0:T(8,128)(2,1)S(1)}, u32[]{:S(2)}, u32[]{:S(2)}) %collective-permute-start.11) | collective-permute-done | bytes 458784 | tf_op jit(solution)/shard_map/ppermute | solution.py:66
  158.3 2.2 collective-permute-start.8
  161.4 1.7 broadcast_select_fusion.1
  163.1 8.8 %collective-permute-done.9 = bf16[160,7168]{1,0:T(8,128)(2,1)S(1)} collective-permute-done((bf16[160,7168]{1,0:T(8,128)(2,1)S(1)}, bf16[160,7168]{1,0:T(8,128)(2,1)S(1)}, u32[]{:S(2)}, u32[]{:S(2)}) %collective-permute-start.9) | collective-permute-done | bytes 2293792 | tf_op jit(solution)/shard_map/ppermute | solution.py:66
  174.4 13.4 %collective-permute-done.8 = bf16[64,7168]{1,0:T(8,128)(2,1)S(1)} collective-permute-done((bf16[64,7168]{1,0:T(8,128)(2,1)S(1)}, bf16[64,7168]{1,0:T(8,128)(2,1)S(1)}, u32[]{:S(2)}, u32[]{:S(2)}) %collective-permute-start.8) | collective-permute-done | bytes 917536 | tf_op jit(solution)/shard_map/ppermute | solution.py:66
  193.2 3.2 collective-permute-start
  196.4 4.5 %collective-permute-start.1 = (bf16[64,7168]{1,0:T(8,128)(2,1)S(1)}, bf16[64,7168]{1,0:T(8,128)(2,1)S(1)}, u32[]{:S(2)}, u32[]{:S(2)}) collective-permute-start(bf16[64,7168]{1,0:T(8,128)(2,1)S(1)} %copy-done.10), channel_id=1, source_target_pairs={{3,7},{0,124},{7,11},{4,0},{11,15},{8,4},{15,19},{12,8},{19,23},{1... | collective-permute-start | bytes 2752520 | tf_op jit(solution)/shard_map/ppermute | solution.py:84
  202.3 18.8 %collective-permute-done.10 = bf16[64,7168]{1,0:T(8,128)(2,1)S(1)} collective-permute-done((bf16[64,7168]{1,0:T(8,128)(2,1)S(1)}, bf16[64,7168]{1,0:T(8,128)(2,1)S(1)}, u32[]{:S(2)}, u32[]{:S(2)}) %collective-permute-start.10) | collective-permute-done | bytes 917536 | tf_op jit(solution)/shard_map/ppermute | solution.py:66
  224.5 9.7 %collective-permute-done.1 = bf16[64,7168]{1,0:T(8,128)(2,1)S(1)} collective-permute-done((bf16[64,7168]{1,0:T(8,128)(2,1)S(1)}, bf16[64,7168]{1,0:T(8,128)(2,1)S(1)}, u32[]{:S(2)}, u32[]{:S(2)}) %collective-permute-start.1) | collective-permute-done | bytes 917536 | tf_op jit(solution)/shard_map/ppermute | solution.py:84
  234.6 1.6 convolution_convert_fusion.3
  236.4 1.6 convolution_convert_fusion.1
  238.9 1.6 convolution_convert_fusion
  241.4 7.9 %collective-permute-start.22 = (bf16[80,4096]{1,0:T(8,128)(2,1)S(1)}, bf16[80,4096]{1,0:T(8,128)(2,1)S(1)}, u32[]{:S(2)}, u32[]{:S(2)}) collective-permute-start(bf16[80,4096]{1,0:T(8,128)(2,1)S(1)} %get-tuple-element.52), channel_id=1, source_target_pairs={{0,1},{1,0},{2,3},{3,2},{4,5},{5,4},{6,7},{7,6},{8,9},{9,8},{10,11... | collective-permute-start | bytes 1966088 | tf_op jit(solution)/shard_map/ppermute | solution.py:66
  251.2 1.7 collective-permute-start.19
  254.6 1.6 convolution_convert_fusion.2
  256.2 18.1 %collective-permute-done.28 = bf16[80,3072]{1,0:T(8,128)(2,1)S(1)} collective-permute-done((bf16[80,3072]{1,0:T(8,128)(2,1)S(1)}, bf16[80,3072]{1,0:T(8,128)(2,1)S(1)}, u32[]{:S(2)}, u32[]{:S(2)}) %collective-permute-start.28) | collective-permute-done | bytes 491552 | tf_op jit(solution)/shard_map/ppermute | solution.py:66
  275.2 25.8 %collective-permute-done.26 = bf16[80,3072]{1,0:T(8,128)(2,1)S(1)} collective-permute-done((bf16[80,3072]{1,0:T(8,128)(2,1)S(1)}, bf16[80,3072]{1,0:T(8,128)(2,1)S(1)}, u32[]{:S(2)}, u32[]{:S(2)}) %collective-permute-start.26) | collective-permute-done | bytes 491552 | tf_op jit(solution)/shard_map/ppermute | solution.py:66
  305.7 6.4 %collective-permute-done.30 = bf16[80,3072]{1,0:T(8,128)(2,1)S(1)} collective-permute-done((bf16[80,3072]{1,0:T(8,128)(2,1)S(1)}, bf16[80,3072]{1,0:T(8,128)(2,1)S(1)}, u32[]{:S(2)}, u32[]{:S(2)}) %collective-permute-start.30) | collective-permute-done | bytes 491552 | tf_op jit(solution)/shard_map/ppermute | solution.py:66
  313.7 9.0 %collective-permute-done.27 = bf16[80,3072]{1,0:T(8,128)(2,1)S(1)} collective-permute-done((bf16[80,3072]{1,0:T(8,128)(2,1)S(1)}, bf16[80,3072]{1,0:T(8,128)(2,1)S(1)}, u32[]{:S(2)}, u32[]{:S(2)}) %collective-permute-start.27) | collective-permute-done | bytes 491552 | tf_op jit(solution)/shard_map/ppermute | solution.py:66
  324.4 12.4 %all-to-all-start.2 = ((bf16[32,5,24,128]{3,2,1,0:T(8,128)(2,1)}), bf16[32,5,24,128]{3,2,1,0:T(8,128)(2,1)S(1)}, u32[]{:S(2)}, u32[]{:S(2)}) async-start(bf16[32,5,24,128]{3,2,1,0:T(8,128)(2,1)} %bitcast.27), calls=%async_computation.2 | async-start | bytes 1966080 | tf_op jit(solution)/shard_map/all_to_all | solution.py:142
  336.8 13.9 %collective-permute-done.21 = bf16[80,4096]{1,0:T(8,128)(2,1)} collective-permute-done((bf16[80,4096]{1,0:T(8,128)(2,1)}, bf16[80,4096]{1,0:T(8,128)(2,1)}, u32[]{:S(2)}, u32[]{:S(2)}) %collective-permute-start.21) | collective-permute-done | bytes 655392 | tf_op jit(solution)/shard_map/ppermute | solution.py:66
  350.8 2.5 add_convert_fusion.2
  355.7 10.3 %all-to-all-start.1 = ((bf16[32,5,32,128]{3,2,1,0:T(8,128)(2,1)}), bf16[32,5,32,128]{3,2,1,0:T(8,128)(2,1)S(1)}, u32[]{:S(2)}, u32[]{:S(2)}) async-start(bf16[32,5,32,128]{3,2,1,0:T(8,128)(2,1)} %bitcast.21), calls=%async_computation.1 | async-start | bytes 2621440 | tf_op jit(solution)/shard_map/all_to_all | solution.py:142
  366.0 2.5 fusion.1
  368.5 17.3 %all-to-all-done.1 = bf16[32,5,32,128]{3,2,1,0:T(8,128)(2,1)S(1)} async-done(((bf16[32,5,32,128]{3,2,1,0:T(8,128)(2,1)}), bf16[32,5,32,128]{3,2,1,0:T(8,128)(2,1)S(1)}, u32[]{:S(2)}, u32[]{:S(2)}) %all-to-all-start.1) | async-done | bytes 1310752 | tf_op jit(solution)/shard_map/all_to_all | solution.py:142
  (125 shorter events, 46.2 us)
Async XLA Ops:
  0.0 2.6 copy-start
  5.2 56.9 %all-to-all-start = ((bf16[32,5,56,128]{3,2,1,0:T(8,128)(2,1)}), bf16[32,5,56,128]{3,2,1,0:T(8,128)(2,1)}, u32[]{:S(2)}, u32[]{:S(2)}) async-start(bf16[32,5,56,128]{3,2,1,0:T(8,128)(2,1)} %bitcast.87), calls=%async_computation | async-start | bytes 4587520 | tf_op jit(solution)/shard_map/all_to_all | solution.py:71
  14.0 11.3 %copy-start.2 = (bf16[1,7168,256]{2,1,0:T(8,128)(2,1)S(1)}, bf16[1,7168,256]{2,1,0:T(8,128)(2,1)}, u32[]{:S(2)}) copy-start(bf16[1,7168,256]{2,1,0:T(8,128)(2,1)} %param.10) | copy-start | bytes 11010052
  18.3 41.8 %collective-permute-start.17 = (bf16[7168,128]{1,0:T(8,128)(2,1)}, bf16[7168,128]{1,0:T(8,128)(2,1)}, u32[]{:S(2)}, u32[]{:S(2)}) collective-permute-start(bf16[7168,128]{1,0:T(8,128)(2,1)} %get-tuple-element.45), channel_id=1, source_target_pairs={{0,1},{3,2},{4,5},{7,6},{8,9},{11,10},{12,13},{15,14},{16,17},{19,... | collective-permute-start | bytes 5505032 | tf_op jit(solution)/shard_map/ppermute | solution.py:63
  22.0 99.1 %collective-permute-start.16 = (bf16[7168,128]{1,0:T(8,128)(2,1)}, bf16[7168,128]{1,0:T(8,128)(2,1)}, u32[]{:S(2)}, u32[]{:S(2)}) collective-permute-start(bf16[7168,128]{1,0:T(8,128)(2,1)} %get-tuple-element.46), channel_id=1, source_target_pairs={{3,7},{0,124},{7,11},{4,0},{11,15},{8,4},{15,19},{12,8},{19,23},{1... | collective-permute-start | bytes 5505032 | tf_op jit(solution)/shard_map/ppermute | solution.py:83
  26.8 72.7 %collective-permute-start.14 = (bf16[7168,128]{1,0:T(8,128)(2,1)}, bf16[7168,128]{1,0:T(8,128)(2,1)}, u32[]{:S(2)}, u32[]{:S(2)}) collective-permute-start(bf16[7168,128]{1,0:T(8,128)(2,1)} %get-tuple-element.43), channel_id=1, source_target_pairs={{0,1},{3,2},{4,5},{7,6},{8,9},{11,10},{12,13},{15,14},{16,17},{19,... | collective-permute-start | bytes 5505032 | tf_op jit(solution)/shard_map/ppermute | solution.py:63
  29.4 100.4 %collective-permute-start.13 = (bf16[7168,128]{1,0:T(8,128)(2,1)S(1)}, bf16[7168,128]{1,0:T(8,128)(2,1)}, u32[]{:S(2)}, u32[]{:S(2)}) collective-permute-start(bf16[7168,128]{1,0:T(8,128)(2,1)S(1)} %get-tuple-element.44), channel_id=1, source_target_pairs={{3,7},{0,124},{7,11},{4,0},{11,15},{8,4},{15,19},{12,8},{19,23},{1... | collective-permute-start | bytes 5505032 | tf_op jit(solution)/shard_map/ppermute | solution.py:82
  33.1 4.6 %copy-start.15 = (s32[128,2]{0,1:T(2,128)S(1)}, s32[128,2]{0,1:T(2,128)}, u32[]{:S(2)}) copy-start(s32[128,2]{0,1:T(2,128)} %param.13) | copy-start | bytes 3076
  60.1 62.0 %collective-permute-start.18 = (bf16[7168,128]{1,0:T(8,128)(2,1)}, bf16[7168,128]{1,0:T(8,128)(2,1)}, u32[]{:S(2)}, u32[]{:S(2)}) collective-permute-start(bf16[7168,128]{1,0:T(8,128)(2,1)} %collective-permute-done.17), channel_id=1, source_target_pairs={{2,6},{1,125},{6,10},{5,1},{10,14},{9,5},{14,18},{13,9},{18,22},{1... | collective-permute-start | bytes 5505032 | tf_op jit(solution)/shard_map/ppermute | solution.py:92
  64.2 1.4 copy-start.4
  66.9 52.2 %collective-permute-start.6 = (bf16[64,7168]{1,0:T(8,128)(2,1)}, bf16[64,7168]{1,0:T(8,128)(2,1)}, u32[]{:S(2)}, u32[]{:S(2)}) collective-permute-start(bf16[64,7168]{1,0:T(8,128)(2,1)} %get-tuple-element.58), channel_id=1, source_target_pairs={{0,1},{1,0},{2,3},{3,2},{4,5},{5,4},{6,7},{7,6},{8,9},{9,8},{10,11... | collective-permute-start | bytes 2752520 | tf_op jit(solution)/shard_map/ppermute | solution.py:66
  73.4 3.8 copy-start.6
  77.2 44.0 %copy-start.5 = (bf16[20,8,56,128]{3,1,2,0:T(8,128)(2,1)S(1)}, bf16[20,8,56,128]{3,1,2,0:T(8,128)(2,1)}, u32[]{:S(2)}) copy-start(bf16[20,8,56,128]{3,1,2,0:T(8,128)(2,1)} %copy-done.4) | copy-start | bytes 6881284
  99.5 96.9 %collective-permute-start.2 = (bf16[96,7168]{1,0:T(8,128)(2,1)S(1)}, bf16[96,7168]{1,0:T(8,128)(2,1)S(1)}, u32[]{:S(2)}, u32[]{:S(2)}) collective-permute-start(bf16[96,7168]{1,0:T(8,128)(2,1)S(1)} %slice_bitcast_fusion), channel_id=1, source_target_pairs={{0,1},{3,2},{4,5},{7,6},{8,9},{11,10},{12,13},{15,14},{16,17},{19,... | collective-permute-start | bytes 4128776 | tf_op jit(solution)/shard_map/ppermute | solution.py:63
  119.1 41.4 %collective-permute-start.15 = (bf16[7168,128]{1,0:T(8,128)(2,1)}, bf16[7168,128]{1,0:T(8,128)(2,1)S(1)}, u32[]{:S(2)}, u32[]{:S(2)}) collective-permute-start(bf16[7168,128]{1,0:T(8,128)(2,1)} %collective-permute-done.14), channel_id=1, source_target_pairs={{2,6},{1,125},{6,10},{5,1},{10,14},{9,5},{14,18},{13,9},{18,22},{1... | collective-permute-start | bytes 5505032 | tf_op jit(solution)/shard_map/ppermute | solution.py:90
  121.1 8.7 %copy-start.14 = (bf16[32,7168]{1,0:T(8,128)(2,1)S(1)}, bf16[32,7168]{1,0:T(8,128)(2,1)}, u32[]{:S(2)}) copy-start(bf16[32,7168]{1,0:T(8,128)(2,1)} %slice_bitcast_fusion.3) | copy-start | bytes 1376260
  121.2 37.2 %copy-start.12 = (bf16[64,7168]{1,0:T(8,128)(2,1)S(1)}, bf16[64,7168]{1,0:T(8,128)(2,1)}, u32[]{:S(2)}) copy-start(bf16[64,7168]{1,0:T(8,128)(2,1)} %get-tuple-element.57) | copy-start | bytes 2752516
  121.2 50.8 %collective-permute-start.9 = (bf16[160,7168]{1,0:T(8,128)(2,1)S(1)}, bf16[160,7168]{1,0:T(8,128)(2,1)S(1)}, u32[]{:S(2)}, u32[]{:S(2)}) collective-permute-start(bf16[160,7168]{1,0:T(8,128)(2,1)S(1)} %bitcast.85), channel_id=1, source_target_pairs={{0,3},{3,0},{1,2},{2,1},{4,7},{7,4},{5,6},{6,5},{8,11},{11,8},{9,1... | collective-permute-start | bytes 6881288 | tf_op jit(solution)/shard_map/ppermute | solution.py:66
  122.1 36.2 %collective-permute-start.11 = (bf16[32,7168]{1,0:T(8,128)(2,1)S(1)}, bf16[32,7168]{1,0:T(8,128)(2,1)S(1)}, u32[]{:S(2)}, u32[]{:S(2)}) collective-permute-start(bf16[32,7168]{1,0:T(8,128)(2,1)S(1)} %slice.185), channel_id=1, source_target_pairs={{0,1},{1,0},{2,3},{3,2},{4,5},{5,4},{6,7},{7,6},{8,9},{9,8},{10,11... | collective-permute-start | bytes 1376264 | tf_op jit(solution)/shard_map/ppermute | solution.py:66
  129.8 63.0 %collective-permute-start.4 = (bf16[32,7168]{1,0:T(8,128)(2,1)S(1)}, bf16[32,7168]{1,0:T(8,128)(2,1)S(1)}, u32[]{:S(2)}, u32[]{:S(2)}) collective-permute-start(bf16[32,7168]{1,0:T(8,128)(2,1)S(1)} %copy-done.14), channel_id=1, source_target_pairs={{0,1},{3,2},{4,5},{7,6},{8,9},{11,10},{12,13},{15,14},{16,17},{19,... | collective-permute-start | bytes 1376264 | tf_op jit(solution)/shard_map/ppermute | solution.py:63
  158.3 14.5 %copy-start.3 = (bf16[1,7168,256]{2,1,0:T(8,128)(2,1)S(1)}, bf16[1,7168,256]{2,1,0:T(8,128)(2,1)}, u32[]{:S(2)}) copy-start(bf16[1,7168,256]{2,1,0:T(8,128)(2,1)} %param.10) | copy-start | bytes 11010052
  158.3 29.5 %collective-permute-start.8 = (bf16[64,7168]{1,0:T(8,128)(2,1)S(1)}, bf16[64,7168]{1,0:T(8,128)(2,1)S(1)}, u32[]{:S(2)}, u32[]{:S(2)}) collective-permute-start(bf16[64,7168]{1,0:T(8,128)(2,1)S(1)} %copy-done.12), channel_id=1, source_target_pairs={{0,1},{1,0},{2,3},{3,2},{4,5},{5,4},{6,7},{7,6},{8,9},{9,8},{10,11... | collective-permute-start | bytes 2752520 | tf_op jit(solution)/shard_map/ppermute | solution.py:66
  160.6 40.3 %collective-permute-start.12 = (bf16[32,7168]{1,0:T(8,128)(2,1)S(1)}, bf16[32,7168]{1,0:T(8,128)(2,1)S(1)}, u32[]{:S(2)}, u32[]{:S(2)}) collective-permute-start(bf16[32,7168]{1,0:T(8,128)(2,1)S(1)} %collective-permute-done.11), channel_id=1, source_target_pairs={{0,3},{3,0},{1,2},{2,1},{4,7},{7,4},{5,6},{6,5},{8,11},{11,8},{9,1... | collective-permute-start | bytes 1376264 | tf_op jit(solution)/shard_map/ppermute | solution.py:66
  172.0 29.6 %collective-permute-start.7 = (bf16[64,7168]{1,0:T(8,128)(2,1)}, bf16[64,7168]{1,0:T(8,128)(2,1)S(1)}, u32[]{:S(2)}, u32[]{:S(2)}) collective-permute-start(bf16[64,7168]{1,0:T(8,128)(2,1)} %collective-permute-done.6), channel_id=1, source_target_pairs={{0,3},{3,0},{1,2},{2,1},{4,7},{7,4},{5,6},{6,5},{8,11},{11,8},{9,1... | collective-permute-start | bytes 2752520 | tf_op jit(solution)/shard_map/ppermute | solution.py:66
  187.8 33.3 %collective-permute-start.10 = (bf16[64,7168]{1,0:T(8,128)(2,1)S(1)}, bf16[64,7168]{1,0:T(8,128)(2,1)S(1)}, u32[]{:S(2)}, u32[]{:S(2)}) collective-permute-start(bf16[64,7168]{1,0:T(8,128)(2,1)S(1)} %collective-permute-done.8), channel_id=1, source_target_pairs={{0,3},{3,0},{1,2},{2,1},{4,7},{7,4},{5,6},{6,5},{8,11},{11,8},{9,1... | collective-permute-start | bytes 2752520 | tf_op jit(solution)/shard_map/ppermute | solution.py:66
  192.0 4.3 %copy-start.10 = (bf16[64,7168]{1,0:T(8,128)(2,1)S(1)}, bf16[64,7168]{1,0:T(8,128)(2,1)}, u32[]{:S(2)}) copy-start(bf16[64,7168]{1,0:T(8,128)(2,1)} %get-tuple-element.47) | copy-start | bytes 2752516
  193.2 31.3 %collective-permute-start = (bf16[64,7168]{1,0:T(8,128)(2,1)S(1)}, bf16[64,7168]{1,0:T(8,128)(2,1)S(1)}, u32[]{:S(2)}, u32[]{:S(2)}) collective-permute-start(bf16[64,7168]{1,0:T(8,128)(2,1)S(1)} %copy-done.11), channel_id=1, source_target_pairs={{3,7},{0,124},{7,11},{4,0},{11,15},{8,4},{15,19},{12,8},{19,23},{1... | collective-permute-start | bytes 2752520 | tf_op jit(solution)/shard_map/ppermute | solution.py:72
  196.4 37.8 %collective-permute-start.1 = (bf16[64,7168]{1,0:T(8,128)(2,1)S(1)}, bf16[64,7168]{1,0:T(8,128)(2,1)S(1)}, u32[]{:S(2)}, u32[]{:S(2)}) collective-permute-start(bf16[64,7168]{1,0:T(8,128)(2,1)S(1)} %copy-done.10), channel_id=1, source_target_pairs={{3,7},{0,124},{7,11},{4,0},{11,15},{8,4},{15,19},{12,8},{19,23},{1... | collective-permute-start | bytes 2752520 | tf_op jit(solution)/shard_map/ppermute | solution.py:84
  200.9 33.3 %collective-permute-start.5 = (bf16[32,7168]{1,0:T(8,128)(2,1)S(1)}, bf16[32,7168]{1,0:T(8,128)(2,1)S(1)}, u32[]{:S(2)}, u32[]{:S(2)}) collective-permute-start(bf16[32,7168]{1,0:T(8,128)(2,1)S(1)} %collective-permute-done.4), channel_id=1, source_target_pairs={{2,6},{1,125},{6,10},{5,1},{10,14},{9,5},{14,18},{13,9},{18,22},{1... | collective-permute-start | bytes 1376264 | tf_op jit(solution)/shard_map/ppermute | solution.py:97
  201.6 32.6 %collective-permute-start.3 = (bf16[96,7168]{1,0:T(8,128)(2,1)S(1)}, bf16[96,7168]{1,0:T(8,128)(2,1)S(1)}, u32[]{:S(2)}, u32[]{:S(2)}) collective-permute-start(bf16[96,7168]{1,0:T(8,128)(2,1)S(1)} %collective-permute-done.2), channel_id=1, source_target_pairs={{2,6},{1,125},{6,10},{5,1},{10,14},{9,5},{14,18},{13,9},{18,22},{1... | collective-permute-start | bytes 4128776 | tf_op jit(solution)/shard_map/ppermute | solution.py:89
  224.5 10.1 %copy-start.7 = (bf16[1,256,7168]{2,1,0:T(8,128)(2,1)S(1)}, bf16[1,256,7168]{2,1,0:T(8,128)(2,1)}, u32[]{:S(2)}) copy-start(bf16[1,256,7168]{2,1,0:T(8,128)(2,1)} %param.12) | copy-start | bytes 11010052
  241.4 59.7 %collective-permute-start.22 = (bf16[80,4096]{1,0:T(8,128)(2,1)S(1)}, bf16[80,4096]{1,0:T(8,128)(2,1)S(1)}, u32[]{:S(2)}, u32[]{:S(2)}) collective-permute-start(bf16[80,4096]{1,0:T(8,128)(2,1)S(1)} %get-tuple-element.52), channel_id=1, source_target_pairs={{0,1},{1,0},{2,3},{3,2},{4,5},{5,4},{6,7},{7,6},{8,9},{9,8},{10,11... | collective-permute-start | bytes 1966088 | tf_op jit(solution)/shard_map/ppermute | solution.py:66
  249.4 53.8 %collective-permute-start.20 = (bf16[80,4096]{1,0:T(8,128)(2,1)S(1)}, bf16[80,4096]{1,0:T(8,128)(2,1)S(1)}, u32[]{:S(2)}, u32[]{:S(2)}) collective-permute-start(bf16[80,4096]{1,0:T(8,128)(2,1)S(1)} %get-tuple-element.51), channel_id=1, source_target_pairs={{0,3},{3,0},{1,2},{2,1},{4,7},{7,4},{5,6},{6,5},{8,11},{11,8},{9,1... | collective-permute-start | bytes 1966088 | tf_op jit(solution)/shard_map/ppermute | solution.py:66
  251.2 85.5 %collective-permute-start.19 = (bf16[80,4096]{1,0:T(8,128)(2,1)}, bf16[80,4096]{1,0:T(8,128)(2,1)S(1)}, u32[]{:S(2)}, u32[]{:S(2)}) collective-permute-start(bf16[80,4096]{1,0:T(8,128)(2,1)} %slice.199), channel_id=1, source_target_pairs={{0,3},{3,0},{1,2},{2,1},{4,7},{7,4},{5,6},{6,5},{8,11},{11,8},{9,1... | collective-permute-start | bytes 1966088 | tf_op jit(solution)/shard_map/ppermute | solution.py:66
  252.9 21.4 %collective-permute-start.28 = (bf16[80,3072]{1,0:T(8,128)(2,1)S(1)}, bf16[80,3072]{1,0:T(8,128)(2,1)S(1)}, u32[]{:S(2)}, u32[]{:S(2)}) collective-permute-start(bf16[80,3072]{1,0:T(8,128)(2,1)S(1)} %get-tuple-element.56), channel_id=1, source_target_pairs={{0,1},{1,0},{2,3},{3,2},{4,5},{5,4},{6,7},{7,6},{8,9},{9,8},{10,11... | collective-permute-start | bytes 1474568 | tf_op jit(solution)/shard_map/ppermute | solution.py:66
  252.9 52.1 %collective-permute-start.25 = (bf16[80,3072]{1,0:T(8,128)(2,1)S(1)}, bf16[80,3072]{1,0:T(8,128)(2,1)S(1)}, u32[]{:S(2)}, u32[]{:S(2)}) collective-permute-start(bf16[80,3072]{1,0:T(8,128)(2,1)S(1)} %slice.205), channel_id=1, source_target_pairs={{0,3},{3,0},{1,2},{2,1},{4,7},{7,4},{5,6},{6,5},{8,11},{11,8},{9,1... | collective-permute-start | bytes 1474568 | tf_op jit(solution)/shard_map/ppermute | solution.py:66
  256.2 66.5 %copy-start.8 = (bf16[160,7168]{1,0:T(8,128)(2,1)}, bf16[160,7168]{1,0:T(8,128)(2,1)S(1)}, u32[]{:S(2)}) copy-start(bf16[160,7168]{1,0:T(8,128)(2,1)S(1)} %convolution_convert_fusion.2) | copy-start | bytes 6881284
  274.3 26.7 %collective-permute-start.26 = (bf16[80,3072]{1,0:T(8,128)(2,1)S(1)}, bf16[80,3072]{1,0:T(8,128)(2,1)S(1)}, u32[]{:S(2)}, u32[]{:S(2)}) collective-permute-start(bf16[80,3072]{1,0:T(8,128)(2,1)S(1)} %get-tuple-element.55), channel_id=1, source_target_pairs={{0,3},{3,0},{1,2},{2,1},{4,7},{7,4},{5,6},{6,5},{8,11},{11,8},{9,1... | collective-permute-start | bytes 1474568 | tf_op jit(solution)/shard_map/ppermute | solution.py:66
  301.0 11.0 %collective-permute-start.30 = (bf16[80,3072]{1,0:T(8,128)(2,1)S(1)}, bf16[80,3072]{1,0:T(8,128)(2,1)S(1)}, u32[]{:S(2)}, u32[]{:S(2)}) collective-permute-start(bf16[80,3072]{1,0:T(8,128)(2,1)S(1)} %slice.209), channel_id=1, source_target_pairs={{0,1},{1,0},{2,3},{3,2},{4,5},{5,4},{6,7},{7,6},{8,9},{9,8},{10,11... | collective-permute-start | bytes 1474568 | tf_op jit(solution)/shard_map/ppermute | solution.py:66
  301.2 12.5 %collective-permute-start.29 = (bf16[80,3072]{1,0:T(8,128)(2,1)S(1)}, bf16[80,3072]{1,0:T(8,128)(2,1)S(1)}, u32[]{:S(2)}, u32[]{:S(2)}) collective-permute-start(bf16[80,3072]{1,0:T(8,128)(2,1)S(1)} %add_convert_fusion.5), channel_id=1, source_target_pairs={{0,3},{3,0},{1,2},{2,1},{4,7},{7,4},{5,6},{6,5},{8,11},{11,8},{9,1... | collective-permute-start | bytes 1474568 | tf_op jit(solution)/shard_map/ppermute | solution.py:66
  303.2 19.5 %collective-permute-start.27 = (bf16[80,3072]{1,0:T(8,128)(2,1)S(1)}, bf16[80,3072]{1,0:T(8,128)(2,1)S(1)}, u32[]{:S(2)}, u32[]{:S(2)}) collective-permute-start(bf16[80,3072]{1,0:T(8,128)(2,1)S(1)} %add_convert_fusion.7), channel_id=1, source_target_pairs={{0,1},{1,0},{2,3},{3,2},{4,5},{5,4},{6,7},{7,6},{8,9},{9,8},{10,11... | collective-permute-start | bytes 1474568 | tf_op jit(solution)/shard_map/ppermute | solution.py:66
  305.1 31.7 %collective-permute-start.24 = (bf16[80,4096]{1,0:T(8,128)(2,1)}, bf16[80,4096]{1,0:T(8,128)(2,1)}, u32[]{:S(2)}, u32[]{:S(2)}) collective-permute-start(bf16[80,4096]{1,0:T(8,128)(2,1)} %slice.203), channel_id=1, source_target_pairs={{0,1},{1,0},{2,3},{3,2},{4,5},{5,4},{6,7},{7,6},{8,9},{9,8},{10,11... | collective-permute-start | bytes 1966088 | tf_op jit(solution)/shard_map/ppermute | solution.py:66
  312.0 24.8 %collective-permute-start.23 = (bf16[80,4096]{1,0:T(8,128)(2,1)}, bf16[80,4096]{1,0:T(8,128)(2,1)}, u32[]{:S(2)}, u32[]{:S(2)}) collective-permute-start(bf16[80,4096]{1,0:T(8,128)(2,1)} %add_convert_fusion.1), channel_id=1, source_target_pairs={{0,3},{3,0},{1,2},{2,1},{4,7},{7,4},{5,6},{6,5},{8,11},{11,8},{9,1... | collective-permute-start | bytes 1966088 | tf_op jit(solution)/shard_map/ppermute | solution.py:66
  313.7 37.1 %collective-permute-start.21 = (bf16[80,4096]{1,0:T(8,128)(2,1)}, bf16[80,4096]{1,0:T(8,128)(2,1)}, u32[]{:S(2)}, u32[]{:S(2)}) collective-permute-start(bf16[80,4096]{1,0:T(8,128)(2,1)} %add_convert_fusion.3), channel_id=1, source_target_pairs={{0,1},{1,0},{2,3},{3,2},{4,5},{5,4},{6,7},{7,6},{8,9},{9,8},{10,11... | collective-permute-start | bytes 1966088 | tf_op jit(solution)/shard_map/ppermute | solution.py:66
  324.4 30.4 %all-to-all-start.2 = ((bf16[32,5,24,128]{3,2,1,0:T(8,128)(2,1)}), bf16[32,5,24,128]{3,2,1,0:T(8,128)(2,1)S(1)}, u32[]{:S(2)}, u32[]{:S(2)}) async-start(bf16[32,5,24,128]{3,2,1,0:T(8,128)(2,1)} %bitcast.27), calls=%async_computation.2 | async-start | bytes 1966080 | tf_op jit(solution)/shard_map/all_to_all | solution.py:142
  353.4 12.6 %copy-start.16 = (f32[128,1]{0,1:T(1,128)S(1)}, f32[128,1]{0,1:T(1,128)}, u32[]{:S(2)}) copy-start(f32[128,1]{0,1:T(1,128)} %param.9) | copy-start | bytes 1540
  355.7 30.1 %all-to-all-start.1 = ((bf16[32,5,32,128]{3,2,1,0:T(8,128)(2,1)}), bf16[32,5,32,128]{3,2,1,0:T(8,128)(2,1)S(1)}, u32[]{:S(2)}, u32[]{:S(2)}) async-start(bf16[32,5,32,128]{3,2,1,0:T(8,128)(2,1)} %bitcast.21), calls=%async_computation.1 | async-start | bytes 2621440 | tf_op jit(solution)/shard_map/all_to_all | solution.py:142
  385.8 2.5 copy-start.1
  (3 other events, 3.3 us)

commit v9 on v8

--- a/solution.py
+++ b/solution.py
@@ -56,7 +56,7 @@
     tiled = (experts, CAPACITY, width // LANES, LANES)
     outgoing = outgoing.reshape(tiled)
     inner = hidden // 2
-    first_down = inner + inner * 3 // 4
+    first_down = inner + 104
     straight, turned = passing(3, 0, experts), passing(2, 1, experts)
 
     def cross(block):
@@ -67,7 +67,6 @@
 
     inward_down = cross(w_down[inner:first_down])
     inward_gate = cross(w_gate[:, inner:])
-    inward_up = cross(w_up[:, inner:])
     arrived = lax.all_to_all(outgoing, PLANE, 0, 0, tiled=True)
     outer_early = lax.ppermute(w_down[: inner // 2], EVERY, straight)
     mid = arrived.reshape(rows, width)
@@ -83,8 +82,9 @@
     outer_up = lax.ppermute(w_up[:, :inner], EVERY, straight)
     outer_late = lax.ppermute(w_down[inner // 2 : inner], EVERY, straight)
     side_a = over(mid[:64], SIDE)
-    side_b = over(mid[64:128], SIDE)
-    side_c = over(mid[128:], SIDE)
+    inward_up = cross(w_up[:, inner:])
+    side_b = over(mid[64:112], SIDE)
+    side_c = over(mid[112:], SIDE)
     inward_last = cross(w_down[first_down:])
     inner_down = lax.ppermute(inward_down, EVERY, turned)
     inner_gate = lax.ppermute(inward_gate, EVERY, turned)
@@ -124,7 +124,7 @@
     f32 = jnp.float32
     half = rows // 2
     upper, lower = slice(None, half), slice(half, None)
-    result = jnp.zeros(tokens.shape, jnp.bfloat16)
+    result = None
     for lo, hi in ((0, 4096), (4096, width)):
         cols = slice(lo, hi)
         far_a = over(far[upper, cols], MIRROR)
@@ -142,7 +142,10 @@
         returned = lax.all_to_all(total, PLANE, 0, 0, tiled=True).reshape(rows, hi - lo)
         expert_out = lax.dot_general(picker, returned, (((0,), (0,)), ((), ())), preferred_element_type=f32)
         mixed = (expert_out * gate_prob.reshape(-1)[:, None]).astype(jnp.bfloat16)
-        result = lax.dynamic_update_slice(result, mixed, (0, lo))
+        if result is None:
+            result = lax.optimization_barrier(jnp.pad(mixed, ((0, 0), (0, width - hi))))
+        else:
+            result = lax.dynamic_update_slice(result, mixed, (0, lo))
     return result
 
 

time: 391 us -> 382 us (0.977)
  waiting for transfers between devices: 224 us -> 218 us
  matrix products: 24.6 us -> 20 us
  local copies, waits for them, and re-layouts: 28.9 us -> 24.8 us
    ppermute x19, waiting for transfers between devices: 158 us -> 142 us  [over(): return lax.ppermute(block, 'x', pairs)]
    ppermute x19, starting transfers between devices: 30.6 us -> 39.4 us  [over(): return lax.ppermute(block, 'x', pairs)]
    all_to_all x2, waiting for transfers between devices: 17.3 us -> 24.3 us  [body(): lax.all_to_all(total, PLANE, 0, 0, tiled=True).reshape(rows, hi - lo)]
    all_to_all x2, starting transfers between devices: 22.7 us -> 17.3 us  [body(): lax.all_to_all(total, PLANE, 0, 0, tiled=True).reshape(rows, hi - lo)]
    dot_general x17, matrix products: 21.5 us -> 16.6 us  [dot(): return jnp.dot(a, b, preferred_element_type=jnp.float32)]
    unnamed x42 -> x32, local copies, waits for them, and re-layouts: 11.3 us -> 7.13 us
  transfers between devices with their start and end apart: 34 -> 34, of which waited for: 15 -> 16; matrix products, arithmetic and copies ran while one was open for 13% -> 13% of each run, Pallas kernels for 0% -> 0%
where the time goes in v9:
time: 382 us; the launch traced here: 379 us
  waiting for transfers between devices  218 us (57%)
  starting transfers between devices  96.5 us (25%)
  local copies, waits for them, and re-layouts  24.8 us (6%)
  matrix products  20 us (5%)
  other arithmetic  18.5 us (5%)
    ppermute x19, waiting for transfers between devices, over(): return lax.ppermute(block, 'x', pairs)  142 us
    ppermute x4, waiting for transfers between devices, cross(): return lax.ppermute(block, 'x', INWARD)  42.5 us
    ppermute x19, starting transfers between devices, over(): return lax.ppermute(block, 'x', pairs)  39.4 us
    all_to_all x2, waiting for transfers between devices, body(): lax.all_to_all(total, PLANE, 0, 0, tiled=True).reshape(rows, hi - lo)  24.3 us
    all_to_all x2, starting transfers between devices, body(): lax.all_to_all(total, PLANE, 0, 0, tiled=True).reshape(rows, hi - lo)  17.3 us
    dot_general x17, matrix products, dot(): return jnp.dot(a, b, preferred_element_type=jnp.float32)  16.6 us
    ppermute x4, starting transfers between devices, cross(): return lax.ppermute(block, 'x', INWARD)  12.4 us
    ppermute x1, waiting for transfers between devices, body(): outer_late = lax.ppermute(w_down[inner // 2:inner], EVERY, straight)  9.71 us
  transfers between devices with their start and end apart: 34, of which 16 were waited for; matrix products, arithmetic and copies ran while one was open for 13% of the time, Pallas kernels for 0%

profile of v9, /device:TPU:7, one launch (start us, length us, event | category | flops | bytes accessed | tf_op | source)
XLA Modules:
  0.0 378.5 jit_solution(7233033059134417975)
XLA Ops:
  3.8 1.9 copy.8
  5.7 8.8 %all-to-all-start = ((bf16[32,5,56,128]{3,2,1,0:T(8,128)(2,1)}), bf16[32,5,56,128]{3,2,1,0:T(8,128)(2,1)S(1)}, u32[]{:S(2)}, u32[]{:S(2)}) async-start(bf16[32,5,56,128]{3,2,1,0:T(8,128)(2,1)} %bitcast.86), calls=%async_computation | async-start | bytes 4587520 | tf_op jit(solution)/shard_map/all_to_all | solution.py:70
  14.5 4.3 %fusion.53 = (bf16[7168,128]{1,0:T(8,128)(2,1)}, bf16[7168,128]{1,0:T(8,128)(2,1)}) fusion(bf16[7168,256]{1,0:T(8,128)(2,1)} %bitcast.91), kind=kLoop, calls=%fused_computation.103 | loop fusion | bytes 7340032 | tf_op jit(solution)/shard_map/slice | solution.py:85
  18.8 3.7 collective-permute-start.17
  22.5 3.2 collective-permute-start.16
  25.7 2.1 fusion.52
  27.8 2.6 collective-permute-start.14
  30.4 3.6 collective-permute-start.13
  34.1 2.5 slice_bitcast_fusion.1
  37.6 1.9 fusion.27
  46.0 2.6 slice_bitcast_fusion
  48.6 12.0 %collective-permute-done.17 = bf16[7168,128]{1,0:T(8,128)(2,1)} collective-permute-done((bf16[7168,128]{1,0:T(8,128)(2,1)}, bf16[7168,128]{1,0:T(8,128)(2,1)}, u32[]{:S(2)}, u32[]{:S(2)}) %collective-permute-start.17) | collective-permute-done | bytes 1835040 | tf_op jit(solution)/shard_map/ppermute | solution.py:63
  60.7 1.9 collective-permute-start.18
  63.1 3.5 collective-permute-start.6
  69.5 30.5 %collective-permute-done.14 = bf16[7168,128]{1,0:T(8,128)(2,1)} collective-permute-done((bf16[7168,128]{1,0:T(8,128)(2,1)}, bf16[7168,128]{1,0:T(8,128)(2,1)}, u32[]{:S(2)}, u32[]{:S(2)}) %collective-permute-start.14) | collective-permute-done | bytes 1835040 | tf_op jit(solution)/shard_map/ppermute | solution.py:63
  100.0 4.2 %collective-permute-start.2 = (bf16[104,7168]{1,0:T(8,128)(2,1)S(1)}, bf16[104,7168]{1,0:T(8,128)(2,1)S(1)}, u32[]{:S(2)}, u32[]{:S(2)}) collective-permute-start(bf16[104,7168]{1,0:T(8,128)(2,1)S(1)} %copy-done.6), channel_id=1, source_target_pairs={{0,1},{3,2},{4,5},{7,6},{8,9},{11,10},{12,13},{15,14},{16,17},{19,... | collective-permute-start | bytes 4472840 | tf_op jit(solution)/shard_map/ppermute | solution.py:63
  104.2 15.4 %collective-permute-done.6 = bf16[64,7168]{1,0:T(8,128)(2,1)S(1)} collective-permute-done((bf16[64,7168]{1,0:T(8,128)(2,1)S(1)}, bf16[64,7168]{1,0:T(8,128)(2,1)S(1)}, u32[]{:S(2)}, u32[]{:S(2)}) %collective-permute-start.6) | collective-permute-done | bytes 917536 | tf_op jit(solution)/shard_map/ppermute | solution.py:66
  121.3 5.9 %collective-permute-start.11 = (bf16[48,7168]{1,0:T(8,128)(2,1)S(1)}, bf16[48,7168]{1,0:T(8,128)(2,1)S(1)}, u32[]{:S(2)}, u32[]{:S(2)}) collective-permute-start(bf16[48,7168]{1,0:T(8,128)(2,1)S(1)} %get-tuple-element.57), channel_id=1, source_target_pairs={{0,1},{1,0},{2,3},{3,2},{4,5},{5,4},{6,7},{7,6},{8,9},{9,8},{10,11... | collective-permute-start | bytes 2064392 | tf_op jit(solution)/shard_map/ppermute | solution.py:66
  127.2 1.7 broadcast_select_fusion
  128.9 1.9 collective-permute-start.4
  130.9 35.3 %collective-permute-done.11 = bf16[48,7168]{1,0:T(8,128)(2,1)S(1)} collective-permute-done((bf16[48,7168]{1,0:T(8,128)(2,1)S(1)}, bf16[48,7168]{1,0:T(8,128)(2,1)S(1)}, u32[]{:S(2)}, u32[]{:S(2)}) %collective-permute-start.11) | collective-permute-done | bytes 688160 | tf_op jit(solution)/shard_map/ppermute | solution.py:66
  166.2 2.2 collective-permute-start.8
  169.3 1.7 broadcast_select_fusion.1
  171.3 1.6 collective-permute-start.7
  174.5 13.8 %collective-permute-done.8 = bf16[48,7168]{1,0:T(8,128)(2,1)S(1)} collective-permute-done((bf16[48,7168]{1,0:T(8,128)(2,1)S(1)}, bf16[48,7168]{1,0:T(8,128)(2,1)S(1)}, u32[]{:S(2)}, u32[]{:S(2)}) %collective-permute-start.8) | collective-permute-done | bytes 688160 | tf_op jit(solution)/shard_map/ppermute | solution.py:66
  193.6 3.1 collective-permute-start
  196.7 4.5 %collective-permute-start.1 = (bf16[64,7168]{1,0:T(8,128)(2,1)S(1)}, bf16[64,7168]{1,0:T(8,128)(2,1)S(1)}, u32[]{:S(2)}, u32[]{:S(2)}) collective-permute-start(bf16[64,7168]{1,0:T(8,128)(2,1)S(1)} %get-tuple-element.47), channel_id=1, source_target_pairs={{3,7},{0,124},{7,11},{4,0},{11,15},{8,4},{15,19},{12,8},{19,23},{1... | collective-permute-start | bytes 2752520 | tf_op jit(solution)/shard_map/ppermute | solution.py:83
  201.9 4.7 %collective-permute-done.7 = bf16[64,7168]{1,0:T(8,128)(2,1)S(1)} collective-permute-done((bf16[64,7168]{1,0:T(8,128)(2,1)S(1)}, bf16[64,7168]{1,0:T(8,128)(2,1)S(1)}, u32[]{:S(2)}, u32[]{:S(2)}) %collective-permute-start.7) | collective-permute-done | bytes 917536 | tf_op jit(solution)/shard_map/ppermute | solution.py:66
  207.4 14.0 %collective-permute-done.10 = bf16[48,7168]{1,0:T(8,128)(2,1)S(1)} collective-permute-done((bf16[48,7168]{1,0:T(8,128)(2,1)S(1)}, bf16[48,7168]{1,0:T(8,128)(2,1)S(1)}, u32[]{:S(2)}, u32[]{:S(2)}) %collective-permute-start.10) | collective-permute-done | bytes 688160 | tf_op jit(solution)/shard_map/ppermute | solution.py:66
  224.8 9.7 %collective-permute-done.1 = bf16[64,7168]{1,0:T(8,128)(2,1)S(1)} collective-permute-done((bf16[64,7168]{1,0:T(8,128)(2,1)S(1)}, bf16[64,7168]{1,0:T(8,128)(2,1)S(1)}, u32[]{:S(2)}, u32[]{:S(2)}) %collective-permute-start.1) | collective-permute-done | bytes 917536 | tf_op jit(solution)/shard_map/ppermute | solution.py:83
  235.0 1.6 convolution_convert_fusion.3
  236.7 1.6 convolution_convert_fusion.1
  238.4 1.6 convolution_convert_fusion
  240.1 14.1 %collective-permute-start.28 = (bf16[80,3072]{1,0:T(8,128)(2,1)S(1)}, bf16[80,3072]{1,0:T(8,128)(2,1)S(1)}, u32[]{:S(2)}, u32[]{:S(2)}) collective-permute-start(bf16[80,3072]{1,0:T(8,128)(2,1)S(1)} %get-tuple-element.52), channel_id=1, source_target_pairs={{0,1},{1,0},{2,3},{3,2},{4,5},{5,4},{6,7},{7,6},{8,9},{9,8},{10,11... | collective-permute-start | bytes 1474568 | tf_op jit(solution)/shard_map/ppermute | solution.py:66
  255.9 1.8 collective-permute-start.25
  259.3 1.6 convolution_convert_fusion.2
  260.9 4.2 %collective-permute-done.28 = bf16[80,3072]{1,0:T(8,128)(2,1)S(1)} collective-permute-done((bf16[80,3072]{1,0:T(8,128)(2,1)S(1)}, bf16[80,3072]{1,0:T(8,128)(2,1)S(1)}, u32[]{:S(2)}, u32[]{:S(2)}) %collective-permute-start.28) | collective-permute-done | bytes 491552 | tf_op jit(solution)/shard_map/ppermute | solution.py:66
  266.5 12.8 %collective-permute-done.22 = bf16[80,4096]{1,0:T(8,128)(2,1)S(1)} collective-permute-done((bf16[80,4096]{1,0:T(8,128)(2,1)S(1)}, bf16[80,4096]{1,0:T(8,128)(2,1)S(1)}, u32[]{:S(2)}, u32[]{:S(2)}) %collective-permute-start.22) | collective-permute-done | bytes 655392 | tf_op jit(solution)/shard_map/ppermute | solution.py:66
  280.5 25.3 %collective-permute-done.20 = bf16[80,4096]{1,0:T(8,128)(2,1)S(1)} collective-permute-done((bf16[80,4096]{1,0:T(8,128)(2,1)S(1)}, bf16[80,4096]{1,0:T(8,128)(2,1)S(1)}, u32[]{:S(2)}, u32[]{:S(2)}) %collective-permute-start.20) | collective-permute-done | bytes 655392 | tf_op jit(solution)/shard_map/ppermute | solution.py:66
  308.9 2.2 collective-permute-start.29
  311.2 10.4 %collective-permute-done.23 = bf16[80,4096]{1,0:T(8,128)(2,1)S(1)} collective-permute-done((bf16[80,4096]{1,0:T(8,128)(2,1)S(1)}, bf16[80,4096]{1,0:T(8,128)(2,1)S(1)}, u32[]{:S(2)}, u32[]{:S(2)}) %collective-permute-start.23) | collective-permute-done | bytes 655392 | tf_op jit(solution)/shard_map/ppermute | solution.py:66
  323.7 12.6 %all-to-all-start.1 = ((bf16[32,5,32,128]{3,2,1,0:T(8,128)(2,1)}), bf16[32,5,32,128]{3,2,1,0:T(8,128)(2,1)}, u32[]{:S(2)}, u32[]{:S(2)}) async-start(bf16[32,5,32,128]{3,2,1,0:T(8,128)(2,1)} %bitcast.21), calls=%async_computation.1 | async-start | bytes 2621440 | tf_op jit(solution)/shard_map/all_to_all | solution.py:142
  336.3 5.2 %collective-permute-done.27 = bf16[80,3072]{1,0:T(8,128)(2,1)} collective-permute-done((bf16[80,3072]{1,0:T(8,128)(2,1)}, bf16[80,3072]{1,0:T(8,128)(2,1)}, u32[]{:S(2)}, u32[]{:S(2)}) %collective-permute-start.27) | collective-permute-done | bytes 491552 | tf_op jit(solution)/shard_map/ppermute | solution.py:66
  341.5 1.9 add_convert_fusion.6
  344.7 11.4 %all-to-all-done.1 = bf16[32,5,32,128]{3,2,1,0:T(8,128)(2,1)} async-done(((bf16[32,5,32,128]{3,2,1,0:T(8,128)(2,1)}), bf16[32,5,32,128]{3,2,1,0:T(8,128)(2,1)}, u32[]{:S(2)}, u32[]{:S(2)}) %all-to-all-start.1) | async-done | bytes 1310752 | tf_op jit(solution)/shard_map/all_to_all | solution.py:142
  356.1 4.7 %all-to-all-start.2 = ((bf16[32,5,24,128]{3,2,1,0:T(8,128)(2,1)}), bf16[32,5,24,128]{3,2,1,0:T(8,128)(2,1)S(1)}, u32[]{:S(2)}, u32[]{:S(2)}) async-start(bf16[32,5,24,128]{3,2,1,0:T(8,128)(2,1)} %bitcast.27), calls=%async_computation.2 | async-start | bytes 1966080 | tf_op jit(solution)/shard_map/all_to_all | solution.py:142
  360.9 2.1 fusion
  364.4 12.9 %all-to-all-done.2 = bf16[32,5,24,128]{3,2,1,0:T(8,128)(2,1)S(1)} async-done(((bf16[32,5,24,128]{3,2,1,0:T(8,128)(2,1)}), bf16[32,5,24,128]{3,2,1,0:T(8,128)(2,1)S(1)}, u32[]{:S(2)}, u32[]{:S(2)}) %all-to-all-start.2) | async-done | bytes 983072 | tf_op jit(solution)/shard_map/all_to_all | solution.py:142
  (115 shorter events, 44.9 us)
Async XLA Ops:
  0.0 3.1 copy-start
  2.5 0.5 copy-start.8
  5.7 56.8 %all-to-all-start = ((bf16[32,5,56,128]{3,2,1,0:T(8,128)(2,1)}), bf16[32,5,56,128]{3,2,1,0:T(8,128)(2,1)S(1)}, u32[]{:S(2)}, u32[]{:S(2)}) async-start(bf16[32,5,56,128]{3,2,1,0:T(8,128)(2,1)} %bitcast.86), calls=%async_computation | async-start | bytes 4587520 | tf_op jit(solution)/shard_map/all_to_all | solution.py:70
  14.5 11.3 %copy-start.2 = (bf16[1,7168,256]{2,1,0:T(8,128)(2,1)S(1)}, bf16[1,7168,256]{2,1,0:T(8,128)(2,1)}, u32[]{:S(2)}) copy-start(bf16[1,7168,256]{2,1,0:T(8,128)(2,1)} %param.10) | copy-start | bytes 11010052
  18.8 41.9 %collective-permute-start.17 = (bf16[7168,128]{1,0:T(8,128)(2,1)}, bf16[7168,128]{1,0:T(8,128)(2,1)}, u32[]{:S(2)}, u32[]{:S(2)}) collective-permute-start(bf16[7168,128]{1,0:T(8,128)(2,1)} %get-tuple-element.45), channel_id=1, source_target_pairs={{0,1},{3,2},{4,5},{7,6},{8,9},{11,10},{12,13},{15,14},{16,17},{19,... | collective-permute-start | bytes 5505032 | tf_op jit(solution)/shard_map/ppermute | solution.py:63
  22.5 97.9 %collective-permute-start.16 = (bf16[7168,128]{1,0:T(8,128)(2,1)}, bf16[7168,128]{1,0:T(8,128)(2,1)}, u32[]{:S(2)}, u32[]{:S(2)}) collective-permute-start(bf16[7168,128]{1,0:T(8,128)(2,1)} %get-tuple-element.46), channel_id=1, source_target_pairs={{3,7},{0,124},{7,11},{4,0},{11,15},{8,4},{15,19},{12,8},{19,23},{1... | collective-permute-start | bytes 5505032 | tf_op jit(solution)/shard_map/ppermute | solution.py:82
  27.8 72.1 %collective-permute-start.14 = (bf16[7168,128]{1,0:T(8,128)(2,1)}, bf16[7168,128]{1,0:T(8,128)(2,1)}, u32[]{:S(2)}, u32[]{:S(2)}) collective-permute-start(bf16[7168,128]{1,0:T(8,128)(2,1)} %get-tuple-element.43), channel_id=1, source_target_pairs={{0,1},{3,2},{4,5},{7,6},{8,9},{11,10},{12,13},{15,14},{16,17},{19,... | collective-permute-start | bytes 5505032 | tf_op jit(solution)/shard_map/ppermute | solution.py:63
  30.4 98.5 %collective-permute-start.13 = (bf16[7168,128]{1,0:T(8,128)(2,1)}, bf16[7168,128]{1,0:T(8,128)(2,1)}, u32[]{:S(2)}, u32[]{:S(2)}) collective-permute-start(bf16[7168,128]{1,0:T(8,128)(2,1)} %get-tuple-element.44), channel_id=1, source_target_pairs={{3,7},{0,124},{7,11},{4,0},{11,15},{8,4},{15,19},{12,8},{19,23},{1... | collective-permute-start | bytes 5505032 | tf_op jit(solution)/shard_map/ppermute | solution.py:81
  60.7 60.7 %collective-permute-start.18 = (bf16[7168,128]{1,0:T(8,128)(2,1)}, bf16[7168,128]{1,0:T(8,128)(2,1)}, u32[]{:S(2)}, u32[]{:S(2)}) collective-permute-start(bf16[7168,128]{1,0:T(8,128)(2,1)} %collective-permute-done.17), channel_id=1, source_target_pairs={{2,6},{1,125},{6,10},{5,1},{10,14},{9,5},{14,18},{13,9},{18,22},{1... | collective-permute-start | bytes 5505032 | tf_op jit(solution)/shard_map/ppermute | solution.py:92
  63.0 3.7 copy-start.3
  63.1 56.5 %collective-permute-start.6 = (bf16[64,7168]{1,0:T(8,128)(2,1)S(1)}, bf16[64,7168]{1,0:T(8,128)(2,1)S(1)}, u32[]{:S(2)}, u32[]{:S(2)}) collective-permute-start(bf16[64,7168]{1,0:T(8,128)(2,1)S(1)} %slice.183), channel_id=1, source_target_pairs={{0,1},{1,0},{2,3},{3,2},{4,5},{5,4},{6,7},{7,6},{8,9},{9,8},{10,11... | collective-permute-start | bytes 2752520 | tf_op jit(solution)/shard_map/ppermute | solution.py:66
  66.7 2.0 copy-start.4
  66.7 2.0 copy-start.11
  68.7 31.2 %copy-start.6 = (bf16[104,7168]{1,0:T(8,128)(2,1)S(1)}, bf16[104,7168]{1,0:T(8,128)(2,1)}, u32[]{:S(2)}) copy-start(bf16[104,7168]{1,0:T(8,128)(2,1)} %slice_bitcast_fusion) | copy-start | bytes 4472836
  100.0 96.7 %collective-permute-start.2 = (bf16[104,7168]{1,0:T(8,128)(2,1)S(1)}, bf16[104,7168]{1,0:T(8,128)(2,1)S(1)}, u32[]{:S(2)}, u32[]{:S(2)}) collective-permute-start(bf16[104,7168]{1,0:T(8,128)(2,1)S(1)} %copy-done.6), channel_id=1, source_target_pairs={{0,1},{3,2},{4,5},{7,6},{8,9},{11,10},{12,13},{15,14},{16,17},{19,... | collective-permute-start | bytes 4472840 | tf_op jit(solution)/shard_map/ppermute | solution.py:63
  119.5 48.9 %collective-permute-start.15 = (bf16[7168,128]{1,0:T(8,128)(2,1)}, bf16[7168,128]{1,0:T(8,128)(2,1)S(1)}, u32[]{:S(2)}, u32[]{:S(2)}) collective-permute-start(bf16[7168,128]{1,0:T(8,128)(2,1)} %collective-permute-done.14), channel_id=1, source_target_pairs={{2,6},{1,125},{6,10},{5,1},{10,14},{9,5},{14,18},{13,9},{18,22},{1... | collective-permute-start | bytes 5505032 | tf_op jit(solution)/shard_map/ppermute | solution.py:90
  120.4 50.9 %collective-permute-start.9 = (bf16[160,7168]{1,0:T(8,128)(2,1)S(1)}, bf16[160,7168]{1,0:T(8,128)(2,1)S(1)}, u32[]{:S(2)}, u32[]{:S(2)}) collective-permute-start(bf16[160,7168]{1,0:T(8,128)(2,1)S(1)} %bitcast.89), channel_id=1, source_target_pairs={{0,3},{3,0},{1,2},{2,1},{4,7},{7,4},{5,6},{6,5},{8,11},{11,8},{9,1... | collective-permute-start | bytes 6881288 | tf_op jit(solution)/shard_map/ppermute | solution.py:66
  121.3 44.9 %collective-permute-start.11 = (bf16[48,7168]{1,0:T(8,128)(2,1)S(1)}, bf16[48,7168]{1,0:T(8,128)(2,1)S(1)}, u32[]{:S(2)}, u32[]{:S(2)}) collective-permute-start(bf16[48,7168]{1,0:T(8,128)(2,1)S(1)} %get-tuple-element.57), channel_id=1, source_target_pairs={{0,1},{1,0},{2,3},{3,2},{4,5},{5,4},{6,7},{7,6},{8,9},{9,8},{10,11... | collective-permute-start | bytes 2064392 | tf_op jit(solution)/shard_map/ppermute | solution.py:66
  128.9 64.3 %collective-permute-start.4 = (bf16[24,7168]{1,0:T(8,128)(2,1)S(1)}, bf16[24,7168]{1,0:T(8,128)(2,1)S(1)}, u32[]{:S(2)}, u32[]{:S(2)}) collective-permute-start(bf16[24,7168]{1,0:T(8,128)(2,1)S(1)} %slice_bitcast_fusion.3), channel_id=1, source_target_pairs={{0,1},{3,2},{4,5},{7,6},{8,9},{11,10},{12,13},{15,14},{16,17},{19,... | collective-permute-start | bytes 1032200 | tf_op jit(solution)/shard_map/ppermute | solution.py:63
  166.2 22.1 %collective-permute-start.8 = (bf16[48,7168]{1,0:T(8,128)(2,1)S(1)}, bf16[48,7168]{1,0:T(8,128)(2,1)S(1)}, u32[]{:S(2)}, u32[]{:S(2)}) collective-permute-start(bf16[48,7168]{1,0:T(8,128)(2,1)S(1)} %get-tuple-element.58), channel_id=1, source_target_pairs={{0,1},{1,0},{2,3},{3,2},{4,5},{5,4},{6,7},{7,6},{8,9},{9,8},{10,11... | collective-permute-start | bytes 2064392 | tf_op jit(solution)/shard_map/ppermute | solution.py:66
  168.4 32.8 %collective-permute-start.12 = (bf16[48,7168]{1,0:T(8,128)(2,1)S(1)}, bf16[48,7168]{1,0:T(8,128)(2,1)S(1)}, u32[]{:S(2)}, u32[]{:S(2)}) collective-permute-start(bf16[48,7168]{1,0:T(8,128)(2,1)S(1)} %collective-permute-done.11), channel_id=1, source_target_pairs={{0,3},{3,0},{1,2},{2,1},{4,7},{7,4},{5,6},{6,5},{8,11},{11,8},{9,1... | collective-permute-start | bytes 2064392 | tf_op jit(solution)/shard_map/ppermute | solution.py:66
  171.3 35.3 %collective-permute-start.7 = (bf16[64,7168]{1,0:T(8,128)(2,1)S(1)}, bf16[64,7168]{1,0:T(8,128)(2,1)S(1)}, u32[]{:S(2)}, u32[]{:S(2)}) collective-permute-start(bf16[64,7168]{1,0:T(8,128)(2,1)S(1)} %collective-permute-done.6), channel_id=1, source_target_pairs={{0,3},{3,0},{1,2},{2,1},{4,7},{7,4},{5,6},{6,5},{8,11},{11,8},{9,1... | collective-permute-start | bytes 2752520 | tf_op jit(solution)/shard_map/ppermute | solution.py:66
  188.4 33.0 %collective-permute-start.10 = (bf16[48,7168]{1,0:T(8,128)(2,1)S(1)}, bf16[48,7168]{1,0:T(8,128)(2,1)S(1)}, u32[]{:S(2)}, u32[]{:S(2)}) collective-permute-start(bf16[48,7168]{1,0:T(8,128)(2,1)S(1)} %collective-permute-done.8), channel_id=1, source_target_pairs={{0,3},{3,0},{1,2},{2,1},{4,7},{7,4},{5,6},{6,5},{8,11},{11,8},{9,1... | collective-permute-start | bytes 2064392 | tf_op jit(solution)/shard_map/ppermute | solution.py:66
  192.4 1.2 copy-start.7
  193.6 31.2 %collective-permute-start = (bf16[64,7168]{1,0:T(8,128)(2,1)S(1)}, bf16[64,7168]{1,0:T(8,128)(2,1)S(1)}, u32[]{:S(2)}, u32[]{:S(2)}) collective-permute-start(bf16[64,7168]{1,0:T(8,128)(2,1)S(1)} %copy-done.7), channel_id=1, source_target_pairs={{3,7},{0,124},{7,11},{4,0},{11,15},{8,4},{15,19},{12,8},{19,23},{1... | collective-permute-start | bytes 2752520 | tf_op jit(solution)/shard_map/ppermute | solution.py:71
  196.7 37.8 %collective-permute-start.1 = (bf16[64,7168]{1,0:T(8,128)(2,1)S(1)}, bf16[64,7168]{1,0:T(8,128)(2,1)S(1)}, u32[]{:S(2)}, u32[]{:S(2)}) collective-permute-start(bf16[64,7168]{1,0:T(8,128)(2,1)S(1)} %get-tuple-element.47), channel_id=1, source_target_pairs={{3,7},{0,124},{7,11},{4,0},{11,15},{8,4},{15,19},{12,8},{19,23},{1... | collective-permute-start | bytes 2752520 | tf_op jit(solution)/shard_map/ppermute | solution.py:83
  201.2 23.6 %collective-permute-start.5 = (bf16[24,7168]{1,0:T(8,128)(2,1)S(1)}, bf16[24,7168]{1,0:T(8,128)(2,1)S(1)}, u32[]{:S(2)}, u32[]{:S(2)}) collective-permute-start(bf16[24,7168]{1,0:T(8,128)(2,1)S(1)} %collective-permute-done.4), channel_id=1, source_target_pairs={{2,6},{1,125},{6,10},{5,1},{10,14},{9,5},{14,18},{13,9},{18,22},{1... | collective-permute-start | bytes 1032200 | tf_op jit(solution)/shard_map/ppermute | solution.py:97
  206.6 27.9 %collective-permute-start.3 = (bf16[104,7168]{1,0:T(8,128)(2,1)S(1)}, bf16[104,7168]{1,0:T(8,128)(2,1)S(1)}, u32[]{:S(2)}, u32[]{:S(2)}) collective-permute-start(bf16[104,7168]{1,0:T(8,128)(2,1)S(1)} %collective-permute-done.2), channel_id=1, source_target_pairs={{2,6},{1,125},{6,10},{5,1},{10,14},{9,5},{14,18},{13,9},{18,22},{1... | collective-permute-start | bytes 4472840 | tf_op jit(solution)/shard_map/ppermute | solution.py:89
  224.8 10.2 %copy-start.5 = (bf16[1,256,7168]{2,1,0:T(8,128)(2,1)S(1)}, bf16[1,256,7168]{2,1,0:T(8,128)(2,1)}, u32[]{:S(2)}) copy-start(bf16[1,256,7168]{2,1,0:T(8,128)(2,1)} %param.12) | copy-start | bytes 11010052
  240.1 25.0 %collective-permute-start.28 = (bf16[80,3072]{1,0:T(8,128)(2,1)S(1)}, bf16[80,3072]{1,0:T(8,128)(2,1)S(1)}, u32[]{:S(2)}, u32[]{:S(2)}) collective-permute-start(bf16[80,3072]{1,0:T(8,128)(2,1)S(1)} %get-tuple-element.52), channel_id=1, source_target_pairs={{0,1},{1,0},{2,3},{3,2},{4,5},{5,4},{6,7},{7,6},{8,9},{9,8},{10,11... | collective-permute-start | bytes 1474568 | tf_op jit(solution)/shard_map/ppermute | solution.py:66
  254.2 52.3 %collective-permute-start.26 = (bf16[80,3072]{1,0:T(8,128)(2,1)S(1)}, bf16[80,3072]{1,0:T(8,128)(2,1)S(1)}, u32[]{:S(2)}, u32[]{:S(2)}) collective-permute-start(bf16[80,3072]{1,0:T(8,128)(2,1)S(1)} %get-tuple-element.51), channel_id=1, source_target_pairs={{0,3},{3,0},{1,2},{2,1},{4,7},{7,4},{5,6},{6,5},{8,11},{11,8},{9,1... | collective-permute-start | bytes 1474568 | tf_op jit(solution)/shard_map/ppermute | solution.py:66
  255.9 80.4 %collective-permute-start.25 = (bf16[80,3072]{1,0:T(8,128)(2,1)S(1)}, bf16[80,3072]{1,0:T(8,128)(2,1)}, u32[]{:S(2)}, u32[]{:S(2)}) collective-permute-start(bf16[80,3072]{1,0:T(8,128)(2,1)S(1)} %slice.205), channel_id=1, source_target_pairs={{0,3},{3,0},{1,2},{2,1},{4,7},{7,4},{5,6},{6,5},{8,11},{11,8},{9,1... | collective-permute-start | bytes 1474568 | tf_op jit(solution)/shard_map/ppermute | solution.py:66
  257.7 21.6 %collective-permute-start.22 = (bf16[80,4096]{1,0:T(8,128)(2,1)S(1)}, bf16[80,4096]{1,0:T(8,128)(2,1)S(1)}, u32[]{:S(2)}, u32[]{:S(2)}) collective-permute-start(bf16[80,4096]{1,0:T(8,128)(2,1)S(1)} %get-tuple-element.56), channel_id=1, source_target_pairs={{0,1},{1,0},{2,3},{3,2},{4,5},{5,4},{6,7},{7,6},{8,9},{9,8},{10,11... | collective-permute-start | bytes 1966088 | tf_op jit(solution)/shard_map/ppermute | solution.py:66
  257.7 49.8 %collective-permute-start.19 = (bf16[80,4096]{1,0:T(8,128)(2,1)S(1)}, bf16[80,4096]{1,0:T(8,128)(2,1)S(1)}, u32[]{:S(2)}, u32[]{:S(2)}) collective-permute-start(bf16[80,4096]{1,0:T(8,128)(2,1)S(1)} %slice.199), channel_id=1, source_target_pairs={{0,3},{3,0},{1,2},{2,1},{4,7},{7,4},{5,6},{6,5},{8,11},{11,8},{9,1... | collective-permute-start | bytes 1966088 | tf_op jit(solution)/shard_map/ppermute | solution.py:66
  265.1 40.7 %collective-permute-start.20 = (bf16[80,4096]{1,0:T(8,128)(2,1)S(1)}, bf16[80,4096]{1,0:T(8,128)(2,1)S(1)}, u32[]{:S(2)}, u32[]{:S(2)}) collective-permute-start(bf16[80,4096]{1,0:T(8,128)(2,1)S(1)} %get-tuple-element.55), channel_id=1, source_target_pairs={{0,3},{3,0},{1,2},{2,1},{4,7},{7,4},{5,6},{6,5},{8,11},{11,8},{9,1... | collective-permute-start | bytes 1966088 | tf_op jit(solution)/shard_map/ppermute | solution.py:66
  279.3 29.7 %collective-permute-start.24 = (bf16[80,4096]{1,0:T(8,128)(2,1)S(1)}, bf16[80,4096]{1,0:T(8,128)(2,1)S(1)}, u32[]{:S(2)}, u32[]{:S(2)}) collective-permute-start(bf16[80,4096]{1,0:T(8,128)(2,1)S(1)} %slice.203), channel_id=1, source_target_pairs={{0,1},{1,0},{2,3},{3,2},{4,5},{5,4},{6,7},{7,6},{8,9},{9,8},{10,11... | collective-permute-start | bytes 1966088 | tf_op jit(solution)/shard_map/ppermute | solution.py:66
  305.8 15.7 %collective-permute-start.23 = (bf16[80,4096]{1,0:T(8,128)(2,1)S(1)}, bf16[80,4096]{1,0:T(8,128)(2,1)S(1)}, u32[]{:S(2)}, u32[]{:S(2)}) collective-permute-start(bf16[80,4096]{1,0:T(8,128)(2,1)S(1)} %add_convert_fusion.1), channel_id=1, source_target_pairs={{0,3},{3,0},{1,2},{2,1},{4,7},{7,4},{5,6},{6,5},{8,11},{11,8},{9,1... | collective-permute-start | bytes 1966088 | tf_op jit(solution)/shard_map/ppermute | solution.py:66
  306.5 15.1 %collective-permute-start.21 = (bf16[80,4096]{1,0:T(8,128)(2,1)S(1)}, bf16[80,4096]{1,0:T(8,128)(2,1)S(1)}, u32[]{:S(2)}, u32[]{:S(2)}) collective-permute-start(bf16[80,4096]{1,0:T(8,128)(2,1)S(1)} %add_convert_fusion.3), channel_id=1, source_target_pairs={{0,1},{1,0},{2,3},{3,2},{4,5},{5,4},{6,7},{7,6},{8,9},{9,8},{10,11... | collective-permute-start | bytes 1966088 | tf_op jit(solution)/shard_map/ppermute | solution.py:66
  307.5 28.8 %collective-permute-start.30 = (bf16[80,3072]{1,0:T(8,128)(2,1)S(1)}, bf16[80,3072]{1,0:T(8,128)(2,1)}, u32[]{:S(2)}, u32[]{:S(2)}) collective-permute-start(bf16[80,3072]{1,0:T(8,128)(2,1)S(1)} %slice.209), channel_id=1, source_target_pairs={{0,1},{1,0},{2,3},{3,2},{4,5},{5,4},{6,7},{7,6},{8,9},{9,8},{10,11... | collective-permute-start | bytes 1474568 | tf_op jit(solution)/shard_map/ppermute | solution.py:66
  308.9 27.4 %collective-permute-start.29 = (bf16[80,3072]{1,0:T(8,128)(2,1)}, bf16[80,3072]{1,0:T(8,128)(2,1)}, u32[]{:S(2)}, u32[]{:S(2)}) collective-permute-start(bf16[80,3072]{1,0:T(8,128)(2,1)} %add_convert_fusion.5), channel_id=1, source_target_pairs={{0,3},{3,0},{1,2},{2,1},{4,7},{7,4},{5,6},{6,5},{8,11},{11,8},{9,1... | collective-permute-start | bytes 1474568 | tf_op jit(solution)/shard_map/ppermute | solution.py:66
  321.5 19.9 %collective-permute-start.27 = (bf16[80,3072]{1,0:T(8,128)(2,1)}, bf16[80,3072]{1,0:T(8,128)(2,1)}, u32[]{:S(2)}, u32[]{:S(2)}) collective-permute-start(bf16[80,3072]{1,0:T(8,128)(2,1)} %add_convert_fusion.7), channel_id=1, source_target_pairs={{0,1},{1,0},{2,3},{3,2},{4,5},{5,4},{6,7},{7,6},{8,9},{9,8},{10,11... | collective-permute-start | bytes 1474568 | tf_op jit(solution)/shard_map/ppermute | solution.py:66
  323.7 32.4 %all-to-all-start.1 = ((bf16[32,5,32,128]{3,2,1,0:T(8,128)(2,1)}), bf16[32,5,32,128]{3,2,1,0:T(8,128)(2,1)}, u32[]{:S(2)}, u32[]{:S(2)}) async-start(bf16[32,5,32,128]{3,2,1,0:T(8,128)(2,1)} %bitcast.21), calls=%async_computation.1 | async-start | bytes 2621440 | tf_op jit(solution)/shard_map/all_to_all | solution.py:142
  343.5 17.3 %copy-start.9 = (s32[128]{0:T(128)S(1)}, s32[128]{0:T(128)}, u32[]{:S(2)}) copy-start(s32[128]{0:T(128)} %copy-done.8) | copy-start | bytes 1540
  343.5 17.3 %copy-start.10 = (f32[128,1]{0,1:T(1,128)S(1)}, f32[128,1]{0,1:T(1,128)}, u32[]{:S(2)}) copy-start(f32[128,1]{0,1:T(1,128)} %param.9) | copy-start | bytes 1540
  356.1 21.1 %all-to-all-start.2 = ((bf16[32,5,24,128]{3,2,1,0:T(8,128)(2,1)}), bf16[32,5,24,128]{3,2,1,0:T(8,128)(2,1)S(1)}, u32[]{:S(2)}, u32[]{:S(2)}) async-start(bf16[32,5,24,128]{3,2,1,0:T(8,128)(2,1)} %bitcast.27), calls=%async_computation.2 | async-start | bytes 1966080 | tf_op jit(solution)/shard_map/all_to_all | solution.py:142
  360.9 17.7 %copy-start.1 = (bf16[128,7168]{1,0:T(8,128)(2,1)S(1)}, bf16[128,7168]{1,0:T(8,128)(2,1)}, u32[]{:S(2)}) copy-start(bf16[128,7168]{1,0:T(8,128)(2,1)} %param.7) | copy-start | bytes 5505028

commit v10 on v9

--- a/solution.py
+++ b/solution.py
@@ -67,8 +67,8 @@
 
     inward_down = cross(w_down[inner:first_down])
     inward_gate = cross(w_gate[:, inner:])
+    inward_up = cross(w_up[:, inner:])
     arrived = lax.all_to_all(outgoing, PLANE, 0, 0, tiled=True)
-    outer_early = lax.ppermute(w_down[: inner // 2], EVERY, straight)
     mid = arrived.reshape(rows, width)
 
     kept, edge = multiplicities(partner, own, slots)
@@ -80,10 +80,9 @@
     mirror = over(mid, MIRROR)
     outer_gate = lax.ppermute(w_gate[:, :inner], EVERY, straight)
     outer_up = lax.ppermute(w_up[:, :inner], EVERY, straight)
-    outer_late = lax.ppermute(w_down[inner // 2 : inner], EVERY, straight)
-    side_a = over(mid[:64], SIDE)
-    inward_up = cross(w_up[:, inner:])
-    side_b = over(mid[64:112], SIDE)
+    outer_down = lax.ppermute(w_down[:inner], EVERY, straight)
+    side_a = over(mid[:56], SIDE)
+    side_b = over(mid[56:112], SIDE)
     side_c = over(mid[112:], SIDE)
     inward_last = cross(w_down[first_down:])
     inner_down = lax.ppermute(inward_down, EVERY, turned)
@@ -109,12 +108,11 @@
         return jnp.concatenate([mine, edge_hidden.astype(jnp.bfloat16)], axis=1)
 
     pairs = ((far, own_hidden(far)), (mirror, mirror_own), (side, own_hidden(side)))
-    downs = (outer_early, outer_late, inner_down, inner_last)
-    tied = lax.optimization_barrier((*downs, *[full_hidden(*p) for p in pairs]))
-    outer_down, inner_down = jnp.concatenate(tied[:2], axis=0), jnp.concatenate(tied[2:4], axis=0)
-    down = jnp.concatenate([w_down, jnp.where(outer, outer_down, inner_down)], axis=0)
-    far = dot(tied[4], down).astype(jnp.bfloat16)
-    far, mirror, side, mid, home_own = lax.optimization_barrier((far, *tied[5:], mid, home_own))
+    tied = lax.optimization_barrier((outer_down, inner_down, inner_last, *[full_hidden(*p) for p in pairs]))
+    edge_down = jnp.where(outer, tied[0], jnp.concatenate(tied[1:3], axis=0))
+    down = jnp.concatenate([w_down, edge_down], axis=0)
+    far = dot(tied[3], down).astype(jnp.bfloat16)
+    far, mirror, side, mid, home_own = lax.optimization_barrier((far, *tied[4:], mid, home_own))
     mirror, side = [dot(h, down).astype(jnp.bfloat16) for h in (mirror, side)]
     home = dot(full_hidden(mid, home_own), down).astype(jnp.bfloat16)
 

time: 382 us -> 373 us (0.976)
  starting transfers between devices: 96.5 us -> 88.4 us
  waiting for transfers between devices: 218 us -> 224 us
    ppermute x4, waiting for transfers between devices: 42.5 us -> 48.6 us  [cross(): return lax.ppermute(block, 'x', INWARD)]
    ppermute x2 -> x1, starting transfers between devices: 7.6 us -> 3.09 us  [body(): outer_down = lax.ppermute(w_down[:inner], EVERY, straight)]
    ppermute x2 -> x1, waiting for transfers between devices: 9.71 us -> 12.5 us  [body(): outer_down = lax.ppermute(w_down[:inner], EVERY, straight)]
  transfers between devices with their start and end apart: 34 -> 33, of which waited for: 16 -> 16; matrix products, arithmetic and copies ran while one was open for 13% -> 12% of each run, Pallas kernels for 0% -> 0%
where the time goes in v10:
time: 373 us; the launch traced here: 370 us
  waiting for transfers between devices  224 us (60%)
  starting transfers between devices  88.4 us (24%)
  local copies, waits for them, and re-layouts  21.8 us (6%)
  matrix products  20 us (5%)
  other arithmetic  15.2 us (4%)
    ppermute x19, waiting for transfers between devices, over(): return lax.ppermute(block, 'x', pairs)  142 us
    ppermute x4, waiting for transfers between devices, cross(): return lax.ppermute(block, 'x', INWARD)  48.6 us
    ppermute x19, starting transfers between devices, over(): return lax.ppermute(block, 'x', pairs)  37.4 us
    all_to_all x2, waiting for transfers between devices, body(): lax.all_to_all(total, PLANE, 0, 0, tiled=True).reshape(rows, hi - lo)  21.2 us
    dot_general x17, matrix products, dot(): return jnp.dot(a, b, preferred_element_type=jnp.float32)  16.6 us
    all_to_all x2, starting transfers between devices, body(): lax.all_to_all(total, PLANE, 0, 0, tiled=True).reshape(rows, hi - lo)  15.5 us
    ppermute x4, starting transfers between devices, cross(): return lax.ppermute(block, 'x', INWARD)  12.6 us
    ppermute x1, waiting for transfers between devices, body(): outer_down = lax.ppermute(w_down[:inner], EVERY, straight)  12.5 us
  transfers between devices with their start and end apart: 33, of which 16 were waited for; matrix products, arithmetic and copies ran while one was open for 12% of the time, Pallas kernels for 0%

profile of v10, /device:TPU:7, one launch (start us, length us, event | category | flops | bytes accessed | tf_op | source)
XLA Modules:
  0.0 370.3 jit_solution(11411789418150375285)
XLA Ops:
  3.3 1.9 copy.8
  5.2 8.8 %all-to-all-start = ((bf16[32,5,56,128]{3,2,1,0:T(8,128)(2,1)}), bf16[32,5,56,128]{3,2,1,0:T(8,128)(2,1)S(1)}, u32[]{:S(2)}, u32[]{:S(2)}) async-start(bf16[32,5,56,128]{3,2,1,0:T(8,128)(2,1)} %bitcast.84), calls=%async_computation | async-start | bytes 4587520 | tf_op jit(solution)/shard_map/all_to_all | solution.py:71
  14.0 4.3 %fusion.53 = (bf16[7168,128]{1,0:T(8,128)(2,1)}, bf16[7168,128]{1,0:T(8,128)(2,1)}) fusion(bf16[7168,256]{1,0:T(8,128)(2,1)} %bitcast.89), kind=kLoop, calls=%fused_computation.102 | loop fusion | bytes 7340032 | tf_op jit(solution)/shard_map/slice | solution.py:70
  18.3 3.7 collective-permute-start.16
  22.0 3.2 collective-permute-start.15
  25.2 2.1 fusion.52
  27.3 2.7 collective-permute-start.13
  30.1 3.6 collective-permute-start.12
  33.8 2.6 slice_bitcast_fusion.1
  40.4 2.8 slice_bitcast_fusion
  43.3 16.9 %collective-permute-done.16 = bf16[7168,128]{1,0:T(8,128)(2,1)} collective-permute-done((bf16[7168,128]{1,0:T(8,128)(2,1)}, bf16[7168,128]{1,0:T(8,128)(2,1)}, u32[]{:S(2)}, u32[]{:S(2)}) %collective-permute-start.16) | collective-permute-done | bytes 1835040 | tf_op jit(solution)/shard_map/ppermute | solution.py:63
  60.2 1.9 collective-permute-start.17
  62.7 3.4 collective-permute-start.5
  67.8 31.7 %collective-permute-done.13 = bf16[7168,128]{1,0:T(8,128)(2,1)} collective-permute-done((bf16[7168,128]{1,0:T(8,128)(2,1)}, bf16[7168,128]{1,0:T(8,128)(2,1)}, u32[]{:S(2)}, u32[]{:S(2)}) %collective-permute-start.13) | collective-permute-done | bytes 1835040 | tf_op jit(solution)/shard_map/ppermute | solution.py:63
  99.5 4.2 %collective-permute-start.1 = (bf16[104,7168]{1,0:T(8,128)(2,1)S(1)}, bf16[104,7168]{1,0:T(8,128)(2,1)S(1)}, u32[]{:S(2)}, u32[]{:S(2)}) collective-permute-start(bf16[104,7168]{1,0:T(8,128)(2,1)S(1)} %copy-done.7), channel_id=1, source_target_pairs={{0,1},{3,2},{4,5},{7,6},{8,9},{11,10},{12,13},{15,14},{16,17},{19,... | collective-permute-start | bytes 4472840 | tf_op jit(solution)/shard_map/ppermute | solution.py:63
  103.7 12.9 %collective-permute-done.5 = bf16[56,7168]{1,0:T(8,128)(2,1)S(1)} collective-permute-done((bf16[56,7168]{1,0:T(8,128)(2,1)S(1)}, bf16[56,7168]{1,0:T(8,128)(2,1)S(1)}, u32[]{:S(2)}, u32[]{:S(2)}) %collective-permute-start.5) | collective-permute-done | bytes 802848 | tf_op jit(solution)/shard_map/ppermute | solution.py:66
  118.4 5.9 %collective-permute-start.10 = (bf16[48,7168]{1,0:T(8,128)(2,1)S(1)}, bf16[48,7168]{1,0:T(8,128)(2,1)S(1)}, u32[]{:S(2)}, u32[]{:S(2)}) collective-permute-start(bf16[48,7168]{1,0:T(8,128)(2,1)S(1)} %slice.177), channel_id=1, source_target_pairs={{0,1},{1,0},{2,3},{3,2},{4,5},{5,4},{6,7},{7,6},{8,9},{9,8},{10,11... | collective-permute-start | bytes 2064392 | tf_op jit(solution)/shard_map/ppermute | solution.py:66
  124.3 1.7 broadcast_select_fusion
  126.0 1.9 collective-permute-start.3
  127.9 35.4 %collective-permute-done.10 = bf16[48,7168]{1,0:T(8,128)(2,1)S(1)} collective-permute-done((bf16[48,7168]{1,0:T(8,128)(2,1)S(1)}, bf16[48,7168]{1,0:T(8,128)(2,1)S(1)}, u32[]{:S(2)}, u32[]{:S(2)}) %collective-permute-start.10) | collective-permute-done | bytes 688160 | tf_op jit(solution)/shard_map/ppermute | solution.py:66
  163.3 2.2 collective-permute-start.7
  166.3 1.7 broadcast_select_fusion.1
  168.3 1.6 collective-permute-start.6
  171.6 16.3 %collective-permute-done.7 = bf16[56,7168]{1,0:T(8,128)(2,1)S(1)} collective-permute-done((bf16[56,7168]{1,0:T(8,128)(2,1)S(1)}, bf16[56,7168]{1,0:T(8,128)(2,1)S(1)}, u32[]{:S(2)}, u32[]{:S(2)}) %collective-permute-start.7) | collective-permute-done | bytes 802848 | tf_op jit(solution)/shard_map/ppermute | solution.py:66
  193.5 3.1 collective-permute-start
  198.0 3.1 collective-permute-done.6
  201.2 17.2 %collective-permute-done.9 = bf16[56,7168]{1,0:T(8,128)(2,1)S(1)} collective-permute-done((bf16[56,7168]{1,0:T(8,128)(2,1)S(1)}, bf16[56,7168]{1,0:T(8,128)(2,1)S(1)}, u32[]{:S(2)}, u32[]{:S(2)}) %collective-permute-start.9) | collective-permute-done | bytes 802848 | tf_op jit(solution)/shard_map/ppermute | solution.py:66
  221.9 12.5 %collective-permute-done = bf16[128,7168]{1,0:T(8,128)(2,1)S(1)} collective-permute-done((bf16[128,7168]{1,0:T(8,128)(2,1)S(1)}, bf16[128,7168]{1,0:T(8,128)(2,1)S(1)}, u32[]{:S(2)}, u32[]{:S(2)}) %collective-permute-start) | collective-permute-done | bytes 1835040 | tf_op jit(solution)/shard_map/ppermute | solution.py:83
  234.8 1.6 convolution_convert_fusion.3
  236.6 1.6 convolution_convert_fusion.1
  238.3 1.6 convolution_convert_fusion
  240.0 2.5 collective-permute-start.27
  242.4 5.2 %collective-permute-start.25 = (bf16[80,3072]{1,0:T(8,128)(2,1)S(1)}, bf16[80,3072]{1,0:T(8,128)(2,1)S(1)}, u32[]{:S(2)}, u32[]{:S(2)}) collective-permute-start(bf16[80,3072]{1,0:T(8,128)(2,1)S(1)} %get-tuple-element.47), channel_id=1, source_target_pairs={{0,3},{3,0},{1,2},{2,1},{4,7},{7,4},{5,6},{6,5},{8,11},{11,8},{9,1... | collective-permute-start | bytes 1474568 | tf_op jit(solution)/shard_map/ppermute | solution.py:66
  248.6 2.6 collective-permute-start.18
  251.9 1.6 convolution_convert_fusion.2
  253.5 5.8 %collective-permute-start.19 = (bf16[80,4096]{1,0:T(8,128)(2,1)S(1)}, bf16[80,4096]{1,0:T(8,128)(2,1)S(1)}, u32[]{:S(2)}, u32[]{:S(2)}) collective-permute-start(bf16[80,4096]{1,0:T(8,128)(2,1)S(1)} %get-tuple-element.51), channel_id=1, source_target_pairs={{0,3},{3,0},{1,2},{2,1},{4,7},{7,4},{5,6},{6,5},{8,11},{11,8},{9,1... | collective-permute-start | bytes 1966088 | tf_op jit(solution)/shard_map/ppermute | solution.py:66
  260.2 5.6 %collective-permute-done.21 = bf16[80,4096]{1,0:T(8,128)(2,1)S(1)} collective-permute-done((bf16[80,4096]{1,0:T(8,128)(2,1)S(1)}, bf16[80,4096]{1,0:T(8,128)(2,1)S(1)}, u32[]{:S(2)}, u32[]{:S(2)}) %collective-permute-start.21) | collective-permute-done | bytes 655392 | tf_op jit(solution)/shard_map/ppermute | solution.py:66
  267.1 30.3 %collective-permute-done.19 = bf16[80,4096]{1,0:T(8,128)(2,1)S(1)} collective-permute-done((bf16[80,4096]{1,0:T(8,128)(2,1)S(1)}, bf16[80,4096]{1,0:T(8,128)(2,1)S(1)}, u32[]{:S(2)}, u32[]{:S(2)}) %collective-permute-start.19) | collective-permute-done | bytes 655392 | tf_op jit(solution)/shard_map/ppermute | solution.py:66
  297.5 2.5 collective-permute-start.22
  301.2 1.5 collective-permute-start.29
  302.8 11.2 %collective-permute-done.22 = bf16[80,4096]{1,0:T(8,128)(2,1)S(1)} collective-permute-done((bf16[80,4096]{1,0:T(8,128)(2,1)S(1)}, bf16[80,4096]{1,0:T(8,128)(2,1)S(1)}, u32[]{:S(2)}, u32[]{:S(2)}) %collective-permute-start.22) | collective-permute-done | bytes 655392 | tf_op jit(solution)/shard_map/ppermute | solution.py:66
  317.3 10.7 %all-to-all-start.1 = ((bf16[32,5,32,128]{3,2,1,0:T(8,128)(2,1)}), bf16[32,5,32,128]{3,2,1,0:T(8,128)(2,1)}, u32[]{:S(2)}, u32[]{:S(2)}) async-start(bf16[32,5,32,128]{3,2,1,0:T(8,128)(2,1)} %bitcast.20), calls=%async_computation.1 | async-start | bytes 2621440 | tf_op jit(solution)/shard_map/all_to_all | solution.py:140
  328.0 8.3 %collective-permute-done.26 = bf16[80,3072]{1,0:T(8,128)(2,1)} collective-permute-done((bf16[80,3072]{1,0:T(8,128)(2,1)}, bf16[80,3072]{1,0:T(8,128)(2,1)}, u32[]{:S(2)}, u32[]{:S(2)}) %collective-permute-start.26) | collective-permute-done | bytes 491552 | tf_op jit(solution)/shard_map/ppermute | solution.py:66
  336.3 1.9 add_convert_fusion.6
  339.5 8.3 %all-to-all-done.1 = bf16[32,5,32,128]{3,2,1,0:T(8,128)(2,1)} async-done(((bf16[32,5,32,128]{3,2,1,0:T(8,128)(2,1)}), bf16[32,5,32,128]{3,2,1,0:T(8,128)(2,1)}, u32[]{:S(2)}, u32[]{:S(2)}) %all-to-all-start.1) | async-done | bytes 1310752 | tf_op jit(solution)/shard_map/all_to_all | solution.py:140
  347.9 4.7 %all-to-all-start.2 = ((bf16[32,5,24,128]{3,2,1,0:T(8,128)(2,1)}), bf16[32,5,24,128]{3,2,1,0:T(8,128)(2,1)S(1)}, u32[]{:S(2)}, u32[]{:S(2)}) async-start(bf16[32,5,24,128]{3,2,1,0:T(8,128)(2,1)} %bitcast.26), calls=%async_computation.2 | async-start | bytes 1966080 | tf_op jit(solution)/shard_map/all_to_all | solution.py:140
  352.6 2.1 fusion
  356.1 12.9 %all-to-all-done.2 = bf16[32,5,24,128]{3,2,1,0:T(8,128)(2,1)S(1)} async-done(((bf16[32,5,24,128]{3,2,1,0:T(8,128)(2,1)}), bf16[32,5,24,128]{3,2,1,0:T(8,128)(2,1)S(1)}, u32[]{:S(2)}, u32[]{:S(2)}) %all-to-all-start.2) | async-done | bytes 983072 | tf_op jit(solution)/shard_map/all_to_all | solution.py:140
  (109 shorter events, 37.5 us)
Async XLA Ops:
  0.0 2.6 copy-start
  5.2 56.9 %all-to-all-start = ((bf16[32,5,56,128]{3,2,1,0:T(8,128)(2,1)}), bf16[32,5,56,128]{3,2,1,0:T(8,128)(2,1)S(1)}, u32[]{:S(2)}, u32[]{:S(2)}) async-start(bf16[32,5,56,128]{3,2,1,0:T(8,128)(2,1)} %bitcast.84), calls=%async_computation | async-start | bytes 4587520 | tf_op jit(solution)/shard_map/all_to_all | solution.py:71
  14.0 11.3 %copy-start.2 = (bf16[1,7168,256]{2,1,0:T(8,128)(2,1)S(1)}, bf16[1,7168,256]{2,1,0:T(8,128)(2,1)}, u32[]{:S(2)}) copy-start(bf16[1,7168,256]{2,1,0:T(8,128)(2,1)} %param.10) | copy-start | bytes 11010052
  18.3 41.9 %collective-permute-start.16 = (bf16[7168,128]{1,0:T(8,128)(2,1)}, bf16[7168,128]{1,0:T(8,128)(2,1)}, u32[]{:S(2)}, u32[]{:S(2)}) collective-permute-start(bf16[7168,128]{1,0:T(8,128)(2,1)} %get-tuple-element.43), channel_id=1, source_target_pairs={{0,1},{3,2},{4,5},{7,6},{8,9},{11,10},{12,13},{15,14},{16,17},{19,... | collective-permute-start | bytes 5505032 | tf_op jit(solution)/shard_map/ppermute | solution.py:63
  22.0 95.4 %collective-permute-start.15 = (bf16[7168,128]{1,0:T(8,128)(2,1)}, bf16[7168,128]{1,0:T(8,128)(2,1)}, u32[]{:S(2)}, u32[]{:S(2)}) collective-permute-start(bf16[7168,128]{1,0:T(8,128)(2,1)} %get-tuple-element.44), channel_id=1, source_target_pairs={{3,7},{0,124},{7,11},{4,0},{11,15},{8,4},{15,19},{12,8},{19,23},{1... | collective-permute-start | bytes 5505032 | tf_op jit(solution)/shard_map/ppermute | solution.py:82
  27.3 10.1 %copy-start.8 = (s32[128,2]{0,1:T(2,128)S(1)}, s32[128,2]{0,1:T(2,128)}, u32[]{:S(2)}) copy-start(s32[128,2]{0,1:T(2,128)} %param.13) | copy-start | bytes 3076
  27.3 72.2 %collective-permute-start.13 = (bf16[7168,128]{1,0:T(8,128)(2,1)}, bf16[7168,128]{1,0:T(8,128)(2,1)}, u32[]{:S(2)}, u32[]{:S(2)}) collective-permute-start(bf16[7168,128]{1,0:T(8,128)(2,1)} %get-tuple-element.41), channel_id=1, source_target_pairs={{0,1},{3,2},{4,5},{7,6},{8,9},{11,10},{12,13},{15,14},{16,17},{19,... | collective-permute-start | bytes 5505032 | tf_op jit(solution)/shard_map/ppermute | solution.py:63
  30.1 95.9 %collective-permute-start.12 = (bf16[7168,128]{1,0:T(8,128)(2,1)}, bf16[7168,128]{1,0:T(8,128)(2,1)}, u32[]{:S(2)}, u32[]{:S(2)}) collective-permute-start(bf16[7168,128]{1,0:T(8,128)(2,1)} %get-tuple-element.42), channel_id=1, source_target_pairs={{3,7},{0,124},{7,11},{4,0},{11,15},{8,4},{15,19},{12,8},{19,23},{1... | collective-permute-start | bytes 5505032 | tf_op jit(solution)/shard_map/ppermute | solution.py:81
  60.2 58.2 %collective-permute-start.17 = (bf16[7168,128]{1,0:T(8,128)(2,1)}, bf16[7168,128]{1,0:T(8,128)(2,1)}, u32[]{:S(2)}, u32[]{:S(2)}) collective-permute-start(bf16[7168,128]{1,0:T(8,128)(2,1)} %collective-permute-done.16), channel_id=1, source_target_pairs={{2,6},{1,125},{6,10},{5,1},{10,14},{9,5},{14,18},{13,9},{18,22},{1... | collective-permute-start | bytes 5505032 | tf_op jit(solution)/shard_map/ppermute | solution.py:91
  62.6 3.6 copy-start.3
  62.7 4.2 %copy-start.4 = (bf16[1,7168,256]{2,1,0:T(8,128)(2,1)S(1)}, bf16[1,7168,256]{2,1,0:T(8,128)(2,1)}, u32[]{:S(2)}) copy-start(bf16[1,7168,256]{2,1,0:T(8,128)(2,1)} %param.11) | copy-start | bytes 11010052
  62.7 53.8 %collective-permute-start.5 = (bf16[56,7168]{1,0:T(8,128)(2,1)S(1)}, bf16[56,7168]{1,0:T(8,128)(2,1)S(1)}, u32[]{:S(2)}, u32[]{:S(2)}) collective-permute-start(bf16[56,7168]{1,0:T(8,128)(2,1)S(1)} %get-tuple-element.54), channel_id=1, source_target_pairs={{0,1},{1,0},{2,3},{3,2},{4,5},{5,4},{6,7},{7,6},{8,9},{9,8},{10,11... | collective-permute-start | bytes 2408456 | tf_op jit(solution)/shard_map/ppermute | solution.py:66
  67.0 32.5 %copy-start.7 = (bf16[104,7168]{1,0:T(8,128)(2,1)S(1)}, bf16[104,7168]{1,0:T(8,128)(2,1)}, u32[]{:S(2)}) copy-start(bf16[104,7168]{1,0:T(8,128)(2,1)} %slice_bitcast_fusion.1) | copy-start | bytes 4472836
  99.5 97.1 %collective-permute-start.1 = (bf16[104,7168]{1,0:T(8,128)(2,1)S(1)}, bf16[104,7168]{1,0:T(8,128)(2,1)S(1)}, u32[]{:S(2)}, u32[]{:S(2)}) collective-permute-start(bf16[104,7168]{1,0:T(8,128)(2,1)S(1)} %copy-done.7), channel_id=1, source_target_pairs={{0,1},{3,2},{4,5},{7,6},{8,9},{11,10},{12,13},{15,14},{16,17},{19,... | collective-permute-start | bytes 4472840 | tf_op jit(solution)/shard_map/ppermute | solution.py:63
  116.6 48.9 %collective-permute-start.14 = (bf16[7168,128]{1,0:T(8,128)(2,1)}, bf16[7168,128]{1,0:T(8,128)(2,1)S(1)}, u32[]{:S(2)}, u32[]{:S(2)}) collective-permute-start(bf16[7168,128]{1,0:T(8,128)(2,1)} %collective-permute-done.13), channel_id=1, source_target_pairs={{2,6},{1,125},{6,10},{5,1},{10,14},{9,5},{14,18},{13,9},{18,22},{1... | collective-permute-start | bytes 5505032 | tf_op jit(solution)/shard_map/ppermute | solution.py:89
  117.4 50.9 %collective-permute-start.8 = (bf16[160,7168]{1,0:T(8,128)(2,1)S(1)}, bf16[160,7168]{1,0:T(8,128)(2,1)S(1)}, u32[]{:S(2)}, u32[]{:S(2)}) collective-permute-start(bf16[160,7168]{1,0:T(8,128)(2,1)S(1)} %bitcast.87), channel_id=1, source_target_pairs={{0,3},{3,0},{1,2},{2,1},{4,7},{7,4},{5,6},{6,5},{8,11},{11,8},{9,1... | collective-permute-start | bytes 6881288 | tf_op jit(solution)/shard_map/ppermute | solution.py:66
  118.4 44.9 %collective-permute-start.10 = (bf16[48,7168]{1,0:T(8,128)(2,1)S(1)}, bf16[48,7168]{1,0:T(8,128)(2,1)S(1)}, u32[]{:S(2)}, u32[]{:S(2)}) collective-permute-start(bf16[48,7168]{1,0:T(8,128)(2,1)S(1)} %slice.177), channel_id=1, source_target_pairs={{0,1},{1,0},{2,3},{3,2},{4,5},{5,4},{6,7},{7,6},{8,9},{9,8},{10,11... | collective-permute-start | bytes 2064392 | tf_op jit(solution)/shard_map/ppermute | solution.py:66
  126.0 66.8 %collective-permute-start.3 = (bf16[24,7168]{1,0:T(8,128)(2,1)S(1)}, bf16[24,7168]{1,0:T(8,128)(2,1)S(1)}, u32[]{:S(2)}, u32[]{:S(2)}) collective-permute-start(bf16[24,7168]{1,0:T(8,128)(2,1)S(1)} %slice_bitcast_fusion.2), channel_id=1, source_target_pairs={{0,1},{3,2},{4,5},{7,6},{8,9},{11,10},{12,13},{15,14},{16,17},{19,... | collective-permute-start | bytes 1032200 | tf_op jit(solution)/shard_map/ppermute | solution.py:63
  163.3 24.6 %collective-permute-start.7 = (bf16[56,7168]{1,0:T(8,128)(2,1)S(1)}, bf16[56,7168]{1,0:T(8,128)(2,1)S(1)}, u32[]{:S(2)}, u32[]{:S(2)}) collective-permute-start(bf16[56,7168]{1,0:T(8,128)(2,1)S(1)} %get-tuple-element.53), channel_id=1, source_target_pairs={{0,1},{1,0},{2,3},{3,2},{4,5},{5,4},{6,7},{7,6},{8,9},{9,8},{10,11... | collective-permute-start | bytes 2408456 | tf_op jit(solution)/shard_map/ppermute | solution.py:66
  165.5 31.8 %collective-permute-start.11 = (bf16[48,7168]{1,0:T(8,128)(2,1)S(1)}, bf16[48,7168]{1,0:T(8,128)(2,1)S(1)}, u32[]{:S(2)}, u32[]{:S(2)}) collective-permute-start(bf16[48,7168]{1,0:T(8,128)(2,1)S(1)} %collective-permute-done.10), channel_id=1, source_target_pairs={{0,3},{3,0},{1,2},{2,1},{4,7},{7,4},{5,6},{6,5},{8,11},{11,8},{9,1... | collective-permute-start | bytes 2064392 | tf_op jit(solution)/shard_map/ppermute | solution.py:66
  168.3 32.9 %collective-permute-start.6 = (bf16[56,7168]{1,0:T(8,128)(2,1)S(1)}, bf16[56,7168]{1,0:T(8,128)(2,1)S(1)}, u32[]{:S(2)}, u32[]{:S(2)}) collective-permute-start(bf16[56,7168]{1,0:T(8,128)(2,1)S(1)} %collective-permute-done.5), channel_id=1, source_target_pairs={{0,3},{3,0},{1,2},{2,1},{4,7},{7,4},{5,6},{6,5},{8,11},{11,8},{9,1... | collective-permute-start | bytes 2408456 | tf_op jit(solution)/shard_map/ppermute | solution.py:66
  187.9 30.5 %collective-permute-start.9 = (bf16[56,7168]{1,0:T(8,128)(2,1)S(1)}, bf16[56,7168]{1,0:T(8,128)(2,1)S(1)}, u32[]{:S(2)}, u32[]{:S(2)}) collective-permute-start(bf16[56,7168]{1,0:T(8,128)(2,1)S(1)} %collective-permute-done.7), channel_id=1, source_target_pairs={{0,3},{3,0},{1,2},{2,1},{4,7},{7,4},{5,6},{6,5},{8,11},{11,8},{9,1... | collective-permute-start | bytes 2408456 | tf_op jit(solution)/shard_map/ppermute | solution.py:66
  192.0 1.5 copy-start.6
  193.5 40.9 %collective-permute-start = (bf16[128,7168]{1,0:T(8,128)(2,1)S(1)}, bf16[128,7168]{1,0:T(8,128)(2,1)S(1)}, u32[]{:S(2)}, u32[]{:S(2)}) collective-permute-start(bf16[128,7168]{1,0:T(8,128)(2,1)S(1)} %copy-done.6), channel_id=1, source_target_pairs={{3,7},{0,124},{7,11},{4,0},{11,15},{8,4},{15,19},{12,8},{19,23},{1... | collective-permute-start | bytes 5505032 | tf_op jit(solution)/shard_map/ppermute | solution.py:83
  196.6 25.3 %collective-permute-start.4 = (bf16[24,7168]{1,0:T(8,128)(2,1)S(1)}, bf16[24,7168]{1,0:T(8,128)(2,1)S(1)}, u32[]{:S(2)}, u32[]{:S(2)}) collective-permute-start(bf16[24,7168]{1,0:T(8,128)(2,1)S(1)} %collective-permute-done.3), channel_id=1, source_target_pairs={{2,6},{1,125},{6,10},{5,1},{10,14},{9,5},{14,18},{13,9},{18,22},{1... | collective-permute-start | bytes 1032200 | tf_op jit(solution)/shard_map/ppermute | solution.py:96
  197.3 37.1 %collective-permute-start.2 = (bf16[104,7168]{1,0:T(8,128)(2,1)S(1)}, bf16[104,7168]{1,0:T(8,128)(2,1)S(1)}, u32[]{:S(2)}, u32[]{:S(2)}) collective-permute-start(bf16[104,7168]{1,0:T(8,128)(2,1)S(1)} %collective-permute-done.1), channel_id=1, source_target_pairs={{2,6},{1,125},{6,10},{5,1},{10,14},{9,5},{14,18},{13,9},{18,22},{1... | collective-permute-start | bytes 4472840 | tf_op jit(solution)/shard_map/ppermute | solution.py:88
  221.8 13.0 %copy-start.5 = (bf16[1,256,7168]{2,1,0:T(8,128)(2,1)S(1)}, bf16[1,256,7168]{2,1,0:T(8,128)(2,1)}, u32[]{:S(2)}) copy-start(bf16[1,256,7168]{2,1,0:T(8,128)(2,1)} %param.12) | copy-start | bytes 11010052
  240.0 13.5 %collective-permute-start.27 = (bf16[80,3072]{1,0:T(8,128)(2,1)S(1)}, bf16[80,3072]{1,0:T(8,128)(2,1)S(1)}, u32[]{:S(2)}, u32[]{:S(2)}) collective-permute-start(bf16[80,3072]{1,0:T(8,128)(2,1)S(1)} %get-tuple-element.48), channel_id=1, source_target_pairs={{0,1},{1,0},{2,3},{3,2},{4,5},{5,4},{6,7},{7,6},{8,9},{9,8},{10,11... | collective-permute-start | bytes 1474568 | tf_op jit(solution)/shard_map/ppermute | solution.py:66
  242.4 57.7 %collective-permute-start.25 = (bf16[80,3072]{1,0:T(8,128)(2,1)S(1)}, bf16[80,3072]{1,0:T(8,128)(2,1)S(1)}, u32[]{:S(2)}, u32[]{:S(2)}) collective-permute-start(bf16[80,3072]{1,0:T(8,128)(2,1)S(1)} %get-tuple-element.47), channel_id=1, source_target_pairs={{0,3},{3,0},{1,2},{2,1},{4,7},{7,4},{5,6},{6,5},{8,11},{11,8},{9,1... | collective-permute-start | bytes 1474568 | tf_op jit(solution)/shard_map/ppermute | solution.py:66
  248.4 79.6 %collective-permute-start.24 = (bf16[80,3072]{1,0:T(8,128)(2,1)S(1)}, bf16[80,3072]{1,0:T(8,128)(2,1)}, u32[]{:S(2)}, u32[]{:S(2)}) collective-permute-start(bf16[80,3072]{1,0:T(8,128)(2,1)S(1)} %slice.197), channel_id=1, source_target_pairs={{0,3},{3,0},{1,2},{2,1},{4,7},{7,4},{5,6},{6,5},{8,11},{11,8},{9,1... | collective-permute-start | bytes 1474568 | tf_op jit(solution)/shard_map/ppermute | solution.py:66
  248.5 17.3 %collective-permute-start.21 = (bf16[80,4096]{1,0:T(8,128)(2,1)S(1)}, bf16[80,4096]{1,0:T(8,128)(2,1)S(1)}, u32[]{:S(2)}, u32[]{:S(2)}) collective-permute-start(bf16[80,4096]{1,0:T(8,128)(2,1)S(1)} %get-tuple-element.52), channel_id=1, source_target_pairs={{0,1},{1,0},{2,3},{3,2},{4,5},{5,4},{6,7},{7,6},{8,9},{9,8},{10,11... | collective-permute-start | bytes 1966088 | tf_op jit(solution)/shard_map/ppermute | solution.py:66
  248.6 52.6 %collective-permute-start.18 = (bf16[80,4096]{1,0:T(8,128)(2,1)S(1)}, bf16[80,4096]{1,0:T(8,128)(2,1)S(1)}, u32[]{:S(2)}, u32[]{:S(2)}) collective-permute-start(bf16[80,4096]{1,0:T(8,128)(2,1)S(1)} %slice.191), channel_id=1, source_target_pairs={{0,3},{3,0},{1,2},{2,1},{4,7},{7,4},{5,6},{6,5},{8,11},{11,8},{9,1... | collective-permute-start | bytes 1966088 | tf_op jit(solution)/shard_map/ppermute | solution.py:66
  253.5 44.0 %collective-permute-start.19 = (bf16[80,4096]{1,0:T(8,128)(2,1)S(1)}, bf16[80,4096]{1,0:T(8,128)(2,1)S(1)}, u32[]{:S(2)}, u32[]{:S(2)}) collective-permute-start(bf16[80,4096]{1,0:T(8,128)(2,1)S(1)} %get-tuple-element.51), channel_id=1, source_target_pairs={{0,3},{3,0},{1,2},{2,1},{4,7},{7,4},{5,6},{6,5},{8,11},{11,8},{9,1... | collective-permute-start | bytes 1966088 | tf_op jit(solution)/shard_map/ppermute | solution.py:66
  265.8 36.8 %collective-permute-start.23 = (bf16[80,4096]{1,0:T(8,128)(2,1)S(1)}, bf16[80,4096]{1,0:T(8,128)(2,1)S(1)}, u32[]{:S(2)}, u32[]{:S(2)}) collective-permute-start(bf16[80,4096]{1,0:T(8,128)(2,1)S(1)} %slice.195), channel_id=1, source_target_pairs={{0,1},{1,0},{2,3},{3,2},{4,5},{5,4},{6,7},{7,6},{8,9},{9,8},{10,11... | collective-permute-start | bytes 1966088 | tf_op jit(solution)/shard_map/ppermute | solution.py:66
  297.5 16.5 %collective-permute-start.22 = (bf16[80,4096]{1,0:T(8,128)(2,1)S(1)}, bf16[80,4096]{1,0:T(8,128)(2,1)S(1)}, u32[]{:S(2)}, u32[]{:S(2)}) collective-permute-start(bf16[80,4096]{1,0:T(8,128)(2,1)S(1)} %add_convert_fusion.1), channel_id=1, source_target_pairs={{0,3},{3,0},{1,2},{2,1},{4,7},{7,4},{5,6},{6,5},{8,11},{11,8},{9,1... | collective-permute-start | bytes 1966088 | tf_op jit(solution)/shard_map/ppermute | solution.py:66
  300.2 15.0 %collective-permute-start.20 = (bf16[80,4096]{1,0:T(8,128)(2,1)S(1)}, bf16[80,4096]{1,0:T(8,128)(2,1)S(1)}, u32[]{:S(2)}, u32[]{:S(2)}) collective-permute-start(bf16[80,4096]{1,0:T(8,128)(2,1)S(1)} %add_convert_fusion.3), channel_id=1, source_target_pairs={{0,1},{1,0},{2,3},{3,2},{4,5},{5,4},{6,7},{7,6},{8,9},{9,8},{10,11... | collective-permute-start | bytes 1966088 | tf_op jit(solution)/shard_map/ppermute | solution.py:66
  301.2 26.8 %collective-permute-start.29 = (bf16[80,3072]{1,0:T(8,128)(2,1)S(1)}, bf16[80,3072]{1,0:T(8,128)(2,1)}, u32[]{:S(2)}, u32[]{:S(2)}) collective-permute-start(bf16[80,3072]{1,0:T(8,128)(2,1)S(1)} %slice.201), channel_id=1, source_target_pairs={{0,1},{1,0},{2,3},{3,2},{4,5},{5,4},{6,7},{7,6},{8,9},{9,8},{10,11... | collective-permute-start | bytes 1474568 | tf_op jit(solution)/shard_map/ppermute | solution.py:66
  302.6 25.4 %collective-permute-start.28 = (bf16[80,3072]{1,0:T(8,128)(2,1)}, bf16[80,3072]{1,0:T(8,128)(2,1)}, u32[]{:S(2)}, u32[]{:S(2)}) collective-permute-start(bf16[80,3072]{1,0:T(8,128)(2,1)} %add_convert_fusion.5), channel_id=1, source_target_pairs={{0,3},{3,0},{1,2},{2,1},{4,7},{7,4},{5,6},{6,5},{8,11},{11,8},{9,1... | collective-permute-start | bytes 1474568 | tf_op jit(solution)/shard_map/ppermute | solution.py:66
  314.0 22.3 %collective-permute-start.26 = (bf16[80,3072]{1,0:T(8,128)(2,1)}, bf16[80,3072]{1,0:T(8,128)(2,1)}, u32[]{:S(2)}, u32[]{:S(2)}) collective-permute-start(bf16[80,3072]{1,0:T(8,128)(2,1)} %add_convert_fusion.7), channel_id=1, source_target_pairs={{0,1},{1,0},{2,3},{3,2},{4,5},{5,4},{6,7},{7,6},{8,9},{9,8},{10,11... | collective-permute-start | bytes 1474568 | tf_op jit(solution)/shard_map/ppermute | solution.py:66
  317.3 30.6 %all-to-all-start.1 = ((bf16[32,5,32,128]{3,2,1,0:T(8,128)(2,1)}), bf16[32,5,32,128]{3,2,1,0:T(8,128)(2,1)}, u32[]{:S(2)}, u32[]{:S(2)}) async-start(bf16[32,5,32,128]{3,2,1,0:T(8,128)(2,1)} %bitcast.20), calls=%async_computation.1 | async-start | bytes 2621440 | tf_op jit(solution)/shard_map/all_to_all | solution.py:140
  338.4 14.2 %copy-start.9 = (f32[128,1]{0,1:T(1,128)S(1)}, f32[128,1]{0,1:T(1,128)}, u32[]{:S(2)}) copy-start(f32[128,1]{0,1:T(1,128)} %param.9) | copy-start | bytes 1540
  347.9 21.1 %all-to-all-start.2 = ((bf16[32,5,24,128]{3,2,1,0:T(8,128)(2,1)}), bf16[32,5,24,128]{3,2,1,0:T(8,128)(2,1)S(1)}, u32[]{:S(2)}, u32[]{:S(2)}) async-start(bf16[32,5,24,128]{3,2,1,0:T(8,128)(2,1)} %bitcast.26), calls=%async_computation.2 | async-start | bytes 1966080 | tf_op jit(solution)/shard_map/all_to_all | solution.py:140
  352.6 17.7 %copy-start.1 = (bf16[128,7168]{1,0:T(8,128)(2,1)S(1)}, bf16[128,7168]{1,0:T(8,128)(2,1)}, u32[]{:S(2)}) copy-start(bf16[128,7168]{1,0:T(8,128)(2,1)} %param.7) | copy-start | bytes 5505028

commit v11 on v10

--- a/solution.py
+++ b/solution.py
@@ -81,26 +81,27 @@
     outer_gate = lax.ppermute(w_gate[:, :inner], EVERY, straight)
     outer_up = lax.ppermute(w_up[:, :inner], EVERY, straight)
     outer_down = lax.ppermute(w_down[:inner], EVERY, straight)
-    side_a = over(mid[:56], SIDE)
-    side_b = over(mid[56:112], SIDE)
-    side_c = over(mid[112:], SIDE)
+    side = []
+    for name, lo in zip("abcd", range(0, rows, rows // 4)):
+        side.append(over(mid[lo : lo + rows // 4], SIDE))
     inward_last = cross(w_down[first_down:])
     inner_down = lax.ppermute(inward_down, EVERY, turned)
     inner_gate = lax.ppermute(inward_gate, EVERY, turned)
-    far_a = over(side_a, MIRROR)
+    far = []
+    far.append(over(side[0], MIRROR))
     inner_up = lax.ppermute(inward_up, EVERY, turned)
     home_own, mirror_own = own_hidden(mid), own_hidden(mirror)
-    side_b, home_own, mirror_own = lax.optimization_barrier((side_b, home_own, mirror_own))
-    far_b = over(side_b, MIRROR)
-    far_c = over(side_c, MIRROR)
+    side[1], home_own, mirror_own = lax.optimization_barrier((side[1], home_own, mirror_own))
+    for name, piece in zip("bcd", side[1:]):
+        far.append(over(piece, MIRROR))
     inner_last = lax.ppermute(inward_last, EVERY, turned)
 
     outer = (place == 0) | (place == SPAN - 1)
     edge_gate = jnp.where(outer, outer_gate, inner_gate)
     edge_up = jnp.where(outer, outer_up, inner_up)
     edge_into = jnp.concatenate([edge_gate, edge_up], axis=1)
-    side = jnp.concatenate([side_a, side_b, side_c], axis=0)
-    far = jnp.concatenate(lax.optimization_barrier((far_a, far_b, far_c)), axis=0)
+    side = jnp.concatenate(side, axis=0)
+    far = jnp.concatenate(lax.optimization_barrier(tuple(far)), axis=0)
 
     def full_hidden(block, mine):
         both = dot(block, edge_into)
@@ -120,11 +121,18 @@
         return (u.astype(jnp.float32) + v.astype(jnp.float32)).astype(jnp.bfloat16)
 
     f32 = jnp.float32
-    half = rows // 2
-    upper, lower = slice(None, half), slice(half, None)
-    result = None
-    for lo, hi in ((0, 4096), (4096, width)):
-        cols = slice(lo, hi)
+
+    def placed(result, returned, lo):
+        expert_out = lax.dot_general(picker, returned, (((0,), (0,)), ((), ())), preferred_element_type=f32)
+        mixed = (expert_out * gate_prob.reshape(-1)[:, None]).astype(jnp.bfloat16)
+        if result is None:
+            return lax.optimization_barrier(jnp.pad(mixed, ((0, 0), (0, width - mixed.shape[1]))))
+        return lax.dynamic_update_slice(result, mixed, (0, lo))
+
+    result, returned = None, None
+    for name, lo, hi in (("one", 0, 3072), ("two", 3072, 5120), ("three", 5120, width)):
+        half = rows // 2 - (8 if name == "three" else 0)
+        upper, lower, cols = slice(None, half), slice(half, None), slice(lo, hi)
         far_a = over(far[upper, cols], MIRROR)
         far_b = over(far[lower, cols], SIDE)
         mirror_a = over(mirror[upper, cols], MIRROR)
@@ -136,15 +144,13 @@
         total_a = home[upper, cols].astype(f32) + mirror_a.astype(f32) + side_a.astype(f32)
         total_b = home[lower, cols].astype(f32) + mirror_b.astype(f32) + side_b.astype(f32)
         total = jnp.concatenate([total_a, total_b], axis=0).astype(jnp.bfloat16)
+        if returned is not None:
+            total, returned = lax.optimization_barrier((total, returned))
+            result = placed(result, returned, last)
+        last = lo
         total = total.reshape(experts, CAPACITY, (hi - lo) // LANES, LANES)
         returned = lax.all_to_all(total, PLANE, 0, 0, tiled=True).reshape(rows, hi - lo)
-        expert_out = lax.dot_general(picker, returned, (((0,), (0,)), ((), ())), preferred_element_type=f32)
-        mixed = (expert_out * gate_prob.reshape(-1)[:, None]).astype(jnp.bfloat16)
-        if result is None:
-            result = lax.optimization_barrier(jnp.pad(mixed, ((0, 0), (0, width - hi))))
-        else:
-            result = lax.dynamic_update_slice(result, mixed, (0, lo))
-    return result
+    return placed(result, returned, last)
 
 
 def solution(mesh):

time: 373 us -> 390 us (1.046)
  starting transfers between devices: 88.4 us -> 140 us
  waiting for transfers between devices: 224 us -> 178 us
  local copies, waits for them, and re-layouts: 21.8 us -> 28.5 us
    ppermute x19 -> x27, waiting for transfers between devices: 142 us -> 98.2 us  [over(): return lax.ppermute(block, 'x', pairs)]
    ppermute x19 -> x27, starting transfers between devices: 37.4 us -> 74.2 us  [over(): return lax.ppermute(block, 'x', pairs)]
    all_to_all x2 -> x3, starting transfers between devices: 15.5 us -> 26.3 us  [body(): lax.all_to_all(total, PLANE, 0, 0, tiled=True).reshape(rows, hi - lo)]
    ppermute x4, starting transfers between devices: 12.6 us -> 17 us  [cross(): return lax.ppermute(block, 'x', INWARD)]
    unnamed x28 -> x43, local copies, waits for them, and re-layouts: 5.69 us -> 9.22 us
    all_to_all x2 -> x3, waiting for transfers between devices: 21.2 us -> 21.8 us  [body(): lax.all_to_all(total, PLANE, 0, 0, tiled=True).reshape(rows, hi - lo)]
  transfers between devices with their start and end apart: 33 -> 42, of which waited for: 16 -> 19; matrix products, arithmetic and copies ran while one was open for 12% -> 14% of each run, Pallas kernels for 0% -> 0%
where the time goes in v11:
time: 390 us; the launch traced here: 386 us
  waiting for transfers between devices  178 us (46%)
  starting transfers between devices  140 us (36%)
  local copies, waits for them, and re-layouts  28.5 us (7%)
  matrix products  19.1 us (5%)
  other arithmetic  19 us (5%)
    ppermute x27, waiting for transfers between devices, over(): return lax.ppermute(block, 'x', pairs)  98.2 us
    ppermute x27, starting transfers between devices, over(): return lax.ppermute(block, 'x', pairs)  74.2 us
    ppermute x4, waiting for transfers between devices, cross(): return lax.ppermute(block, 'x', INWARD)  46.8 us
    all_to_all x3, starting transfers between devices, body(): lax.all_to_all(total, PLANE, 0, 0, tiled=True).reshape(rows, hi - lo)  26.3 us
    all_to_all x3, waiting for transfers between devices, body(): lax.all_to_all(total, PLANE, 0, 0, tiled=True).reshape(rows, hi - lo)  21.8 us
    ppermute x4, starting transfers between devices, cross(): return lax.ppermute(block, 'x', INWARD)  17 us
    dot_general x17, matrix products, dot(): return jnp.dot(a, b, preferred_element_type=jnp.float32)  16.4 us
    ppermute x1, waiting for transfers between devices, body(): outer_down = lax.ppermute(w_down[:inner], EVERY, straight)  11.5 us
  transfers between devices with their start and end apart: 42, of which 19 were waited for; matrix products, arithmetic and copies ran while one was open for 14% of the time, Pallas kernels for 0%

profile of v11, /device:TPU:7, one launch (start us, length us, event | category | flops | bytes accessed | tf_op | source)
XLA Modules:
  0.0 386.1 jit_solution(17696656735532958736)
XLA Ops:
  3.3 1.9 copy.8
  5.2 8.8 %all-to-all-start = ((bf16[32,5,56,128]{3,2,1,0:T(8,128)(2,1)}), bf16[32,5,56,128]{3,2,1,0:T(8,128)(2,1)S(1)}, u32[]{:S(2)}, u32[]{:S(2)}) async-start(bf16[32,5,56,128]{3,2,1,0:T(8,128)(2,1)} %bitcast.113), calls=%async_computation | async-start | bytes 4587520 | tf_op jit(solution)/shard_map/all_to_all | solution.py:71
  14.0 4.3 %fusion.54 = (bf16[7168,128]{1,0:T(8,128)(2,1)}, bf16[7168,128]{1,0:T(8,128)(2,1)}) fusion(bf16[7168,256]{1,0:T(8,128)(2,1)} %bitcast.116), kind=kLoop, calls=%fused_computation.117 | loop fusion | bytes 7340032 | tf_op jit(solution)/shard_map/slice | solution.py:70
  18.3 3.7 collective-permute-start.18
  22.0 3.2 collective-permute-start.17
  25.3 2.1 fusion.53
  27.4 2.6 collective-permute-start.15
  29.9 3.6 collective-permute-start.14
  33.7 2.6 slice_bitcast_fusion.1
  36.3 2.9 slice_bitcast_fusion
  43.1 17.0 %collective-permute-done.18 = bf16[7168,128]{1,0:T(8,128)(2,1)} collective-permute-done((bf16[7168,128]{1,0:T(8,128)(2,1)}, bf16[7168,128]{1,0:T(8,128)(2,1)}, u32[]{:S(2)}, u32[]{:S(2)}) %collective-permute-start.18) | collective-permute-done | bytes 1835040 | tf_op jit(solution)/shard_map/ppermute | solution.py:63
  60.1 1.9 collective-permute-start.19
  62.5 3.5 collective-permute-start.5
  69.6 29.8 %collective-permute-done.15 = bf16[7168,128]{1,0:T(8,128)(2,1)} collective-permute-done((bf16[7168,128]{1,0:T(8,128)(2,1)}, bf16[7168,128]{1,0:T(8,128)(2,1)}, u32[]{:S(2)}, u32[]{:S(2)}) %collective-permute-start.15) | collective-permute-done | bytes 1835040 | tf_op jit(solution)/shard_map/ppermute | solution.py:63
  99.5 4.2 %collective-permute-start.1 = (bf16[104,7168]{1,0:T(8,128)(2,1)S(1)}, bf16[104,7168]{1,0:T(8,128)(2,1)S(1)}, u32[]{:S(2)}, u32[]{:S(2)}) collective-permute-start(bf16[104,7168]{1,0:T(8,128)(2,1)S(1)} %copy-done.8), channel_id=1, source_target_pairs={{0,1},{3,2},{4,5},{7,6},{8,9},{11,10},{12,13},{15,14},{16,17},{19,... | collective-permute-start | bytes 4472840 | tf_op jit(solution)/shard_map/ppermute | solution.py:63
  103.7 8.0 %collective-permute-done.5 = bf16[40,7168]{1,0:T(8,128)(2,1)S(1)} collective-permute-done((bf16[40,7168]{1,0:T(8,128)(2,1)S(1)}, bf16[40,7168]{1,0:T(8,128)(2,1)S(1)}, u32[]{:S(2)}, u32[]{:S(2)}) %collective-permute-start.5) | collective-permute-done | bytes 573472 | tf_op jit(solution)/shard_map/ppermute | solution.py:66
  112.5 6.4 %collective-permute-start.3 = (bf16[24,7168]{1,0:T(8,128)(2,1)S(1)}, bf16[24,7168]{1,0:T(8,128)(2,1)S(1)}, u32[]{:S(2)}, u32[]{:S(2)}) collective-permute-start(bf16[24,7168]{1,0:T(8,128)(2,1)S(1)} %slice_bitcast_fusion.2), channel_id=1, source_target_pairs={{0,1},{3,2},{4,5},{7,6},{8,9},{11,10},{12,13},{15,14},{16,17},{19,... | collective-permute-start | bytes 1032200 | tf_op jit(solution)/shard_map/ppermute | solution.py:63
  118.9 2.9 collective-permute-start.8
  121.9 1.7 broadcast_select_fusion
  123.7 30.8 %collective-permute-start.10 = (bf16[40,7168]{1,0:T(8,128)(2,1)S(1)}, bf16[40,7168]{1,0:T(8,128)(2,1)S(1)}, u32[]{:S(2)}, u32[]{:S(2)}) collective-permute-start(bf16[40,7168]{1,0:T(8,128)(2,1)S(1)} %bitcast.133), channel_id=1, source_target_pairs={{0,1},{1,0},{2,3},{3,2},{4,5},{5,4},{6,7},{7,6},{8,9},{9,8},{10,11... | collective-permute-start | bytes 1720328 | tf_op jit(solution)/shard_map/ppermute | solution.py:66
  154.5 1.7 broadcast_select_fusion.1
  156.2 13.1 %collective-permute-done.8 = bf16[160,7168]{1,0:T(8,128)(2,1)S(1)} collective-permute-done((bf16[160,7168]{1,0:T(8,128)(2,1)S(1)}, bf16[160,7168]{1,0:T(8,128)(2,1)S(1)}, u32[]{:S(2)}, u32[]{:S(2)}) %collective-permute-start.8) | collective-permute-done | bytes 2293792 | tf_op jit(solution)/shard_map/ppermute | solution.py:66
  170.9 3.1 collective-permute-start.6
  176.4 11.4 %collective-permute-done.12 = bf16[40,7168]{1,0:T(8,128)(2,1)S(1)} collective-permute-done((bf16[40,7168]{1,0:T(8,128)(2,1)S(1)}, bf16[40,7168]{1,0:T(8,128)(2,1)S(1)}, u32[]{:S(2)}, u32[]{:S(2)}) %collective-permute-start.12) | collective-permute-done | bytes 573472 | tf_op jit(solution)/shard_map/ppermute | solution.py:66
  191.2 1.9 collective-permute-start.9
  195.2 3.1 collective-permute-start
  199.0 9.7 %collective-permute-done.13 = bf16[40,7168]{1,0:T(8,128)(2,1)S(1)} collective-permute-done((bf16[40,7168]{1,0:T(8,128)(2,1)S(1)}, bf16[40,7168]{1,0:T(8,128)(2,1)S(1)}, u32[]{:S(2)}, u32[]{:S(2)}) %collective-permute-start.13) | collective-permute-done | bytes 573472 | tf_op jit(solution)/shard_map/ppermute | solution.py:66
  209.5 11.5 %collective-permute-done.9 = bf16[40,7168]{1,0:T(8,128)(2,1)S(1)} collective-permute-done((bf16[40,7168]{1,0:T(8,128)(2,1)S(1)}, bf16[40,7168]{1,0:T(8,128)(2,1)S(1)}, u32[]{:S(2)}, u32[]{:S(2)}) %collective-permute-start.9) | collective-permute-done | bytes 573472 | tf_op jit(solution)/shard_map/ppermute | solution.py:66
  224.3 11.5 %collective-permute-done = bf16[128,7168]{1,0:T(8,128)(2,1)S(1)} collective-permute-done((bf16[128,7168]{1,0:T(8,128)(2,1)S(1)}, bf16[128,7168]{1,0:T(8,128)(2,1)S(1)}, u32[]{:S(2)}, u32[]{:S(2)}) %collective-permute-start) | collective-permute-done | bytes 1835040 | tf_op jit(solution)/shard_map/ppermute | solution.py:83
  236.3 1.6 convolution_convert_fusion.3
  238.0 1.6 convolution_convert_fusion
  239.6 4.9 %collective-permute-start.33 = (bf16[72,2048]{1,0:T(8,128)(2,1)S(1)}, bf16[72,2048]{1,0:T(8,128)(2,1)S(1)}, u32[]{:S(2)}, u32[]{:S(2)}) collective-permute-start(bf16[72,2048]{1,0:T(8,128)(2,1)S(1)} %slice.222), channel_id=1, source_target_pairs={{0,3},{3,0},{1,2},{2,1},{4,7},{7,4},{5,6},{6,5},{8,11},{11,8},{9,1... | collective-permute-start | bytes 884744 | tf_op jit(solution)/shard_map/ppermute | solution.py:66
  250.6 12.4 %collective-permute-start.35 = (bf16[88,2048]{1,0:T(8,128)(2,1)S(1)}, bf16[88,2048]{1,0:T(8,128)(2,1)S(1)}, u32[]{:S(2)}, u32[]{:S(2)}) collective-permute-start(bf16[88,2048]{1,0:T(8,128)(2,1)S(1)} %slice.225), channel_id=1, source_target_pairs={{0,1},{1,0},{2,3},{3,2},{4,5},{5,4},{6,7},{7,6},{8,9},{9,8},{10,11... | collective-permute-start | bytes 1081352 | tf_op jit(solution)/shard_map/ppermute | solution.py:66
  263.7 2.1 collective-permute-start.26
  268.8 19.6 %collective-permute-done.23 = bf16[80,2048]{1,0:T(8,128)(2,1)S(1)} collective-permute-done((bf16[80,2048]{1,0:T(8,128)(2,1)S(1)}, bf16[80,2048]{1,0:T(8,128)(2,1)S(1)}, u32[]{:S(2)}, u32[]{:S(2)}) %collective-permute-start.23) | collective-permute-done | bytes 327712 | tf_op jit(solution)/shard_map/ppermute | solution.py:66
  288.4 1.7 collective-permute-start.31
  293.9 7.2 %collective-permute-done.21 = bf16[80,2048]{1,0:T(8,128)(2,1)S(1)} collective-permute-done((bf16[80,2048]{1,0:T(8,128)(2,1)S(1)}, bf16[80,2048]{1,0:T(8,128)(2,1)S(1)}, u32[]{:S(2)}, u32[]{:S(2)}) %collective-permute-start.21) | collective-permute-done | bytes 327712 | tf_op jit(solution)/shard_map/ppermute | solution.py:66
  306.3 5.3 %collective-permute-done.30 = bf16[80,3072]{1,0:T(8,128)(2,1)S(1)} collective-permute-done((bf16[80,3072]{1,0:T(8,128)(2,1)S(1)}, bf16[80,3072]{1,0:T(8,128)(2,1)S(1)}, u32[]{:S(2)}, u32[]{:S(2)}) %collective-permute-start.30) | collective-permute-done | bytes 491552 | tf_op jit(solution)/shard_map/ppermute | solution.py:66
  314.8 12.1 %all-to-all-start.1 = ((bf16[32,5,24,128]{3,2,1,0:T(8,128)(2,1)}), bf16[32,5,24,128]{3,2,1,0:T(8,128)(2,1)S(1)}, u32[]{:S(2)}, u32[]{:S(2)}) async-start(bf16[32,5,24,128]{3,2,1,0:T(8,128)(2,1)} %bitcast.32), calls=%async_computation.1 | async-start | bytes 1966080 | tf_op jit(solution)/shard_map/all_to_all | solution.py:152
  327.0 6.2 %collective-permute-done.34 = bf16[72,2048]{1,0:T(8,128)(2,1)} collective-permute-done((bf16[72,2048]{1,0:T(8,128)(2,1)}, bf16[72,2048]{1,0:T(8,128)(2,1)}, u32[]{:S(2)}, u32[]{:S(2)}) %collective-permute-start.34) | collective-permute-done | bytes 294944 | tf_op jit(solution)/shard_map/ppermute | solution.py:66
  333.5 1.9 add_convert_fusion.10
  335.6 1.9 collective-permute-done.24
  337.5 2.4 collective-permute-done.22
  341.4 1.8 all-to-all-done.1
  344.4 8.9 %all-to-all-start.2 = ((bf16[32,5,16,128]{3,2,1,0:T(8,128)(2,1)}), bf16[32,5,16,128]{3,2,1,0:T(8,128)(2,1)S(1)}, u32[]{:S(2)}, u32[]{:S(2)}) async-start(bf16[32,5,16,128]{3,2,1,0:T(8,128)(2,1)} %bitcast.38), calls=%async_computation.2 | async-start | bytes 1310720 | tf_op jit(solution)/shard_map/all_to_all | solution.py:152
  354.8 10.7 %all-to-all-done.2 = bf16[32,5,16,128]{3,2,1,0:T(8,128)(2,1)S(1)} async-done(((bf16[32,5,16,128]{3,2,1,0:T(8,128)(2,1)}), bf16[32,5,16,128]{3,2,1,0:T(8,128)(2,1)S(1)}, u32[]{:S(2)}, u32[]{:S(2)}) %all-to-all-start.2) | async-done | bytes 655392 | tf_op jit(solution)/shard_map/all_to_all | solution.py:152
  367.4 5.3 %all-to-all-start.3 = ((bf16[32,5,16,128]{3,2,1,0:T(8,128)(2,1)}), bf16[32,5,16,128]{3,2,1,0:T(8,128)(2,1)S(1)}, u32[]{:S(2)}, u32[]{:S(2)}) async-start(bf16[32,5,16,128]{3,2,1,0:T(8,128)(2,1)} %bitcast.44), calls=%async_computation.3 | async-start | bytes 1310720 | tf_op jit(solution)/shard_map/all_to_all | solution.py:152
  375.7 9.2 %all-to-all-done.3 = bf16[32,5,16,128]{3,2,1,0:T(8,128)(2,1)S(1)} async-done(((bf16[32,5,16,128]{3,2,1,0:T(8,128)(2,1)}), bf16[32,5,16,128]{3,2,1,0:T(8,128)(2,1)S(1)}, u32[]{:S(2)}, u32[]{:S(2)}) %all-to-all-start.3) | async-done | bytes 655392 | tf_op jit(solution)/shard_map/all_to_all | solution.py:152
  (151 shorter events, 59.3 us)
Async XLA Ops:
  5.2 56.9 %all-to-all-start = ((bf16[32,5,56,128]{3,2,1,0:T(8,128)(2,1)}), bf16[32,5,56,128]{3,2,1,0:T(8,128)(2,1)S(1)}, u32[]{:S(2)}, u32[]{:S(2)}) async-start(bf16[32,5,56,128]{3,2,1,0:T(8,128)(2,1)} %bitcast.113), calls=%async_computation | async-start | bytes 4587520 | tf_op jit(solution)/shard_map/all_to_all | solution.py:71
  13.9 11.3 %copy-start.2 = (bf16[1,7168,256]{2,1,0:T(8,128)(2,1)S(1)}, bf16[1,7168,256]{2,1,0:T(8,128)(2,1)}, u32[]{:S(2)}) copy-start(bf16[1,7168,256]{2,1,0:T(8,128)(2,1)} %param.10) | copy-start | bytes 11010052
  18.3 41.9 %collective-permute-start.18 = (bf16[7168,128]{1,0:T(8,128)(2,1)}, bf16[7168,128]{1,0:T(8,128)(2,1)}, u32[]{:S(2)}, u32[]{:S(2)}) collective-permute-start(bf16[7168,128]{1,0:T(8,128)(2,1)} %get-tuple-element.53), channel_id=1, source_target_pairs={{0,1},{3,2},{4,5},{7,6},{8,9},{11,10},{12,13},{15,14},{16,17},{19,... | collective-permute-start | bytes 5505032 | tf_op jit(solution)/shard_map/ppermute | solution.py:63
  22.0 90.5 %collective-permute-start.17 = (bf16[7168,128]{1,0:T(8,128)(2,1)}, bf16[7168,128]{1,0:T(8,128)(2,1)}, u32[]{:S(2)}, u32[]{:S(2)}) collective-permute-start(bf16[7168,128]{1,0:T(8,128)(2,1)} %get-tuple-element.54), channel_id=1, source_target_pairs={{3,7},{0,124},{7,11},{4,0},{11,15},{8,4},{15,19},{12,8},{19,23},{1... | collective-permute-start | bytes 5505032 | tf_op jit(solution)/shard_map/ppermute | solution.py:82
  27.4 72.1 %collective-permute-start.15 = (bf16[7168,128]{1,0:T(8,128)(2,1)}, bf16[7168,128]{1,0:T(8,128)(2,1)}, u32[]{:S(2)}, u32[]{:S(2)}) collective-permute-start(bf16[7168,128]{1,0:T(8,128)(2,1)} %get-tuple-element.51), channel_id=1, source_target_pairs={{0,1},{3,2},{4,5},{7,6},{8,9},{11,10},{12,13},{15,14},{16,17},{19,... | collective-permute-start | bytes 5505032 | tf_op jit(solution)/shard_map/ppermute | solution.py:63
  29.9 93.6 %collective-permute-start.14 = (bf16[7168,128]{1,0:T(8,128)(2,1)}, bf16[7168,128]{1,0:T(8,128)(2,1)}, u32[]{:S(2)}, u32[]{:S(2)}) collective-permute-start(bf16[7168,128]{1,0:T(8,128)(2,1)} %get-tuple-element.52), channel_id=1, source_target_pairs={{3,7},{0,124},{7,11},{4,0},{11,15},{8,4},{15,19},{12,8},{19,23},{1... | collective-permute-start | bytes 5505032 | tf_op jit(solution)/shard_map/ppermute | solution.py:81
  60.1 58.8 %collective-permute-start.19 = (bf16[7168,128]{1,0:T(8,128)(2,1)}, bf16[7168,128]{1,0:T(8,128)(2,1)}, u32[]{:S(2)}, u32[]{:S(2)}) collective-permute-start(bf16[7168,128]{1,0:T(8,128)(2,1)} %collective-permute-done.18), channel_id=1, source_target_pairs={{2,6},{1,125},{6,10},{5,1},{10,14},{9,5},{14,18},{13,9},{18,22},{1... | collective-permute-start | bytes 5505032 | tf_op jit(solution)/shard_map/ppermute | solution.py:92
  62.5 49.1 %collective-permute-start.5 = (bf16[40,7168]{1,0:T(8,128)(2,1)S(1)}, bf16[40,7168]{1,0:T(8,128)(2,1)S(1)}, u32[]{:S(2)}, u32[]{:S(2)}) collective-permute-start(bf16[40,7168]{1,0:T(8,128)(2,1)S(1)} %bitcast.135), channel_id=1, source_target_pairs={{0,1},{1,0},{2,3},{3,2},{4,5},{5,4},{6,7},{7,6},{8,9},{9,8},{10,11... | collective-permute-start | bytes 1720328 | tf_op jit(solution)/shard_map/ppermute | solution.py:66
  68.8 30.6 %copy-start.8 = (bf16[104,7168]{1,0:T(8,128)(2,1)S(1)}, bf16[104,7168]{1,0:T(8,128)(2,1)}, u32[]{:S(2)}) copy-start(bf16[104,7168]{1,0:T(8,128)(2,1)} %slice_bitcast_fusion.1) | copy-start | bytes 4472836
  99.5 95.0 %collective-permute-start.1 = (bf16[104,7168]{1,0:T(8,128)(2,1)S(1)}, bf16[104,7168]{1,0:T(8,128)(2,1)S(1)}, u32[]{:S(2)}, u32[]{:S(2)}) collective-permute-start(bf16[104,7168]{1,0:T(8,128)(2,1)S(1)} %copy-done.8), channel_id=1, source_target_pairs={{0,1},{3,2},{4,5},{7,6},{8,9},{11,10},{12,13},{15,14},{16,17},{19,... | collective-permute-start | bytes 4472840 | tf_op jit(solution)/shard_map/ppermute | solution.py:63
  111.6 12.0 %collective-permute-start.16 = (bf16[7168,128]{1,0:T(8,128)(2,1)}, bf16[7168,128]{1,0:T(8,128)(2,1)S(1)}, u32[]{:S(2)}, u32[]{:S(2)}) collective-permute-start(bf16[7168,128]{1,0:T(8,128)(2,1)} %collective-permute-done.15), channel_id=1, source_target_pairs={{2,6},{1,125},{6,10},{5,1},{10,14},{9,5},{14,18},{13,9},{18,22},{1... | collective-permute-start | bytes 5505032 | tf_op jit(solution)/shard_map/ppermute | solution.py:89
  112.5 78.7 %collective-permute-start.3 = (bf16[24,7168]{1,0:T(8,128)(2,1)S(1)}, bf16[24,7168]{1,0:T(8,128)(2,1)S(1)}, u32[]{:S(2)}, u32[]{:S(2)}) collective-permute-start(bf16[24,7168]{1,0:T(8,128)(2,1)S(1)} %slice_bitcast_fusion.2), channel_id=1, source_target_pairs={{0,1},{3,2},{4,5},{7,6},{8,9},{11,10},{12,13},{15,14},{16,17},{19,... | collective-permute-start | bytes 1032200 | tf_op jit(solution)/shard_map/ppermute | solution.py:63
  118.9 50.4 %collective-permute-start.8 = (bf16[160,7168]{1,0:T(8,128)(2,1)S(1)}, bf16[160,7168]{1,0:T(8,128)(2,1)S(1)}, u32[]{:S(2)}, u32[]{:S(2)}) collective-permute-start(bf16[160,7168]{1,0:T(8,128)(2,1)S(1)} %bitcast.128), channel_id=1, source_target_pairs={{0,3},{3,0},{1,2},{2,1},{4,7},{7,4},{5,6},{6,5},{8,11},{11,8},{9,1... | collective-permute-start | bytes 6881288 | tf_op jit(solution)/shard_map/ppermute | solution.py:66
  123.6 47.3 %collective-permute-start.7 = (bf16[40,7168]{1,0:T(8,128)(2,1)S(1)}, bf16[40,7168]{1,0:T(8,128)(2,1)S(1)}, u32[]{:S(2)}, u32[]{:S(2)}) collective-permute-start(bf16[40,7168]{1,0:T(8,128)(2,1)S(1)} %bitcast.134), channel_id=1, source_target_pairs={{0,1},{1,0},{2,3},{3,2},{4,5},{5,4},{6,7},{7,6},{8,9},{9,8},{10,11... | collective-permute-start | bytes 1720328 | tf_op jit(solution)/shard_map/ppermute | solution.py:66
  123.7 51.9 %collective-permute-start.10 = (bf16[40,7168]{1,0:T(8,128)(2,1)S(1)}, bf16[40,7168]{1,0:T(8,128)(2,1)S(1)}, u32[]{:S(2)}, u32[]{:S(2)}) collective-permute-start(bf16[40,7168]{1,0:T(8,128)(2,1)S(1)} %bitcast.133), channel_id=1, source_target_pairs={{0,1},{1,0},{2,3},{3,2},{4,5},{5,4},{6,7},{7,6},{8,9},{9,8},{10,11... | collective-permute-start | bytes 1720328 | tf_op jit(solution)/shard_map/ppermute | solution.py:66
  169.3 18.5 %collective-permute-start.12 = (bf16[40,7168]{1,0:T(8,128)(2,1)S(1)}, bf16[40,7168]{1,0:T(8,128)(2,1)S(1)}, u32[]{:S(2)}, u32[]{:S(2)}) collective-permute-start(bf16[40,7168]{1,0:T(8,128)(2,1)S(1)} %bitcast.132), channel_id=1, source_target_pairs={{0,1},{1,0},{2,3},{3,2},{4,5},{5,4},{6,7},{7,6},{8,9},{9,8},{10,11... | collective-permute-start | bytes 1720328 | tf_op jit(solution)/shard_map/ppermute | solution.py:66
  170.9 38.6 %collective-permute-start.6 = (bf16[40,7168]{1,0:T(8,128)(2,1)S(1)}, bf16[40,7168]{1,0:T(8,128)(2,1)S(1)}, u32[]{:S(2)}, u32[]{:S(2)}) collective-permute-start(bf16[40,7168]{1,0:T(8,128)(2,1)S(1)} %collective-permute-done.5), channel_id=1, source_target_pairs={{0,3},{3,0},{1,2},{2,1},{4,7},{7,4},{5,6},{6,5},{8,11},{11,8},{9,1... | collective-permute-start | bytes 1720328 | tf_op jit(solution)/shard_map/ppermute | solution.py:66
  175.5 22.7 %collective-permute-start.11 = (bf16[40,7168]{1,0:T(8,128)(2,1)S(1)}, bf16[40,7168]{1,0:T(8,128)(2,1)S(1)}, u32[]{:S(2)}, u32[]{:S(2)}) collective-permute-start(bf16[40,7168]{1,0:T(8,128)(2,1)S(1)} %collective-permute-done.10), channel_id=1, source_target_pairs={{0,3},{3,0},{1,2},{2,1},{4,7},{7,4},{5,6},{6,5},{8,11},{11,8},{9,1... | collective-permute-start | bytes 1720328 | tf_op jit(solution)/shard_map/ppermute | solution.py:66
  187.8 20.9 %collective-permute-start.13 = (bf16[40,7168]{1,0:T(8,128)(2,1)S(1)}, bf16[40,7168]{1,0:T(8,128)(2,1)S(1)}, u32[]{:S(2)}, u32[]{:S(2)}) collective-permute-start(bf16[40,7168]{1,0:T(8,128)(2,1)S(1)} %collective-permute-done.12), channel_id=1, source_target_pairs={{0,3},{3,0},{1,2},{2,1},{4,7},{7,4},{5,6},{6,5},{8,11},{11,8},{9,1... | collective-permute-start | bytes 1720328 | tf_op jit(solution)/shard_map/ppermute | solution.py:66
  191.2 29.8 %collective-permute-start.9 = (bf16[40,7168]{1,0:T(8,128)(2,1)S(1)}, bf16[40,7168]{1,0:T(8,128)(2,1)S(1)}, u32[]{:S(2)}, u32[]{:S(2)}) collective-permute-start(bf16[40,7168]{1,0:T(8,128)(2,1)S(1)} %collective-permute-done.7), channel_id=1, source_target_pairs={{0,3},{3,0},{1,2},{2,1},{4,7},{7,4},{5,6},{6,5},{8,11},{11,8},{9,1... | collective-permute-start | bytes 1720328 | tf_op jit(solution)/shard_map/ppermute | solution.py:66
  195.2 40.6 %collective-permute-start = (bf16[128,7168]{1,0:T(8,128)(2,1)S(1)}, bf16[128,7168]{1,0:T(8,128)(2,1)S(1)}, u32[]{:S(2)}, u32[]{:S(2)}) collective-permute-start(bf16[128,7168]{1,0:T(8,128)(2,1)S(1)} %copy-done.7), channel_id=1, source_target_pairs={{3,7},{0,124},{7,11},{4,0},{11,15},{8,4},{15,19},{12,8},{19,23},{1... | collective-permute-start | bytes 5505032 | tf_op jit(solution)/shard_map/ppermute | solution.py:83
  198.3 26.0 %collective-permute-start.4 = (bf16[24,7168]{1,0:T(8,128)(2,1)S(1)}, bf16[24,7168]{1,0:T(8,128)(2,1)S(1)}, u32[]{:S(2)}, u32[]{:S(2)}) collective-permute-start(bf16[24,7168]{1,0:T(8,128)(2,1)S(1)} %collective-permute-done.3), channel_id=1, source_target_pairs={{2,6},{1,125},{6,10},{5,1},{10,14},{9,5},{14,18},{13,9},{18,22},{1... | collective-permute-start | bytes 1032200 | tf_op jit(solution)/shard_map/ppermute | solution.py:97
  208.7 27.1 %collective-permute-start.2 = (bf16[104,7168]{1,0:T(8,128)(2,1)S(1)}, bf16[104,7168]{1,0:T(8,128)(2,1)S(1)}, u32[]{:S(2)}, u32[]{:S(2)}) collective-permute-start(bf16[104,7168]{1,0:T(8,128)(2,1)S(1)} %collective-permute-done.1), channel_id=1, source_target_pairs={{2,6},{1,125},{6,10},{5,1},{10,14},{9,5},{14,18},{13,9},{18,22},{1... | collective-permute-start | bytes 4472840 | tf_op jit(solution)/shard_map/ppermute | solution.py:88
  224.3 12.0 %copy-start.5 = (bf16[1,256,7168]{2,1,0:T(8,128)(2,1)S(1)}, bf16[1,256,7168]{2,1,0:T(8,128)(2,1)}, u32[]{:S(2)}) copy-start(bf16[1,256,7168]{2,1,0:T(8,128)(2,1)} %param.12) | copy-start | bytes 11010052
  239.6 27.7 %collective-permute-start.33 = (bf16[72,2048]{1,0:T(8,128)(2,1)S(1)}, bf16[72,2048]{1,0:T(8,128)(2,1)S(1)}, u32[]{:S(2)}, u32[]{:S(2)}) collective-permute-start(bf16[72,2048]{1,0:T(8,128)(2,1)S(1)} %slice.222), channel_id=1, source_target_pairs={{0,3},{3,0},{1,2},{2,1},{4,7},{7,4},{5,6},{6,5},{8,11},{11,8},{9,1... | collective-permute-start | bytes 884744 | tf_op jit(solution)/shard_map/ppermute | solution.py:66
  250.6 51.3 %collective-permute-start.35 = (bf16[88,2048]{1,0:T(8,128)(2,1)S(1)}, bf16[88,2048]{1,0:T(8,128)(2,1)S(1)}, u32[]{:S(2)}, u32[]{:S(2)}) collective-permute-start(bf16[88,2048]{1,0:T(8,128)(2,1)S(1)} %slice.225), channel_id=1, source_target_pairs={{0,1},{1,0},{2,3},{3,2},{4,5},{5,4},{6,7},{7,6},{8,9},{9,8},{10,11... | collective-permute-start | bytes 1081352 | tf_op jit(solution)/shard_map/ppermute | solution.py:66
  263.1 27.8 %collective-permute-start.29 = (bf16[80,3072]{1,0:T(8,128)(2,1)S(1)}, bf16[80,3072]{1,0:T(8,128)(2,1)S(1)}, u32[]{:S(2)}, u32[]{:S(2)}) collective-permute-start(bf16[80,3072]{1,0:T(8,128)(2,1)S(1)} %get-tuple-element.58), channel_id=1, source_target_pairs={{0,1},{1,0},{2,3},{3,2},{4,5},{5,4},{6,7},{7,6},{8,9},{9,8},{10,11... | collective-permute-start | bytes 1474568 | tf_op jit(solution)/shard_map/ppermute | solution.py:66
  263.1 29.5 %collective-permute-start.27 = (bf16[80,3072]{1,0:T(8,128)(2,1)S(1)}, bf16[80,3072]{1,0:T(8,128)(2,1)S(1)}, u32[]{:S(2)}, u32[]{:S(2)}) collective-permute-start(bf16[80,3072]{1,0:T(8,128)(2,1)S(1)} %get-tuple-element.57), channel_id=1, source_target_pairs={{0,3},{3,0},{1,2},{2,1},{4,7},{7,4},{5,6},{6,5},{8,11},{11,8},{9,1... | collective-permute-start | bytes 1474568 | tf_op jit(solution)/shard_map/ppermute | solution.py:66
  263.7 40.1 %collective-permute-start.26 = (bf16[80,3072]{1,0:T(8,128)(2,1)S(1)}, bf16[80,3072]{1,0:T(8,128)(2,1)S(1)}, u32[]{:S(2)}, u32[]{:S(2)}) collective-permute-start(bf16[80,3072]{1,0:T(8,128)(2,1)S(1)} %slice.250), channel_id=1, source_target_pairs={{0,3},{3,0},{1,2},{2,1},{4,7},{7,4},{5,6},{6,5},{8,11},{11,8},{9,1... | collective-permute-start | bytes 1474568 | tf_op jit(solution)/shard_map/ppermute | solution.py:66
  267.4 72.5 %copy-start.6 = (bf16[160,7168]{1,0:T(8,128)(2,1)}, bf16[160,7168]{1,0:T(8,128)(2,1)S(1)}, u32[]{:S(2)}) copy-start(bf16[160,7168]{1,0:T(8,128)(2,1)S(1)} %convolution_convert_fusion.2) | copy-start | bytes 6881284
  267.4 21.0 %collective-permute-start.23 = (bf16[80,2048]{1,0:T(8,128)(2,1)S(1)}, bf16[80,2048]{1,0:T(8,128)(2,1)S(1)}, u32[]{:S(2)}, u32[]{:S(2)}) collective-permute-start(bf16[80,2048]{1,0:T(8,128)(2,1)S(1)} %get-tuple-element.62), channel_id=1, source_target_pairs={{0,1},{1,0},{2,3},{3,2},{4,5},{5,4},{6,7},{7,6},{8,9},{9,8},{10,11... | collective-permute-start | bytes 983048 | tf_op jit(solution)/shard_map/ppermute | solution.py:66
  288.4 16.4 %collective-permute-start.31 = (bf16[80,3072]{1,0:T(8,128)(2,1)S(1)}, bf16[80,3072]{1,0:T(8,128)(2,1)S(1)}, u32[]{:S(2)}, u32[]{:S(2)}) collective-permute-start(bf16[80,3072]{1,0:T(8,128)(2,1)S(1)} %slice.254), channel_id=1, source_target_pairs={{0,1},{1,0},{2,3},{3,2},{4,5},{5,4},{6,7},{7,6},{8,9},{9,8},{10,11... | collective-permute-start | bytes 1474568 | tf_op jit(solution)/shard_map/ppermute | solution.py:66
  290.9 10.2 %collective-permute-start.21 = (bf16[80,2048]{1,0:T(8,128)(2,1)S(1)}, bf16[80,2048]{1,0:T(8,128)(2,1)S(1)}, u32[]{:S(2)}, u32[]{:S(2)}) collective-permute-start(bf16[80,2048]{1,0:T(8,128)(2,1)S(1)} %get-tuple-element.61), channel_id=1, source_target_pairs={{0,3},{3,0},{1,2},{2,1},{4,7},{7,4},{5,6},{6,5},{8,11},{11,8},{9,1... | collective-permute-start | bytes 983048 | tf_op jit(solution)/shard_map/ppermute | solution.py:66
  292.6 19.1 %collective-permute-start.30 = (bf16[80,3072]{1,0:T(8,128)(2,1)S(1)}, bf16[80,3072]{1,0:T(8,128)(2,1)S(1)}, u32[]{:S(2)}, u32[]{:S(2)}) collective-permute-start(bf16[80,3072]{1,0:T(8,128)(2,1)S(1)} %add_convert_fusion.1), channel_id=1, source_target_pairs={{0,3},{3,0},{1,2},{2,1},{4,7},{7,4},{5,6},{6,5},{8,11},{11,8},{9,1... | collective-permute-start | bytes 1474568 | tf_op jit(solution)/shard_map/ppermute | solution.py:66
  301.1 10.9 %collective-permute-start.28 = (bf16[80,3072]{1,0:T(8,128)(2,1)S(1)}, bf16[80,3072]{1,0:T(8,128)(2,1)S(1)}, u32[]{:S(2)}, u32[]{:S(2)}) collective-permute-start(bf16[80,3072]{1,0:T(8,128)(2,1)S(1)} %add_convert_fusion.3), channel_id=1, source_target_pairs={{0,1},{1,0},{2,3},{3,2},{4,5},{5,4},{6,7},{7,6},{8,9},{9,8},{10,11... | collective-permute-start | bytes 1474568 | tf_op jit(solution)/shard_map/ppermute | solution.py:66
  301.9 25.0 %collective-permute-start.32 = (bf16[72,2048]{1,0:T(8,128)(2,1)}, bf16[72,2048]{1,0:T(8,128)(2,1)}, u32[]{:S(2)}, u32[]{:S(2)}) collective-permute-start(bf16[72,2048]{1,0:T(8,128)(2,1)} %slice.256), channel_id=1, source_target_pairs={{0,3},{3,0},{1,2},{2,1},{4,7},{7,4},{5,6},{6,5},{8,11},{11,8},{9,1... | collective-permute-start | bytes 884744 | tf_op jit(solution)/shard_map/ppermute | solution.py:66
  303.9 49.5 %collective-permute-start.37 = (bf16[88,2048]{1,0:T(8,128)(2,1)}, bf16[88,2048]{1,0:T(8,128)(2,1)}, u32[]{:S(2)}, u32[]{:S(2)}) collective-permute-start(bf16[88,2048]{1,0:T(8,128)(2,1)} %slice.260), channel_id=1, source_target_pairs={{0,1},{1,0},{2,3},{3,2},{4,5},{5,4},{6,7},{7,6},{8,9},{9,8},{10,11... | collective-permute-start | bytes 1081352 | tf_op jit(solution)/shard_map/ppermute | solution.py:66
  304.7 30.6 %collective-permute-start.20 = (bf16[80,2048]{1,0:T(8,128)(2,1)}, bf16[80,2048]{1,0:T(8,128)(2,1)}, u32[]{:S(2)}, u32[]{:S(2)}) collective-permute-start(bf16[80,2048]{1,0:T(8,128)(2,1)} %slice.244), channel_id=1, source_target_pairs={{0,3},{3,0},{1,2},{2,1},{4,7},{7,4},{5,6},{6,5},{8,11},{11,8},{9,1... | collective-permute-start | bytes 983048 | tf_op jit(solution)/shard_map/ppermute | solution.py:66
  311.6 23.9 %collective-permute-start.25 = (bf16[80,2048]{1,0:T(8,128)(2,1)}, bf16[80,2048]{1,0:T(8,128)(2,1)}, u32[]{:S(2)}, u32[]{:S(2)}) collective-permute-start(bf16[80,2048]{1,0:T(8,128)(2,1)} %slice.248), channel_id=1, source_target_pairs={{0,1},{1,0},{2,3},{3,2},{4,5},{5,4},{6,7},{7,6},{8,9},{9,8},{10,11... | collective-permute-start | bytes 983048 | tf_op jit(solution)/shard_map/ppermute | solution.py:66
  312.0 21.2 %collective-permute-start.34 = (bf16[72,2048]{1,0:T(8,128)(2,1)}, bf16[72,2048]{1,0:T(8,128)(2,1)}, u32[]{:S(2)}, u32[]{:S(2)}) collective-permute-start(bf16[72,2048]{1,0:T(8,128)(2,1)} %add_convert_fusion.11), channel_id=1, source_target_pairs={{0,1},{1,0},{2,3},{3,2},{4,5},{5,4},{6,7},{7,6},{8,9},{9,8},{10,11... | collective-permute-start | bytes 884744 | tf_op jit(solution)/shard_map/ppermute | solution.py:66
  314.8 28.4 %all-to-all-start.1 = ((bf16[32,5,24,128]{3,2,1,0:T(8,128)(2,1)}), bf16[32,5,24,128]{3,2,1,0:T(8,128)(2,1)S(1)}, u32[]{:S(2)}, u32[]{:S(2)}) async-start(bf16[32,5,24,128]{3,2,1,0:T(8,128)(2,1)} %bitcast.32), calls=%async_computation.1 | async-start | bytes 1966080 | tf_op jit(solution)/shard_map/all_to_all | solution.py:152
  326.9 10.5 %collective-permute-start.24 = (bf16[80,2048]{1,0:T(8,128)(2,1)}, bf16[80,2048]{1,0:T(8,128)(2,1)S(1)}, u32[]{:S(2)}, u32[]{:S(2)}) collective-permute-start(bf16[80,2048]{1,0:T(8,128)(2,1)} %add_convert_fusion.7), channel_id=1, source_target_pairs={{0,3},{3,0},{1,2},{2,1},{4,7},{7,4},{5,6},{6,5},{8,11},{11,8},{9,1... | collective-permute-start | bytes 983048 | tf_op jit(solution)/shard_map/ppermute | solution.py:66
  333.2 6.7 %collective-permute-start.22 = (bf16[80,2048]{1,0:T(8,128)(2,1)}, bf16[80,2048]{1,0:T(8,128)(2,1)S(1)}, u32[]{:S(2)}, u32[]{:S(2)}) collective-permute-start(bf16[80,2048]{1,0:T(8,128)(2,1)} %add_convert_fusion.9), channel_id=1, source_target_pairs={{0,1},{1,0},{2,3},{3,2},{4,5},{5,4},{6,7},{7,6},{8,9},{9,8},{10,11... | collective-permute-start | bytes 983048 | tf_op jit(solution)/shard_map/ppermute | solution.py:66
  335.3 18.0 %collective-permute-start.36 = (bf16[88,2048]{1,0:T(8,128)(2,1)}, bf16[88,2048]{1,0:T(8,128)(2,1)}, u32[]{:S(2)}, u32[]{:S(2)}) collective-permute-start(bf16[88,2048]{1,0:T(8,128)(2,1)} %add_convert_fusion.5), channel_id=1, source_target_pairs={{0,3},{3,0},{1,2},{2,1},{4,7},{7,4},{5,6},{6,5},{8,11},{11,8},{9,1... | collective-permute-start | bytes 1081352 | tf_op jit(solution)/shard_map/ppermute | solution.py:66
  344.4 21.1 %all-to-all-start.2 = ((bf16[32,5,16,128]{3,2,1,0:T(8,128)(2,1)}), bf16[32,5,16,128]{3,2,1,0:T(8,128)(2,1)S(1)}, u32[]{:S(2)}, u32[]{:S(2)}) async-start(bf16[32,5,16,128]{3,2,1,0:T(8,128)(2,1)} %bitcast.38), calls=%async_computation.2 | async-start | bytes 1310720 | tf_op jit(solution)/shard_map/all_to_all | solution.py:152
  354.7 18.0 %copy-start.12 = (f32[128,1]{0,1:T(1,128)S(1)}, f32[128,1]{0,1:T(1,128)}, u32[]{:S(2)}) copy-start(f32[128,1]{0,1:T(1,128)} %param.9) | copy-start | bytes 1540
  367.4 17.5 %all-to-all-start.3 = ((bf16[32,5,16,128]{3,2,1,0:T(8,128)(2,1)}), bf16[32,5,16,128]{3,2,1,0:T(8,128)(2,1)S(1)}, u32[]{:S(2)}, u32[]{:S(2)}) async-start(bf16[32,5,16,128]{3,2,1,0:T(8,128)(2,1)} %bitcast.44), calls=%async_computation.3 | async-start | bytes 1310720 | tf_op jit(solution)/shard_map/all_to_all | solution.py:152
  372.7 13.4 %copy-start.1 = (bf16[128,7168]{1,0:T(8,128)(2,1)S(1)}, bf16[128,7168]{1,0:T(8,128)(2,1)}, u32[]{:S(2)}) copy-start(bf16[128,7168]{1,0:T(8,128)(2,1)} %param.7) | copy-start | bytes 5505028
  (7 other events, 26.1 us)
